TPU v7x, 32 devices: a whole 2x2x4 slice. The times are simulated.
32 devices in a mesh: dp: 4 (over z), ctx: 2 (over x), tp: 4 (over y, core).
Axes of the slice: x: 2, y: 2, z: 4, core: 2. Of those that a mesh axis runs over, the one named last changes fastest.
Arguments:
- tokens: bfloat16 [2, 4, 2048, 768], P(None, 'dp', ('ctx', 'tp')), may hold values from -6 to 6
- cotangent: bfloat16 [2, 4, 2048, 768], P(None, 'dp', ('ctx', 'tp')), may hold values from -6 to 6
- ln1_gain: bfloat16 [768], P(('dp', 'ctx')), may hold values from 0.5 to 1.5
- ln1_bias: bfloat16 [768], P(('dp', 'ctx')), may hold values from -1.25 to 1.25
- qkv_weight: bfloat16 [3, 768, 768], P(None, ('dp', 'ctx'), 'tp'), may hold values from -0.3125 to 0.3125
- qkv_bias: bfloat16 [3, 12, 64], P(None, 'tp', ('dp', 'ctx')), may hold values from -1.25 to 1.25
- out_weight: bfloat16 [768, 768], P('tp', ('dp', 'ctx')), may hold values from -1.5 to 1.5
- out_bias: bfloat16 [768], P(('dp', 'ctx')), may hold values from -1.25 to 1.25
- ln2_gain: bfloat16 [768], P(('dp', 'ctx')), may hold values from 0.5 to 1.5
- ln2_bias: bfloat16 [768], P(('dp', 'ctx')), may hold values from -1.25 to 1.25
- fc_weight: bfloat16 [768, 3072], P(('dp', 'ctx'), 'tp'), may hold values from -0.21875 to 0.21875
- fc_bias: bfloat16 [24, 128], P('tp', ('dp', 'ctx')), may hold values from -1.25 to 1.25
- proj_weight: bfloat16 [3072, 768], P('tp', ('dp', 'ctx')), may hold values from -0.21875 to 0.21875
- proj_bias: bfloat16 [768], P(('dp', 'ctx')), may hold values from -1.25 to 1.25
Outputs:
- activations: bfloat16 [2, 4, 2048, 768], P(None, 'dp', ('ctx', 'tp'))
- grad_tokens: float32 [2, 4, 2048, 768], P(None, 'dp', ('ctx', 'tp'))
- grad_ln1_gain: float32 [768], P(('dp', 'ctx'))
- grad_ln1_bias: float32 [768], P(('dp', 'ctx'))
- grad_qkv_weight: float32 [3, 768, 768], P(None, ('dp', 'ctx'), 'tp')
- grad_qkv_bias: float32 [3, 12, 64], P(None, 'tp', ('dp', 'ctx'))
- grad_out_weight: float32 [768, 768], P('tp', ('dp', 'ctx'))
- grad_out_bias: float32 [768], P(('dp', 'ctx'))
- grad_ln2_gain: float32 [768], P(('dp', 'ctx'))
- grad_ln2_bias: float32 [768], P(('dp', 'ctx'))
- grad_fc_weight: float32 [768, 3072], P(('dp', 'ctx'), 'tp')
- grad_fc_bias: float32 [24, 128], P('tp', ('dp', 'ctx'))
- grad_proj_weight: float32 [3072, 768], P('tp', ('dp', 'ctx'))
- grad_proj_bias: float32 [768], P(('dp', 'ctx'))
All inputs are finite; a program needn't handle non-finite values.
Results may differ from a plain program's by a relative error of at most 0.013.
The roundings to bfloat16 on the way count: a program that leaves them out, or rounds other values in their place, can miss the bound.
Values may be sent and summed in bfloat16 or wider, within the bound.
No kernel may reach another device: no remote copies, remote signals or barrier semaphores. Data moves between devices by JAX's collectives and lax.ppermute only.
A program may use at most 128 MiB of HBM per device.

v0:
```python
import jax
import jax.numpy as jnp
from jax import lax
from jax.sharding import PartitionSpec as P

HD = 64


epsilon = 1e-05


def layer_norm(rows, gain, shift):
    mean = jnp.mean(rows, axis=-1, keepdims=True)
    centered = rows - mean
    spread = jnp.mean(centered * centered, axis=-1, keepdims=True)
    return centered * lax.rsqrt(spread + epsilon) * gain + shift


def gelu_tanh(values):
    return jax.nn.gelu(values, approximate=True)


def fetch(shards):
    return (
        lax.all_gather(shards[0], ("dp", "ctx"), axis=1, tiled=True),
        lax.all_gather(shards[1], ("dp", "ctx"), axis=2, tiled=True),
        lax.all_gather(shards[2], ("dp", "ctx"), axis=1, tiled=True),
        lax.all_gather(shards[3], ("dp", "ctx"), axis=0, tiled=True),
        lax.all_gather(shards[4], ("dp", "ctx"), axis=1, tiled=True),
        lax.all_gather(shards[5], ("dp", "ctx"), axis=1, tiled=True),
        lax.all_gather(shards[6], ("dp", "ctx"), axis=1, tiled=True),
    )


def settle(gradients):
    vector_total = lax.psum(gradients[6], "tp")
    return (
        lax.psum_scatter(gradients[0], ("dp", "ctx"), scatter_dimension=1, tiled=True),
        lax.psum_scatter(gradients[1], ("dp", "ctx"), scatter_dimension=2, tiled=True),
        lax.psum_scatter(gradients[2], ("dp", "ctx"), scatter_dimension=1, tiled=True),
        lax.psum_scatter(gradients[3], ("dp", "ctx"), scatter_dimension=0, tiled=True),
        lax.psum_scatter(gradients[4], ("dp", "ctx"), scatter_dimension=1, tiled=True),
        lax.psum_scatter(gradients[5], ("dp", "ctx"), scatter_dimension=1, tiled=True),
        lax.psum_scatter(vector_total, ("dp", "ctx"), scatter_dimension=1, tiled=True),
    )


def rows_gather(rows):
    return lax.all_gather(rows, "tp", axis=0, tiled=True)


def rows_sum(terms):
    return lax.psum_scatter(terms, "tp", scatter_dimension=0, tiled=True)


def widened(part, along, factor):
    layout = list(part.shape)
    layout[along] = layout[along] * factor
    return jnp.zeros(tuple(layout), jnp.float32)


def head_blocks(matrix, heads, block):
    length = matrix.shape[0]
    width = matrix.shape[1] // heads
    split = matrix.reshape(length // block, block, heads, width)
    return split.transpose(2, 0, 1, 3).reshape(heads * (length // block), block, width)


def join_blocks(blocks, heads):
    count = blocks.shape[0] // heads
    split = blocks.reshape(heads, count, blocks.shape[1], blocks.shape[2])
    return split.transpose(1, 2, 0, 3).reshape(count * blocks.shape[1], heads * blocks.shape[2])


def by_heads(matrix, heads):
    return matrix.reshape(matrix.shape[0], heads, matrix.shape[1] // heads).transpose(1, 0, 2)


def from_heads(stacked):
    return stacked.transpose(1, 0, 2).reshape(stacked.shape[1], stacked.shape[0] * stacked.shape[2])


def block_scores(query, key_head, index, count, first_row, scale):
    block = query.shape[0]
    scores = jnp.einsum("qd,kd->qk", query, key_head, preferred_element_type=jnp.float32) * scale
    row_pos = first_row + index % count * block + lax.broadcasted_iota(jnp.int32, (block, 1), 0)
    key_pos = lax.broadcasted_iota(jnp.int32, (1, key_head.shape[0]), 1)
    allowed = key_pos <= row_pos
    return (jnp.where(allowed, scores, 0.0), allowed)


def attend(query_blocks, key_heads, value_heads, count, first_row, scale):

    def one(index):
        head = index // count
        masked, allowed = block_scores(
            query_blocks[index], key_heads[head], index, count, first_row, scale
        )
        peak = jnp.max(jnp.abs(masked), axis=1, keepdims=True)
        upper = jnp.where(allowed, jnp.exp(masked - peak), 0.0)
        lower = jnp.where(allowed, jnp.exp(-masked - peak), 0.0)
        total = 0.5 * jnp.sum(upper + lower, axis=1, keepdims=True)
        weights = (0.5 * (upper - lower) / total).astype(jnp.bfloat16)
        mixed = jnp.dot(weights, value_heads[head], preferred_element_type=jnp.float32)
        return (mixed.astype(jnp.bfloat16), peak + jnp.log(total))

    return lax.map(one, jnp.arange(query_blocks.shape[0], dtype=jnp.int32))


def attend_back(query_blocks, key_heads, value_heads, grad_blocks, logsum, count, first_row, scale):

    def one(index):
        head = index // count
        query = query_blocks[index]
        key_head = key_heads[head]
        masked, allowed = block_scores(query, key_head, index, count, first_row, scale)
        level = logsum[index]
        upper = jnp.where(allowed, jnp.exp(masked - level), 0.0)
        lower = jnp.where(allowed, jnp.exp(-masked - level), 0.0)
        weights = 0.5 * (upper - lower)
        cosh_part = 0.5 * (upper + lower)
        grad_mix = grad_blocks[index]
        grad_weights = jnp.einsum(
            "qd,kd->qk", grad_mix, value_heads[head], preferred_element_type=jnp.float32
        )
        grad_value = jnp.einsum(
            "qk,qd->kd", weights.astype(jnp.bfloat16), grad_mix, preferred_element_type=jnp.float32
        )
        inner = jnp.sum(grad_weights * weights, axis=1, keepdims=True)
        grad_scores = (cosh_part * grad_weights - weights * inner).astype(jnp.bfloat16)
        grad_query = jnp.dot(grad_scores, key_head, preferred_element_type=jnp.float32) * scale
        grad_key = (
            jnp.einsum("qk,qd->kd", grad_scores, query, preferred_element_type=jnp.float32) * scale
        )
        return (grad_query, grad_key, grad_value)

    return lax.map(one, jnp.arange(query_blocks.shape[0], dtype=jnp.int32))


def micro_step(full, refetch, tokens_rows, cot_rows, first_row, scale):
    w_qkv, b_qkv, w_out, w_fc, b_fc, w_proj, vectors = full
    heads = b_qkv.shape[1]
    local_width = heads * b_qkv.shape[2]
    vector_rows = vectors.astype(jnp.float32)
    rows = tokens_rows.astype(jnp.float32)
    norm_one, back_one = jax.vjp(layer_norm, rows, vector_rows[0], vector_rows[1])
    normed = rows_gather(norm_one.astype(jnp.bfloat16))
    block = min(512, normed.shape[0])
    count = normed.shape[0] // block
    projected = jnp.einsum("rd,idc->irc", normed, w_qkv, preferred_element_type=jnp.float32)
    triple = (projected + b_qkv.reshape(3, 1, local_width).astype(jnp.float32)).astype(jnp.bfloat16)
    keys, values = (
        lax.all_gather(triple[1], "ctx", axis=0, tiled=True),
        lax.all_gather(triple[2], "ctx", axis=0, tiled=True),
    )
    query_blocks = head_blocks(triple[0], heads, block)
    key_heads = by_heads(keys, heads)
    value_heads = by_heads(values, heads)
    mixed_blocks, logsum = attend(query_blocks, key_heads, value_heads, count, first_row, scale)
    mixed = join_blocks(mixed_blocks, heads)
    attn_part = rows_sum(jnp.dot(mixed, w_out, preferred_element_type=jnp.float32))
    hidden = rows + attn_part + vector_rows[4]
    norm_two, back_two = jax.vjp(layer_norm, hidden, vector_rows[2], vector_rows[3])
    normed_two = rows_gather(norm_two.astype(jnp.bfloat16))
    lifted = jnp.dot(normed_two, w_fc, preferred_element_type=jnp.float32) + b_fc.reshape(
        -1
    ).astype(jnp.float32)
    activated_wide, back_act = jax.vjp(gelu_tanh, lifted)
    activated = activated_wide.astype(jnp.bfloat16)
    mlp_part = rows_sum(jnp.dot(activated, w_proj, preferred_element_type=jnp.float32))
    output = hidden + mlp_part + vector_rows[5]
    full_back = refetch(output)
    back_qkv = full_back[0]
    back_out = full_back[2]
    back_fc = full_back[3]
    back_proj = full_back[5]
    cot_local = cot_rows.astype(jnp.float32)
    cot_all = rows_gather(cot_rows)
    grad_proj = jnp.einsum("rf,rd->fd", activated, cot_all, preferred_element_type=jnp.float32)
    grad_proj_bias = jnp.sum(cot_local, axis=0)
    grad_activated = jnp.einsum("rd,fd->rf", cot_all, back_proj, preferred_element_type=jnp.float32)
    grad_lifted = back_act(grad_activated)[0].astype(jnp.bfloat16)
    grad_fc_bias = jnp.sum(grad_lifted, axis=0, dtype=jnp.float32).reshape(b_fc.shape)
    grad_fc = jnp.einsum("rd,rf->df", normed_two, grad_lifted, preferred_element_type=jnp.float32)
    grad_norm_two = rows_sum(
        jnp.einsum("rf,df->rd", grad_lifted, back_fc, preferred_element_type=jnp.float32)
    )
    grad_hidden_norm, grad_gain_two, grad_shift_two = back_two(grad_norm_two)
    grad_hidden = cot_local + grad_hidden_norm
    grad_branch = grad_hidden.astype(jnp.bfloat16)
    grad_out_bias = jnp.sum(grad_branch, axis=0, dtype=jnp.float32)
    grad_branch_all = rows_gather(grad_branch)
    grad_out = jnp.einsum("rc,rd->cd", mixed, grad_branch_all, preferred_element_type=jnp.float32)
    grad_mixed = jnp.einsum(
        "rd,cd->rc", grad_branch_all, back_out, preferred_element_type=jnp.float32
    ).astype(jnp.bfloat16)
    grad_query, grad_key, grad_value = attend_back(
        query_blocks,
        key_heads,
        value_heads,
        head_blocks(grad_mixed, heads, block),
        logsum,
        count,
        first_row,
        scale,
    )
    span = keys.shape[0]
    grad_key = from_heads(grad_key.reshape(heads, count, span, -1).sum(axis=1))
    grad_value = from_heads(grad_value.reshape(heads, count, span, -1).sum(axis=1))
    grad_keys, grad_values = (
        lax.psum_scatter(
            grad_key.astype(jnp.bfloat16), "ctx", scatter_dimension=0, tiled=True
        ).astype(jnp.float32),
        lax.psum_scatter(
            grad_value.astype(jnp.bfloat16), "ctx", scatter_dimension=0, tiled=True
        ).astype(jnp.float32),
    )
    grad_triple = jnp.stack([join_blocks(grad_query, heads), grad_keys, grad_values]).astype(
        jnp.bfloat16
    )
    grad_qkv_bias = jnp.sum(grad_triple, axis=1, dtype=jnp.float32).reshape(b_qkv.shape)
    grad_qkv_weight = jnp.einsum(
        "rd,irc->idc", normed, grad_triple, preferred_element_type=jnp.float32
    )
    grad_norm_one = rows_sum(
        jnp.einsum("irc,idc->rd", grad_triple, back_qkv, preferred_element_type=jnp.float32)
    )
    grad_rows_norm, grad_gain_one, grad_shift_one = back_one(grad_norm_one)
    grad_tokens = grad_hidden + grad_rows_norm
    grad_vectors = jnp.stack(
        [
            grad_gain_one,
            grad_shift_one,
            grad_gain_two,
            grad_shift_two,
            grad_out_bias,
            grad_proj_bias,
        ]
    )
    gradients = (
        grad_qkv_weight,
        grad_qkv_bias,
        grad_out,
        grad_fc,
        grad_fc_bias,
        grad_proj,
        grad_vectors,
    )
    return (output.astype(jnp.bfloat16), grad_tokens, gradients)


def local(
    tokens,
    cotangent,
    ln1_gain,
    ln1_bias,
    qkv_weight,
    qkv_bias,
    out_weight,
    out_bias,
    ln2_gain,
    ln2_bias,
    fc_weight,
    fc_bias,
    proj_weight,
    proj_bias,
):
    vectors = jnp.stack([ln1_gain, ln1_bias, ln2_gain, ln2_bias, out_bias, proj_bias])
    shards = (qkv_weight, qkv_bias, out_weight, fc_weight, fc_bias, proj_weight, vectors)
    first_row = lax.axis_index("ctx") * (tokens.shape[2] * lax.axis_size("tp"))
    scale = HD ** (-0.5)
    share = lax.axis_size(("dp", "ctx"))
    gather_dims = (1, 2, 1, 0, 1, 1, 1)
    zeros = tuple((widened(part, along, share) for part, along in zip(shards, gather_dims)))

    def step(totals, pair):
        tokens_rows, cot_rows = pair
        full = fetch(shards)

        def refetch(dependency):
            later, ignored = lax.optimization_barrier((shards, dependency))
            return fetch(later)

        output, grad_tokens, gradients = micro_step(
            full, refetch, tokens_rows, cot_rows, first_row, scale
        )
        totals = tuple((total + gradient for total, gradient in zip(totals, gradients)))
        return (totals, (output, grad_tokens))

    totals, (outputs, grad_rows) = lax.scan(step, zeros, (tokens[:, 0], cotangent[:, 0]))
    totals = settle(totals)
    grad_joint, grad_joint_bias, grad_out, grad_fc, grad_fc_bias, grad_proj, grad_vectors = totals
    return (
        outputs[:, None],
        grad_rows[:, None],
        grad_vectors[0],
        grad_vectors[1],
        grad_joint,
        grad_joint_bias,
        grad_out,
        grad_vectors[4],
        grad_vectors[2],
        grad_vectors[3],
        grad_fc,
        grad_fc_bias,
        grad_proj,
        grad_vectors[5],
    )


def solution(mesh):
    return jax.shard_map(
        local,
        mesh=mesh,
        in_specs=(
            P(None, "dp", ("ctx", "tp"), None),
            P(None, "dp", ("ctx", "tp"), None),
            P(("dp", "ctx")),
            P(("dp", "ctx")),
            P(None, ("dp", "ctx"), "tp"),
            P(None, "tp", ("dp", "ctx")),
            P("tp", ("dp", "ctx")),
            P(("dp", "ctx")),
            P(("dp", "ctx")),
            P(("dp", "ctx")),
            P(("dp", "ctx"), "tp"),
            P("tp", ("dp", "ctx")),
            P("tp", ("dp", "ctx")),
            P(("dp", "ctx")),
        ),
        out_specs=(
            P(None, "dp", ("ctx", "tp"), None),
            P(None, "dp", ("ctx", "tp"), None),
            P(("dp", "ctx")),
            P(("dp", "ctx")),
            P(None, ("dp", "ctx"), "tp"),
            P(None, "tp", ("dp", "ctx")),
            P("tp", ("dp", "ctx")),
            P(("dp", "ctx")),
            P(("dp", "ctx")),
            P(("dp", "ctx")),
            P(("dp", "ctx"), "tp"),
            P("tp", ("dp", "ctx")),
            P("tp", ("dp", "ctx")),
            P(("dp", "ctx")),
        ),
        check_vma=False,
    )
```

profile of v0, /device:TPU:0, one launch (start us, length us, event | category | flops | bytes accessed | tf_op | source)
XLA Modules:
  0.0 2026.1 jit_solution(1083775102349154934)
XLA Ops:
  12.3 1590.8 %while.91 = (s32[]{:T(128)}, f32[3,768,192]{1,2,0:T(8,128)}, f32[3,3,64]{2,1,0:T(4,128)}, f32[192,768]{1,0:T(8,128)}, f32[768,768]{1,0:T(8,128)}, /*index=5*/f32...) while((s32[]{:T(128)}, f32[3,768,192]{1,2,0:T(8,128)}, ...), condition=%wide.region_32.33_spmd.clone, body=%wide.region_0.32_spmd.clone.sunk | while | flops 11935105024 | bytes 334181536 | solution.py:290
  77.7 35.8 %all_gather.144 = bf16[3,768,192]{2,0,1:T(4,128)(2,1)S(1)} all-gather(bf16[3,96,192]{2,0,1:T(4,128)(2,1)S(1)} %copy.120), channel_id=1, replica_groups=mesh['dp'=4,'ctx'=2,'tp'=4] {'dp','ctx'}, dimensions={1}, use_global_device_ids=true | all-gather | bytes 995328 | tf_op jit(solution)/shard_map/while/body/eval_jaxpr/all_gather | solution.py:25
  114.4 33.4 %all_gather.146 = bf16[192,768]{0,1:T(8,128)(2,1)} all-gather(bf16[192,96]{0,1:T(8,128)(2,1)} %get-tuple-element.1244), channel_id=1, replica_groups=mesh['dp'=4,'ctx'=2,'tp'=4] {'dp','ctx'}, dimensions={1}, use_global_device_ids=true | all-gather | bytes 331776 | tf_op jit(solution)/shard_map/while/body/eval_jaxpr/all_gather | solution.py:27
  170.8 73.5 %while.92 = (s32[]{:T(128)}, bf16[6,512,64]{1,2,0:T(8,128)(2,1)}, f32[6,512,1]{1,2,0:T(1,128)}, s32[6]{0:T(128)S(1)}, s32[]{:T(128)}, /*index=5*/bf16[6,512,64]{...) while((s32[]{:T(128)}, bf16[6,512,64]{1,2,0:T(8,128)(2,1)}, ...), condition=%wide.region_6.6_spmd, body=%wide.region_3.5_spmd.sunk | while | flops 292586016 | bytes 13859271 | solution.py:107
  249.8 35.9 %reduce-scatter.32.cloned.1.call-done = f32[256,768]{1,0:T(8,128)} async-done(((f32[1024,768]{1,0:T(8,128)}), f32[256,768]{1,0:T(8,128)}) %reduce-scatter.32.cloned.1.call-update) | async-done | bytes 786448 | tf_op jit(solution)/shard_map/while/body/eval_jaxpr/reduce_scatter | solution.py:53
  320.6 33.9 %all-gather.35.cloned.1.call-done = bf16[768,768]{0,1:T(8,128)(2,1)} async-done(((bf16[768,96]{0,1:T(8,128)(2,1)}), bf16[768,768]{0,1:T(8,128)(2,1)}) %all-gather.35.cloned.1.call-update) | async-done | bytes 1179664 | tf_op jit(solution)/shard_map/while/body/eval_jaxpr/all_gather | solution.py:30
  362.5 35.1 %reduce-scatter.34.cloned.1.call-done = f32[256,768]{1,0:T(8,128)} async-done(((f32[1024,768]{1,0:T(8,128)}), f32[256,768]{1,0:T(8,128)}) %reduce-scatter.34.cloned.1.call-update) | async-done | bytes 786448 | tf_op jit(solution)/shard_map/while/body/eval_jaxpr/reduce_scatter | solution.py:53
  400.3 40.6 %all-gather.37.cloned.1.call-done = bf16[768,768]{0,1:T(8,128)(2,1)} async-done(((bf16[768,96]{0,1:T(8,128)(2,1)}), bf16[768,768]{0,1:T(8,128)(2,1)}) %all-gather.37.cloned.1.call-update) | async-done | bytes 1179664 | tf_op jit(solution)/shard_map/while/body/eval_jaxpr/all_gather | solution.py:30
  448.3 34.4 %all-gather.41.cloned.1.call-done = bf16[768,768]{1,0:T(8,128)(2,1)} async-done(((bf16[96,768]{1,0:T(8,128)(2,1)}), bf16[768,768]{1,0:T(8,128)(2,1)}) %all-gather.41.cloned.1.call-update) | async-done | bytes 1179664 | tf_op jit(solution)/shard_map/while/body/eval_jaxpr/all_gather | solution.py:28
  487.7 36.5 %reduce-scatter.36.cloned.1.call-done = f32[256,768]{1,0:T(8,128)} async-done(((f32[1024,768]{1,0:T(8,128)}), f32[256,768]{1,0:T(8,128)}) %reduce-scatter.36.cloned.1.call-update) | async-done | bytes 786448 | tf_op jit(solution)/shard_map/while/body/eval_jaxpr/reduce_scatter | solution.py:53
  530.3 31.7 %all_gather.153 = bf16[192,768]{0,1:T(8,128)(2,1)S(1)} all-gather(bf16[192,96]{0,1:T(8,128)(2,1)} %get-tuple-element.1244), channel_id=1, replica_groups=mesh['dp'=4,'ctx'=2,'tp'=4] {'dp','ctx'}, dimensions={1}, use_global_device_ids=true | all-gather | bytes 331776 | tf_op jit(solution)/shard_map/while/body/eval_jaxpr/all_gather | solution.py:27
  565.7 138.0 %while.93 = (s32[]{:T(128)}, bf16[6,512,64]{1,2,0:T(8,128)(2,1)}, f32[6,2048,64]{1,2,0:T(8,128)}, f32[6,2048,64]{1,2,0:T(8,128)}, s32[6]{0:T(128)S(1)}, /*index=...) while((s32[]{:T(128)}, bf16[6,512,64]{1,2,0:T(8,128)(2,1)}, ...), condition=%wide.region_16.16_spmd, body=%wide.region_14.15_spmd.sunk | while | flops 711098880 | bytes 34761208 | solution.py:137
  710.4 38.0 %all_gather.154 = bf16[3,768,192]{2,1,0:T(8,128)(2,1)S(1)} all-gather(bf16[3,96,192]{2,1,0:T(8,128)(2,1)S(1)} %copy-done.11), channel_id=1, replica_groups=mesh['dp'=4,'ctx'=2,'tp'=4] {'dp','ctx'}, dimensions={1}, use_global_device_ids=true | all-gather | bytes 995328 | tf_op jit(solution)/shard_map/while/body/eval_jaxpr/all_gather | solution.py:25
  839.7 30.8 %all_gather.145 = bf16[3,3,64]{1,0,2:T(4,128)(2,1)S(1)} all-gather(bf16[3,3,8]{1,0,2:T(4,128)(2,1)} %get-tuple-element.1470), channel_id=1, replica_groups=mesh['dp'=4,'ctx'=2,'tp'=4] {'dp','ctx'}, dimensions={2}, use_global_device_ids=true | all-gather | bytes 1296 | tf_op jit(solution)/shard_map/while/body/eval_jaxpr/all_gather | solution.py:26
  871.7 35.1 %all_gather.144 = bf16[3,768,192]{2,0,1:T(4,128)(2,1)S(1)} all-gather(bf16[3,96,192]{2,0,1:T(4,128)(2,1)S(1)} %copy.120), channel_id=1, replica_groups=mesh['dp'=4,'ctx'=2,'tp'=4] {'dp','ctx'}, dimensions={1}, use_global_device_ids=true | all-gather | bytes 995328 | tf_op jit(solution)/shard_map/while/body/eval_jaxpr/all_gather | solution.py:25
  907.7 33.4 %all_gather.146 = bf16[192,768]{0,1:T(8,128)(2,1)} all-gather(bf16[192,96]{0,1:T(8,128)(2,1)} %get-tuple-element.1244), channel_id=1, replica_groups=mesh['dp'=4,'ctx'=2,'tp'=4] {'dp','ctx'}, dimensions={1}, use_global_device_ids=true | all-gather | bytes 331776 | tf_op jit(solution)/shard_map/while/body/eval_jaxpr/all_gather | solution.py:27
  964.1 73.5 %while.92 = (s32[]{:T(128)}, bf16[6,512,64]{1,2,0:T(8,128)(2,1)}, f32[6,512,1]{1,2,0:T(1,128)}, s32[6]{0:T(128)S(1)}, s32[]{:T(128)}, /*index=5*/bf16[6,512,64]{...) while((s32[]{:T(128)}, bf16[6,512,64]{1,2,0:T(8,128)(2,1)}, ...), condition=%wide.region_6.6_spmd, body=%wide.region_3.5_spmd.sunk | while | flops 292586016 | bytes 13859271 | solution.py:107
  1043.1 35.8 %reduce-scatter.32.cloned.1.call-done = f32[256,768]{1,0:T(8,128)} async-done(((f32[1024,768]{1,0:T(8,128)}), f32[256,768]{1,0:T(8,128)}) %reduce-scatter.32.cloned.1.call-update) | async-done | bytes 786448 | tf_op jit(solution)/shard_map/while/body/eval_jaxpr/reduce_scatter | solution.py:53
  1113.4 34.3 %all-gather.35.cloned.1.call-done = bf16[768,768]{0,1:T(8,128)(2,1)} async-done(((bf16[768,96]{0,1:T(8,128)(2,1)}), bf16[768,768]{0,1:T(8,128)(2,1)}) %all-gather.35.cloned.1.call-update) | async-done | bytes 1179664 | tf_op jit(solution)/shard_map/while/body/eval_jaxpr/all_gather | solution.py:30
  1155.6 35.1 %reduce-scatter.34.cloned.1.call-done = f32[256,768]{1,0:T(8,128)} async-done(((f32[1024,768]{1,0:T(8,128)}), f32[256,768]{1,0:T(8,128)}) %reduce-scatter.34.cloned.1.call-update) | async-done | bytes 786448 | tf_op jit(solution)/shard_map/while/body/eval_jaxpr/reduce_scatter | solution.py:53
  1193.6 40.4 %all-gather.37.cloned.1.call-done = bf16[768,768]{0,1:T(8,128)(2,1)} async-done(((bf16[768,96]{0,1:T(8,128)(2,1)}), bf16[768,768]{0,1:T(8,128)(2,1)}) %all-gather.37.cloned.1.call-update) | async-done | bytes 1179664 | tf_op jit(solution)/shard_map/while/body/eval_jaxpr/all_gather | solution.py:30
  1241.4 34.6 %all-gather.41.cloned.1.call-done = bf16[768,768]{1,0:T(8,128)(2,1)} async-done(((bf16[96,768]{1,0:T(8,128)(2,1)}), bf16[768,768]{1,0:T(8,128)(2,1)}) %all-gather.41.cloned.1.call-update) | async-done | bytes 1179664 | tf_op jit(solution)/shard_map/while/body/eval_jaxpr/all_gather | solution.py:28
  1281.0 36.5 %reduce-scatter.36.cloned.1.call-done = f32[256,768]{1,0:T(8,128)} async-done(((f32[1024,768]{1,0:T(8,128)}), f32[256,768]{1,0:T(8,128)}) %reduce-scatter.36.cloned.1.call-update) | async-done | bytes 786448 | tf_op jit(solution)/shard_map/while/body/eval_jaxpr/reduce_scatter | solution.py:53
  1323.6 31.8 %all_gather.153 = bf16[192,768]{0,1:T(8,128)(2,1)S(1)} all-gather(bf16[192,96]{0,1:T(8,128)(2,1)} %get-tuple-element.1244), channel_id=1, replica_groups=mesh['dp'=4,'ctx'=2,'tp'=4] {'dp','ctx'}, dimensions={1}, use_global_device_ids=true | all-gather | bytes 331776 | tf_op jit(solution)/shard_map/while/body/eval_jaxpr/all_gather | solution.py:27
  1359.0 138.0 %while.93 = (s32[]{:T(128)}, bf16[6,512,64]{1,2,0:T(8,128)(2,1)}, f32[6,2048,64]{1,2,0:T(8,128)}, f32[6,2048,64]{1,2,0:T(8,128)}, s32[6]{0:T(128)S(1)}, /*index=...) while((s32[]{:T(128)}, bf16[6,512,64]{1,2,0:T(8,128)(2,1)}, ...), condition=%wide.region_16.16_spmd, body=%wide.region_14.15_spmd.sunk | while | flops 711098880 | bytes 34761208 | solution.py:137
  1503.7 38.3 %all_gather.154 = bf16[3,768,192]{2,1,0:T(8,128)(2,1)S(1)} all-gather(bf16[3,96,192]{2,1,0:T(8,128)(2,1)S(1)} %copy-done.11), channel_id=1, replica_groups=mesh['dp'=4,'ctx'=2,'tp'=4] {'dp','ctx'}, dimensions={1}, use_global_device_ids=true | all-gather | bytes 995328 | tf_op jit(solution)/shard_map/while/body/eval_jaxpr/all_gather | solution.py:25
  1638.0 32.1 %reduce-scatter.28.cloned.1.call-done = f32[16,6]{1,0:T(8,128)} async-done(((f32[128,6]{1,0:T(8,128)}), f32[16,6]{1,0:T(8,128)}) %reduce-scatter.28.cloned.1.call-update) | async-done | bytes 400
  1671.5 63.1 %reduce-scatter.30.cloned.1.call-done = f32[96,6]{1,0:T(8,128)} async-done(((f32[768,6]{1,0:T(8,128)}), f32[96,6]{1,0:T(8,128)}) %reduce-scatter.30.cloned.1.call-update) | async-done | bytes 2320
  1741.6 58.7 %reduce-scatter.26.cloned.1.call-done = f32[96,192]{1,0:T(8,128)} async-done(((f32[768,192]{1,0:T(8,128)}), f32[96,192]{1,0:T(8,128)}) %reduce-scatter.26.cloned.1.call-update) | async-done | bytes 73744
  1801.9 70.9 %reduce-scatter.20.cloned.1.call-done = f32[3,96,192]{2,1,0:T(8,128)} async-done(((f32[3,768,192]{2,1,0:T(8,128)}), f32[3,96,192]{2,1,0:T(8,128)}) %reduce-scatter.20.cloned.1.call-update) | async-done | bytes 221200 | tf_op jit(solution)/shard_map/reduce_scatter | solution.py:38
  1872.8 72.8 %reduce-scatter.22.cloned.1.call-done = f32[96,768]{1,0:T(8,128)} async-done(((f32[768,768]{1,0:T(8,128)}), f32[96,768]{1,0:T(8,128)}) %reduce-scatter.22.cloned.1.call-update) | async-done | bytes 294928 | tf_op jit(solution)/shard_map/reduce_scatter | solution.py:41
  1945.6 72.9 %reduce-scatter.24.cloned.1.call-done = f32[768,96]{0,1:T(8,128)} async-done(((f32[768,768]{0,1:T(8,128)}), f32[768,96]{0,1:T(8,128)}) %reduce-scatter.24.cloned.1.call-update) | async-done | bytes 294928 | tf_op jit(solution)/shard_map/reduce_scatter | solution.py:43
  (650 shorter events, 799.1 us)
Async XLA Ops:
  12.3 135.5 %all-gather.29.cloned.1.call-start = ((), (), s32[]{:S(2)}) async-start(), calls=%async_computation.18 | async-start | bytes 1966080 | tf_op jit(solution)/shard_map/while/body/eval_jaxpr/all_gather | solution.py:49
  45.6 240.1 %reduce-scatter.32.cloned.1.call-start = ((), (), s32[]{:S(2)}) async-start(), calls=%async_computation.19 | async-start | bytes 3932160 | tf_op jit(solution)/shard_map/while/body/eval_jaxpr/reduce_scatter | solution.py:53
  249.1 66.6 %all-gather.33.cloned.1.call-start = ((), (), s32[]{:S(2)}) async-start(), calls=%async_computation.21 | async-start | bytes 1327104 | tf_op jit(solution)/shard_map/while/body/eval_jaxpr/all_gather | solution.py:28
  249.7 66.1 %all-gather.31.cloned.1.call-start = ((), (), s32[]{:S(2)}) async-start(), calls=%async_computation.20 | async-start | bytes 1966080 | tf_op jit(solution)/shard_map/while/body/eval_jaxpr/all_gather | solution.py:49
  288.3 66.3 %all-gather.35.cloned.1.call-start = ((), (), s32[]{:S(2)}) async-start(), calls=%async_computation.22 | async-start | bytes 1327104 | tf_op jit(solution)/shard_map/while/body/eval_jaxpr/all_gather | solution.py:30
  288.8 108.8 %reduce-scatter.34.cloned.1.call-start = ((), (), s32[]{:S(2)}) async-start(), calls=%async_computation.23 | async-start | bytes 3932160 | tf_op jit(solution)/shard_map/while/body/eval_jaxpr/reduce_scatter | solution.py:53
  362.5 78.4 %all-gather.37.cloned.1.call-start = ((), (), s32[]{:S(2)}) async-start(), calls=%async_computation.24 | async-start | bytes 1327104 | tf_op jit(solution)/shard_map/while/body/eval_jaxpr/all_gather | solution.py:30
  399.6 83.1 %all-gather.41.cloned.1.call-start = ((), (), s32[]{:S(2)}) async-start(), calls=%async_computation.26 | async-start | bytes 1327104 | tf_op jit(solution)/shard_map/while/body/eval_jaxpr/all_gather | solution.py:28
  400.2 124.0 %reduce-scatter.36.cloned.1.call-start = ((), (), s32[]{:S(2)}) async-start(), calls=%async_computation.27 | async-start | bytes 3932160 | tf_op jit(solution)/shard_map/while/body/eval_jaxpr/reduce_scatter | solution.py:53
  487.7 74.4 %all-gather.43.cloned.1.call-start = ((), (), s32[]{:S(2)}) async-start(), calls=%async_computation.28 | async-start | bytes 1966080 | tf_op jit(solution)/shard_map/while/body/eval_jaxpr/all_gather | solution.py:49
  530.3 218.8 %reduce-scatter.38.cloned.1.call-start = ((), (), s32[]{:S(2)}) async-start(), calls=%async_computation.29 | async-start | bytes 1179648 | tf_op jit(solution)/shard_map/while/body/eval_jaxpr/reduce_scatter | solution.py:214
  707.0 52.9 %reduce-scatter.40.cloned.1.call-start = ((), (), s32[]{:S(2)}) async-start(), calls=%async_computation.30 | async-start | bytes 1179648 | tf_op jit(solution)/shard_map/while/body/eval_jaxpr/reduce_scatter | solution.py:211
  710.3 91.7 %reduce-scatter.42.cloned.1.call-start = ((), (), s32[]{:S(2)}) async-start(), calls=%async_computation.31 | async-start | bytes 3932160 | tf_op jit(solution)/shard_map/while/body/eval_jaxpr/reduce_scatter | solution.py:53
  808.0 133.0 %all-gather.29.cloned.1.call-start = ((), (), s32[]{:S(2)}) async-start(), calls=%async_computation.18 | async-start | bytes 1966080 | tf_op jit(solution)/shard_map/while/body/eval_jaxpr/all_gather | solution.py:49
  839.6 239.2 %reduce-scatter.32.cloned.1.call-start = ((), (), s32[]{:S(2)}) async-start(), calls=%async_computation.19 | async-start | bytes 3932160 | tf_op jit(solution)/shard_map/while/body/eval_jaxpr/reduce_scatter | solution.py:53
  1042.4 66.1 %all-gather.33.cloned.1.call-start = ((), (), s32[]{:S(2)}) async-start(), calls=%async_computation.21 | async-start | bytes 1327104 | tf_op jit(solution)/shard_map/while/body/eval_jaxpr/all_gather | solution.py:28
  1043.0 65.6 %all-gather.31.cloned.1.call-start = ((), (), s32[]{:S(2)}) async-start(), calls=%async_computation.20 | async-start | bytes 1966080 | tf_op jit(solution)/shard_map/while/body/eval_jaxpr/all_gather | solution.py:49
  1081.4 66.2 %all-gather.35.cloned.1.call-start = ((), (), s32[]{:S(2)}) async-start(), calls=%async_computation.22 | async-start | bytes 1327104 | tf_op jit(solution)/shard_map/while/body/eval_jaxpr/all_gather | solution.py:30
  1082.0 108.7 %reduce-scatter.34.cloned.1.call-start = ((), (), s32[]{:S(2)}) async-start(), calls=%async_computation.23 | async-start | bytes 3932160 | tf_op jit(solution)/shard_map/while/body/eval_jaxpr/reduce_scatter | solution.py:53
  1155.6 78.4 %all-gather.37.cloned.1.call-start = ((), (), s32[]{:S(2)}) async-start(), calls=%async_computation.24 | async-start | bytes 1327104 | tf_op jit(solution)/shard_map/while/body/eval_jaxpr/all_gather | solution.py:30
  1192.7 83.3 %all-gather.41.cloned.1.call-start = ((), (), s32[]{:S(2)}) async-start(), calls=%async_computation.26 | async-start | bytes 1327104 | tf_op jit(solution)/shard_map/while/body/eval_jaxpr/all_gather | solution.py:28
  1193.5 123.9 %reduce-scatter.36.cloned.1.call-start = ((), (), s32[]{:S(2)}) async-start(), calls=%async_computation.27 | async-start | bytes 3932160 | tf_op jit(solution)/shard_map/while/body/eval_jaxpr/reduce_scatter | solution.py:53
  1280.9 74.5 %all-gather.43.cloned.1.call-start = ((), (), s32[]{:S(2)}) async-start(), calls=%async_computation.28 | async-start | bytes 1966080 | tf_op jit(solution)/shard_map/while/body/eval_jaxpr/all_gather | solution.py:49
  1323.5 219.2 %reduce-scatter.38.cloned.1.call-start = ((), (), s32[]{:S(2)}) async-start(), calls=%async_computation.29 | async-start | bytes 1179648 | tf_op jit(solution)/shard_map/while/body/eval_jaxpr/reduce_scatter | solution.py:214
  1500.3 52.8 %reduce-scatter.40.cloned.1.call-start = ((), (), s32[]{:S(2)}) async-start(), calls=%async_computation.30 | async-start | bytes 1179648 | tf_op jit(solution)/shard_map/while/body/eval_jaxpr/reduce_scatter | solution.py:211
  1503.6 91.7 %reduce-scatter.42.cloned.1.call-start = ((), (), s32[]{:S(2)}) async-start(), calls=%async_computation.31 | async-start | bytes 3932160 | tf_op jit(solution)/shard_map/while/body/eval_jaxpr/reduce_scatter | solution.py:53
  1603.1 67.0 %reduce-scatter.28.cloned.1.call-start = ((), (), s32[]{:S(2)}) async-start(), calls=%async_computation.16 | async-start | bytes 73728
  1604.7 129.8 %reduce-scatter.30.cloned.1.call-start = ((), (), s32[]{:S(2)}) async-start(), calls=%async_computation.17 | async-start | bytes 442368
  1606.5 193.8 %reduce-scatter.26.cloned.1.call-start = ((), (), s32[]{:S(2)}) async-start(), calls=%async_computation.15 | async-start | bytes 884736
  1608.8 263.9 %reduce-scatter.20.cloned.1.call-start = ((), (), s32[]{:S(2)}) async-start(), calls=%async_computation.12 | async-start | bytes 2654208 | tf_op jit(solution)/shard_map/reduce_scatter | solution.py:38
  1610.8 334.7 %reduce-scatter.22.cloned.1.call-start = ((), (), s32[]{:S(2)}) async-start(), calls=%async_computation.13 | async-start | bytes 2654208 | tf_op jit(solution)/shard_map/reduce_scatter | solution.py:41
  1611.6 406.9 %reduce-scatter.24.cloned.1.call-start = ((), (), s32[]{:S(2)}) async-start(), calls=%async_computation.14 | async-start | bytes 2654208 | tf_op jit(solution)/shard_map/reduce_scatter | solution.py:43
  (90 other events, 1554.2 us)
Sparse Core Ops, SparseCore 0:
  45.7 18.8 all-gather.28
  249.3 36.3 reduce-scatter.31
  363.0 18.3 all-gather.38
  399.7 41.1 all-gather.36
  442.9 39.8 all-gather.40
  530.4 19.6 all-gather.42
  707.1 29.7 reduce-scatter.37
  739.2 20.6 reduce-scatter.39
  839.7 17.8 all-gather.28
  1042.5 36.2 reduce-scatter.31
  1156.1 18.3 all-gather.38
  1192.8 41.1 all-gather.36
  1236.2 39.8 all-gather.40
  1323.6 19.6 all-gather.42
  1500.4 29.9 reduce-scatter.37
  1532.5 20.6 reduce-scatter.39
  1607.6 62.4 reduce-scatter.27
  1673.2 61.2 reduce-scatter.29
  1737.8 62.3 reduce-scatter.25
  1804.2 68.5 reduce-scatter.19
  1876.8 68.6 reduce-scatter.21
  1949.6 68.7 reduce-scatter.23
Sparse Core Ops, SparseCore 1:
  251.8 39.9 all-gather.32
  293.2 17.8 all-gather.30
  313.1 41.4 all-gather.34
  360.7 36.9 reduce-scatter.33
  487.7 36.4 reduce-scatter.35
  764.3 37.7 reduce-scatter.41
  1045.1 39.7 all-gather.32
  1086.3 17.8 all-gather.30
  1106.2 41.4 all-gather.34
  1153.8 36.9 reduce-scatter.33
  1281.0 36.4 reduce-scatter.35
  1557.5 37.7 reduce-scatter.41
where the time goes:
time: 2030 us
  waiting for transfers between devices  871 us (43%)
  blocking collectives  508 us (25%)
  matrix products  310 us (15%)
  other arithmetic  141 us (7%)
  loops' own time  98.8 us (5%)
  local copies, waits for them, and re-layouts  79.5 us (4%)
    reduce_scatter x8, waiting for transfers between devices, rows_sum(): return lax.psum_scatter(terms, 'tp', scatter_dimension=0, tiled=True)  257 us
    unnamed x9, waiting for transfers between devices  155 us
    all_gather x4, waiting for transfers between devices, fetch(): lax.all_gather(shards[5], ('dp', 'ctx'), axis=1, tiled=True)  149 us
    all_gather x4, blocking collectives, fetch(): lax.all_gather(shards[0], ('dp', 'ctx'), axis=1, tiled=True)  147 us
    all_gather x4, blocking collectives, fetch(): lax.all_gather(shards[2], ('dp', 'ctx'), axis=1, tiled=True)  130 us
    reduce_scatter x1, waiting for transfers between devices, settle(): lax.psum_scatter(gradients[5], ('dp', 'ctx'), scatter_dimension=1, tiled=...  72.9 us
    reduce_scatter x1, waiting for transfers between devices, settle(): lax.psum_scatter(gradients[3], ('dp', 'ctx'), scatter_dimension=0, tiled=...  72.8 us
    reduce_scatter x1, waiting for transfers between devices, settle(): lax.psum_scatter(gradients[0], ('dp', 'ctx'), scatter_dimension=1, tiled=...  70.9 us
  transfers between devices with their start and end apart: 34, of which 22 were waited for; matrix products, arithmetic and copies ran while one was open for 5% of the time, Pallas kernels for 0%

commit v1 on v0

v1 whole, which is shorter than its diff:
```python
import functools

import jax
import jax.numpy as jnp
from jax import lax
from jax.experimental import pallas as pl
from jax.experimental.pallas import tpu as pltpu
from jax.sharding import PartitionSpec as P

HD = 64
EPS = 1e-05
LOG2E = 1.4426950408889634
F32 = jnp.float32
BF16 = jnp.bfloat16
VMEM_LIMIT = 60 * 1024 * 1024
EXT = 64


def dot(a, b):
    return lax.dot_general(a, b, (((1,), (0,)), ((), ())), preferred_element_type=F32)


def dot_nt(a, b):
    return lax.dot_general(a, b, (((1,), (1,)), ((), ())), preferred_element_type=F32)


def norm_parts(rows):
    mean = jnp.mean(rows, axis=-1, keepdims=True)
    centered = rows - mean
    spread = jnp.mean(centered * centered, axis=-1, keepdims=True)
    scale = lax.rsqrt(spread + EPS)
    return (centered * scale, scale)


def norm_back(incoming, gain, n, scale):
    e = incoming * gain
    return (e - jnp.mean(e, axis=-1, keepdims=True) - n * jnp.mean(e * n, axis=-1, keepdims=True)) * scale


def params(steps=1):
    return pltpu.CompilerParams(
        dimension_semantics=("arbitrary",) * steps, vmem_limit_bytes=VMEM_LIMIT
    )


def cost(flops, moved, exps=0):
    return pl.CostEstimate(flops=int(flops), bytes_accessed=int(moved), transcendentals=int(exps))


def project_kernel(me_ref, own_ref, far_ref, w_ref, order_ref, out_ref, vec_ref, bias_ref):
    i = pl.program_id(0)
    width = out_ref.shape[2]

    @pl.when(i == 0)
    def _():
        turned = jnp.transpose(w_ref[:, 512:640].astype(F32))
        vec_ref[...] = turned[64:72]
        bias_ref[...] = dot(turned[64:72].astype(BF16), order_ref[...])

    far = ((i ^ me_ref[0]) & 1) == 1
    rows = jnp.where(far, far_ref[0], own_ref[0]).astype(F32)
    n, _ = norm_parts(rows)
    normed = (n * vec_ref[0:1] + vec_ref[1:2]).astype(BF16)
    full = dot(normed, w_ref[...])[:, : 3 * width] + bias_ref[2:3, :]
    full = full.astype(BF16)
    out_ref[0] = full[:, :width] * jnp.asarray(HD ** (-0.5), BF16)
    out_ref[1] = full[:, width : 2 * width]
    out_ref[2] = full[:, 2 * width :]


def project(me, own, far, w, order):
    half, rows, d = own.shape
    blocks = 2 * half
    width = order.shape[1] // 3
    return pl.pallas_call(
        project_kernel,
        out_shape=jax.ShapeDtypeStruct((3, blocks * rows, width), BF16),
        grid_spec=pltpu.PrefetchScalarGridSpec(
            num_scalar_prefetch=1,
            grid=(blocks,),
            in_specs=[
                pl.BlockSpec((1, rows, d), lambda i, me: ((i ^ me[0]) // 2, 0, 0)),
                pl.BlockSpec((1, rows, d), lambda i, me: ((i ^ me[0]) // 2, 0, 0)),
                pl.BlockSpec(w.shape, lambda i, me: (0, 0)),
                pl.BlockSpec(order.shape, lambda i, me: (0, 0)),
            ],
            out_specs=pl.BlockSpec((3, rows, width), lambda i, me: (0, i, 0)),
            scratch_shapes=[pltpu.VMEM((8, d), F32), pltpu.VMEM((8, 3 * width), F32)],
        ),
        compiler_params=params(),
        cost_estimate=cost(2 * blocks * rows * d * 3 * width, 8e6),
        name="project",
    )(me, own, far, w, order)


def head_mask(shape, h):
    lane = lax.broadcasted_iota(jnp.int32, shape, 1)
    return (lane >= h * HD) & (lane < (h + 1) * HD)


def attend_kernel(q_ref, k_ref, v_ref, o_ref, ot_ref, level_ref, vt_ref, qm_ref, m_ref, l_ref):
    i = pl.program_id(0)
    heads = q_ref.shape[2] // HD
    bq = q_ref.shape[1]
    half = bq // 2

    @pl.when(i == 0)
    def _():
        vt_ref[...] = jnp.transpose(v_ref[0].astype(F32)).astype(BF16)

    for h in range(heads):
        q = q_ref[0]
        qm_ref[h] = jnp.where(head_mask(q.shape, h), q, jnp.zeros_like(q))
    m_ref[...] = jnp.zeros_like(m_ref)
    l_ref[...] = jnp.zeros_like(l_ref)
    ot_ref[...] = jnp.zeros_like(ot_ref)

    def chunk(start, size, first, masked):
        cols = slice(first, bq)
        keys = k_ref[0, pl.ds(start, size), :]
        for h in range(heads):
            u = dot_nt(keys, qm_ref[h, first:bq, :]) * LOG2E
            if masked:
                key_pos = lax.broadcasted_iota(jnp.int32, u.shape, 0)
                row_pos = lax.broadcasted_iota(jnp.int32, u.shape, 1)
                allowed = key_pos <= row_pos
                u = jnp.where(allowed, u, 0.0)
            before = m_ref[h : h + 1, cols]
            peak = jnp.maximum(before, jnp.max(jnp.abs(u), axis=0, keepdims=True))
            fade = jnp.exp2(before - peak)
            upper = jnp.exp2(u - peak)
            lower = jnp.exp2(-peak - u)
            both = upper + lower
            if masked:
                both = jnp.where(allowed, both, 0.0)
            m_ref[h : h + 1, cols] = peak
            l_ref[h : h + 1, cols] = l_ref[h : h + 1, cols] * fade + jnp.sum(both, axis=0, keepdims=True)
            part = dot(vt_ref[h * HD : (h + 1) * HD, pl.ds(start, size)], (upper - lower).astype(BF16))
            ot_ref[h * HD : (h + 1) * HD, cols] = ot_ref[h * HD : (h + 1) * HD, cols] * fade + part

    def body(j, carry):
        chunk(pl.multiple_of(j * bq, bq), bq, 0, False)
        return carry

    lax.fori_loop(0, i, body, 0)
    base = pl.multiple_of(i * bq, bq)
    chunk(base, half, 0, True)
    chunk(pl.multiple_of(base + half, half), half, half, True)
    for h in range(heads):
        total = l_ref[h : h + 1, :]
        level_ref[h : h + 1, :] = m_ref[h : h + 1, :] + jnp.log2(total)
        ot_ref[h * HD : (h + 1) * HD, :] = ot_ref[h * HD : (h + 1) * HD, :] * (1.0 / total)
    o_ref[...] = jnp.transpose(ot_ref[...]).astype(BF16)


def attend(triple):
    _, span, width = triple.shape
    bq = min(512, span)
    heads = width // HD
    return pl.pallas_call(
        attend_kernel,
        out_shape=(
            jax.ShapeDtypeStruct((span, width), BF16),
            jax.ShapeDtypeStruct((width, span), F32),
            jax.ShapeDtypeStruct((8, span), F32),
        ),
        grid=(span // bq,),
        in_specs=[
            pl.BlockSpec((1, bq, width), lambda i: (0, i, 0)),
            pl.BlockSpec((1, span, width), lambda i: (1, 0, 0)),
            pl.BlockSpec((1, span, width), lambda i: (2, 0, 0)),
        ],
        out_specs=(
            pl.BlockSpec((bq, width), lambda i: (i, 0)),
            pl.BlockSpec((width, bq), lambda i: (0, i)),
            pl.BlockSpec((8, bq), lambda i: (0, i)),
        ),
        scratch_shapes=[
            pltpu.VMEM((width, span), BF16),
            pltpu.VMEM((heads, bq, width), BF16),
            pltpu.VMEM((8, bq), F32),
            pltpu.VMEM((8, bq), F32),
        ],
        compiler_params=params(),
        cost_estimate=cost(4 * span * span * width, 8e6, span * span * heads),
        name="attend",
    )(triple, triple, triple)


def attend_back_kernel(
    qkv_ref, grad_ref, ot_ref, level_ref, out_ref, qm_ref, gm_ref, kt_ref, dqt_ref, dot_ref, dk_ref, dv_ref
):
    j = pl.program_id(0)
    blocks = pl.num_programs(0)
    span, width = grad_ref.shape
    heads = width // HD
    count = qm_ref.shape[0]
    b = span // count
    half = b // 2

    @pl.when(j == 0)
    def _():
        turned = jnp.transpose(grad_ref[...].astype(F32))
        prod = turned * ot_ref[...]
        for h in range(heads):
            dot_ref[h : h + 1, :] = jnp.sum(prod[h * HD : (h + 1) * HD], axis=0, keepdims=True)
        kt_ref[...] = jnp.transpose(qkv_ref[1].astype(F32)).astype(BF16)
        dqt_ref[...] = jnp.zeros_like(dqt_ref)
        for n in range(count):
            q = qkv_ref[0, n * b : (n + 1) * b, :]
            g = grad_ref[n * b : (n + 1) * b, :]
            for h in range(heads):
                mask = head_mask(q.shape, h)
                qm_ref[n, h * b : (h + 1) * b, :] = jnp.where(mask, q, jnp.zeros_like(q))
                gm_ref[n, h * b : (h + 1) * b, :] = jnp.where(mask, g, jnp.zeros_like(g))

    dk_ref[...] = jnp.zeros_like(dk_ref)
    dv_ref[...] = jnp.zeros_like(dv_ref)

    def chunk(i, key_first, key_size, first, masked):
        start = pl.multiple_of(j * b + key_first, half)
        keys = qkv_ref[1, pl.ds(start, key_size), :]
        vals = qkv_ref[2, pl.ds(start, key_size), :]
        cols = b - first
        at = pl.multiple_of(i * b + first, half)
        for h in range(heads):
            lo = h * b + first
            qm = qm_ref[i, lo : lo + cols, :]
            gm = gm_ref[i, lo : lo + cols, :]
            level = level_ref[h : h + 1, pl.ds(at, cols)]
            inner = dot_ref[h : h + 1, pl.ds(at, cols)]
            u = dot_nt(keys, qm) * LOG2E
            upper = jnp.exp2(u - level)
            lower = jnp.exp2(-level - u)
            gw = dot_nt(vals, gm)
            weights = upper - lower
            gs = upper * (gw - inner) + lower * (gw + inner)
            if masked:
                key_pos = lax.broadcasted_iota(jnp.int32, u.shape, 0)
                row_pos = lax.broadcasted_iota(jnp.int32, u.shape, 1)
                allowed = key_pos <= row_pos
                weights = jnp.where(allowed, weights, 0.0)
                gs = jnp.where(allowed, gs, 0.0)
            weights = weights.astype(BF16)
            gs = gs.astype(BF16)
            rows = slice(key_first, key_first + key_size)
            dv_ref[rows, :] += dot(weights, gm)
            dk_ref[rows, :] += dot(gs, qm)
            dqt_ref[h * HD : (h + 1) * HD, pl.ds(at, cols)] += dot(
                kt_ref[h * HD : (h + 1) * HD, pl.ds(start, key_size)], gs
            )

    def body(i, carry):
        chunk(i, 0, b, 0, False)
        return carry

    chunk(j, 0, half, 0, True)
    chunk(j, half, half, half, True)
    lax.fori_loop(j + 1, blocks, body, 0)
    here = pl.ds(pl.multiple_of(j * b, b), b)
    out_ref[1, here, :] = dk_ref[...].astype(BF16)
    out_ref[2, here, :] = dv_ref[...].astype(BF16)

    @pl.when(j == blocks - 1)
    def _():
        out_ref[0] = jnp.transpose(dqt_ref[...] * (HD ** (-0.5))).astype(BF16)


def attend_back(triple, grad, ot, level):
    _, span, width = triple.shape
    b = min(512, span)
    count = span // b
    heads = width // HD
    whole = lambda *shape: pl.BlockSpec(shape, lambda j: (0,) * len(shape))
    return pl.pallas_call(
        attend_back_kernel,
        out_shape=jax.ShapeDtypeStruct(triple.shape, BF16),
        grid=(count,),
        in_specs=[
            whole(*triple.shape),
            whole(*grad.shape),
            whole(*ot.shape),
            whole(*level.shape),
        ],
        out_specs=whole(*triple.shape),
        scratch_shapes=[
            pltpu.VMEM((count, heads * b, width), BF16),
            pltpu.VMEM((count, heads * b, width), BF16),
            pltpu.VMEM((width, span), BF16),
            pltpu.VMEM((width, span), F32),
            pltpu.VMEM((8, span), F32),
            pltpu.VMEM((b, width), F32),
            pltpu.VMEM((b, width), F32),
        ],
        compiler_params=params(),
        cost_estimate=cost(10 * span * span * width, 1e7, span * span * heads),
        name="attend_back",
    )(triple, grad, ot, level)


def gelu_parts(u):
    c = 0.7978845608028654
    square = u * u
    th = jnp.tanh(c * u * (1.0 + 0.044715 * square))
    near = 0.5 * (1.0 + th)
    slope = near + (0.5 * c) * u * (1.0 - th * th) * (1.0 + (3.0 * 0.044715) * square)
    return (u * near, slope)


def middle_kernel(
    tok_ref,
    cot_ref,
    mix_ref,
    g_ref,
    gout_ref,
    order_ref,
    y_ref,
    gh_ref,
    dmix_ref,
    n2_ref,
    act_ref,
    gl_ref,
    gb_ref,
    vec_ref,
    gfb_ref,
    hid_ref,
    acc_ref,
    back_ref,
    ext_ref,
):
    t = pl.program_id(0)
    steps = pl.num_programs(0)
    half = mix_ref.shape[1]
    parts = gout_ref.shape[0]
    d = tok_ref.shape[1]
    width = mix_ref.shape[2]

    @pl.when(t == 0)
    def _():
        ext_ref[...] = jnp.transpose(gout_ref[0, :, 128:256].astype(F32))[64:72]
        total = tok_ref[...].astype(F32) + ext_ref[2:3]
        for s in range(parts):
            lhs = jnp.concatenate([mix_ref[s], mix_ref[parts + s]], axis=0)
            total = total + dot_nt(lhs, gout_ref[s, :, :width])
        hid_ref[...] = total
        n, _ = norm_parts(total)
        n2_ref[...] = (n * ext_ref[0:1] + ext_ref[1:2]).astype(BF16)
        acc_ref[...] = total + ext_ref[3:4]
        back_ref[...] = jnp.zeros_like(back_ref)

    ext = jnp.transpose(g_ref[0, :, 2 * d + 128 : 2 * d + 256].astype(F32))[64:72].astype(BF16)
    bias = dot(ext, order_ref[...])[4:5]
    fc = g_ref[0, :, :d]
    pj = g_ref[0, :, d : 2 * d]
    lifted = dot(n2_ref[...], fc) + bias
    act, slope = gelu_parts(lifted)
    act = act.astype(BF16)
    act_ref[0] = act
    gl32 = dot(cot_ref[...], pj) * slope
    gl = gl32.astype(BF16)
    gl_ref[0] = gl
    gfb_ref[0, 0:1, :] = jnp.sum(gl.astype(F32), axis=0, keepdims=True)
    acc_ref[...] += dot_nt(act, pj)
    back_ref[...] += dot_nt(gl, fc)

    @pl.when(t == steps - 1)
    def _():
        y_ref[...] = acc_ref[...].astype(BF16)
        n, scale = norm_parts(hid_ref[...])
        back = back_ref[...]
        cot = cot_ref[...].astype(F32)
        gh = cot + norm_back(back, ext_ref[0:1], n, scale)
        gh_ref[...] = gh
        gb = gh.astype(BF16)
        gb_ref[...] = gb
        vec_ref[0:1, :] = jnp.sum(back * n, axis=0, keepdims=True)
        vec_ref[1:2, :] = jnp.sum(back, axis=0, keepdims=True)
        vec_ref[2:3, :] = jnp.sum(gb.astype(F32), axis=0, keepdims=True)
        vec_ref[3:4, :] = jnp.sum(cot, axis=0, keepdims=True)
        vec_ref[4:8, :] = jnp.zeros((4, d), F32)
        for s in range(parts):
            dm = dot(gb, gout_ref[s, :, :width]).astype(BF16)
            dmix_ref[s] = dm[:half]
            dmix_ref[parts + s] = dm[half:]


def middle(tok, cot, mix, gathered, order):
    rows, d = tok.shape
    parts = gathered.shape[0]
    cols = gathered.shape[2]
    whole = lambda *shape: pl.BlockSpec(shape, lambda t: (0,) * len(shape))
    piece = lambda *shape: pl.BlockSpec(shape, lambda t: (t,) + (0,) * (len(shape) - 1))
    sds = jax.ShapeDtypeStruct
    return pl.pallas_call(
        middle_kernel,
        out_shape=(
            sds((rows, d), BF16),
            sds((rows, d), F32),
            sds(mix.shape, BF16),
            sds((rows, d), BF16),
            sds((parts, rows, d), BF16),
            sds((parts, rows, d), BF16),
            sds((rows, d), BF16),
            sds((8, d), F32),
            sds((parts, 8, d), F32),
        ),
        grid=(parts,),
        in_specs=[
            whole(rows, d),
            whole(rows, d),
            whole(*mix.shape),
            piece(1, d, cols),
            pl.BlockSpec((parts, d, 256), lambda t: (0, 0, cols // 256 - 1)),
            whole(*order.shape),
        ],
        out_specs=(
            whole(rows, d),
            whole(rows, d),
            whole(*mix.shape),
            whole(rows, d),
            piece(1, rows, d),
            piece(1, rows, d),
            whole(rows, d),
            whole(8, d),
            piece(1, 8, d),
        ),
        scratch_shapes=[
            pltpu.VMEM((rows, d), F32),
            pltpu.VMEM((rows, d), F32),
            pltpu.VMEM((rows, d), F32),
            pltpu.VMEM((8, d), F32),
        ],
        compiler_params=params(),
        cost_estimate=cost(2 * rows * d * d * 18, 3e7),
        name="middle",
    )(tok, cot, mix, gathered, gathered, order)


def weights_kernel(
    n2_ref, cot_ref, gb_ref, mix_ref, act_ref, gl_ref, vec_ref, gfb_ref, order_ref, out_ref, nt_ref, ct_ref, bt_ref
):
    t = pl.program_id(0)
    d = n2_ref.shape[1]
    width = mix_ref.shape[3]

    @pl.when(t == 0)
    def _():
        nt_ref[...] = jnp.transpose(n2_ref[...].astype(F32)).astype(BF16)
        ct_ref[...] = jnp.transpose(cot_ref[...].astype(F32)).astype(BF16)
        bt_ref[...] = jnp.transpose(gb_ref[...].astype(F32)).astype(BF16)

    out_ref[0, :, :d] = dot(nt_ref[...], gl_ref[0]).astype(BF16)
    out_ref[0, :, d : 2 * d] = dot(ct_ref[...], act_ref[0]).astype(BF16)
    mix = jnp.concatenate([mix_ref[0, 0], mix_ref[1, 0]], axis=0)
    out_ref[0, :, 2 * d : 2 * d + width] = dot(bt_ref[...], mix).astype(BF16)
    turned = dot_nt(gfb_ref[0].astype(BF16), order_ref[...])
    line = lax.broadcasted_iota(jnp.int32, turned.shape, 0)
    rows = jnp.where(line == 4, turned[0:1], vec_ref[...])
    tall = jnp.concatenate([rows, jnp.zeros((EXT - 8, d), F32)], axis=0)
    out_ref[0, :, 2 * d + width :] = jnp.transpose(tall).astype(BF16)


def weights(n2, cot, gb, mix, act, gl, vec, gfb, order):
    rows, d = n2.shape
    parts = act.shape[0]
    width = mix.shape[2]
    cols = 2 * d + width + EXT
    whole = lambda *shape: pl.BlockSpec(shape, lambda t: (0,) * len(shape))
    piece = lambda *shape: pl.BlockSpec(shape, lambda t: (t,) + (0,) * (len(shape) - 1))
    mix = mix.reshape(mix.shape[0] // parts, parts, mix.shape[1], width)
    return pl.pallas_call(
        weights_kernel,
        out_shape=jax.ShapeDtypeStruct((parts, d, cols), BF16),
        grid=(parts,),
        in_specs=[
            whole(rows, d),
            whole(rows, d),
            whole(rows, d),
            pl.BlockSpec((mix.shape[0], 1, mix.shape[2], width), lambda t: (0, t, 0, 0)),
            piece(1, rows, d),
            piece(1, rows, d),
            whole(8, d),
            piece(1, 8, d),
            whole(*order.shape),
        ],
        out_specs=piece(1, d, cols),
        scratch_shapes=[
            pltpu.VMEM((d, rows), BF16),
            pltpu.VMEM((d, rows), BF16),
            pltpu.VMEM((d, rows), BF16),
        ],
        compiler_params=params(),
        cost_estimate=cost(2 * rows * d * d * 9, 2.5e7),
        name="weights",
    )(n2, cot, gb, mix, act, gl, vec, gfb, order)


def project_back_kernel(
    me_ref, own_ref, far_ref, grad_ref, w_ref, keep_ref, send_ref, dw_ref, vec_ref, bias_ref, w3_ref, dw3_ref, gain_ref
):
    i = pl.program_id(0)
    steps = pl.num_programs(0)
    width = grad_ref.shape[2]

    @pl.when(i == 0)
    def _():
        gain_ref[...] = jnp.transpose(w_ref[:, 512:640].astype(F32))[64:72]
        for s in range(3):
            w3_ref[s] = w_ref[:, s * width : (s + 1) * width]
        dw3_ref[...] = jnp.zeros_like(dw3_ref)
        vec_ref[...] = jnp.zeros_like(vec_ref)
        bias_ref[...] = jnp.zeros_like(bias_ref)

    far = ((i ^ me_ref[0]) & 1) == 1
    rows = jnp.where(far, far_ref[0], own_ref[0]).astype(F32)
    n, _ = norm_parts(rows)
    normed = n * gain_ref[0:1] + gain_ref[1:2]
    turned = jnp.transpose(normed).astype(BF16)
    part = dot_nt(grad_ref[0], w3_ref[0])
    for s in range(1, 3):
        part = part + dot_nt(grad_ref[s], w3_ref[s])
    for s in range(3):
        dw3_ref[s] += dot(turned, grad_ref[s])
        bias_ref[s : s + 1, :] += jnp.sum(grad_ref[s].astype(F32), axis=0, keepdims=True)
    vec_ref[0:1, :] += jnp.sum(part * n, axis=0, keepdims=True)
    vec_ref[1:2, :] += jnp.sum(part, axis=0, keepdims=True)

    @pl.when(far)
    def _():
        send_ref[0] = part.astype(BF16)

    @pl.when(jnp.logical_not(far))
    def _():
        keep_ref[0] = part

    @pl.when(i == steps - 1)
    def _():
        dw_ref[...] = dw3_ref[...].astype(BF16)


def project_back(me, own, far, grad, w):
    half, rows, d = own.shape
    width = grad.shape[2]
    blocks = 2 * half
    sds = jax.ShapeDtypeStruct
    rel = lambda i, me: ((i ^ me[0]) // 2, 0, 0)
    return pl.pallas_call(
        project_back_kernel,
        out_shape=(
            sds((half, rows, d), F32),
            sds((half, rows, d), BF16),
            sds((3, d, width), BF16),
            sds((8, d), F32),
            sds((8, width), F32),
        ),
        grid_spec=pltpu.PrefetchScalarGridSpec(
            num_scalar_prefetch=1,
            grid=(blocks,),
            in_specs=[
                pl.BlockSpec((1, rows, d), rel),
                pl.BlockSpec((1, rows, d), rel),
                pl.BlockSpec((3, rows, width), lambda i, me: (0, i, 0)),
                pl.BlockSpec(w.shape, lambda i, me: (0, 0)),
            ],
            out_specs=(
                pl.BlockSpec((1, rows, d), rel),
                pl.BlockSpec((1, rows, d), rel),
                pl.BlockSpec((3, d, width), lambda i, me: (0, 0, 0)),
                pl.BlockSpec((8, d), lambda i, me: (0, 0)),
                pl.BlockSpec((8, width), lambda i, me: (0, 0)),
            ),
            scratch_shapes=[
                pltpu.VMEM((3, d, width), BF16),
                pltpu.VMEM((3, d, width), F32),
                pltpu.VMEM((8, d), F32),
            ],
        ),
        compiler_params=params(),
        cost_estimate=cost(4 * blocks * rows * d * 3 * width, 1.5e7),
        name="project_back",
    )(me, own, far, grad, w)


def one_hot_order(sources, targets, size, width):
    row = lax.broadcasted_iota(jnp.int32, (size, width), 0)
    return jnp.where(row == sources, 1.0, 0.0).astype(BF16)


def local(
    tokens,
    cotangent,
    ln1_gain,
    ln1_bias,
    qkv_weight,
    qkv_bias,
    out_weight,
    out_bias,
    ln2_gain,
    ln2_bias,
    fc_weight,
    fc_bias,
    proj_weight,
    proj_bias,
):
    sides = lax.axis_size("ctx")
    parts = lax.axis_size("tp")
    shards = lax.axis_size(("dp", "ctx"))
    group = sides * parts
    micro, _, rows, d = tokens.shape
    assert micro == sides == 2 and parts % 2 == 0
    side = lax.axis_index("ctx")
    me = side * parts + lax.axis_index("tp")
    me_array = jnp.full((1,), me, jnp.int32)
    tall = qkv_weight.shape[1]
    heads, piece = qkv_bias.shape[1], qkv_bias.shape[2]
    width = heads * HD
    lines, strip = fc_bias.shape

    def swap(array, mask):
        return lax.ppermute(array, ("ctx", "tp"), [(n, n ^ mask) for n in range(group)])

    tok = tokens[:, 0]
    cot = cotangent[:, 0]

    mine = lax.dynamic_index_in_dim(tok, side, 0, keepdims=False)
    other = lax.dynamic_index_in_dim(tok, 1 - side, 0, keepdims=False)
    blocks = []
    for mask in range(0, group, 2):
        block = other if mask >= parts else mine
        blocks.append(block if mask == 0 else swap(block, mask))
    own = jnp.stack(blocks)
    far = swap(own, 1)

    def column(values):
        return jnp.pad(values.reshape(-1, 1), ((0, tall - values.size), (0, 0)))

    narrow = jnp.concatenate(
        [
            qkv_weight.transpose(1, 0, 2).reshape(tall, 3 * width),
            column(ln1_gain),
            column(ln1_bias),
            column(qkv_bias),
            jnp.zeros((tall, EXT - 3), BF16),
        ],
        axis=1,
    )
    w_in = lax.all_to_all(
        jnp.broadcast_to(narrow[None], (shards,) + narrow.shape), ("dp", "ctx"), 0, 0, tiled=True
    ).reshape(d, 3 * width + EXT)

    wide = jnp.concatenate(
        [
            fc_weight,
            proj_weight.T,
            out_weight.T,
            column(ln2_gain),
            column(ln2_bias),
            column(out_bias),
            column(proj_bias),
            column(fc_bias),
            jnp.zeros((tall, EXT - 5), BF16),
        ],
        axis=1,
    )
    gathered = lax.all_gather(wide, ("tp", "dp", "ctx"), axis=0, tiled=True)
    gathered = gathered.reshape(parts, d, wide.shape[1])

    unit = lax.broadcasted_iota(jnp.int32, (1, 3 * width), 1)
    shard = unit % HD // piece
    order_in = one_hot_order(shard * tall + unit // HD * piece + unit % piece, None, d, 3 * width)
    unit = lax.broadcasted_iota(jnp.int32, (1, d), 1)
    shard = unit % 128 // strip
    order_fc = one_hot_order(shard * tall + unit // 128 * strip + unit % strip, None, d, d)

    triple = project(me_array, own, far, w_in, order_in)
    mixed, mixed_turned, level = attend(triple)
    mix = lax.all_to_all(mixed.reshape(group, rows, width), ("ctx", "tp"), 0, 0, tiled=True)

    tok_rows = tok.reshape(micro * rows, d)
    cot_rows = cot.reshape(micro * rows, d)
    y, grad_hidden, grad_mix, n2, act, gl, gb, vec, gfb = middle(
        tok_rows, cot_rows, mix, gathered, order_fc
    )
    grad_mix = lax.all_to_all(grad_mix, ("ctx", "tp"), 0, 0, tiled=True)
    grad_wide = weights(n2, cot_rows, gb, mix, act, gl, vec, gfb, order_fc)
    grad_wide = lax.psum_scatter(
        grad_wide.reshape(parts * d, wide.shape[1]), ("tp", "dp", "ctx"), scatter_dimension=0, tiled=True
    ).astype(F32)

    grad_triple = attend_back(triple, grad_mix.reshape(group * rows, width), mixed_turned, level)
    keep, send, grad_in, vec_in, bias_in = project_back(me_array, own, far, grad_triple, w_in)

    pair = keep + swap(send, 1).astype(F32)
    arrived = []
    for n, mask in enumerate(range(0, group, 2)):
        arrived.append(pair[n] if mask == 0 else swap(pair[n].astype(BF16), mask).astype(F32))
    near = sum(arrived[1 : parts // 2], arrived[0])
    away = sum(arrived[parts // 2 + 1 :], arrived[parts // 2])
    swapped = side == 1
    grad_normed = jnp.stack([jnp.where(swapped, away, near), jnp.where(swapped, near, away)])

    vec_in = vec_in[:2]
    mask = 1
    while mask < parts:
        vec_in = vec_in + swap(vec_in, mask)
        mask *= 2
    bias_cols = bias_in[:3].reshape(3, heads, shards, piece).transpose(2, 0, 1, 3).reshape(shards, 3 * heads * piece)
    bias_cols = jnp.pad(bias_cols, ((0, 0), (0, tall - 3 * heads * piece))).reshape(d, 1)
    narrow_grad = jnp.concatenate(
        [
            grad_in.transpose(1, 0, 2).reshape(d, 3 * width),
            vec_in.T.astype(BF16),
            bias_cols.astype(BF16),
            jnp.zeros((d, EXT - 3), BF16),
        ],
        axis=1,
    )
    narrow_grad = lax.all_to_all(
        narrow_grad.reshape(shards, tall, 3 * width + EXT), ("dp", "ctx"), 0, 0, tiled=True
    )
    narrow_grad = jnp.sum(narrow_grad.astype(F32), axis=0)

    n, scale = norm_parts(tok.astype(F32))
    gain = w_in[:, 3 * width].astype(F32)
    grad_tokens = grad_hidden.reshape(micro, rows, d) + norm_back(grad_normed, gain, n, scale)

    base = 3 * width
    grad_qkv_weight = narrow_grad[:, :base].reshape(tall, 3, width).transpose(1, 0, 2)
    grad_qkv_bias = narrow_grad[: 3 * heads * piece, base + 2].reshape(3, heads, piece)
    edge = 2 * d + width
    return (
        y.reshape(micro, 1, rows, d),
        grad_tokens[:, None],
        narrow_grad[:, base],
        narrow_grad[:, base + 1],
        grad_qkv_weight,
        grad_qkv_bias,
        grad_wide[:, 2 * d : edge].T,
        grad_wide[:, edge + 2],
        grad_wide[:, edge],
        grad_wide[:, edge + 1],
        grad_wide[:, :d],
        grad_wide[:, edge + 4].reshape(lines, strip),
        grad_wide[:, d : 2 * d].T,
        grad_wide[:, edge + 3],
    )


def solution(mesh):
    rows = P(None, "dp", ("ctx", "tp"), None)
    vector = P(("dp", "ctx"))
    joint = P(None, ("dp", "ctx"), "tp")
    joint_bias = P(None, "tp", ("dp", "ctx"))
    down = P("tp", ("dp", "ctx"))
    up = P(("dp", "ctx"), "tp")
    inner = (vector, vector, joint, joint_bias, down, vector, vector, vector, up, down, down, vector)
    return jax.shard_map(
        local,
        mesh=mesh,
        in_specs=(rows, rows) + inner,
        out_specs=(rows, rows) + inner,
        check_vma=False,
    )
```

time: 2030 us -> 323 us (0.16)
  waiting for transfers between devices: 871 us -> 95.8 us
  blocking collectives: 508 us -> 14.3 us
  matrix products: 310 us -> 0 us
  Pallas kernels: 0 us -> 120 us
  other arithmetic: 141 us -> 23.2 us
  loops' own time: 98.8 us -> 0 us
  local copies, waits for them, and re-layouts: 79.5 us -> 29.9 us
  starting transfers between devices: 1.43 us -> 24.6 us
    all_gather x18 -> x0, blocking collectives: 480 us -> none  [the longest x4 147 us: fetch(): lax.all_gather(shards[0], ('dp', 'ctx'), axis=1, tiled=True)]
    reduce_scatter x15 -> x1, waiting for transfers between devices: 494 us -> 31.9 us  [local(): lax.psum_scatter(grad_wide.reshape(parts * d, wide.shape[1]), ('tp', 'dp'...]
    dot_general x106 -> x0, matrix products: 305 us -> none  [the longest x12 49.3 us: one(): jnp.einsum('qk,qd->kd', weights.astype(jnp.bfloat16), grad_mix, preferred...]
    all_gather x16 -> x1, waiting for transfers between devices: 218 us -> 0.01 us  [local(): gathered = lax.all_gather(wide, ('tp', 'dp', 'ctx'), axis=0, tiled=True)]
    unnamed x9 -> x2, waiting for transfers between devices: 155 us -> 0.03 us
    pallas_call x0 -> x6, Pallas kernels: none -> 120 us  [the longest x1 32.3 us: attend_back(): pl.pallas_call(attend_back_kernel, out_shape=jax.ShapeDtypeStruct(triple....]
    another operation x5 -> x0, loops' own time: 98.8 us -> none  [the longest x2 47.3 us: attend_back(): return lax.map(one, jnp.arange(query_blocks.shape[0], dtype=jnp.int32))]
    reduce_sum x38 -> x4, other arithmetic: 65.6 us -> 1.26 us  [the longest x1 0.58 us: norm_back(): jnp.mean(e, axis=-1, keepdims=True)]
  transfers between devices with their start and end apart: 34 -> 15, of which waited for: 22 -> 8; matrix products, arithmetic and copies ran while one was open for 5% -> 12% of each run, Pallas kernels for 0% -> 26%
where the time goes in v1:
time: 323 us; the launch traced here: 322 us
  Pallas kernels  120 us (37%)
  waiting for transfers between devices  95.8 us (30%)
  local copies, waits for them, and re-layouts  29.9 us (9%)
  starting transfers between devices  24.6 us (8%)
  other arithmetic  23.2 us (7%)
  between operations  14.4 us (4%)
  blocking collectives  14.3 us (4%)
    pallas_call x1, Pallas kernels, attend_back(): pl.pallas_call(attend_back_kernel, out_shape=jax.ShapeDtypeStruct(triple....  32.3 us
    reduce_scatter x1, waiting for transfers between devices, local(): lax.psum_scatter(grad_wide.reshape(parts * d, wide.shape[1]), ('tp', 'dp'...  31.9 us
    pallas_call x1, Pallas kernels, attend(): pl.pallas_call(attend_kernel, out_shape=(jax.ShapeDtypeStruct((span, widt...  29 us
    ppermute x10, waiting for transfers between devices, swap(): lax.ppermute(array, ('ctx', 'tp'), [(n, n ^ mask) for n in range(group)])  27.7 us
    pallas_call x1, Pallas kernels, middle(): pl.pallas_call(middle_kernel, out_shape=(sds((rows, d), BF16), sds((rows,...  21.6 us
    all_to_all x1, blocking collectives, local(): grad_mix = lax.all_to_all(grad_mix, ('ctx', 'tp'), 0, 0, tiled=True)  14.3 us
    all_to_all x1, waiting for transfers between devices, local(): lax.all_to_all(narrow_grad.reshape(shards, tall, 3 * width + EXT), ('dp',...  14.3 us
    pallas_call x1, Pallas kernels, weights(): pl.pallas_call(weights_kernel, out_shape=jax.ShapeDtypeStruct((parts, d,...  13.6 us
  transfers between devices with their start and end apart: 15, of which 8 were waited for; matrix products, arithmetic and copies ran while one was open for 12% of the time, Pallas kernels for 26%

profile of v1, /device:TPU:0, one launch (start us, length us, event | category | flops | bytes accessed | tf_op | source)
XLA Modules:
  0.0 321.6 jit_solution(8926948870252744925)
XLA Ops:
  12.1 1.9 concatenate.22
  14.2 3.0 collective-permute-start.1
  17.2 1.5 collective-permute-start.2
  20.6 6.3 %all-to-all-start = ((bf16[8,96,640]{2,1,0:T(8,128)(2,1)}), bf16[8,96,640]{2,1,0:T(8,128)(2,1)S(1)}, u32[]{:S(2)}, u32[]{:S(2)}) async-start(bf16[8,96,640]{2,1,0:T(8,128)(2,1)} %broadcast_in_dim.42), calls=%async_computation | async-start | bytes 1966080 | tf_op jit(solution)/shard_map/all_to_all | solution.py:647
  27.5 16.3 %collective-permute-done.2 = bf16[256,768]{1,0:T(8,128)(2,1)} collective-permute-done((bf16[256,768]{1,0:T(8,128)(2,1)S(1)}, bf16[256,768]{1,0:T(8,128)(2,1)}, u32[]{:S(2)}, u32[]{:S(2)}) %collective-permute-start.2) | collective-permute-done | bytes 393248 | tf_op jit(solution)/shard_map/ppermute | solution.py:620
  43.9 1.3 pad_maximum_fusion.own_ref
  45.3 1.4 select_convert_fusion.1.order_ref
  46.7 12.0 %all-to-all-done = bf16[8,96,640]{2,1,0:T(8,128)(2,1)S(1)} async-done(((bf16[8,96,640]{2,1,0:T(8,128)(2,1)}), bf16[8,96,640]{2,1,0:T(8,128)(2,1)S(1)}, u32[]{:S(2)}, u32[]{:S(2)}) %all-to-all-start) | async-done | bytes 983072 | tf_op jit(solution)/shard_map/all_to_all | solution.py:647
  59.6 10.2 %project.1.q_ref.k_ref.v_ref.qkv_ref = bf16[3,2048,192]{2,1,0:T(8,128)(2,1)} custom-call(s32[1]{0:T(128)} %bitcast.2.me_ref, bf16[4,256,768]{2,1,0:T(8,128)(2,1)} %copy-done.2, bf16[4,256,768]{2,1,0:T(8,128)(2,1)} %collective-permute-done.3.far_ref, bf16[768,640]{1,0:T(8,128)(2,1)} %bitcast.105, bf16[768,576]{1,0:T(8,128)(2,1)} %select_convert_fusion.1.order_ref), custom_call_target="tpu_custom_call" | custom-call | flops 1811939328 | bytes 8000000 | tf_op jit(solution)/shard_map/project/pallas_call | solution.py:75
  69.8 29.0 %attend.1 = (bf16[2048,192]{1,0:T(8,128)(2,1)}, f32[192,2048]{1,0:T(8,128)}, f32[8,2048]{1,0:T(8,128)}) custom-call(bf16[3,2048,192]{2,1,0:T(8,128)(2,1)} %project.1.q_ref.k_ref.v_ref.qkv_ref, bf16[3,2048,192]{2,1,0:T(8,128)(2,1)} %project.1.q_ref.k_ref.v_ref.qkv_ref, bf16[3,2048,192]{2,1,0:T(8,128)(2,1)} %project.1.q_ref.k_ref.v_ref.qkv_ref), custom_call_target="tpu_custom_call" | custom-call | flops 3221225472 | bytes 8000000 | tf_op jit(solution)/shard_map/attend/pallas_call | solution.py:160
  98.8 2.2 copy.102
  101.0 4.0 %all-to-all-start.1 = ((bf16[8,256,192]{1,2,0:T(8,128)(2,1)}), bf16[8,256,192]{1,2,0:T(8,128)(2,1)S(1)}, u32[]{:S(2)}, u32[]{:S(2)}) async-start(bf16[8,256,192]{1,2,0:T(8,128)(2,1)} %copy.102), calls=%async_computation.1 | async-start | bytes 1572864 | tf_op jit(solution)/shard_map/all_to_all | solution.py:677
  105.2 1.5 select_convert_fusion.order_ref
  106.8 9.9 %all-to-all-done.1 = bf16[8,256,192]{1,2,0:T(8,128)(2,1)S(1)} async-done(((bf16[8,256,192]{1,2,0:T(8,128)(2,1)}), bf16[8,256,192]{1,2,0:T(8,128)(2,1)S(1)}, u32[]{:S(2)}, u32[]{:S(2)}) %all-to-all-start.1) | async-done | bytes 786464 | tf_op jit(solution)/shard_map/all_to_all | solution.py:677
  117.9 21.6 %middle.1 = (bf16[512,768]{1,0:T(8,128)(2,1)}, f32[512,768]{1,0:T(8,128)}, bf16[8,256,192]{2,1,0:T(8,128)(2,1)}, bf16[512,768]{1,0:T(8,128)(2,1)}, bf16[4,512,76...) custom-call(bf16[512,768]{1,0:T(8,128)(2,1)} %bitcast.104, ...), custom_call_target="tpu_custom_call" | custom-call | flops 10871635968 | bytes 30000000 | tf_op jit(solution)/shard_map/middle/pallas_call | solution.py:394
  139.6 13.6 %weights.1 = bf16[4,768,1792]{2,1,0:T(8,128)(2,1)} custom-call(bf16[512,768]{1,0:T(8,128)(2,1)} %get-tuple-element.42.n2_ref, bf16[512,768]{1,0:T(8,128)(2,1)} %bitcast.116, bf16[512,768]{1,0:T(8,128)(2,1)} %get-tuple-element.43.gb_ref, bf16[2,4,256,192]{3,2,1,0:T(8,128)(2,1)} %bitcast.108, bf16[4,512,768]{2,1,0:T(8,128)(2,1)} %get-tuple-element.44.act_ref, ...), custom_call_target="tpu_custom_call" | custom-call | flops 5435817984 | bytes 25000000 | tf_op jit(solution)/shard_map/weights/pallas_call | solution.py:471
  154.9 14.3 %all_to_all.20 = bf16[8,256,192]{1,2,0:T(8,128)(2,1)S(1)} all-to-all(bf16[8,256,192]{1,2,0:T(8,128)(2,1)S(1)} %copy.110), channel_id=1, replica_groups=mesh['dp'=4,'ctx'=2,'tp'=4] {'ctx','tp'}, dimensions={0} | all-to-all | bytes 1572864 | tf_op jit(solution)/shard_map/all_to_all | solution.py:684
  169.3 1.3 copy.111
  170.6 32.3 %attend_back.1.grad_ref = bf16[3,2048,192]{2,1,0:T(8,128)(2,1)} custom-call(bf16[3,2048,192]{2,1,0:T(8,128)(2,1)} %project.1.q_ref.k_ref.v_ref.qkv_ref, bf16[2048,192]{1,0:T(8,128)(2,1)} %bitcast.113, f32[192,2048]{1,0:T(8,128)} %get-tuple-element.35.ot_ref, f32[8,2048]{1,0:T(8,128)} %get-tuple-element.36.level_ref), custom_call_target="tpu_custom_call" | custom-call | flops 8053063680 | bytes 10000000 | tf_op jit(solution)/shard_map/attend_back/pallas_call | solution.py:275
  202.9 12.7 %project_back.1 = (f32[4,256,768]{2,1,0:T(8,128)}, bf16[4,256,768]{2,1,0:T(8,128)(2,1)}, bf16[3,768,192]{2,1,0:T(8,128)(2,1)}, f32[8,768]{1,0:T(8,128)}, f32[8,192]{1,0:T(8,128)}) custom-call(s32[1]{0:T(128)} %bitcast.2.me_ref, bf16[4,256,768]{2,1,0:T(8,128)(2,1)} %copy-done.2, bf16[4,256,768]{2,1,0:T(8,128)(2,1)} %collective-permute-done.3.far_ref, ...), custom_call_target="tpu_custom_call" | custom-call | flops 3623878656 | bytes 15000000 | tf_op jit(solution)/shard_map/project_back/pallas_call | solution.py:547
  218.6 1.4 collective-permute-start.9
  220.1 1.7 copy.113
  223.0 6.7 %maximum_maximum_fusion = bf16[8,96,640]{1,0,2:T(8,128)(2,1)S(1)} fusion(bf16[8,96,1]{1,0,2:T(8,128)(2,1)S(1)} %pad_bitcast_fusion, bf16[8,96,2]{1,0,2:T(8,128)(2,1)S(1)} %concatenate.24, bf16[8,96,576]{1,0,2:T(8,128)(2,1)S(1)} %concatenate.23, bf16[640]{0:T(1024)(128)(2,1)S(1)} %pad.14.clone), kind=kLoop, calls=%fused_computation.25 | loop fusion | flops 1474560 | bytes 1873664 | tf_op jit(solution)/shard_map/concatenate | solution.py:709
  229.7 1.9 copy.115
  231.6 4.0 %all-to-all-start.3 = ((bf16[8,96,640]{2,1,0:T(8,128)(2,1)}), bf16[8,96,640]{2,1,0:T(8,128)(2,1)S(1)}, u32[]{:S(2)}, u32[]{:S(2)}) async-start(bf16[8,96,640]{2,1,0:T(8,128)(2,1)} %copy.115), calls=%async_computation.3 | async-start | bytes 1966080 | tf_op jit(solution)/shard_map/all_to_all | solution.py:718
  236.2 4.6 %fusion.64 = (bf16[4,256,768]{2,1,0:T(8,128)(2,1)S(1)}, f32[4,256,768]{2,1,0:T(8,128)}) fusion(f32[4,256,768]{2,1,0:T(8,128)} %get-tuple-element.37, bf16[4,256,768]{2,1,0:T(8,128)(2,1)} %collective-permute-done.4), kind=kLoop, calls=%fused_computation.123 | loop fusion | flops 2359296 | bytes 9437184 | tf_op jit(solution)/shard_map/convert.9
  240.9 2.0 collective-permute-start.5
  245.6 14.3 %all-to-all-done.3 = bf16[8,96,640]{2,1,0:T(8,128)(2,1)S(1)} async-done(((bf16[8,96,640]{2,1,0:T(8,128)(2,1)}), bf16[8,96,640]{2,1,0:T(8,128)(2,1)S(1)}, u32[]{:S(2)}, u32[]{:S(2)}) %all-to-all-start.3) | async-done | bytes 983072 | tf_op jit(solution)/shard_map/all_to_all | solution.py:718
  262.8 10.4 %collective-permute-done.6 = bf16[256,768]{1,0:T(8,128)(2,1)} collective-permute-done((bf16[256,768]{1,0:T(8,128)(2,1)S(1)}, bf16[256,768]{1,0:T(8,128)(2,1)}, u32[]{:S(2)}, u32[]{:S(2)}) %collective-permute-start.6) | collective-permute-done | bytes 393248 | tf_op jit(solution)/shard_map/ppermute | solution.py:620
  273.2 1.7 fusion.17
  276.4 1.7 fusion.5
  278.1 31.9 %reduce-scatter.2.cloned.1.call-done = bf16[96,1792]{1,0:T(8,128)(2,1)} async-done(((bf16[3072,1792]{1,0:T(8,128)(2,1)}), bf16[96,1792]{1,0:T(8,128)(2,1)}) %reduce-scatter.2.cloned.1.call-update) | async-done | bytes 344080 | tf_op jit(solution)/shard_map/reduce_scatter | solution.py:686
  (93 shorter events, 28.5 us)
Async XLA Ops:
  7.2 6.9 %copy-start = (bf16[2,1,256,768]{3,2,1,0:T(8,128)(2,1)S(1)}, bf16[2,1,256,768]{3,2,1,0:T(8,128)(2,1)}, u32[]{:S(2)}) copy-start(bf16[2,1,256,768]{3,2,1,0:T(8,128)(2,1)} %param.14) | copy-start | bytes 2359300
  7.2 110.8 %all-gather.2.cloned.1.call-start = ((), (), s32[]{:S(2)}) async-start(), calls=%async_computation.5 | async-start | bytes 11354112 | tf_op jit(solution)/shard_map/all_gather | solution.py:665
  12.1 6.7 %copy-start.7 = (bf16[3,96,192]{2,1,0:T(8,128)(2,1)S(1)}, bf16[3,96,192]{2,1,0:T(8,128)(2,1)}, u32[]{:S(2)}) copy-start(bf16[3,96,192]{2,1,0:T(8,128)(2,1)} %param.18) | copy-start | bytes 331780
  12.1 6.8 %copy-start.8 = (bf16[3,3,8]{2,1,0:T(4,128)(2,1)S(1)}, bf16[3,3,8]{2,1,0:T(4,128)(2,1)}, u32[]{:S(2)}) copy-start(bf16[3,3,8]{2,1,0:T(4,128)(2,1)} %param.19) | copy-start | bytes 436
  12.1 6.9 %copy-start.9 = (bf16[96]{0:T(256)(128)(2,1)S(1)}, bf16[96]{0:T(256)(128)(2,1)}, u32[]{:S(2)}) copy-start(bf16[96]{0:T(256)(128)(2,1)} %param.16) | copy-start | bytes 580
  12.1 6.9 %copy-start.10 = (bf16[96]{0:T(256)(128)(2,1)S(1)}, bf16[96]{0:T(256)(128)(2,1)}, u32[]{:S(2)}) copy-start(bf16[96]{0:T(256)(128)(2,1)} %param.17) | copy-start | bytes 580
  14.2 13.4 %collective-permute-start.1 = (bf16[256,768]{1,0:T(8,128)(2,1)S(1)}, bf16[256,768]{1,0:T(8,128)(2,1)S(1)}, u32[]{:S(2)}, u32[]{:S(2)}) collective-permute-start(bf16[256,768]{1,0:T(8,128)(2,1)S(1)} %get-tuple-element.138), channel_id=1, source_target_pairs={{0,4},{1,5},{2,6},{3,7},{4,0},{5,1},{6,2},{7,3},{8,12},{9,13},{10,... | collective-permute-start | bytes 1179656 | tf_op jit(solution)/shard_map/ppermute | solution.py:620
  17.2 26.7 %collective-permute-start.2 = (bf16[256,768]{1,0:T(8,128)(2,1)S(1)}, bf16[256,768]{1,0:T(8,128)(2,1)}, u32[]{:S(2)}, u32[]{:S(2)}) collective-permute-start(bf16[256,768]{1,0:T(8,128)(2,1)S(1)} %get-tuple-element.138), channel_id=1, source_target_pairs={{0,6},{1,7},{2,4},{3,5},{4,2},{5,3},{6,0},{7,1},{8,14},{9,15},{10,... | collective-permute-start | bytes 1179656 | tf_op jit(solution)/shard_map/ppermute | solution.py:620
  18.7 25.2 %collective-permute-start = (bf16[256,768]{1,0:T(8,128)(2,1)S(1)}, bf16[256,768]{1,0:T(8,128)(2,1)}, u32[]{:S(2)}, u32[]{:S(2)}) collective-permute-start(bf16[256,768]{1,0:T(8,128)(2,1)S(1)} %get-tuple-element.137), channel_id=1, source_target_pairs={{0,2},{1,3},{2,0},{3,1},{4,6},{5,7},{6,4},{7,5},{8,10},{9,11},{10,... | collective-permute-start | bytes 1179656 | tf_op jit(solution)/shard_map/ppermute | solution.py:620
  20.6 38.1 %all-to-all-start = ((bf16[8,96,640]{2,1,0:T(8,128)(2,1)}), bf16[8,96,640]{2,1,0:T(8,128)(2,1)S(1)}, u32[]{:S(2)}, u32[]{:S(2)}) async-start(bf16[8,96,640]{2,1,0:T(8,128)(2,1)} %broadcast_in_dim.42), calls=%async_computation | async-start | bytes 1966080 | tf_op jit(solution)/shard_map/all_to_all | solution.py:647
  45.2 13.4 %copy-start.2 = (bf16[4,256,768]{2,1,0:T(8,128)(2,1)}, bf16[4,256,768]{2,1,0:T(8,128)(2,1)S(1)}, u32[]{:S(2)}) copy-start(bf16[4,256,768]{2,1,0:T(8,128)(2,1)S(1)} %pad_maximum_fusion.own_ref) | copy-start | bytes 4718596
  45.2 13.4 %collective-permute-start.3 = (bf16[4,256,768]{2,1,0:T(8,128)(2,1)S(1)}, bf16[4,256,768]{2,1,0:T(8,128)(2,1)}, u32[]{:S(2)}, u32[]{:S(2)}) collective-permute-start(bf16[4,256,768]{2,1,0:T(8,128)(2,1)S(1)} %pad_maximum_fusion.own_ref), channel_id=1, source_target_pairs={{0,1},{1,0},{2,3},{3,2},{4,5},{5,4},{6,7},{7,6},{8,9},{9,8},{10,11... | collective-permute-start | bytes 4718600 | tf_op jit(solution)/shard_map/ppermute | solution.py:620
  58.6 1.0 copy-start.3
  101.0 15.6 %all-to-all-start.1 = ((bf16[8,256,192]{1,2,0:T(8,128)(2,1)}), bf16[8,256,192]{1,2,0:T(8,128)(2,1)S(1)}, u32[]{:S(2)}, u32[]{:S(2)}) async-start(bf16[8,256,192]{1,2,0:T(8,128)(2,1)} %copy.102), calls=%async_computation.1 | async-start | bytes 1572864 | tf_op jit(solution)/shard_map/all_to_all | solution.py:677
  105.0 205.0 %reduce-scatter.2.cloned.1.call-start = ((), (), s32[]{:S(2)}) async-start(), calls=%async_computation.6 | async-start | bytes 11354112 | tf_op jit(solution)/shard_map/reduce_scatter | solution.py:686
  153.2 1.2 copy-start.6
  216.4 1.5 collective-permute-start.8
  217.4 18.8 %collective-permute-start.4 = (bf16[4,256,768]{2,1,0:T(8,128)(2,1)}, bf16[4,256,768]{2,1,0:T(8,128)(2,1)}, u32[]{:S(2)}, u32[]{:S(2)}) collective-permute-start(bf16[4,256,768]{2,1,0:T(8,128)(2,1)} %get-tuple-element.38), channel_id=1, source_target_pairs={{0,1},{1,0},{2,3},{3,2},{4,5},{5,4},{6,7},{7,6},{8,9},{9,8},{10,11... | collective-permute-start | bytes 4718600 | tf_op jit(solution)/shard_map/ppermute | solution.py:620
  218.6 4.3 %collective-permute-start.9 = (f32[2,768]{1,0:T(2,128)S(1)}, f32[2,768]{1,0:T(2,128)S(1)}, u32[]{:S(2)}, u32[]{:S(2)}) collective-permute-start(f32[2,768]{1,0:T(2,128)S(1)} %slice_add_fusion), channel_id=1, source_target_pairs={{0,2},{1,3},{2,0},{3,1},{4,6},{5,7},{6,4},{7,5},{8,10},{9,11},{10,... | collective-permute-start | bytes 18440 | tf_op jit(solution)/shard_map/ppermute | solution.py:620
  229.7 5.9 %copy-start.1 = (bf16[2,1,256,768]{3,2,1,0:T(8,128)(2,1)S(1)}, bf16[2,1,256,768]{3,2,1,0:T(8,128)(2,1)}, u32[]{:S(2)}) copy-start(bf16[2,1,256,768]{3,2,1,0:T(8,128)(2,1)} %param.14) | copy-start | bytes 2359300
  231.6 28.3 %all-to-all-start.3 = ((bf16[8,96,640]{2,1,0:T(8,128)(2,1)}), bf16[8,96,640]{2,1,0:T(8,128)(2,1)S(1)}, u32[]{:S(2)}, u32[]{:S(2)}) async-start(bf16[8,96,640]{2,1,0:T(8,128)(2,1)} %copy.115), calls=%async_computation.3 | async-start | bytes 1966080 | tf_op jit(solution)/shard_map/all_to_all | solution.py:718
  240.9 21.9 %collective-permute-start.5 = (bf16[256,768]{1,0:T(8,128)(2,1)S(1)}, bf16[256,768]{1,0:T(8,128)(2,1)}, u32[]{:S(2)}, u32[]{:S(2)}) collective-permute-start(bf16[256,768]{1,0:T(8,128)(2,1)S(1)} %get-tuple-element.135), channel_id=1, source_target_pairs={{0,4},{1,5},{2,6},{3,7},{4,0},{5,1},{6,2},{7,3},{8,12},{9,13},{10,... | collective-permute-start | bytes 1179656 | tf_op jit(solution)/shard_map/ppermute | solution.py:620
  242.9 30.3 %collective-permute-start.6 = (bf16[256,768]{1,0:T(8,128)(2,1)S(1)}, bf16[256,768]{1,0:T(8,128)(2,1)}, u32[]{:S(2)}, u32[]{:S(2)}) collective-permute-start(bf16[256,768]{1,0:T(8,128)(2,1)S(1)} %get-tuple-element.134), channel_id=1, source_target_pairs={{0,6},{1,7},{2,4},{3,5},{4,2},{5,3},{6,0},{7,1},{8,14},{9,15},{10,... | collective-permute-start | bytes 1179656 | tf_op jit(solution)/shard_map/ppermute | solution.py:620
  243.7 29.5 %collective-permute-start.7 = (bf16[256,768]{1,0:T(8,128)(2,1)S(1)}, bf16[256,768]{1,0:T(8,128)(2,1)}, u32[]{:S(2)}, u32[]{:S(2)}) collective-permute-start(bf16[256,768]{1,0:T(8,128)(2,1)S(1)} %get-tuple-element.133), channel_id=1, source_target_pairs={{0,2},{1,3},{2,0},{3,1},{4,6},{5,7},{6,4},{7,5},{8,10},{9,11},{10,... | collective-permute-start | bytes 1179656 | tf_op jit(solution)/shard_map/ppermute | solution.py:620
  275.0 1.4 copy-start.4
  310.0 4.1 %copy-start.5 = (bf16[96,1792]{1,0:T(8,128)(2,1)S(1)}, bf16[96,1792]{1,0:T(8,128)(2,1)}, u32[]{:S(2)}) copy-start(bf16[96,1792]{1,0:T(8,128)(2,1)} %reduce-scatter.2.cloned.1.call-done) | copy-start | bytes 1032196
Sparse Core Ops, SparseCore 0:
  14.2 101.2 all-gather.1
  153.3 156.6 reduce-scatter.1

commit v2 on v1

--- a/solution.py
+++ b/solution.py
@@ -47,7 +47,61 @@
     return pl.CostEstimate(flops=int(flops), bytes_accessed=int(moved), transcendentals=int(exps))
 
 
-def project_kernel(me_ref, own_ref, far_ref, w_ref, order_ref, out_ref, vec_ref, bias_ref):
+def pack_kernel(fc_ref, pj_ref, out_ref, qkv_ref, vec_ref, qb_ref, fb_ref, wide_ref, narrow_ref):
+    tall, d = fc_ref.shape
+    width = out_ref.shape[0]
+    copies = narrow_ref.shape[0]
+    columns = jnp.transpose(vec_ref[...].astype(F32)).astype(BF16)
+    wide_ref[:, :d] = fc_ref[...]
+    wide_ref[:, d : 2 * d] = jnp.transpose(pj_ref[...].astype(F32)).astype(BF16)
+    wide_ref[:, 2 * d : 2 * d + width] = jnp.transpose(out_ref[...].astype(F32)).astype(BF16)
+    edge = 2 * d + width
+    wide_ref[:, edge:] = jnp.zeros((tall, EXT), BF16)
+    wide_ref[:, edge : edge + 4] = columns[:, 2:6]
+    rows, strip = fb_ref.shape
+    wide_ref[:rows, edge + 8 : edge + 8 + strip] = fb_ref[...]
+    for s in range(3):
+        narrow_ref[0, :, s * width : (s + 1) * width] = qkv_ref[s]
+    edge = 3 * width
+    narrow_ref[0, :, edge:] = jnp.zeros((tall, EXT), BF16)
+    narrow_ref[0, :, edge : edge + 2] = columns[:, :2]
+    heads, piece = qb_ref.shape[1:]
+    for s in range(3):
+        narrow_ref[0, s * heads : (s + 1) * heads, edge + 8 : edge + 8 + piece] = qb_ref[s]
+    whole = narrow_ref[0]
+    for n in range(1, copies):
+        narrow_ref[n] = whole
+
+
+def pack(fc, pj, out, qkv, vec, qb, fb, copies):
+    tall, d = fc.shape
+    width = out.shape[0]
+    return pl.pallas_call(
+        pack_kernel,
+        out_shape=(
+            jax.ShapeDtypeStruct((tall, 2 * d + width + EXT), BF16),
+            jax.ShapeDtypeStruct((copies, tall, 3 * width + EXT), BF16),
+        ),
+        compiler_params=pltpu.CompilerParams(vmem_limit_bytes=VMEM_LIMIT),
+        cost_estimate=cost(0, 2e6),
+        name="pack",
+    )(fc, pj, out, qkv, vec, qb, fb)
+
+
+def pick_rows(table, period):
+    line = lax.broadcasted_iota(jnp.int32, table.shape, 0)
+    lane = lax.broadcasted_iota(jnp.int32, table.shape, 1)
+    return jnp.sum(jnp.where(line == (lane & (period - 1)), table, 0.0), axis=0, keepdims=True)
+
+
+def spread_rows(row, lines, period):
+    shape = (lines, row.shape[1])
+    line = lax.broadcasted_iota(jnp.int32, shape, 0)
+    lane = lax.broadcasted_iota(jnp.int32, shape, 1)
+    return jnp.where(line == (lane & (period - 1)), jnp.broadcast_to(row, shape), 0.0).astype(BF16)
+
+
+def project_kernel(piece, me_ref, own_ref, far_ref, w_ref, order_ref, out_ref, vec_ref, bias_ref):
     i = pl.program_id(0)
     width = out_ref.shape[2]
 
@@ -55,25 +109,26 @@
     def _():
         turned = jnp.transpose(w_ref[:, 512:640].astype(F32))
         vec_ref[...] = turned[64:72]
-        bias_ref[...] = dot(turned[64:72].astype(BF16), order_ref[...])
+        table = dot(turned[72:80].astype(BF16), order_ref[...])
+        bias_ref[...] = jnp.broadcast_to(pick_rows(table, piece), bias_ref.shape)
 
     far = ((i ^ me_ref[0]) & 1) == 1
     rows = jnp.where(far, far_ref[0], own_ref[0]).astype(F32)
     n, _ = norm_parts(rows)
     normed = (n * vec_ref[0:1] + vec_ref[1:2]).astype(BF16)
-    full = dot(normed, w_ref[...])[:, : 3 * width] + bias_ref[2:3, :]
+    full = dot(normed, w_ref[...])[:, : 3 * width] + bias_ref[0:1, :]
     full = full.astype(BF16)
     out_ref[0] = full[:, :width] * jnp.asarray(HD ** (-0.5), BF16)
     out_ref[1] = full[:, width : 2 * width]
     out_ref[2] = full[:, 2 * width :]
 
 
-def project(me, own, far, w, order):
+def project(me, own, far, w, order, piece):
     half, rows, d = own.shape
     blocks = 2 * half
     width = order.shape[1] // 3
     return pl.pallas_call(
-        project_kernel,
+        functools.partial(project_kernel, piece),
         out_shape=jax.ShapeDtypeStruct((3, blocks * rows, width), BF16),
         grid_spec=pltpu.PrefetchScalarGridSpec(
             num_scalar_prefetch=1,
@@ -150,17 +205,19 @@
         total = l_ref[h : h + 1, :]
         level_ref[h : h + 1, :] = m_ref[h : h + 1, :] + jnp.log2(total)
         ot_ref[h * HD : (h + 1) * HD, :] = ot_ref[h * HD : (h + 1) * HD, :] * (1.0 / total)
-    o_ref[...] = jnp.transpose(ot_ref[...]).astype(BF16)
-
-
-def attend(triple):
+    rows = o_ref.shape[2]
+    for n in range(bq // rows):
+        o_ref[n] = ot_ref[:, n * rows : (n + 1) * rows].astype(BF16)
+
+
+def attend(triple, rows):
     _, span, width = triple.shape
     bq = min(512, span)
     heads = width // HD
     return pl.pallas_call(
         attend_kernel,
         out_shape=(
-            jax.ShapeDtypeStruct((span, width), BF16),
+            jax.ShapeDtypeStruct((span // rows, width, rows), BF16),
             jax.ShapeDtypeStruct((width, span), F32),
             jax.ShapeDtypeStruct((8, span), F32),
         ),
@@ -171,7 +228,7 @@
             pl.BlockSpec((1, span, width), lambda i: (2, 0, 0)),
         ],
         out_specs=(
-            pl.BlockSpec((bq, width), lambda i: (i, 0)),
+            pl.BlockSpec((bq // rows, width, rows), lambda i: (i, 0, 0)),
             pl.BlockSpec((width, bq), lambda i: (0, i)),
             pl.BlockSpec((8, bq), lambda i: (0, i)),
         ),
@@ -192,7 +249,8 @@
 ):
     j = pl.program_id(0)
     blocks = pl.num_programs(0)
-    span, width = grad_ref.shape
+    span, width = qkv_ref.shape[1:]
+    rows = grad_ref.shape[2]
     heads = width // HD
     count = qm_ref.shape[0]
     b = span // count
@@ -200,19 +258,24 @@
 
     @pl.when(j == 0)
     def _():
-        turned = jnp.transpose(grad_ref[...].astype(F32))
-        prod = turned * ot_ref[...]
-        for h in range(heads):
-            dot_ref[h : h + 1, :] = jnp.sum(prod[h * HD : (h + 1) * HD], axis=0, keepdims=True)
+        for n in range(span // rows):
+            cols = slice(n * rows, (n + 1) * rows)
+            turned = grad_ref[n].astype(F32)
+            prod = turned * ot_ref[:, cols]
+            for h in range(heads):
+                dot_ref[h : h + 1, cols] = jnp.sum(prod[h * HD : (h + 1) * HD], axis=0, keepdims=True)
+            g = jnp.transpose(turned).astype(BF16)
+            at = n * rows % b
+            for h in range(heads):
+                mask = head_mask(g.shape, h)
+                gm_ref[n * rows // b, h * b + at : h * b + at + rows, :] = jnp.where(mask, g, jnp.zeros_like(g))
         kt_ref[...] = jnp.transpose(qkv_ref[1].astype(F32)).astype(BF16)
         dqt_ref[...] = jnp.zeros_like(dqt_ref)
         for n in range(count):
             q = qkv_ref[0, n * b : (n + 1) * b, :]
-            g = grad_ref[n * b : (n + 1) * b, :]
             for h in range(heads):
                 mask = head_mask(q.shape, h)
                 qm_ref[n, h * b : (h + 1) * b, :] = jnp.where(mask, q, jnp.zeros_like(q))
-                gm_ref[n, h * b : (h + 1) * b, :] = jnp.where(mask, g, jnp.zeros_like(g))
 
     dk_ref[...] = jnp.zeros_like(dk_ref)
     dv_ref[...] = jnp.zeros_like(dv_ref)
@@ -308,6 +371,7 @@
 
 
 def middle_kernel(
+    strip,
     tok_ref,
     cot_ref,
     mix_ref,
@@ -330,17 +394,18 @@
 ):
     t = pl.program_id(0)
     steps = pl.num_programs(0)
-    half = mix_ref.shape[1]
+    half = mix_ref.shape[2]
     parts = gout_ref.shape[0]
     d = tok_ref.shape[1]
-    width = mix_ref.shape[2]
+    width = mix_ref.shape[1]
 
     @pl.when(t == 0)
     def _():
         ext_ref[...] = jnp.transpose(gout_ref[0, :, 128:256].astype(F32))[64:72]
         total = tok_ref[...].astype(F32) + ext_ref[2:3]
         for s in range(parts):
-            lhs = jnp.concatenate([mix_ref[s], mix_ref[parts + s]], axis=0)
+            lhs = jnp.concatenate([mix_ref[s], mix_ref[parts + s]], axis=1)
+            lhs = jnp.transpose(lhs.astype(F32)).astype(BF16)
             total = total + dot_nt(lhs, gout_ref[s, :, :width])
         hid_ref[...] = total
         n, _ = norm_parts(total)
@@ -348,8 +413,8 @@
         acc_ref[...] = total + ext_ref[3:4]
         back_ref[...] = jnp.zeros_like(back_ref)
 
-    ext = jnp.transpose(g_ref[0, :, 2 * d + 128 : 2 * d + 256].astype(F32))[64:72].astype(BF16)
-    bias = dot(ext, order_ref[...])[4:5]
+    ext = jnp.transpose(g_ref[0, :, 2 * d + 128 : 2 * d + 256].astype(F32))[72:88].astype(BF16)
+    bias = pick_rows(dot(ext, order_ref[...]), strip)
     fc = g_ref[0, :, :d]
     pj = g_ref[0, :, d : 2 * d]
     lifted = dot(n2_ref[...], fc) + bias
@@ -379,12 +444,12 @@
         vec_ref[3:4, :] = jnp.sum(cot, axis=0, keepdims=True)
         vec_ref[4:8, :] = jnp.zeros((4, d), F32)
         for s in range(parts):
-            dm = dot(gb, gout_ref[s, :, :width]).astype(BF16)
-            dmix_ref[s] = dm[:half]
-            dmix_ref[parts + s] = dm[half:]
-
-
-def middle(tok, cot, mix, gathered, order):
+            dm = jnp.transpose(dot(gb, gout_ref[s, :, :width])).astype(BF16)
+            dmix_ref[s] = dm[:, :half]
+            dmix_ref[parts + s] = dm[:, half:]
+
+
+def middle(tok, cot, mix, gathered, order, strip):
     rows, d = tok.shape
     parts = gathered.shape[0]
     cols = gathered.shape[2]
@@ -392,7 +457,7 @@
     piece = lambda *shape: pl.BlockSpec(shape, lambda t: (t,) + (0,) * (len(shape) - 1))
     sds = jax.ShapeDtypeStruct
     return pl.pallas_call(
-        middle_kernel,
+        functools.partial(middle_kernel, strip),
         out_shape=(
             sds((rows, d), BF16),
             sds((rows, d), F32),
@@ -437,70 +502,164 @@
 
 
 def weights_kernel(
-    n2_ref, cot_ref, gb_ref, mix_ref, act_ref, gl_ref, vec_ref, gfb_ref, order_ref, out_ref, nt_ref, ct_ref, bt_ref
+    mode, strip, index_ref, n2_ref, cot_ref, gb_ref, mix_ref, act_ref, gl_ref, vec_ref, gfb_ref, order_ref, *rest
 ):
-    t = pl.program_id(0)
+    s = pl.program_id(0)
     d = n2_ref.shape[1]
-    width = mix_ref.shape[3]
-
-    @pl.when(t == 0)
+    width = mix_ref.shape[2]
+    cols = 2 * d + width + EXT
+    nt_ref, ct_ref, bt_ref = rest[-3:]
+
+    @pl.when(s == 0)
     def _():
         nt_ref[...] = jnp.transpose(n2_ref[...].astype(F32)).astype(BF16)
         ct_ref[...] = jnp.transpose(cot_ref[...].astype(F32)).astype(BF16)
         bt_ref[...] = jnp.transpose(gb_ref[...].astype(F32)).astype(BF16)
 
-    out_ref[0, :, :d] = dot(nt_ref[...], gl_ref[0]).astype(BF16)
-    out_ref[0, :, d : 2 * d] = dot(ct_ref[...], act_ref[0]).astype(BF16)
-    mix = jnp.concatenate([mix_ref[0, 0], mix_ref[1, 0]], axis=0)
-    out_ref[0, :, 2 * d : 2 * d + width] = dot(bt_ref[...], mix).astype(BF16)
-    turned = dot_nt(gfb_ref[0].astype(BF16), order_ref[...])
-    line = lax.broadcasted_iota(jnp.int32, turned.shape, 0)
-    rows = jnp.where(line == 4, turned[0:1], vec_ref[...])
-    tall = jnp.concatenate([rows, jnp.zeros((EXT - 8, d), F32)], axis=0)
-    out_ref[0, :, 2 * d + width :] = jnp.transpose(tall).astype(BF16)
-
-
-def weights(n2, cot, gb, mix, act, gl, vec, gfb, order):
+    mix = jnp.concatenate([mix_ref[0, 0], mix_ref[1, 0]], axis=1)
+    turned = dot_nt(spread_rows(gfb_ref[0, 0:1], 16, strip), order_ref[...])
+    tall = jnp.concatenate([vec_ref[...], turned, jnp.zeros((EXT - 24, d), F32)], axis=0)
+    if mode != "keep":
+        out_ref = rest[0]
+        out_ref[0, :, :d] = dot(nt_ref[...], gl_ref[0]).astype(BF16)
+        out_ref[0, :, d : 2 * d] = dot(ct_ref[...], act_ref[0]).astype(BF16)
+        out_ref[0, :, 2 * d : 2 * d + width] = dot_nt(bt_ref[...], mix).astype(BF16)
+        out_ref[0, :, 2 * d + width :] = jnp.transpose(tall).astype(BF16)
+        return
+    came_ref, as_ref, ak_ref, bs_ref, bk_ref, sum_ref = rest[:6]
+    sum_ref[:, 2 * d : 2 * d + width] = dot_nt(bt_ref[...], mix).astype(BF16)
+    sum_ref[:, 2 * d + width :] = jnp.transpose(tall).astype(BF16)
+    sum_ref[:, 2 * d :] = (sum_ref[:, 2 * d :].astype(F32) + came_ref[0, :, 2 * d :].astype(F32)).astype(BF16)
+    sum_ref[:, :d] = (dot(nt_ref[...], gl_ref[0]) + came_ref[0, :, :d].astype(F32)).astype(BF16)
+    sum_ref[:, d : 2 * d] = (dot(ct_ref[...], act_ref[0]) + came_ref[0, :, d : 2 * d].astype(F32)).astype(BF16)
+    depth, step = as_ref.shape[1], as_ref.shape[2]
+    order = halving_order(depth)
+    cut = cols // 2
+
+    def block(xr, zr):
+        at = ((order[zr] ^ index_ref[2]) * 2 + (xr ^ index_ref[3])) * step
+        return pl.ds(pl.multiple_of(at, 16), step)
+
+    for zr in range(depth):
+        bk_ref[0, zr] = sum_ref[block(0, zr), cut:]
+        bs_ref[0, zr] = sum_ref[block(1, zr), cut:]
+
+    @pl.when(s == 0)
+    def _():
+        for xr in range(2):
+            for zr in range(depth):
+                as_ref[xr, zr] = sum_ref[block(xr, zr), :cut]
+
+    @pl.when(s == 1)
+    def _():
+        for xr in range(2):
+            for zr in range(depth):
+                ak_ref[xr, zr] = sum_ref[block(xr, zr), :cut]
+
+
+def halving_order(count):
+    bits = count.bit_length() - 1
+    return [int(format(n, "b").zfill(bits)[::-1], 2) if bits else 0 for n in range(count)]
+
+
+def weights(mode, index, n2, cot, gb, mix, act, gl, vec, gfb, order, strip, came=None, shards=None):
     rows, d = n2.shape
     parts = act.shape[0]
-    width = mix.shape[2]
+    width = mix.shape[1]
     cols = 2 * d + width + EXT
-    whole = lambda *shape: pl.BlockSpec(shape, lambda t: (0,) * len(shape))
-    piece = lambda *shape: pl.BlockSpec(shape, lambda t: (t,) + (0,) * (len(shape) - 1))
-    mix = mix.reshape(mix.shape[0] // parts, parts, mix.shape[1], width)
+    steps = parts if mode == "all" else 2
+    whole = lambda *shape: pl.BlockSpec(shape, lambda s, ix: (0,) * len(shape))
+    piece = lambda *shape: pl.BlockSpec(shape, lambda s, ix: (ix[s],) + (0,) * (len(shape) - 1))
+    mix = mix.reshape(mix.shape[0] // parts, parts, width, mix.shape[2])
+    operands = [index, n2, cot, gb, mix, act, gl, vec, gfb, order]
+    specs = [
+        whole(rows, d),
+        whole(rows, d),
+        whole(rows, d),
+        pl.BlockSpec((mix.shape[0], 1, width, mix.shape[3]), lambda s, ix: (0, ix[s], 0, 0)),
+        piece(1, rows, d),
+        piece(1, rows, d),
+        whole(8, d),
+        piece(1, 8, d),
+        whole(*order.shape),
+    ]
+    scratch = [pltpu.VMEM((d, rows), BF16) for _ in range(3)]
+    if mode == "keep":
+        operands.append(came)
+        specs.append(pl.BlockSpec((1, d, cols), lambda s, ix: (s, 0, 0)))
+        block = (2, shards // 2, d // shards, cols // 2)
+        sds = jax.ShapeDtypeStruct(block, BF16)
+        out_shape = (sds,) * 4
+        turn = pl.BlockSpec((1,) + block[1:], lambda s, ix: (1 - s, 0, 0, 0))
+        out_specs = (whole(*block), whole(*block), turn, turn)
+        scratch = [pltpu.VMEM((d, cols), BF16)] + scratch
+    else:
+        out_shape = jax.ShapeDtypeStruct((steps, d, cols), BF16)
+        out_specs = pl.BlockSpec((1, d, cols), lambda s, ix: (s, 0, 0))
     return pl.pallas_call(
-        weights_kernel,
-        out_shape=jax.ShapeDtypeStruct((parts, d, cols), BF16),
-        grid=(parts,),
-        in_specs=[
-            whole(rows, d),
-            whole(rows, d),
-            whole(rows, d),
-            pl.BlockSpec((mix.shape[0], 1, mix.shape[2], width), lambda t: (0, t, 0, 0)),
-            piece(1, rows, d),
-            piece(1, rows, d),
-            whole(8, d),
-            piece(1, 8, d),
-            whole(*order.shape),
-        ],
-        out_specs=piece(1, d, cols),
-        scratch_shapes=[
-            pltpu.VMEM((d, rows), BF16),
-            pltpu.VMEM((d, rows), BF16),
-            pltpu.VMEM((d, rows), BF16),
-        ],
+        functools.partial(weights_kernel, mode, strip),
+        out_shape=out_shape,
+        grid_spec=pltpu.PrefetchScalarGridSpec(
+            num_scalar_prefetch=1,
+            grid=(steps,),
+            in_specs=specs,
+            out_specs=out_specs,
+            scratch_shapes=scratch,
+        ),
         compiler_params=params(),
-        cost_estimate=cost(2 * rows * d * d * 9, 2.5e7),
-        name="weights",
-    )(n2, cot, gb, mix, act, gl, vec, gfb, order)
+        cost_estimate=cost(2 * rows * d * cols * steps, 6e6 * steps),
+        name="weights_" + mode,
+    )(*operands)
+
+
+def finish_wide_kernel(ak_ref, ar_ref, bk_ref, br_ref, fc_ref, pj_ref, out_ref, g_ref, b_ref, ob_ref, pb_ref, fb_ref):
+    tall, d = fc_ref.shape
+    width = out_ref.shape[0]
+    cut = ak_ref.shape[1]
+    a = ak_ref[...].astype(F32) + ar_ref[...].astype(F32)
+    b = bk_ref[...].astype(F32) + br_ref[...].astype(F32)
+    fc_ref[...] = a[:, :d]
+    pj_ref[: cut - d, :] = jnp.transpose(a[:, d:])
+    pj_ref[cut - d :, :] = jnp.transpose(b[:, : 2 * d - cut])
+    rest = jnp.transpose(b[:, 2 * d - cut :])
+    out_ref[...] = rest[:width]
+    g_ref[...] = rest[width : width + 1]
+    b_ref[...] = rest[width + 1 : width + 2]
+    ob_ref[...] = rest[width + 2 : width + 3]
+    pb_ref[...] = rest[width + 3 : width + 4]
+    rows, strip = fb_ref.shape
+    at = 2 * d - cut + width + 8
+    fb_ref[...] = b[:rows, at : at + strip]
+
+
+def finish_wide(ak, ar, bk, br, d, width, bias_shape):
+    tall = ak.shape[0]
+    sds = lambda *shape: jax.ShapeDtypeStruct(shape, F32)
+    return pl.pallas_call(
+        finish_wide_kernel,
+        out_shape=(
+            sds(tall, d),
+            sds(d, tall),
+            sds(width, tall),
+            sds(1, tall),
+            sds(1, tall),
+            sds(1, tall),
+            sds(1, tall),
+            sds(*bias_shape),
+        ),
+        compiler_params=pltpu.CompilerParams(vmem_limit_bytes=VMEM_LIMIT),
+        cost_estimate=cost(0, 2e6),
+        name="finish_wide",
+    )(ak, ar, bk, br)
 
 
 def project_back_kernel(
-    me_ref, own_ref, far_ref, grad_ref, w_ref, keep_ref, send_ref, dw_ref, vec_ref, bias_ref, w3_ref, dw3_ref, gain_ref
+    piece, me_ref, own_ref, far_ref, grad_ref, w_ref, order_ref, keep_ref, send_ref, dw_ref, w3_ref, dw3_ref, gain_ref, vec_ref, bias_ref
 ):
     i = pl.program_id(0)
     steps = pl.num_programs(0)
     width = grad_ref.shape[2]
+    d = w_ref.shape[0]
 
     @pl.when(i == 0)
     def _():
@@ -535,23 +694,27 @@
 
     @pl.when(i == steps - 1)
     def _():
-        dw_ref[...] = dw3_ref[...].astype(BF16)
-
-
-def project_back(me, own, far, grad, w):
+        turned_bias = jnp.zeros((8, d), F32)
+        for s in range(3):
+            dw_ref[:, s * width : (s + 1) * width] = dw3_ref[s].astype(BF16)
+            spread = spread_rows(bias_ref[s : s + 1, :], 8, piece)
+            turned_bias = turned_bias + dot_nt(spread, order_ref[s])
+        tall = jnp.concatenate([vec_ref[...], turned_bias, jnp.zeros((EXT - 16, d), F32)], axis=0)
+        dw_ref[:, 3 * width :] = jnp.transpose(tall).astype(BF16)
+
+
+def project_back(me, own, far, grad, w, order, piece):
     half, rows, d = own.shape
     width = grad.shape[2]
     blocks = 2 * half
     sds = jax.ShapeDtypeStruct
     rel = lambda i, me: ((i ^ me[0]) // 2, 0, 0)
     return pl.pallas_call(
-        project_back_kernel,
+        functools.partial(project_back_kernel, piece),
         out_shape=(
             sds((half, rows, d), F32),
             sds((half, rows, d), BF16),
-            sds((3, d, width), BF16),
-            sds((8, d), F32),
-            sds((8, width), F32),
+            sds(w.shape, BF16),
         ),
         grid_spec=pltpu.PrefetchScalarGridSpec(
             num_scalar_prefetch=1,
@@ -561,29 +724,126 @@
                 pl.BlockSpec((1, rows, d), rel),
                 pl.BlockSpec((3, rows, width), lambda i, me: (0, i, 0)),
                 pl.BlockSpec(w.shape, lambda i, me: (0, 0)),
+                pl.BlockSpec(order.shape, lambda i, me: (0, 0, 0)),
             ],
             out_specs=(
                 pl.BlockSpec((1, rows, d), rel),
                 pl.BlockSpec((1, rows, d), rel),
-                pl.BlockSpec((3, d, width), lambda i, me: (0, 0, 0)),
-                pl.BlockSpec((8, d), lambda i, me: (0, 0)),
-                pl.BlockSpec((8, width), lambda i, me: (0, 0)),
+                pl.BlockSpec(w.shape, lambda i, me: (0, 0)),
             ),
             scratch_shapes=[
                 pltpu.VMEM((3, d, width), BF16),
                 pltpu.VMEM((3, d, width), F32),
                 pltpu.VMEM((8, d), F32),
+                pltpu.VMEM((8, d), F32),
+                pltpu.VMEM((8, width), F32),
             ],
         ),
         compiler_params=params(),
         cost_estimate=cost(4 * blocks * rows * d * 3 * width, 1.5e7),
         name="project_back",
-    )(me, own, far, grad, w)
-
-
-def one_hot_order(sources, targets, size, width):
-    row = lax.broadcasted_iota(jnp.int32, (size, width), 0)
+    )(me, own, far, grad, w, order)
+
+
+def pair_kernel(keep_ref, came_ref, own_ref, *send_refs):
+    n = pl.program_id(0)
+    total = keep_ref[0] + came_ref[0].astype(F32)
+
+    @pl.when(n == 0)
+    def _():
+        own_ref[...] = total
+
+    for m, ref in enumerate(send_refs):
+
+        @pl.when(n == m + 1)
+        def _(ref=ref):
+            ref[...] = total.astype(BF16)
+
+
+def pair_sum(keep, came):
+    half, rows, d = keep.shape
+    piece = pl.BlockSpec((1, rows, d), lambda n: (n, 0, 0))
+    flat = pl.BlockSpec((rows, d), lambda n: (0, 0))
+    return pl.pallas_call(
+        pair_kernel,
+        out_shape=(jax.ShapeDtypeStruct((rows, d), F32),)
+        + (jax.ShapeDtypeStruct((rows, d), BF16),) * (half - 1),
+        grid=(half,),
+        in_specs=[piece, piece],
+        out_specs=(flat,) * half,
+        compiler_params=params(),
+        cost_estimate=cost(0, 7e6),
+        name="pair_sum",
+    )(keep, came)
+
+
+def finish_narrow_kernel(g_ref, qkv_ref, qb_ref, vec_ref):
+    total = g_ref[0].astype(F32)
+    for n in range(1, g_ref.shape[0]):
+        total = total + g_ref[n].astype(F32)
+    width = qkv_ref.shape[2]
+    for s in range(3):
+        qkv_ref[s] = total[:, s * width : (s + 1) * width]
+    heads, piece = qb_ref.shape[1:]
+    edge = 3 * width + 8
+    for s in range(3):
+        qb_ref[s] = total[s * heads : (s + 1) * heads, edge : edge + piece]
+    vec_ref[...] = jnp.transpose(total[:, 512:640])[64:72]
+
+
+def finish_narrow(g, width, bias_shape):
+    tall = g.shape[1]
+    sds = lambda *shape: jax.ShapeDtypeStruct(shape, F32)
+    return pl.pallas_call(
+        finish_narrow_kernel,
+        out_shape=(sds(3, tall, width), sds(*bias_shape), sds(8, tall)),
+        compiler_params=pltpu.CompilerParams(vmem_limit_bytes=VMEM_LIMIT),
+        cost_estimate=cost(0, 2e6),
+        name="finish_narrow",
+    )(g)
+
+
+def finish_rows_kernel(side_ref, tok_ref, near_ref, near2_ref, away_ref, away2_ref, gh_ref, w_ref, out_ref, gain_ref):
+    m = pl.program_id(0)
+
+    @pl.when(m == 0)
+    def _():
+        gain_ref[...] = jnp.transpose(w_ref[:, 512:640].astype(F32))[64:72]
+
+    n, scale = norm_parts(tok_ref[0].astype(F32))
+    near = near_ref[...] + near2_ref[...].astype(F32)
+    away = away_ref[...].astype(F32) + away2_ref[...].astype(F32)
+    incoming = jnp.where(m == side_ref[0], near, away)
+    out_ref[0] = gh_ref[0] + norm_back(incoming, gain_ref[0:1], n, scale)
+
+
+def finish_rows(side, tok, near, near2, away, away2, gh, w):
+    micro, rows, d = tok.shape
+    piece = pl.BlockSpec((1, rows, d), lambda m, ix: (m, 0, 0))
+    flat = pl.BlockSpec((rows, d), lambda m, ix: (0, 0))
+    return pl.pallas_call(
+        finish_rows_kernel,
+        out_shape=jax.ShapeDtypeStruct((micro, rows, d), F32),
+        grid_spec=pltpu.PrefetchScalarGridSpec(
+            num_scalar_prefetch=1,
+            grid=(micro,),
+            in_specs=[piece, flat, flat, flat, flat, piece, pl.BlockSpec(w.shape, lambda m, ix: (0, 0))],
+            out_specs=piece,
+            scratch_shapes=[pltpu.VMEM((8, d), F32)],
+        ),
+        compiler_params=params(),
+        cost_estimate=cost(0, 6e6),
+        name="finish_rows",
+    )(side, tok, near, near2, away, away2, gh, w)
+
+
+def one_hot_order(sources, size):
+    row = lax.broadcasted_iota(jnp.int32, (size, sources.shape[1]), 0)
     return jnp.where(row == sources, 1.0, 0.0).astype(BF16)
+
+
+def plus(a, b):
+    return (a.astype(F32) + b.astype(F32)).astype(BF16)
 
 
 def local(
@@ -607,10 +867,14 @@
     shards = lax.axis_size(("dp", "ctx"))
     group = sides * parts
     micro, _, rows, d = tokens.shape
-    assert micro == sides == 2 and parts % 2 == 0
+    assert micro == sides == 2 and parts == 4
     side = lax.axis_index("ctx")
-    me = side * parts + lax.axis_index("tp")
+    slot = lax.axis_index("tp")
+    deep = lax.axis_index("dp")
+    depth = lax.axis_size("dp")
+    me = side * parts + slot
     me_array = jnp.full((1,), me, jnp.int32)
+    side_array = jnp.full((1,), side, jnp.int32)
     tall = qkv_weight.shape[1]
     heads, piece = qkv_bias.shape[1], qkv_bias.shape[2]
     width = heads * HD
@@ -619,8 +883,17 @@
     def swap(array, mask):
         return lax.ppermute(array, ("ctx", "tp"), [(n, n ^ mask) for n in range(group)])
 
+    def swap_deep(array, mask):
+        return lax.ppermute(array, "dp", [(n, n ^ mask) for n in range(depth)])
+
     tok = tokens[:, 0]
     cot = cotangent[:, 0]
+
+    vectors = jnp.stack([ln1_gain, ln1_bias, ln2_gain, ln2_bias, out_bias, proj_bias])
+    wide, narrow = pack(fc_weight, proj_weight, out_weight, qkv_weight, vectors, qkv_bias, fc_bias, shards)
+
+    gathered = lax.all_gather(wide, ("tp", "dp", "ctx"), axis=0, tiled=True)
+    gathered = gathered.reshape(parts, d, wide.shape[1])
 
     mine = lax.dynamic_index_in_dim(tok, side, 0, keepdims=False)
     other = lax.dynamic_index_in_dim(tok, 1 - side, 0, keepdims=False)
@@ -631,118 +904,86 @@
     own = jnp.stack(blocks)
     far = swap(own, 1)
 
-    def column(values):
-        return jnp.pad(values.reshape(-1, 1), ((0, tall - values.size), (0, 0)))
-
-    narrow = jnp.concatenate(
-        [
-            qkv_weight.transpose(1, 0, 2).reshape(tall, 3 * width),
-            column(ln1_gain),
-            column(ln1_bias),
-            column(qkv_bias),
-            jnp.zeros((tall, EXT - 3), BF16),
-        ],
-        axis=1,
-    )
-    w_in = lax.all_to_all(
-        jnp.broadcast_to(narrow[None], (shards,) + narrow.shape), ("dp", "ctx"), 0, 0, tiled=True
-    ).reshape(d, 3 * width + EXT)
-
-    wide = jnp.concatenate(
-        [
-            fc_weight,
-            proj_weight.T,
-            out_weight.T,
-            column(ln2_gain),
-            column(ln2_bias),
-            column(out_bias),
-            column(proj_bias),
-            column(fc_bias),
-            jnp.zeros((tall, EXT - 5), BF16),
-        ],
-        axis=1,
-    )
-    gathered = lax.all_gather(wide, ("tp", "dp", "ctx"), axis=0, tiled=True)
-    gathered = gathered.reshape(parts, d, wide.shape[1])
+    w_in = lax.all_to_all(narrow, ("dp", "ctx"), 0, 0, tiled=True).reshape(d, narrow.shape[2])
 
     unit = lax.broadcasted_iota(jnp.int32, (1, 3 * width), 1)
-    shard = unit % HD // piece
-    order_in = one_hot_order(shard * tall + unit // HD * piece + unit % piece, None, d, 3 * width)
+    order_in = one_hot_order(unit % HD // piece * tall + unit // HD, d)
     unit = lax.broadcasted_iota(jnp.int32, (1, d), 1)
-    shard = unit % 128 // strip
-    order_fc = one_hot_order(shard * tall + unit // 128 * strip + unit % strip, None, d, d)
-
-    triple = project(me_array, own, far, w_in, order_in)
-    mixed, mixed_turned, level = attend(triple)
-    mix = lax.all_to_all(mixed.reshape(group, rows, width), ("ctx", "tp"), 0, 0, tiled=True)
+    order_fc = one_hot_order(unit % 128 // strip * tall + unit // 128, d)
+
+    triple = project(me_array, own, far, w_in, order_in, piece)
+    mixed, mixed_turned, level = attend(triple, rows)
+    mix = lax.all_to_all(mixed, ("ctx", "tp"), 0, 0, tiled=True)
 
     tok_rows = tok.reshape(micro * rows, d)
     cot_rows = cot.reshape(micro * rows, d)
     y, grad_hidden, grad_mix, n2, act, gl, gb, vec, gfb = middle(
-        tok_rows, cot_rows, mix, gathered, order_fc
+        tok_rows, cot_rows, mix, gathered, order_fc, strip
     )
     grad_mix = lax.all_to_all(grad_mix, ("ctx", "tp"), 0, 0, tiled=True)
-    grad_wide = weights(n2, cot_rows, gb, mix, act, gl, vec, gfb, order_fc)
-    grad_wide = lax.psum_scatter(
-        grad_wide.reshape(parts * d, wide.shape[1]), ("tp", "dp", "ctx"), scatter_dimension=0, tiled=True
-    ).astype(F32)
-
-    grad_triple = attend_back(triple, grad_mix.reshape(group * rows, width), mixed_turned, level)
-    keep, send, grad_in, vec_in, bias_in = project_back(me_array, own, far, grad_triple, w_in)
-
-    pair = keep + swap(send, 1).astype(F32)
-    arrived = []
-    for n, mask in enumerate(range(0, group, 2)):
-        arrived.append(pair[n] if mask == 0 else swap(pair[n].astype(BF16), mask).astype(F32))
-    near = sum(arrived[1 : parts // 2], arrived[0])
-    away = sum(arrived[parts // 2 + 1 :], arrived[parts // 2])
-    swapped = side == 1
-    grad_normed = jnp.stack([jnp.where(swapped, away, near), jnp.where(swapped, near, away)])
-
-    vec_in = vec_in[:2]
-    mask = 1
-    while mask < parts:
+
+    parcels = (n2, cot_rows, gb, mix, act, gl, vec, gfb, order_fc, strip)
+    cut = wide.shape[1] // 2
+    if tall % 16 == 0 and depth & (depth - 1) == 0:
+        core, row = slot % 2, slot // 2
+        index = lambda lane: jnp.stack([(1 - row) * 2 + lane, row * 2 + lane, deep, side]).astype(jnp.int32)
+        came = swap(weights("send", index(1 - core), *parcels), 1)
+        a_send, a_keep, b_send, b_keep = weights("keep", index(core), *parcels, came=came, shards=shards)
+        a_came, b_came = swap(a_send, 2), swap(b_send, parts)
+        a_send, a_keep = plus(a_keep[1], a_came[1]), plus(a_keep[0], a_came[0])
+        b_send, b_keep = plus(b_keep[1], b_came[1]), plus(b_keep[0], b_came[0])
+        a_came, b_came = swap(a_send, parts), swap(b_send, 2)
+        left, mask = depth, 1
+        while left > 1:
+            left //= 2
+            a_send, a_keep = plus(a_keep[left:], a_came[left:]), plus(a_keep[:left], a_came[:left])
+            b_send, b_keep = plus(b_keep[left:], b_came[left:]), plus(b_keep[:left], b_came[:left])
+            a_came, b_came = swap_deep(a_send, mask), swap_deep(b_send, mask)
+            mask *= 2
+        a_keep, a_came, b_keep, b_came = a_keep[0], a_came[0], b_keep[0], b_came[0]
+    else:
+        grad_wide = weights("all", jnp.arange(parts, dtype=jnp.int32), *parcels)
+        grad_wide = lax.psum_scatter(
+            grad_wide.reshape(parts * d, wide.shape[1]), ("tp", "dp", "ctx"), scatter_dimension=0, tiled=True
+        )
+        a_keep, b_keep = grad_wide[:, :cut], grad_wide[:, cut:]
+        a_came, b_came = jnp.zeros_like(a_keep), jnp.zeros_like(b_keep)
+
+    grad_triple = attend_back(triple, grad_mix, mixed_turned, level)
+    order_back = order_in.reshape(d, 3, width).transpose(1, 0, 2)
+    keep, send, grad_in = project_back(me_array, own, far, grad_triple, w_in, order_back, piece)
+
+    near, *sends = pair_sum(keep, swap(send, 1))
+    arrived = [swap(sends[n - 1], 2 * n) for n in range(1, group // 2)]
+
+    grad_in = lax.all_to_all(grad_in.reshape(narrow.shape), ("dp", "ctx"), 0, 0, tiled=True)
+    grad_qkv_weight, grad_qkv_bias, vec_in = finish_narrow(grad_in, width, qkv_bias.shape)
+    mask = parts // 2
+    while mask:
         vec_in = vec_in + swap(vec_in, mask)
-        mask *= 2
-    bias_cols = bias_in[:3].reshape(3, heads, shards, piece).transpose(2, 0, 1, 3).reshape(shards, 3 * heads * piece)
-    bias_cols = jnp.pad(bias_cols, ((0, 0), (0, tall - 3 * heads * piece))).reshape(d, 1)
-    narrow_grad = jnp.concatenate(
-        [
-            grad_in.transpose(1, 0, 2).reshape(d, 3 * width),
-            vec_in.T.astype(BF16),
-            bias_cols.astype(BF16),
-            jnp.zeros((d, EXT - 3), BF16),
-        ],
-        axis=1,
+        mask //= 2
+
+    grad_tokens = finish_rows(
+        side_array, tok, near, *arrived, grad_hidden.reshape(micro, rows, d), w_in
     )
-    narrow_grad = lax.all_to_all(
-        narrow_grad.reshape(shards, tall, 3 * width + EXT), ("dp", "ctx"), 0, 0, tiled=True
+    fc_grad, proj_grad, out_grad, gain2, shift2, out_b, proj_b, fc_b = finish_wide(
+        a_keep, a_came, b_keep, b_came, d, width, fc_bias.shape
     )
-    narrow_grad = jnp.sum(narrow_grad.astype(F32), axis=0)
-
-    n, scale = norm_parts(tok.astype(F32))
-    gain = w_in[:, 3 * width].astype(F32)
-    grad_tokens = grad_hidden.reshape(micro, rows, d) + norm_back(grad_normed, gain, n, scale)
-
-    base = 3 * width
-    grad_qkv_weight = narrow_grad[:, :base].reshape(tall, 3, width).transpose(1, 0, 2)
-    grad_qkv_bias = narrow_grad[: 3 * heads * piece, base + 2].reshape(3, heads, piece)
-    edge = 2 * d + width
     return (
         y.reshape(micro, 1, rows, d),
         grad_tokens[:, None],
-        narrow_grad[:, base],
-        narrow_grad[:, base + 1],
+        vec_in[0],
+        vec_in[1],
         grad_qkv_weight,
         grad_qkv_bias,
-        grad_wide[:, 2 * d : edge].T,
-        grad_wide[:, edge + 2],
-        grad_wide[:, edge],
-        grad_wide[:, edge + 1],
-        grad_wide[:, :d],
-        grad_wide[:, edge + 4].reshape(lines, strip),
-        grad_wide[:, d : 2 * d].T,
-        grad_wide[:, edge + 3],
+        out_grad,
+        out_b[0],
+        gain2[0],
+        shift2[0],
+        fc_grad,
+        fc_b,
+        proj_grad,
+        proj_b[0],
     )
 
 

time: 323 us -> 303 us (0.938)
  Pallas kernels: 120 us -> 143 us
  waiting for transfers between devices: 95.8 us -> 77.9 us
  local copies, waits for them, and re-layouts: 29.9 us -> 13.5 us
  blocking collectives: 14.3 us -> 0 us
  starting transfers between devices: 24.6 us -> 37.2 us
  other arithmetic: 23.2 us -> 16.8 us
    reduce_scatter x1 -> x0, waiting for transfers between devices: 31.9 us -> none  [local(): lax.psum_scatter(grad_wide.reshape(parts * d, wide.shape[1]), ('tp', 'dp'...]
    ppermute x10 -> x15, waiting for transfers between devices: 27.7 us -> 59.3 us  [swap(): lax.ppermute(array, ('ctx', 'tp'), [(n, n ^ mask) for n in range(group)])]
    pallas_call x5 -> x11, Pallas kernels: 87.2 us -> 111 us  [the longest x1 28.7 us: attend(): pl.pallas_call(attend_kernel, out_shape=(jax.ShapeDtypeStruct((span // ro...]
    all_to_all x3 -> x4, waiting for transfers between devices: 36.2 us -> 18.5 us  [the longest x1 9.3 us: local(): mix = lax.all_to_all(mixed, ('ctx', 'tp'), 0, 0, tiled=True)]
    all_to_all x1 -> x0, blocking collectives: 14.3 us -> none  [local(): grad_mix = lax.all_to_all(grad_mix, ('ctx', 'tp'), 0, 0, tiled=True)]
    convert_element_type x3 -> x6, other arithmetic: 2.25 us -> 9.12 us  [plus(): return (a.astype(F32) + b.astype(F32)).astype(BF16)]
    concatenate x1 -> x0, other arithmetic: 6.67 us -> none  [local(): jnp.concatenate([grad_in.transpose(1, 0, 2).reshape(d, 3 * width), vec_in...]
    reshape x10 -> x0, local copies, waits for them, and re-layouts: 6.37 us -> none  [the longest x6 3.96 us: column(): return jnp.pad(values.reshape(-1, 1), ((0, tall - values.size), (0, 0)))]
  transfers between devices with their start and end apart: 15 -> 24, of which waited for: 8 -> 10; matrix products, arithmetic and copies ran while one was open for 12% -> 6% of each run, Pallas kernels for 26% -> 35%
where the time goes in v2:
time: 303 us; the launch traced here: 302 us
  Pallas kernels  143 us (47%)
  waiting for transfers between devices  77.9 us (26%)
  starting transfers between devices  37.2 us (12%)
  other arithmetic  16.8 us (6%)
  between operations  14.3 us (5%)
  local copies, waits for them, and re-layouts  13.5 us (4%)
    ppermute x15, waiting for transfers between devices, swap(): lax.ppermute(array, ('ctx', 'tp'), [(n, n ^ mask) for n in range(group)])  59.3 us
    pallas_call x1, Pallas kernels, attend_back(): pl.pallas_call(attend_back_kernel, out_shape=jax.ShapeDtypeStruct(triple....  31.9 us
    pallas_call x1, Pallas kernels, attend(): pl.pallas_call(attend_kernel, out_shape=(jax.ShapeDtypeStruct((span // ro...  28.7 us
    pallas_call x1, Pallas kernels, middle(): pl.pallas_call(functools.partial(middle_kernel, strip), out_shape=(sds((r...  21.6 us
    pallas_call x2, Pallas kernels, weights(): pl.pallas_call(functools.partial(weights_kernel, mode, strip), out_shape=...  20.7 us
    ppermute x15, starting transfers between devices, swap(): lax.ppermute(array, ('ctx', 'tp'), [(n, n ^ mask) for n in range(group)])  14.6 us
    pallas_call x1, Pallas kernels, project_back(): pl.pallas_call(functools.partial(project_back_kernel, piece), out_shape=(...  13.6 us
    unnamed x34, local copies, waits for them, and re-layouts  10.9 us
  transfers between devices with their start and end apart: 24, of which 10 were waited for; matrix products, arithmetic and copies ran while one was open for 6% of the time, Pallas kernels for 35%

profile of v2, /device:TPU:0, one launch (start us, length us, event | category | flops | bytes accessed | tf_op | source)
XLA Modules:
  0.0 302.2 jit_solution(3874277663889016906)
XLA Ops:
  7.2 1.8 copy.28.pj_ref
  10.4 2.5 pack.1
  13.7 3.9 %collective-permute-start.2 = (bf16[256,768]{1,0:T(8,128)(2,1)S(1)}, bf16[256,768]{1,0:T(8,128)(2,1)S(1)}, u32[]{:S(2)}, u32[]{:S(2)}) collective-permute-start(bf16[256,768]{1,0:T(8,128)(2,1)S(1)} %get-tuple-element.110), channel_id=1, source_target_pairs={{0,6},{1,7},{2,4},{3,5},{4,2},{5,3},{6,0},{7,1},{8,14},{9,15},{10,... | collective-permute-start | bytes 1179656 | tf_op jit(solution)/shard_map/ppermute | solution.py:884
  18.2 6.3 %all-to-all-start = ((bf16[8,96,640]{2,1,0:T(8,128)(2,1)}), bf16[8,96,640]{2,1,0:T(8,128)(2,1)S(1)}, u32[]{:S(2)}, u32[]{:S(2)}) async-start(bf16[8,96,640]{2,1,0:T(8,128)(2,1)} %get-tuple-element.50), calls=%async_computation | async-start | bytes 1966080 | tf_op jit(solution)/shard_map/all_to_all | solution.py:907
  24.5 7.8 %collective-permute-done.2 = bf16[256,768]{1,0:T(8,128)(2,1)S(1)} collective-permute-done((bf16[256,768]{1,0:T(8,128)(2,1)S(1)}, bf16[256,768]{1,0:T(8,128)(2,1)S(1)}, u32[]{:S(2)}, u32[]{:S(2)}) %collective-permute-start.2) | collective-permute-done | bytes 393248 | tf_op jit(solution)/shard_map/ppermute | solution.py:884
  32.3 12.6 %collective-permute-done.1 = bf16[256,768]{1,0:T(8,128)(2,1)S(1)} collective-permute-done((bf16[256,768]{1,0:T(8,128)(2,1)S(1)}, bf16[256,768]{1,0:T(8,128)(2,1)S(1)}, u32[]{:S(2)}, u32[]{:S(2)}) %collective-permute-start.1) | collective-permute-done | bytes 393248 | tf_op jit(solution)/shard_map/ppermute | solution.py:884
  48.7 9.2 %all-to-all-done = bf16[8,96,640]{2,1,0:T(8,128)(2,1)S(1)} async-done(((bf16[8,96,640]{2,1,0:T(8,128)(2,1)}), bf16[8,96,640]{2,1,0:T(8,128)(2,1)S(1)}, u32[]{:S(2)}, u32[]{:S(2)}) %all-to-all-start) | async-done | bytes 983072 | tf_op jit(solution)/shard_map/all_to_all | solution.py:907
  58.9 10.2 %project.1.q_ref.k_ref.v_ref.qkv_ref = bf16[3,2048,192]{2,1,0:T(8,128)(2,1)} custom-call(s32[1]{0:T(128)} %bitcast.2.me_ref, bf16[4,256,768]{2,1,0:T(8,128)(2,1)} %copy-done.2, bf16[4,256,768]{2,1,0:T(8,128)(2,1)} %collective-permute-done.3.far_ref, bf16[768,640]{1,0:T(8,128)(2,1)} %bitcast.74, bf16[768,576]{1,0:T(8,128)(2,1)} %select_convert_fusion.2.order_ref), custom_call_target="tpu_custom_call" | custom-call | flops 1811939328 | bytes 8000000 | tf_op jit(solution)/shard_map/project/pallas_call | solution.py:130
  69.1 28.7 %attend.1 = (bf16[8,192,256]{2,1,0:T(8,128)(2,1)}, f32[192,2048]{1,0:T(8,128)}, f32[8,2048]{1,0:T(8,128)}) custom-call(bf16[3,2048,192]{2,1,0:T(8,128)(2,1)} %project.1.q_ref.k_ref.v_ref.qkv_ref, bf16[3,2048,192]{2,1,0:T(8,128)(2,1)} %project.1.q_ref.k_ref.v_ref.qkv_ref, bf16[3,2048,192]{2,1,0:T(8,128)(2,1)} %project.1.q_ref.k_ref.v_ref.qkv_ref), custom_call_target="tpu_custom_call" | custom-call | flops 3221225472 | bytes 8000000 | tf_op jit(solution)/shard_map/attend/pallas_call | solution.py:217
  97.9 3.7 %all-to-all-start.1 = ((bf16[8,192,256]{2,1,0:T(8,128)(2,1)}), bf16[8,192,256]{2,1,0:T(8,128)(2,1)S(1)}, u32[]{:S(2)}, u32[]{:S(2)}) async-start(bf16[8,192,256]{2,1,0:T(8,128)(2,1)} %get-tuple-element.51), calls=%async_computation.1 | async-start | bytes 1572864 | tf_op jit(solution)/shard_map/all_to_all | solution.py:916
  103.7 9.3 %all-to-all-done.1.mix_ref = bf16[8,192,256]{2,1,0:T(8,128)(2,1)S(1)} async-done(((bf16[8,192,256]{2,1,0:T(8,128)(2,1)}), bf16[8,192,256]{2,1,0:T(8,128)(2,1)S(1)}, u32[]{:S(2)}, u32[]{:S(2)}) %all-to-all-start.1) | async-done | bytes 786464 | tf_op jit(solution)/shard_map/all_to_all | solution.py:916
  113.9 21.6 %middle.1 = (bf16[512,768]{1,0:T(8,128)(2,1)}, f32[512,768]{1,0:T(8,128)}, bf16[8,192,256]{2,1,0:T(8,128)(2,1)}, bf16[512,768]{1,0:T(8,128)(2,1)}, bf16[4,512,76...) custom-call(bf16[512,768]{1,0:T(8,128)(2,1)} %bitcast.82, ...), custom_call_target="tpu_custom_call" | custom-call | flops 10871635968 | bytes 30000000 | tf_op jit(solution)/shard_map/middle/pallas_call | solution.py:459
  135.5 9.4 %weights_send.1 = bf16[2,768,1792]{2,1,0:T(8,128)(2,1)} custom-call(s32[4]{0:T(128)} %add_add_fusion.1.index_ref, bf16[512,768]{1,0:T(8,128)(2,1)} %get-tuple-element.68.n2_ref, bf16[512,768]{1,0:T(8,128)(2,1)} %bitcast.80, bf16[512,768]{1,0:T(8,128)(2,1)} %get-tuple-element.69.gb_ref, bf16[2,4,192,256]{3,2,1,0:T(8,128)(2,1)} %bitcast.77, ...), custom_call_target="tpu_custom_call" | custom-call | flops 2818572288 | bytes 12000000 | tf_op jit(solution)/shard_map/weights_send/pallas_call | solution.py:599
  144.9 3.8 %all-to-all-start.2 = ((bf16[8,192,256]{2,1,0:T(8,128)(2,1)}), bf16[8,192,256]{2,1,0:T(8,128)(2,1)S(1)}, u32[]{:S(2)}, u32[]{:S(2)}) async-start(bf16[8,192,256]{2,1,0:T(8,128)(2,1)} %get-tuple-element.54), calls=%async_computation.2 | async-start | bytes 1572864 | tf_op jit(solution)/shard_map/all_to_all | solution.py:923
  149.3 5.0 %collective-permute-done.10.rest_0_ = bf16[2,768,1792]{2,1,0:T(8,128)(2,1)} collective-permute-done((bf16[2,768,1792]{2,1,0:T(8,128)(2,1)}, bf16[2,768,1792]{2,1,0:T(8,128)(2,1)}, u32[]{:S(2)}, u32[]{:S(2)}) %collective-permute-start.10) | collective-permute-done | bytes 5505056 | tf_op jit(solution)/shard_map/ppermute | solution.py:884
  154.3 11.3 %weights_keep.1 = (bf16[2,4,96,896]{3,2,1,0:T(8,128)(2,1)}, bf16[2,4,96,896]{3,2,1,0:T(8,128)(2,1)}, bf16[2,4,96,896]{3,2,1,0:T(8,128)(2,1)}, bf16[2,4,96,896]{3,2,1,0:T(8,128)(2,1)}) custom-call(s32[4]{0:T(128)} %add_add_fusion.index_ref, bf16[512,768]{1,0:T(8,128)(2,1)} %get-tuple-element.68.n2_ref, bf16[512,768]{1,0:T(8,128)(2,1)} %bitcast.81, ...), custom_call_target="tpu_custom_call" | custom-call | flops 2818572288 | bytes 12000000 | tf_op jit(solution)/shard_map/weights_keep/pallas_call | solution.py:599
  170.0 31.9 %attend_back.1.grad_ref = bf16[3,2048,192]{2,1,0:T(8,128)(2,1)} custom-call(bf16[3,2048,192]{2,1,0:T(8,128)(2,1)} %project.1.q_ref.k_ref.v_ref.qkv_ref, bf16[8,192,256]{2,1,0:T(8,128)(2,1)} %copy-done.8, f32[192,2048]{1,0:T(8,128)} %get-tuple-element.55.ot_ref, f32[8,2048]{1,0:T(8,128)} %get-tuple-element.56.level_ref), custom_call_target="tpu_custom_call" | custom-call | flops 8053063680 | bytes 10000000 | tf_op jit(solution)/shard_map/attend_back/pallas_call | solution.py:338
  201.9 13.6 %project_back.1 = (f32[4,256,768]{2,1,0:T(8,128)}, bf16[4,256,768]{2,1,0:T(8,128)(2,1)}, bf16[768,640]{1,0:T(8,128)(2,1)}) custom-call(s32[1]{0:T(128)} %bitcast.2.me_ref, bf16[4,256,768]{2,1,0:T(8,128)(2,1)} %copy-done.2, bf16[4,256,768]{2,1,0:T(8,128)(2,1)} %collective-permute-done.3.far_ref, bf16[3,2048,192]{2,1,0:T(8,128)(2,1)} %attend_back.1.grad_ref, ...), custom_call_target="tpu_custom_call" | custom-call | flops 3623878656 | bytes 15000000 | tf_op jit(solution)/shard_map/project_back/pallas_call | solution.py:712
  215.5 3.8 %all-to-all-start.3 = ((bf16[8,96,640]{2,1,0:T(8,128)(2,1)}), bf16[8,96,640]{2,1,0:T(8,128)(2,1)S(1)}, u32[]{:S(2)}, u32[]{:S(2)}) async-start(bf16[8,96,640]{2,1,0:T(8,128)(2,1)} %bitcast.86), calls=%async_computation.3 | async-start | bytes 1966080 | tf_op jit(solution)/shard_map/all_to_all | solution.py:959
  219.4 2.2 add_convert_fusion.3
  221.5 1.9 collective-permute-start.12
  226.4 20.5 %collective-permute-done.12 = bf16[4,96,896]{2,1,0:T(8,128)(2,1)S(1)} collective-permute-done((bf16[4,96,896]{2,1,0:T(8,128)(2,1)S(1)}, bf16[4,96,896]{2,1,0:T(8,128)(2,1)S(1)}, u32[]{:S(2)}, u32[]{:S(2)}) %collective-permute-start.12) | collective-permute-done | bytes 688160 | tf_op jit(solution)/shard_map/ppermute | solution.py:884
  251.7 2.1 finish_narrow.1
  255.0 2.5 collective-permute-done.8
  259.4 4.5 %pair_sum.1 = (f32[256,768]{1,0:T(8,128)}, bf16[256,768]{1,0:T(8,128)(2,1)}, bf16[256,768]{1,0:T(8,128)(2,1)}, bf16[256,768]{1,0:T(8,128)(2,1)}) custom-call(f32[4,256,768]{2,1,0:T(8,128)} %get-tuple-element.57.keep_ref, bf16[4,256,768]{2,1,0:T(8,128)(2,1)} %copy-done.6), custom_call_target="tpu_custom_call" | custom-call | bytes 7000000 | tf_op jit(solution)/shard_map/pair_sum/pallas_call | solution.py:767
  267.4 1.8 add_convert_fusion.6
  269.2 2.1 collective-permute-start.14
  271.3 1.8 add_convert_fusion.4
  277.4 7.9 %collective-permute-done.7.away2_ref = bf16[256,768]{1,0:T(8,128)(2,1)S(1)} collective-permute-done((bf16[256,768]{1,0:T(8,128)(2,1)}, bf16[256,768]{1,0:T(8,128)(2,1)S(1)}, u32[]{:S(2)}, u32[]{:S(2)}) %collective-permute-start.7) | collective-permute-done | bytes 393248 | tf_op jit(solution)/shard_map/ppermute | solution.py:884
  286.0 4.5 %finish_rows.1 = f32[2,256,768]{2,1,0:T(8,128)} custom-call(s32[1]{0:T(128)} %bitcast.19.side_ref, bf16[2,256,768]{2,1,0:T(8,128)(2,1)} %bitcast.83, f32[256,768]{1,0:T(8,128)} %get-tuple-element.59.near_ref, bf16[256,768]{1,0:T(8,128)(2,1)} %copy-done.11, bf16[256,768]{1,0:T(8,128)(2,1)} %copy-done.12, bf16[256,768]{1,0:T(8,128)(2,1)} %copy-done.13, ...), custom_call_target="tpu_custom_call" | custom-call | bytes 6000000 | tf_op jit(solution)/shard_map/finish_rows/pallas_call | solution.py:824
  291.2 2.2 finish_wide.1
  293.5 1.9 copy.31
  (83 shorter events, 35.7 us)
Async XLA Ops:
  7.2 5.7 %copy-start.4 = (bf16[2,1,256,768]{3,2,1,0:T(8,128)(2,1)S(1)}, bf16[2,1,256,768]{3,2,1,0:T(8,128)(2,1)}, u32[]{:S(2)}) copy-start(bf16[2,1,256,768]{3,2,1,0:T(8,128)(2,1)} %param.14) | copy-start | bytes 2359300
  7.2 105.8 %all-gather.2.cloned.1.call-start = ((), (), s32[]{:S(2)}) async-start(), calls=%async_computation.4 | async-start | bytes 11354112 | tf_op jit(solution)/shard_map/all_gather | solution.py:895
  13.7 32.1 %copy-start.5 = (bf16[1,256,768]{2,1,0:T(8,128)(2,1)S(1)}, bf16[1,256,768]{2,1,0:T(8,128)(2,1)}, u32[]{:S(2)}) copy-start(bf16[1,256,768]{2,1,0:T(8,128)(2,1)} %get-tuple-element.108) | copy-start | bytes 1179652
  13.7 18.6 %collective-permute-start.2 = (bf16[256,768]{1,0:T(8,128)(2,1)S(1)}, bf16[256,768]{1,0:T(8,128)(2,1)S(1)}, u32[]{:S(2)}, u32[]{:S(2)}) collective-permute-start(bf16[256,768]{1,0:T(8,128)(2,1)S(1)} %get-tuple-element.110), channel_id=1, source_target_pairs={{0,6},{1,7},{2,4},{3,5},{4,2},{5,3},{6,0},{7,1},{8,14},{9,15},{10,... | collective-permute-start | bytes 1179656 | tf_op jit(solution)/shard_map/ppermute | solution.py:884
  17.7 27.3 %collective-permute-start.1 = (bf16[256,768]{1,0:T(8,128)(2,1)S(1)}, bf16[256,768]{1,0:T(8,128)(2,1)S(1)}, u32[]{:S(2)}, u32[]{:S(2)}) collective-permute-start(bf16[256,768]{1,0:T(8,128)(2,1)S(1)} %get-tuple-element.110), channel_id=1, source_target_pairs={{0,4},{1,5},{2,6},{3,7},{4,0},{5,1},{6,2},{7,3},{8,12},{9,13},{10,... | collective-permute-start | bytes 1179656 | tf_op jit(solution)/shard_map/ppermute | solution.py:884
  18.2 26.7 %collective-permute-start = (bf16[256,768]{1,0:T(8,128)(2,1)S(1)}, bf16[256,768]{1,0:T(8,128)(2,1)S(1)}, u32[]{:S(2)}, u32[]{:S(2)}) collective-permute-start(bf16[256,768]{1,0:T(8,128)(2,1)S(1)} %get-tuple-element.109), channel_id=1, source_target_pairs={{0,2},{1,3},{2,0},{3,1},{4,6},{5,7},{6,4},{7,5},{8,10},{9,11},{10,... | collective-permute-start | bytes 1179656 | tf_op jit(solution)/shard_map/ppermute | solution.py:884
  18.2 39.7 %all-to-all-start = ((bf16[8,96,640]{2,1,0:T(8,128)(2,1)}), bf16[8,96,640]{2,1,0:T(8,128)(2,1)S(1)}, u32[]{:S(2)}, u32[]{:S(2)}) async-start(bf16[8,96,640]{2,1,0:T(8,128)(2,1)} %get-tuple-element.50), calls=%async_computation | async-start | bytes 1966080 | tf_op jit(solution)/shard_map/all_to_all | solution.py:907
  47.2 10.8 %copy-start.2 = (bf16[4,256,768]{2,1,0:T(8,128)(2,1)}, bf16[4,256,768]{2,1,0:T(8,128)(2,1)S(1)}, u32[]{:S(2)}) copy-start(bf16[4,256,768]{2,1,0:T(8,128)(2,1)S(1)} %pad_maximum_fusion.own_ref) | copy-start | bytes 4718596
  47.2 10.8 %collective-permute-start.3 = (bf16[4,256,768]{2,1,0:T(8,128)(2,1)S(1)}, bf16[4,256,768]{2,1,0:T(8,128)(2,1)}, u32[]{:S(2)}, u32[]{:S(2)}) collective-permute-start(bf16[4,256,768]{2,1,0:T(8,128)(2,1)S(1)} %pad_maximum_fusion.own_ref), channel_id=1, source_target_pairs={{0,1},{1,0},{2,3},{3,2},{4,5},{5,4},{6,7},{7,6},{8,9},{9,8},{10,11... | collective-permute-start | bytes 4718600 | tf_op jit(solution)/shard_map/ppermute | solution.py:884
  97.9 15.1 %all-to-all-start.1 = ((bf16[8,192,256]{2,1,0:T(8,128)(2,1)}), bf16[8,192,256]{2,1,0:T(8,128)(2,1)S(1)}, u32[]{:S(2)}, u32[]{:S(2)}) async-start(bf16[8,192,256]{2,1,0:T(8,128)(2,1)} %get-tuple-element.51), calls=%async_computation.1 | async-start | bytes 1572864 | tf_op jit(solution)/shard_map/all_to_all | solution.py:916
  144.9 9.4 %collective-permute-start.10 = (bf16[2,768,1792]{2,1,0:T(8,128)(2,1)}, bf16[2,768,1792]{2,1,0:T(8,128)(2,1)}, u32[]{:S(2)}, u32[]{:S(2)}) collective-permute-start(bf16[2,768,1792]{2,1,0:T(8,128)(2,1)} %weights_send.1), channel_id=1, source_target_pairs={{0,1},{1,0},{2,3},{3,2},{4,5},{5,4},{6,7},{7,6},{8,9},{9,8},{10,11... | collective-permute-start | bytes 16515080 | tf_op jit(solution)/shard_map/ppermute | solution.py:884
  144.9 24.2 %all-to-all-start.2 = ((bf16[8,192,256]{2,1,0:T(8,128)(2,1)}), bf16[8,192,256]{2,1,0:T(8,128)(2,1)S(1)}, u32[]{:S(2)}, u32[]{:S(2)}) async-start(bf16[8,192,256]{2,1,0:T(8,128)(2,1)} %get-tuple-element.54), calls=%async_computation.2 | async-start | bytes 1572864 | tf_op jit(solution)/shard_map/all_to_all | solution.py:923
  165.6 53.8 %collective-permute-start.11 = (bf16[2,4,96,896]{3,2,1,0:T(8,128)(2,1)}, bf16[2,4,96,896]{3,2,1,0:T(8,128)(2,1)}, u32[]{:S(2)}, u32[]{:S(2)}) collective-permute-start(bf16[2,4,96,896]{3,2,1,0:T(8,128)(2,1)} %get-tuple-element.75), channel_id=1, source_target_pairs={{0,2},{1,3},{2,0},{3,1},{4,6},{5,7},{6,4},{7,5},{8,10},{9,11},{10,... | collective-permute-start | bytes 4128776 | tf_op jit(solution)/shard_map/ppermute | solution.py:884
  168.5 54.9 %collective-permute-start.15 = (bf16[2,4,96,896]{3,2,1,0:T(8,128)(2,1)}, bf16[2,4,96,896]{3,2,1,0:T(8,128)(2,1)}, u32[]{:S(2)}, u32[]{:S(2)}) collective-permute-start(bf16[2,4,96,896]{3,2,1,0:T(8,128)(2,1)} %get-tuple-element.77), channel_id=1, source_target_pairs={{0,4},{1,5},{2,6},{3,7},{4,0},{5,1},{6,2},{7,3},{8,12},{9,13},{10,... | collective-permute-start | bytes 4128776 | tf_op jit(solution)/shard_map/ppermute | solution.py:884
  215.5 35.3 %all-to-all-start.3 = ((bf16[8,96,640]{2,1,0:T(8,128)(2,1)}), bf16[8,96,640]{2,1,0:T(8,128)(2,1)S(1)}, u32[]{:S(2)}, u32[]{:S(2)}) async-start(bf16[8,96,640]{2,1,0:T(8,128)(2,1)} %bitcast.86), calls=%async_computation.3 | async-start | bytes 1966080 | tf_op jit(solution)/shard_map/all_to_all | solution.py:959
  219.3 39.0 %collective-permute-start.4 = (bf16[4,256,768]{2,1,0:T(8,128)(2,1)}, bf16[4,256,768]{2,1,0:T(8,128)(2,1)S(1)}, u32[]{:S(2)}, u32[]{:S(2)}) collective-permute-start(bf16[4,256,768]{2,1,0:T(8,128)(2,1)} %get-tuple-element.58), channel_id=1, source_target_pairs={{0,1},{1,0},{2,3},{3,2},{4,5},{5,4},{6,7},{7,6},{8,9},{9,8},{10,11... | collective-permute-start | bytes 4718600 | tf_op jit(solution)/shard_map/ppermute | solution.py:884
  219.4 4.1 %copy-start.7 = (bf16[2,4,96,896]{3,2,1,0:T(8,128)(2,1)S(1)}, bf16[2,4,96,896]{3,2,1,0:T(8,128)(2,1)}, u32[]{:S(2)}) copy-start(bf16[2,4,96,896]{3,2,1,0:T(8,128)(2,1)} %get-tuple-element.76) | copy-start | bytes 4128772
  221.5 25.3 %collective-permute-start.12 = (bf16[4,96,896]{2,1,0:T(8,128)(2,1)S(1)}, bf16[4,96,896]{2,1,0:T(8,128)(2,1)S(1)}, u32[]{:S(2)}, u32[]{:S(2)}) collective-permute-start(bf16[4,96,896]{2,1,0:T(8,128)(2,1)S(1)} %get-tuple-element.103), channel_id=1, source_target_pairs={{0,4},{1,5},{2,6},{3,7},{4,0},{5,1},{6,2},{7,3},{8,12},{9,13},{10,... | collective-permute-start | bytes 2064392 | tf_op jit(solution)/shard_map/ppermute | solution.py:884
  225.1 24.2 %collective-permute-start.16 = (bf16[4,96,896]{2,1,0:T(8,128)(2,1)S(1)}, bf16[4,96,896]{2,1,0:T(8,128)(2,1)S(1)}, u32[]{:S(2)}, u32[]{:S(2)}) collective-permute-start(bf16[4,96,896]{2,1,0:T(8,128)(2,1)S(1)} %get-tuple-element.101), channel_id=1, source_target_pairs={{0,2},{1,3},{2,0},{3,1},{4,6},{5,7},{6,4},{7,5},{8,10},{9,11},{10,... | collective-permute-start | bytes 2064392 | tf_op jit(solution)/shard_map/ppermute | solution.py:884
  247.8 19.6 %collective-permute-start.13 = (bf16[2,96,896]{2,1,0:T(8,128)(2,1)}, bf16[2,96,896]{2,1,0:T(8,128)(2,1)}, u32[]{:S(2)}, u32[]{:S(2)}) collective-permute-start(bf16[2,96,896]{2,1,0:T(8,128)(2,1)} %get-tuple-element.107), channel_id=1, source_target_pairs={{0,8},{8,0},{16,24},{24,16},{1,9},{9,1},{17,25},{25,17},{2,10},{10... | collective-permute-start | bytes 1032200 | tf_op jit(solution)/shard_map/ppermute | solution.py:887
  250.2 21.1 %collective-permute-start.17 = (bf16[2,96,896]{2,1,0:T(8,128)(2,1)}, bf16[2,96,896]{2,1,0:T(8,128)(2,1)}, u32[]{:S(2)}, u32[]{:S(2)}) collective-permute-start(bf16[2,96,896]{2,1,0:T(8,128)(2,1)} %get-tuple-element.105), channel_id=1, source_target_pairs={{0,8},{8,0},{16,24},{24,16},{1,9},{9,1},{17,25},{25,17},{2,10},{10... | collective-permute-start | bytes 1032200 | tf_op jit(solution)/shard_map/ppermute | solution.py:887
  250.7 0.9 copy-start.3
  253.8 3.8 %collective-permute-start.8 = (f32[8,96]{1,0:T(8,128)}, f32[8,96]{1,0:T(8,128)S(1)}, u32[]{:S(2)}, u32[]{:S(2)}) collective-permute-start(f32[8,96]{1,0:T(8,128)} %get-tuple-element.65), channel_id=1, source_target_pairs={{0,2},{1,3},{2,0},{3,1},{4,6},{5,7},{6,4},{7,5},{8,10},{9,11},{10,... | collective-permute-start | bytes 9224 | tf_op jit(solution)/shard_map/ppermute | solution.py:884
  258.3 7.5 %collective-permute-start.9 = (f32[8,96]{1,0:T(8,128)S(1)}, f32[8,96]{1,0:T(8,128)S(1)}, u32[]{:S(2)}, u32[]{:S(2)}) collective-permute-start(f32[8,96]{1,0:T(8,128)S(1)} %add.165), channel_id=1, source_target_pairs={{0,1},{1,0},{2,3},{3,2},{4,5},{5,4},{6,7},{7,6},{8,9},{9,8},{10,11... | collective-permute-start | bytes 9224 | tf_op jit(solution)/shard_map/ppermute | solution.py:884
  258.3 1.1 copy-start.6
  263.9 11.7 %collective-permute-start.5 = (bf16[256,768]{1,0:T(8,128)(2,1)}, bf16[256,768]{1,0:T(8,128)(2,1)S(1)}, u32[]{:S(2)}, u32[]{:S(2)}) collective-permute-start(bf16[256,768]{1,0:T(8,128)(2,1)} %get-tuple-element.60), channel_id=1, source_target_pairs={{0,2},{1,3},{2,0},{3,1},{4,6},{5,7},{6,4},{7,5},{8,10},{9,11},{10,... | collective-permute-start | bytes 1179656 | tf_op jit(solution)/shard_map/ppermute | solution.py:884
  265.2 12.2 %collective-permute-start.6 = (bf16[256,768]{1,0:T(8,128)(2,1)}, bf16[256,768]{1,0:T(8,128)(2,1)S(1)}, u32[]{:S(2)}, u32[]{:S(2)}) collective-permute-start(bf16[256,768]{1,0:T(8,128)(2,1)} %get-tuple-element.61), channel_id=1, source_target_pairs={{0,4},{1,5},{2,6},{3,7},{4,0},{5,1},{6,2},{7,3},{8,12},{9,13},{10,... | collective-permute-start | bytes 1179656 | tf_op jit(solution)/shard_map/ppermute | solution.py:884
  265.8 19.5 %collective-permute-start.7 = (bf16[256,768]{1,0:T(8,128)(2,1)}, bf16[256,768]{1,0:T(8,128)(2,1)S(1)}, u32[]{:S(2)}, u32[]{:S(2)}) collective-permute-start(bf16[256,768]{1,0:T(8,128)(2,1)} %get-tuple-element.62), channel_id=1, source_target_pairs={{0,6},{1,7},{2,4},{3,5},{4,2},{5,3},{6,0},{7,1},{8,14},{9,15},{10,... | collective-permute-start | bytes 1179656 | tf_op jit(solution)/shard_map/ppermute | solution.py:884
  269.2 21.3 %collective-permute-start.14 = (bf16[1,96,896]{2,1,0:T(8,128)(2,1)S(1)}, bf16[1,96,896]{2,1,0:T(8,128)(2,1)S(1)}, u32[]{:S(2)}, u32[]{:S(2)}) collective-permute-start(bf16[1,96,896]{2,1,0:T(8,128)(2,1)S(1)} %get-tuple-element.113), channel_id=1, source_target_pairs={{0,16},{8,24},{16,0},{24,8},{1,17},{9,25},{17,1},{25,9},{2,18},{10... | collective-permute-start | bytes 516104 | tf_op jit(solution)/shard_map/ppermute | solution.py:887
  273.1 17.5 %collective-permute-start.18 = (bf16[1,96,896]{2,1,0:T(8,128)(2,1)S(1)}, bf16[1,96,896]{2,1,0:T(8,128)(2,1)S(1)}, u32[]{:S(2)}, u32[]{:S(2)}) collective-permute-start(bf16[1,96,896]{2,1,0:T(8,128)(2,1)S(1)} %get-tuple-element.111), channel_id=1, source_target_pairs={{0,16},{8,24},{16,0},{24,8},{1,17},{9,25},{17,1},{25,9},{2,18},{10... | collective-permute-start | bytes 516104 | tf_op jit(solution)/shard_map/ppermute | solution.py:887
  275.7 9.6 %copy-start.11 = (bf16[256,768]{1,0:T(8,128)(2,1)}, bf16[256,768]{1,0:T(8,128)(2,1)S(1)}, u32[]{:S(2)}) copy-start(bf16[256,768]{1,0:T(8,128)(2,1)S(1)} %collective-permute-done.5.near2_ref) | copy-start | bytes 1179652
  277.4 7.9 %copy-start.12 = (bf16[256,768]{1,0:T(8,128)(2,1)}, bf16[256,768]{1,0:T(8,128)(2,1)S(1)}, u32[]{:S(2)}) copy-start(bf16[256,768]{1,0:T(8,128)(2,1)S(1)} %collective-permute-done.6.away_ref) | copy-start | bytes 1179652
  (8 other events, 6.5 us)
Sparse Core Ops, SparseCore 0:
  13.0 99.8 all-gather.1

commit v3 on v2

--- a/solution.py
+++ b/solution.py
@@ -13,6 +13,7 @@
 F32 = jnp.float32
 BF16 = jnp.bfloat16
 VMEM_LIMIT = 60 * 1024 * 1024
+SMALL_LIMIT = 60 * 1024 * 1024
 EXT = 64
 
 
@@ -37,10 +38,8 @@
     return (e - jnp.mean(e, axis=-1, keepdims=True) - n * jnp.mean(e * n, axis=-1, keepdims=True)) * scale
 
 
-def params(steps=1):
-    return pltpu.CompilerParams(
-        dimension_semantics=("arbitrary",) * steps, vmem_limit_bytes=VMEM_LIMIT
-    )
+def params(limit=VMEM_LIMIT):
+    return pltpu.CompilerParams(dimension_semantics=("arbitrary",), vmem_limit_bytes=limit)
 
 
 def cost(flops, moved, exps=0):
@@ -82,7 +81,7 @@
             jax.ShapeDtypeStruct((tall, 2 * d + width + EXT), BF16),
             jax.ShapeDtypeStruct((copies, tall, 3 * width + EXT), BF16),
         ),
-        compiler_params=pltpu.CompilerParams(vmem_limit_bytes=VMEM_LIMIT),
+        compiler_params=pltpu.CompilerParams(vmem_limit_bytes=SMALL_LIMIT),
         cost_estimate=cost(0, 2e6),
         name="pack",
     )(fc, pj, out, qkv, vec, qb, fb)
@@ -533,11 +532,10 @@
     sum_ref[:, :d] = (dot(nt_ref[...], gl_ref[0]) + came_ref[0, :, :d].astype(F32)).astype(BF16)
     sum_ref[:, d : 2 * d] = (dot(ct_ref[...], act_ref[0]) + came_ref[0, :, d : 2 * d].astype(F32)).astype(BF16)
     depth, step = as_ref.shape[1], as_ref.shape[2]
-    order = halving_order(depth)
     cut = cols // 2
 
     def block(xr, zr):
-        at = ((order[zr] ^ index_ref[2]) * 2 + (xr ^ index_ref[3])) * step
+        at = (zr * 2 + (xr ^ index_ref[2])) * step
         return pl.ds(pl.multiple_of(at, 16), step)
 
     for zr in range(depth):
@@ -555,11 +553,6 @@
         for xr in range(2):
             for zr in range(depth):
                 ak_ref[xr, zr] = sum_ref[block(xr, zr), :cut]
-
-
-def halving_order(count):
-    bits = count.bit_length() - 1
-    return [int(format(n, "b").zfill(bits)[::-1], 2) if bits else 0 for n in range(count)]
 
 
 def weights(mode, index, n2, cot, gb, mix, act, gl, vec, gfb, order, strip, came=None, shards=None):
@@ -612,31 +605,89 @@
     )(*operands)
 
 
-def finish_wide_kernel(ak_ref, ar_ref, bk_ref, br_ref, fc_ref, pj_ref, out_ref, g_ref, b_ref, ob_ref, pb_ref, fb_ref):
-    tall, d = fc_ref.shape
+def merge_kernel(side_ref, ak_ref, ac_ref, bk_ref, bc_ref, nk_ref, nc_ref, vec_ref, out_ref, turn_ref):
+    depth, step, cut = ak_ref.shape
+    at = 2 * cut + nk_ref.shape[2] - EXT
+    turn_ref[...] = jnp.transpose(vec_ref[...])
+    for z in range(depth):
+        out_ref[z, :, :cut] = (ak_ref[z].astype(F32) + ac_ref[z].astype(F32)).astype(BF16)
+        out_ref[z, :, cut : 2 * cut] = (bk_ref[z].astype(F32) + bc_ref[z].astype(F32)).astype(BF16)
+        out_ref[z, :, 2 * cut :] = (nk_ref[z].astype(F32) + nc_ref[z].astype(F32)).astype(BF16)
+        here = pl.ds(pl.multiple_of((2 * z + side_ref[0]) * step, 8), step)
+        out_ref[z, :, at : at + 8] = turn_ref[here, :].astype(BF16)
+
+
+def merge(side, *parts):
+    depth, step, cut = parts[0].shape
+    cols = 2 * cut + parts[4].shape[2]
+    whole = lambda array: pl.BlockSpec(array.shape, lambda i, ix: (0,) * array.ndim)
+    out = jax.ShapeDtypeStruct((depth, step, cols), BF16)
+    return pl.pallas_call(
+        merge_kernel,
+        out_shape=out,
+        grid_spec=pltpu.PrefetchScalarGridSpec(
+            num_scalar_prefetch=1,
+            grid=(1,),
+            in_specs=[whole(p) for p in parts],
+            out_specs=whole(out),
+            scratch_shapes=[pltpu.VMEM(parts[6].shape[::-1], F32)],
+        ),
+        compiler_params=params(),
+        cost_estimate=cost(0, 6e6),
+        name="merge",
+    )(side, *parts)
+
+
+def finish_wide(t, fc_ref, pj_ref, out_ref, g_ref, b_ref, ob_ref, pb_ref, fb_ref):
+    d = fc_ref.shape[1]
     width = out_ref.shape[0]
-    cut = ak_ref.shape[1]
-    a = ak_ref[...].astype(F32) + ar_ref[...].astype(F32)
-    b = bk_ref[...].astype(F32) + br_ref[...].astype(F32)
-    fc_ref[...] = a[:, :d]
-    pj_ref[: cut - d, :] = jnp.transpose(a[:, d:])
-    pj_ref[cut - d :, :] = jnp.transpose(b[:, : 2 * d - cut])
-    rest = jnp.transpose(b[:, 2 * d - cut :])
+    fc_ref[...] = t[:, :d]
+    pj_ref[...] = jnp.transpose(t[:, d : 2 * d])
+    rest = jnp.transpose(t[:, 2 * d : 2 * d + width + EXT])
     out_ref[...] = rest[:width]
     g_ref[...] = rest[width : width + 1]
     b_ref[...] = rest[width + 1 : width + 2]
     ob_ref[...] = rest[width + 2 : width + 3]
     pb_ref[...] = rest[width + 3 : width + 4]
     rows, strip = fb_ref.shape
-    at = 2 * d - cut + width + 8
-    fb_ref[...] = b[:rows, at : at + strip]
-
-
-def finish_wide(ak, ar, bk, br, d, width, bias_shape):
-    tall = ak.shape[0]
+    at = 2 * d + width + 8
+    fb_ref[...] = t[:rows, at : at + strip]
+
+
+def finish_narrow(t, qkv_ref, qb_ref, vec_ref):
+    width = qkv_ref.shape[2]
+    for s in range(3):
+        qkv_ref[s] = t[:, s * width : (s + 1) * width]
+    heads, piece = qb_ref.shape[1:]
+    edge = 3 * width + 8
+    for s in range(3):
+        qb_ref[s] = t[s * heads : (s + 1) * heads, edge : edge + piece]
+    vec_ref[...] = jnp.transpose(t[:, 512:640])[64:72]
+
+
+def total_of(ref):
+    total = ref[0].astype(F32)
+    for n in range(1, ref.shape[0]):
+        total = total + ref[n].astype(F32)
+    return total
+
+
+def finish_kernel(*refs):
+    total = total_of(refs[0])
+    if len(refs) == 12:
+        edge = total.shape[1] - 640
+        finish_wide(total[:, :edge], *refs[1:9])
+        finish_narrow(total[:, edge:], *refs[9:])
+    else:
+        finish_wide(total, *refs[2:10])
+        finish_narrow(total_of(refs[1]), *refs[10:])
+
+
+def finish(parts, d, width, fc_bias_shape, qkv_bias_shape):
+    tall = parts[0].shape[1]
     sds = lambda *shape: jax.ShapeDtypeStruct(shape, F32)
     return pl.pallas_call(
-        finish_wide_kernel,
+        finish_kernel,
         out_shape=(
             sds(tall, d),
             sds(d, tall),
@@ -645,17 +696,20 @@
             sds(1, tall),
             sds(1, tall),
             sds(1, tall),
-            sds(*bias_shape),
+            sds(*fc_bias_shape),
+            sds(3, tall, width),
+            sds(*qkv_bias_shape),
+            sds(8, tall),
         ),
-        compiler_params=pltpu.CompilerParams(vmem_limit_bytes=VMEM_LIMIT),
-        cost_estimate=cost(0, 2e6),
-        name="finish_wide",
-    )(ak, ar, bk, br)
-
-
-def project_back_kernel(
-    piece, me_ref, own_ref, far_ref, grad_ref, w_ref, order_ref, keep_ref, send_ref, dw_ref, w3_ref, dw3_ref, gain_ref, vec_ref, bias_ref
-):
+        compiler_params=pltpu.CompilerParams(vmem_limit_bytes=SMALL_LIMIT),
+        cost_estimate=cost(0, 4e6),
+        name="finish",
+    )(*parts)
+
+
+def project_back_kernel(piece, me_ref, own_ref, far_ref, grad_ref, w_ref, order_ref, keep_ref, send_ref, sum_ref, *rest):
+    parted = rest[:-6]
+    dw_ref, w3_ref, dw3_ref, gain_ref, vec_ref, bias_ref = rest[-6:]
     i = pl.program_id(0)
     steps = pl.num_programs(0)
     width = grad_ref.shape[2]
@@ -701,21 +755,34 @@
             turned_bias = turned_bias + dot_nt(spread, order_ref[s])
         tall = jnp.concatenate([vec_ref[...], turned_bias, jnp.zeros((EXT - 16, d), F32)], axis=0)
         dw_ref[:, 3 * width :] = jnp.transpose(tall).astype(BF16)
-
-
-def project_back(me, own, far, grad, w, order, piece):
+        if not parted:
+            sum_ref[...] = dw_ref[...]
+            return
+        sum_ref[...] = vec_ref[...]
+        near_ref, away_ref = parted
+        depth, step = near_ref.shape[:2]
+        for z in range(depth):
+            near_ref[z] = dw_ref[pl.ds(pl.multiple_of((2 * z + me_ref[1]) * step, 16), step), :]
+            away_ref[z] = dw_ref[pl.ds(pl.multiple_of((2 * z + 1 - me_ref[1]) * step, 16), step), :]
+
+
+def project_back(me, own, far, grad, w, order, piece, shards):
     half, rows, d = own.shape
     width = grad.shape[2]
     blocks = 2 * half
     sds = jax.ShapeDtypeStruct
     rel = lambda i, me: ((i ^ me[0]) // 2, 0, 0)
+    whole = lambda *shape: pl.BlockSpec(shape, lambda i, me: (0,) * len(shape))
+    last = [w.shape]
+    if shards:
+        last = [(8, d)] + [(shards // 2, d // shards, w.shape[1])] * 2
     return pl.pallas_call(
         functools.partial(project_back_kernel, piece),
         out_shape=(
             sds((half, rows, d), F32),
             sds((half, rows, d), BF16),
-            sds(w.shape, BF16),
-        ),
+        )
+        + tuple(sds(shape, BF16 if len(shape) == 3 or not shards else F32) for shape in last),
         grid_spec=pltpu.PrefetchScalarGridSpec(
             num_scalar_prefetch=1,
             grid=(blocks,),
@@ -729,9 +796,10 @@
             out_specs=(
                 pl.BlockSpec((1, rows, d), rel),
                 pl.BlockSpec((1, rows, d), rel),
-                pl.BlockSpec(w.shape, lambda i, me: (0, 0)),
-            ),
+            )
+            + tuple(whole(*shape) for shape in last),
             scratch_shapes=[
+                pltpu.VMEM(w.shape, BF16),
                 pltpu.VMEM((3, d, width), BF16),
                 pltpu.VMEM((3, d, width), F32),
                 pltpu.VMEM((8, d), F32),
@@ -771,36 +839,10 @@
         grid=(half,),
         in_specs=[piece, piece],
         out_specs=(flat,) * half,
-        compiler_params=params(),
+        compiler_params=params(SMALL_LIMIT),
         cost_estimate=cost(0, 7e6),
         name="pair_sum",
     )(keep, came)
-
-
-def finish_narrow_kernel(g_ref, qkv_ref, qb_ref, vec_ref):
-    total = g_ref[0].astype(F32)
-    for n in range(1, g_ref.shape[0]):
-        total = total + g_ref[n].astype(F32)
-    width = qkv_ref.shape[2]
-    for s in range(3):
-        qkv_ref[s] = total[:, s * width : (s + 1) * width]
-    heads, piece = qb_ref.shape[1:]
-    edge = 3 * width + 8
-    for s in range(3):
-        qb_ref[s] = total[s * heads : (s + 1) * heads, edge : edge + piece]
-    vec_ref[...] = jnp.transpose(total[:, 512:640])[64:72]
-
-
-def finish_narrow(g, width, bias_shape):
-    tall = g.shape[1]
-    sds = lambda *shape: jax.ShapeDtypeStruct(shape, F32)
-    return pl.pallas_call(
-        finish_narrow_kernel,
-        out_shape=(sds(3, tall, width), sds(*bias_shape), sds(8, tall)),
-        compiler_params=pltpu.CompilerParams(vmem_limit_bytes=VMEM_LIMIT),
-        cost_estimate=cost(0, 2e6),
-        name="finish_narrow",
-    )(g)
 
 
 def finish_rows_kernel(side_ref, tok_ref, near_ref, near2_ref, away_ref, away2_ref, gh_ref, w_ref, out_ref, gain_ref):
@@ -831,7 +873,7 @@
             out_specs=piece,
             scratch_shapes=[pltpu.VMEM((8, d), F32)],
         ),
-        compiler_params=params(),
+        compiler_params=params(SMALL_LIMIT),
         cost_estimate=cost(0, 6e6),
         name="finish_rows",
     )(side, tok, near, near2, away, away2, gh, w)
@@ -840,6 +882,9 @@
 def one_hot_order(sources, size):
     row = lax.broadcasted_iota(jnp.int32, (size, sources.shape[1]), 0)
     return jnp.where(row == sources, 1.0, 0.0).astype(BF16)
+
+
+barrier = lax.optimization_barrier
 
 
 def plus(a, b):
@@ -870,10 +915,8 @@
     assert micro == sides == 2 and parts == 4
     side = lax.axis_index("ctx")
     slot = lax.axis_index("tp")
-    deep = lax.axis_index("dp")
-    depth = lax.axis_size("dp")
     me = side * parts + slot
-    me_array = jnp.full((1,), me, jnp.int32)
+    me_array = jnp.stack([me, side]).astype(jnp.int32)
     side_array = jnp.full((1,), side, jnp.int32)
     tall = qkv_weight.shape[1]
     heads, piece = qkv_bias.shape[1], qkv_bias.shape[2]
@@ -882,9 +925,6 @@
 
     def swap(array, mask):
         return lax.ppermute(array, ("ctx", "tp"), [(n, n ^ mask) for n in range(group)])
-
-    def swap_deep(array, mask):
-        return lax.ppermute(array, "dp", [(n, n ^ mask) for n in range(depth)])
 
     tok = tokens[:, 0]
     cot = cotangent[:, 0]
@@ -923,52 +963,62 @@
     grad_mix = lax.all_to_all(grad_mix, ("ctx", "tp"), 0, 0, tiled=True)
 
     parcels = (n2, cot_rows, gb, mix, act, gl, vec, gfb, order_fc, strip)
-    cut = wide.shape[1] // 2
-    if tall % 16 == 0 and depth & (depth - 1) == 0:
+    exchange = tall % 16 == 0
+    if exchange:
         core, row = slot % 2, slot // 2
-        index = lambda lane: jnp.stack([(1 - row) * 2 + lane, row * 2 + lane, deep, side]).astype(jnp.int32)
+        index = lambda lane: jnp.stack([(1 - row) * 2 + lane, row * 2 + lane, side]).astype(jnp.int32)
         came = swap(weights("send", index(1 - core), *parcels), 1)
         a_send, a_keep, b_send, b_keep = weights("keep", index(core), *parcels, came=came, shards=shards)
         a_came, b_came = swap(a_send, 2), swap(b_send, parts)
-        a_send, a_keep = plus(a_keep[1], a_came[1]), plus(a_keep[0], a_came[0])
-        b_send, b_keep = plus(b_keep[1], b_came[1]), plus(b_keep[0], b_came[0])
-        a_came, b_came = swap(a_send, parts), swap(b_send, 2)
-        left, mask = depth, 1
-        while left > 1:
-            left //= 2
-            a_send, a_keep = plus(a_keep[left:], a_came[left:]), plus(a_keep[:left], a_came[:left])
-            b_send, b_keep = plus(b_keep[left:], b_came[left:]), plus(b_keep[:left], b_came[:left])
-            a_came, b_came = swap_deep(a_send, mask), swap_deep(b_send, mask)
-            mask *= 2
-        a_keep, a_came, b_keep, b_came = a_keep[0], a_came[0], b_keep[0], b_came[0]
     else:
         grad_wide = weights("all", jnp.arange(parts, dtype=jnp.int32), *parcels)
         grad_wide = lax.psum_scatter(
             grad_wide.reshape(parts * d, wide.shape[1]), ("tp", "dp", "ctx"), scatter_dimension=0, tiled=True
         )
-        a_keep, b_keep = grad_wide[:, :cut], grad_wide[:, cut:]
-        a_came, b_came = jnp.zeros_like(a_keep), jnp.zeros_like(b_keep)
 
     grad_triple = attend_back(triple, grad_mix, mixed_turned, level)
+    if exchange:
+        a_came, b_came, grad_triple = barrier((a_came, b_came, grad_triple))
+        a_send, b_send = plus(a_keep[1], a_came[1]), plus(b_keep[1], b_came[1])
+        a_send, b_send, grad_triple = barrier((a_send, b_send, grad_triple))
+        a_keep, b_keep = plus(a_keep[0], a_came[0]), plus(b_keep[0], b_came[0])
+        a_came, b_came = swap(a_send, parts), swap(b_send, 2)
     order_back = order_in.reshape(d, 3, width).transpose(1, 0, 2)
-    keep, send, grad_in = project_back(me_array, own, far, grad_triple, w_in, order_back, piece)
-
-    near, *sends = pair_sum(keep, swap(send, 1))
+    back = project_back(me_array, own, far, grad_triple, w_in, order_back, piece, shards if exchange else 0)
+    if exchange:
+        a_came, b_came, back = barrier((a_came, b_came, back))
+    keep, send = back[:2]
+
+    send_came = swap(send, 1)
+    if exchange:
+        vec_in, n_keep, n_send = back[2:]
+        n_came = swap(n_send, parts)
+        vec_in = vec_in + swap(vec_in, 1)
+        vec_in, send_came = barrier((vec_in, send_came))
+        vec_came = swap(vec_in, 2)
+    near, *sends = pair_sum(keep, send_came)
     arrived = [swap(sends[n - 1], 2 * n) for n in range(1, group // 2)]
 
-    grad_in = lax.all_to_all(grad_in.reshape(narrow.shape), ("dp", "ctx"), 0, 0, tiled=True)
-    grad_qkv_weight, grad_qkv_bias, vec_in = finish_narrow(grad_in, width, qkv_bias.shape)
-    mask = parts // 2
-    while mask:
-        vec_in = vec_in + swap(vec_in, mask)
-        mask //= 2
+    if exchange:
+        vec_came, near = barrier((vec_came, near))
+        vec_in = vec_in + vec_came
+        vec_in = vec_in + swap(vec_in, parts)
+        total = merge(side_array, a_keep, a_came, b_keep, b_came, n_keep, n_came, vec_in)
+        totals = (lax.all_to_all(total, "dp", 0, 0, tiled=True),)
+    else:
+        grad_in = back[2].reshape(narrow.shape)
+        totals = (grad_wide[None], lax.all_to_all(grad_in, ("dp", "ctx"), 0, 0, tiled=True))
 
     grad_tokens = finish_rows(
         side_array, tok, near, *arrived, grad_hidden.reshape(micro, rows, d), w_in
     )
-    fc_grad, proj_grad, out_grad, gain2, shift2, out_b, proj_b, fc_b = finish_wide(
-        a_keep, a_came, b_keep, b_came, d, width, fc_bias.shape
-    )
+    done = finish(totals, d, width, fc_bias.shape, qkv_bias.shape)
+    fc_grad, proj_grad, out_grad, gain2, shift2, out_b, proj_b, fc_b, grad_qkv_weight, grad_qkv_bias, vec_in = done
+    if not exchange:
+        mask = parts // 2
+        while mask:
+            vec_in = vec_in + swap(vec_in, mask)
+            mask //= 2
     return (
         y.reshape(micro, 1, rows, d),
         grad_tokens[:, None],

time: 303 us -> 305 us (level)
  waiting for transfers between devices: 77.9 us -> 83 us
  other arithmetic: 16.8 us -> 12.3 us
  Pallas kernels: 143 us -> 147 us
  starting transfers between devices: 37.2 us -> 33.9 us
    all_to_all x1, waiting for transfers between devices: 0.01 us -> 17.8 us  [local(): totals = (lax.all_to_all(total, 'dp', 0, 0, tiled=True),)]
    ppermute x15 -> x17, waiting for transfers between devices: 59.3 us -> 46.5 us  [swap(): lax.ppermute(array, ('ctx', 'tp'), [(n, n ^ mask) for n in range(group)])]
    convert_element_type x6 -> x1, other arithmetic: 9.12 us -> 3.35 us  [plus(): return (a.astype(F32) + b.astype(F32)).astype(BF16)]
    ppermute x4 -> x0, starting transfers between devices: 4.95 us -> none  [swap_deep(): return lax.ppermute(array, 'dp', [(n, n ^ mask) for n in range(depth)])]
    ppermute x15 -> x17, starting transfers between devices: 14.6 us -> 16.4 us  [swap(): lax.ppermute(array, ('ctx', 'tp'), [(n, n ^ mask) for n in range(group)])]
    unnamed x34 -> x40, local copies, waits for them, and re-layouts: 10.9 us -> 10 us
  transfers between devices with their start and end apart: 24 -> 22, of which waited for: 10 -> 12; matrix products, arithmetic and copies ran while one was open for 6% -> 3% of each run, Pallas kernels for 35% -> 35%
where the time goes in v3:
time: 305 us; the launch traced here: 304 us
  Pallas kernels  147 us (48%)
  waiting for transfers between devices  83 us (27%)
  starting transfers between devices  33.9 us (11%)
  between operations  14.2 us (5%)
  local copies, waits for them, and re-layouts  13.5 us (4%)
  other arithmetic  12.3 us (4%)
    ppermute x17, waiting for transfers between devices, swap(): lax.ppermute(array, ('ctx', 'tp'), [(n, n ^ mask) for n in range(group)])  46.5 us
    pallas_call x1, Pallas kernels, attend_back(): pl.pallas_call(attend_back_kernel, out_shape=jax.ShapeDtypeStruct(triple....  32 us
    pallas_call x1, Pallas kernels, attend(): pl.pallas_call(attend_kernel, out_shape=(jax.ShapeDtypeStruct((span // ro...  28.8 us
    pallas_call x1, Pallas kernels, middle(): pl.pallas_call(functools.partial(middle_kernel, strip), out_shape=(sds((r...  21.6 us
    pallas_call x2, Pallas kernels, weights(): pl.pallas_call(functools.partial(weights_kernel, mode, strip), out_shape=...  20.7 us
    all_to_all x1, waiting for transfers between devices, local(): totals = (lax.all_to_all(total, 'dp', 0, 0, tiled=True),)  17.8 us
    ppermute x17, starting transfers between devices, swap(): lax.ppermute(array, ('ctx', 'tp'), [(n, n ^ mask) for n in range(group)])  16.4 us
    pallas_call x1, Pallas kernels, project_back(): pl.pallas_call(functools.partial(project_back_kernel, piece), out_shape=(...  14.7 us
  transfers between devices with their start and end apart: 22, of which 12 were waited for; matrix products, arithmetic and copies ran while one was open for 3% of the time, Pallas kernels for 35%

profile of v3, /device:TPU:0, one launch (start us, length us, event | category | flops | bytes accessed | tf_op | source)
XLA Modules:
  0.0 304.0 jit_solution(4303425706278313451)
XLA Ops:
  7.2 1.8 copy.28.pj_ref
  10.4 2.5 pack.1
  13.7 3.0 collective-permute-start.1
  18.2 6.3 %all-to-all-start = ((bf16[8,96,640]{2,1,0:T(8,128)(2,1)}), bf16[8,96,640]{2,1,0:T(8,128)(2,1)S(1)}, u32[]{:S(2)}, u32[]{:S(2)}) async-start(bf16[8,96,640]{2,1,0:T(8,128)(2,1)} %get-tuple-element.69), calls=%async_computation | async-start | bytes 1966080 | tf_op jit(solution)/shard_map/all_to_all | solution.py:947
  24.5 4.1 %collective-permute-done.1 = bf16[256,768]{1,0:T(8,128)(2,1)S(1)} collective-permute-done((bf16[256,768]{1,0:T(8,128)(2,1)S(1)}, bf16[256,768]{1,0:T(8,128)(2,1)S(1)}, u32[]{:S(2)}, u32[]{:S(2)}) %collective-permute-start.1) | collective-permute-done | bytes 393248 | tf_op jit(solution)/shard_map/ppermute | solution.py:927
  28.5 15.9 %collective-permute-done.2 = bf16[256,768]{1,0:T(8,128)(2,1)} collective-permute-done((bf16[256,768]{1,0:T(8,128)(2,1)S(1)}, bf16[256,768]{1,0:T(8,128)(2,1)}, u32[]{:S(2)}, u32[]{:S(2)}) %collective-permute-start.2) | collective-permute-done | bytes 393248 | tf_op jit(solution)/shard_map/ppermute | solution.py:927
  48.6 9.3 %all-to-all-done = bf16[8,96,640]{2,1,0:T(8,128)(2,1)S(1)} async-done(((bf16[8,96,640]{2,1,0:T(8,128)(2,1)}), bf16[8,96,640]{2,1,0:T(8,128)(2,1)S(1)}, u32[]{:S(2)}, u32[]{:S(2)}) %all-to-all-start) | async-done | bytes 983072 | tf_op jit(solution)/shard_map/all_to_all | solution.py:947
  58.9 10.9 %project.1.q_ref.k_ref.v_ref.qkv_ref = bf16[3,2048,192]{2,1,0:T(8,128)(2,1)} custom-call(s32[2]{0:T(128)} %pad_add_fusion.me_ref, bf16[4,256,768]{2,1,0:T(8,128)(2,1)} %copy-done.3, bf16[4,256,768]{2,1,0:T(8,128)(2,1)} %collective-permute-done.3.far_ref, bf16[768,640]{1,0:T(8,128)(2,1)} %bitcast.50, bf16[768,576]{1,0:T(8,128)(2,1)} %select_convert_fusion.2.order_ref), custom_call_target="tpu_custom_call" | custom-call | flops 1811939328 | bytes 8000000 | tf_op jit(solution)/shard_map/project/pallas_call | solution.py:129
  69.8 28.8 %attend.1 = (bf16[8,192,256]{2,1,0:T(8,128)(2,1)}, f32[192,2048]{1,0:T(8,128)}, f32[8,2048]{1,0:T(8,128)}) custom-call(bf16[3,2048,192]{2,1,0:T(8,128)(2,1)} %project.1.q_ref.k_ref.v_ref.qkv_ref, bf16[3,2048,192]{2,1,0:T(8,128)(2,1)} %project.1.q_ref.k_ref.v_ref.qkv_ref, bf16[3,2048,192]{2,1,0:T(8,128)(2,1)} %project.1.q_ref.k_ref.v_ref.qkv_ref), custom_call_target="tpu_custom_call" | custom-call | flops 3221225472 | bytes 8000000 | tf_op jit(solution)/shard_map/attend/pallas_call | solution.py:216
  98.6 3.7 %all-to-all-start.1 = ((bf16[8,192,256]{2,1,0:T(8,128)(2,1)}), bf16[8,192,256]{2,1,0:T(8,128)(2,1)S(1)}, u32[]{:S(2)}, u32[]{:S(2)}) async-start(bf16[8,192,256]{2,1,0:T(8,128)(2,1)} %get-tuple-element.70), calls=%async_computation.1 | async-start | bytes 1572864 | tf_op jit(solution)/shard_map/all_to_all | solution.py:956
  104.4 9.4 %all-to-all-done.1.mix_ref = bf16[8,192,256]{2,1,0:T(8,128)(2,1)S(1)} async-done(((bf16[8,192,256]{2,1,0:T(8,128)(2,1)}), bf16[8,192,256]{2,1,0:T(8,128)(2,1)S(1)}, u32[]{:S(2)}, u32[]{:S(2)}) %all-to-all-start.1) | async-done | bytes 786464 | tf_op jit(solution)/shard_map/all_to_all | solution.py:956
  114.6 21.6 %middle.1 = (bf16[512,768]{1,0:T(8,128)(2,1)}, f32[512,768]{1,0:T(8,128)}, bf16[8,192,256]{2,1,0:T(8,128)(2,1)}, bf16[512,768]{1,0:T(8,128)(2,1)}, bf16[4,512,76...) custom-call(bf16[512,768]{1,0:T(8,128)(2,1)} %bitcast.58, ...), custom_call_target="tpu_custom_call" | custom-call | flops 10871635968 | bytes 30000000 | tf_op jit(solution)/shard_map/middle/pallas_call | solution.py:458
  136.2 9.4 %weights_send.1 = bf16[2,768,1792]{2,1,0:T(8,128)(2,1)} custom-call(s32[3]{0:T(128)} %add_add_fusion.1.index_ref, bf16[512,768]{1,0:T(8,128)(2,1)} %get-tuple-element.73.n2_ref, bf16[512,768]{1,0:T(8,128)(2,1)} %bitcast.56, bf16[512,768]{1,0:T(8,128)(2,1)} %get-tuple-element.74.gb_ref, bf16[2,4,192,256]{3,2,1,0:T(8,128)(2,1)} %bitcast.53, ...), custom_call_target="tpu_custom_call" | custom-call | flops 2818572288 | bytes 12000000 | tf_op jit(solution)/shard_map/weights_send/pallas_call | solution.py:592
  146.2 3.8 %all-to-all-start.2 = ((bf16[8,192,256]{2,1,0:T(8,128)(2,1)}), bf16[8,192,256]{2,1,0:T(8,128)(2,1)S(1)}, u32[]{:S(2)}, u32[]{:S(2)}) async-start(bf16[8,192,256]{2,1,0:T(8,128)(2,1)} %get-tuple-element.82), calls=%async_computation.2 | async-start | bytes 1572864 | tf_op jit(solution)/shard_map/all_to_all | solution.py:963
  150.0 5.0 %collective-permute-done.4.rest_0_ = bf16[2,768,1792]{2,1,0:T(8,128)(2,1)} collective-permute-done((bf16[2,768,1792]{2,1,0:T(8,128)(2,1)}, bf16[2,768,1792]{2,1,0:T(8,128)(2,1)}, u32[]{:S(2)}, u32[]{:S(2)}) %collective-permute-start.4) | collective-permute-done | bytes 5505056 | tf_op jit(solution)/shard_map/ppermute | solution.py:927
  155.0 11.4 %weights_keep.1 = (bf16[2,4,96,896]{3,2,1,0:T(8,128)(2,1)}, bf16[2,4,96,896]{3,2,1,0:T(8,128)(2,1)}, bf16[2,4,96,896]{3,2,1,0:T(8,128)(2,1)}, bf16[2,4,96,896]{3,2,1,0:T(8,128)(2,1)}) custom-call(s32[3]{0:T(128)} %add_add_fusion.index_ref, bf16[512,768]{1,0:T(8,128)(2,1)} %get-tuple-element.73.n2_ref, bf16[512,768]{1,0:T(8,128)(2,1)} %bitcast.57, ...), custom_call_target="tpu_custom_call" | custom-call | flops 2818572288 | bytes 12000000 | tf_op jit(solution)/shard_map/weights_keep/pallas_call | solution.py:592
  169.3 32.0 %attend_back.1.grad_ref = bf16[3,2048,192]{2,1,0:T(8,128)(2,1)} custom-call(bf16[3,2048,192]{2,1,0:T(8,128)(2,1)} %project.1.q_ref.k_ref.v_ref.qkv_ref, bf16[8,192,256]{2,1,0:T(8,128)(2,1)} %copy-done.9, f32[192,2048]{1,0:T(8,128)} %get-tuple-element.83.ot_ref, f32[8,2048]{1,0:T(8,128)} %get-tuple-element.84.level_ref), custom_call_target="tpu_custom_call" | custom-call | flops 8053063680 | bytes 10000000 | tf_op jit(solution)/shard_map/attend_back/pallas_call | solution.py:337
  201.3 3.3 %fusion.2 = (bf16[4,96,896]{2,1,0:T(8,128)(2,1)}, bf16[4,96,896]{2,1,0:T(8,128)(2,1)}, bf16[4,96,896]{2,1,0:T(8,128)(2,1)}, bf16[4,96,896]{2,1,0:T(8,128)(2,1)}) fusion(bf16[2,4,96,896]{3,2,1,0:T(8,128)(2,1)S(1)} %collective-permute-done.5, bf16[2,4,96,896]{3,2,1,0:T(8,128)(2,1)S(1)} %copy-done.7, bf16[2,4,96,896]{3,2,1,0:T(8,128)(2,1)} %collective-permute-done.6, ...), kind=kLoop, calls=%fused_computation.13 | loop fusion | flops 5505024 | bytes 8257536 | tf_op jit(solution)/shard_map/convert_element_type | solution.py:891
  208.3 14.7 %project_back.1 = (f32[4,256,768]{2,1,0:T(8,128)}, bf16[4,256,768]{2,1,0:T(8,128)(2,1)}, f32[8,768]{1,0:T(8,128)}, bf16[4,96,640]{2,1,0:T(8,128)(2,1)}, bf16[4,96,640]{2,1,0:T(8,128)(2,1)}) custom-call(s32[2]{0:T(128)} %pad_add_fusion.me_ref, bf16[4,256,768]{2,1,0:T(8,128)(2,1)} %copy-done.3, bf16[4,256,768]{2,1,0:T(8,128)(2,1)} %collective-permute-done.3.far_ref, ...), custom_call_target="tpu_custom_call" | custom-call | flops 3623878656 | bytes 15000000 | tf_op jit(solution)/shard_map/project_back/pallas_call | solution.py:779
  224.7 2.0 collective-permute-done.9
  227.5 1.5 collective-permute-start.11
  229.0 4.5 %pair_sum.1 = (f32[256,768]{1,0:T(8,128)}, bf16[256,768]{1,0:T(8,128)(2,1)}, bf16[256,768]{1,0:T(8,128)(2,1)}, bf16[256,768]{1,0:T(8,128)(2,1)}) custom-call(f32[4,256,768]{2,1,0:T(8,128)} %get-tuple-element.100.keep_ref, bf16[4,256,768]{2,1,0:T(8,128)(2,1)} %copy-done.6), custom_call_target="tpu_custom_call" | custom-call | bytes 7000000 | tf_op jit(solution)/shard_map/pair_sum/pallas_call | solution.py:835
  234.6 2.8 collective-permute-done.16
  238.8 4.1 %merge.1 = bf16[4,96,2432]{2,1,0:T(8,128)(2,1)} custom-call(s32[1]{0:T(128)} %bitcast.3.side_ref, bf16[4,96,896]{2,1,0:T(8,128)(2,1)} %get-tuple-element.140.ak_ref, bf16[4,96,896]{2,1,0:T(8,128)(2,1)} %copy-done.10, bf16[4,96,896]{2,1,0:T(8,128)(2,1)} %get-tuple-element.148.bk_ref, bf16[4,96,896]{2,1,0:T(8,128)(2,1)} %copy-done.11, ...), custom_call_target="tpu_custom_call" | custom-call | bytes 6000000 | tf_op jit(solution)/shard_map/merge/pallas_call | solution.py:625
  243.0 3.7 %all-to-all-start.3 = ((bf16[4,96,2432]{2,1,0:T(8,128)(2,1)}), bf16[4,96,2432]{2,1,0:T(8,128)(2,1)S(1)}, u32[]{:S(2)}, u32[]{:S(2)}) async-start(bf16[4,96,2432]{2,1,0:T(8,128)(2,1)} %merge.1), calls=%async_computation.3 | async-start | bytes 3735552 | tf_op jit(solution)/shard_map/all_to_all | solution.py:1007
  250.3 8.0 %collective-permute-done.12.near2_ref = bf16[256,768]{1,0:T(8,128)(2,1)S(1)} collective-permute-done((bf16[256,768]{1,0:T(8,128)(2,1)}, bf16[256,768]{1,0:T(8,128)(2,1)S(1)}, u32[]{:S(2)}, u32[]{:S(2)}) %collective-permute-start.12) | collective-permute-done | bytes 393248 | tf_op jit(solution)/shard_map/ppermute | solution.py:927
  258.3 1.9 collective-permute-done.13.away_ref
  260.2 6.7 %collective-permute-done.14.away2_ref = bf16[256,768]{1,0:T(8,128)(2,1)S(1)} collective-permute-done((bf16[256,768]{1,0:T(8,128)(2,1)S(1)}, bf16[256,768]{1,0:T(8,128)(2,1)S(1)}, u32[]{:S(2)}, u32[]{:S(2)}) %collective-permute-start.14) | collective-permute-done | bytes 393248 | tf_op jit(solution)/shard_map/ppermute | solution.py:927
  267.7 4.5 %finish_rows.1 = f32[2,256,768]{2,1,0:T(8,128)} custom-call(s32[1]{0:T(128)} %bitcast.3.side_ref, bf16[2,256,768]{2,1,0:T(8,128)(2,1)} %bitcast.59, f32[256,768]{1,0:T(8,128)} %get-tuple-element.103.near_ref, bf16[256,768]{1,0:T(8,128)(2,1)} %copy-done.14, bf16[256,768]{1,0:T(8,128)(2,1)} %copy-done.15, bf16[256,768]{1,0:T(8,128)(2,1)} %copy-done.16, ...), custom_call_target="tpu_custom_call" | custom-call | bytes 6000000 | tf_op jit(solution)/shard_map/finish_rows/pallas_call | solution.py:866
  272.2 17.8 %all-to-all-done.3.refs_0_ = bf16[4,96,2432]{2,1,0:T(8,128)(2,1)S(1)} async-done(((bf16[4,96,2432]{2,1,0:T(8,128)(2,1)}), bf16[4,96,2432]{2,1,0:T(8,128)(2,1)S(1)}, u32[]{:S(2)}, u32[]{:S(2)}) %all-to-all-start.3) | async-done | bytes 1867808 | tf_op jit(solution)/shard_map/all_to_all | solution.py:1007
  291.3 2.7 finish.1
  294.0 1.9 copy.31
  (82 shorter events, 30.8 us)
Async XLA Ops:
  7.2 5.7 %copy-start.4 = (bf16[2,1,256,768]{3,2,1,0:T(8,128)(2,1)S(1)}, bf16[2,1,256,768]{3,2,1,0:T(8,128)(2,1)}, u32[]{:S(2)}) copy-start(bf16[2,1,256,768]{3,2,1,0:T(8,128)(2,1)} %param.14) | copy-start | bytes 2359300
  7.2 106.5 %all-gather.2.cloned.1.call-start = ((), (), s32[]{:S(2)}) async-start(), calls=%async_computation.4 | async-start | bytes 11354112 | tf_op jit(solution)/shard_map/all_gather | solution.py:935
  13.7 31.4 %copy-start.5 = (bf16[1,256,768]{2,1,0:T(8,128)(2,1)S(1)}, bf16[1,256,768]{2,1,0:T(8,128)(2,1)}, u32[]{:S(2)}) copy-start(bf16[1,256,768]{2,1,0:T(8,128)(2,1)} %get-tuple-element.142) | copy-start | bytes 1179652
  13.7 14.8 %collective-permute-start.1 = (bf16[256,768]{1,0:T(8,128)(2,1)S(1)}, bf16[256,768]{1,0:T(8,128)(2,1)S(1)}, u32[]{:S(2)}, u32[]{:S(2)}) collective-permute-start(bf16[256,768]{1,0:T(8,128)(2,1)S(1)} %get-tuple-element.144), channel_id=1, source_target_pairs={{0,4},{1,5},{2,6},{3,7},{4,0},{5,1},{6,2},{7,3},{8,12},{9,13},{10,... | collective-permute-start | bytes 1179656 | tf_op jit(solution)/shard_map/ppermute | solution.py:927
  16.7 27.7 %collective-permute-start.2 = (bf16[256,768]{1,0:T(8,128)(2,1)S(1)}, bf16[256,768]{1,0:T(8,128)(2,1)}, u32[]{:S(2)}, u32[]{:S(2)}) collective-permute-start(bf16[256,768]{1,0:T(8,128)(2,1)S(1)} %get-tuple-element.144), channel_id=1, source_target_pairs={{0,6},{1,7},{2,4},{3,5},{4,2},{5,3},{6,0},{7,1},{8,14},{9,15},{10,... | collective-permute-start | bytes 1179656 | tf_op jit(solution)/shard_map/ppermute | solution.py:927
  18.1 26.2 %collective-permute-start = (bf16[256,768]{1,0:T(8,128)(2,1)S(1)}, bf16[256,768]{1,0:T(8,128)(2,1)S(1)}, u32[]{:S(2)}, u32[]{:S(2)}) collective-permute-start(bf16[256,768]{1,0:T(8,128)(2,1)S(1)} %get-tuple-element.143), channel_id=1, source_target_pairs={{0,2},{1,3},{2,0},{3,1},{4,6},{5,7},{6,4},{7,5},{8,10},{9,11},{10,... | collective-permute-start | bytes 1179656 | tf_op jit(solution)/shard_map/ppermute | solution.py:927
  18.2 39.8 %all-to-all-start = ((bf16[8,96,640]{2,1,0:T(8,128)(2,1)}), bf16[8,96,640]{2,1,0:T(8,128)(2,1)S(1)}, u32[]{:S(2)}, u32[]{:S(2)}) async-start(bf16[8,96,640]{2,1,0:T(8,128)(2,1)} %get-tuple-element.69), calls=%async_computation | async-start | bytes 1966080 | tf_op jit(solution)/shard_map/all_to_all | solution.py:947
  46.4 11.5 %copy-start.3 = (bf16[4,256,768]{2,1,0:T(8,128)(2,1)}, bf16[4,256,768]{2,1,0:T(8,128)(2,1)S(1)}, u32[]{:S(2)}) copy-start(bf16[4,256,768]{2,1,0:T(8,128)(2,1)S(1)} %pad_maximum_fusion.own_ref) | copy-start | bytes 4718596
  46.5 11.5 %collective-permute-start.3 = (bf16[4,256,768]{2,1,0:T(8,128)(2,1)S(1)}, bf16[4,256,768]{2,1,0:T(8,128)(2,1)}, u32[]{:S(2)}, u32[]{:S(2)}) collective-permute-start(bf16[4,256,768]{2,1,0:T(8,128)(2,1)S(1)} %pad_maximum_fusion.own_ref), channel_id=1, source_target_pairs={{0,1},{1,0},{2,3},{3,2},{4,5},{5,4},{6,7},{7,6},{8,9},{9,8},{10,11... | collective-permute-start | bytes 4718600 | tf_op jit(solution)/shard_map/ppermute | solution.py:927
  98.6 15.1 %all-to-all-start.1 = ((bf16[8,192,256]{2,1,0:T(8,128)(2,1)}), bf16[8,192,256]{2,1,0:T(8,128)(2,1)S(1)}, u32[]{:S(2)}, u32[]{:S(2)}) async-start(bf16[8,192,256]{2,1,0:T(8,128)(2,1)} %get-tuple-element.70), calls=%async_computation.1 | async-start | bytes 1572864 | tf_op jit(solution)/shard_map/all_to_all | solution.py:956
  145.6 9.4 %collective-permute-start.4 = (bf16[2,768,1792]{2,1,0:T(8,128)(2,1)}, bf16[2,768,1792]{2,1,0:T(8,128)(2,1)}, u32[]{:S(2)}, u32[]{:S(2)}) collective-permute-start(bf16[2,768,1792]{2,1,0:T(8,128)(2,1)} %weights_send.1), channel_id=1, source_target_pairs={{0,1},{1,0},{2,3},{3,2},{4,5},{5,4},{6,7},{7,6},{8,9},{9,8},{10,11... | collective-permute-start | bytes 16515080 | tf_op jit(solution)/shard_map/ppermute | solution.py:927
  146.2 22.2 %all-to-all-start.2 = ((bf16[8,192,256]{2,1,0:T(8,128)(2,1)}), bf16[8,192,256]{2,1,0:T(8,128)(2,1)S(1)}, u32[]{:S(2)}, u32[]{:S(2)}) async-start(bf16[8,192,256]{2,1,0:T(8,128)(2,1)} %get-tuple-element.82), calls=%async_computation.2 | async-start | bytes 1572864 | tf_op jit(solution)/shard_map/all_to_all | solution.py:963
  166.3 35.0 %collective-permute-start.5 = (bf16[2,4,96,896]{3,2,1,0:T(8,128)(2,1)}, bf16[2,4,96,896]{3,2,1,0:T(8,128)(2,1)S(1)}, u32[]{:S(2)}, u32[]{:S(2)}) collective-permute-start(bf16[2,4,96,896]{3,2,1,0:T(8,128)(2,1)} %get-tuple-element.80), channel_id=1, source_target_pairs={{0,2},{1,3},{2,0},{3,1},{4,6},{5,7},{6,4},{7,5},{8,10},{9,11},{10,... | collective-permute-start | bytes 4128776 | tf_op jit(solution)/shard_map/ppermute | solution.py:927
  167.8 33.5 %collective-permute-start.6 = (bf16[2,4,96,896]{3,2,1,0:T(8,128)(2,1)}, bf16[2,4,96,896]{3,2,1,0:T(8,128)(2,1)}, u32[]{:S(2)}, u32[]{:S(2)}) collective-permute-start(bf16[2,4,96,896]{3,2,1,0:T(8,128)(2,1)} %get-tuple-element.81), channel_id=1, source_target_pairs={{0,4},{1,5},{2,6},{3,7},{4,0},{5,1},{6,2},{7,3},{8,12},{9,13},{10,... | collective-permute-start | bytes 4128776 | tf_op jit(solution)/shard_map/ppermute | solution.py:927
  169.3 32.0 %copy-start.7 = (bf16[2,4,96,896]{3,2,1,0:T(8,128)(2,1)S(1)}, bf16[2,4,96,896]{3,2,1,0:T(8,128)(2,1)}, u32[]{:S(2)}) copy-start(bf16[2,4,96,896]{3,2,1,0:T(8,128)(2,1)} %get-tuple-element.79) | copy-start | bytes 4128772
  169.3 32.0 %copy-start.8 = (bf16[2,4,96,896]{3,2,1,0:T(8,128)(2,1)S(1)}, bf16[2,4,96,896]{3,2,1,0:T(8,128)(2,1)}, u32[]{:S(2)}) copy-start(bf16[2,4,96,896]{3,2,1,0:T(8,128)(2,1)} %get-tuple-element.86) | copy-start | bytes 4128772
  204.7 18.3 %collective-permute-start.7 = (bf16[4,96,896]{2,1,0:T(8,128)(2,1)}, bf16[4,96,896]{2,1,0:T(8,128)(2,1)S(1)}, u32[]{:S(2)}, u32[]{:S(2)}) collective-permute-start(bf16[4,96,896]{2,1,0:T(8,128)(2,1)} %get-tuple-element.89), channel_id=1, source_target_pairs={{0,4},{1,5},{2,6},{3,7},{4,0},{5,1},{6,2},{7,3},{8,12},{9,13},{10,... | collective-permute-start | bytes 2064392 | tf_op jit(solution)/shard_map/ppermute | solution.py:927
  206.2 16.8 %collective-permute-start.8 = (bf16[4,96,896]{2,1,0:T(8,128)(2,1)}, bf16[4,96,896]{2,1,0:T(8,128)(2,1)S(1)}, u32[]{:S(2)}, u32[]{:S(2)}) collective-permute-start(bf16[4,96,896]{2,1,0:T(8,128)(2,1)} %get-tuple-element.90), channel_id=1, source_target_pairs={{0,2},{1,3},{2,0},{3,1},{4,6},{5,7},{6,4},{7,5},{8,10},{9,11},{10,... | collective-permute-start | bytes 2064392 | tf_op jit(solution)/shard_map/ppermute | solution.py:927
  223.0 15.1 %copy-start.10 = (bf16[4,96,896]{2,1,0:T(8,128)(2,1)}, bf16[4,96,896]{2,1,0:T(8,128)(2,1)S(1)}, u32[]{:S(2)}) copy-start(bf16[4,96,896]{2,1,0:T(8,128)(2,1)S(1)} %collective-permute-done.7.ac_ref) | copy-start | bytes 2064388
  223.0 15.0 %copy-start.11 = (bf16[4,96,896]{2,1,0:T(8,128)(2,1)}, bf16[4,96,896]{2,1,0:T(8,128)(2,1)S(1)}, u32[]{:S(2)}) copy-start(bf16[4,96,896]{2,1,0:T(8,128)(2,1)S(1)} %collective-permute-done.8.bc_ref) | copy-start | bytes 2064388
  223.0 4.4 %collective-permute-start.10 = (bf16[4,256,768]{2,1,0:T(8,128)(2,1)}, bf16[4,256,768]{2,1,0:T(8,128)(2,1)S(1)}, u32[]{:S(2)}, u32[]{:S(2)}) collective-permute-start(bf16[4,256,768]{2,1,0:T(8,128)(2,1)} %get-tuple-element.98), channel_id=1, source_target_pairs={{0,1},{1,0},{2,3},{3,2},{4,5},{5,4},{6,7},{7,6},{8,9},{9,8},{10,11... | collective-permute-start | bytes 4718600 | tf_op jit(solution)/shard_map/ppermute | solution.py:927
  223.1 15.0 %collective-permute-start.15 = (bf16[4,96,640]{2,1,0:T(8,128)(2,1)}, bf16[4,96,640]{2,1,0:T(8,128)(2,1)S(1)}, u32[]{:S(2)}, u32[]{:S(2)}) collective-permute-start(bf16[4,96,640]{2,1,0:T(8,128)(2,1)} %get-tuple-element.111), channel_id=1, source_target_pairs={{0,4},{1,5},{2,6},{3,7},{4,0},{5,1},{6,2},{7,3},{8,12},{9,13},{10,... | collective-permute-start | bytes 1474568 | tf_op jit(solution)/shard_map/ppermute | solution.py:927
  224.5 2.2 collective-permute-start.9
  227.5 6.1 %collective-permute-start.11 = (f32[8,768]{1,0:T(8,128)S(1)}, f32[8,768]{1,0:T(8,128)S(1)}, u32[]{:S(2)}, u32[]{:S(2)}) collective-permute-start(f32[8,768]{1,0:T(8,128)S(1)} %add.151), channel_id=1, source_target_pairs={{0,2},{1,3},{2,0},{3,1},{4,6},{5,7},{6,4},{7,5},{8,10},{9,11},{10,... | collective-permute-start | bytes 73736 | tf_op jit(solution)/shard_map/ppermute | solution.py:927
  233.6 3.9 %collective-permute-start.16 = (f32[8,768]{1,0:T(8,128)S(1)}, f32[8,768]{1,0:T(8,128)S(1)}, u32[]{:S(2)}, u32[]{:S(2)}) collective-permute-start(f32[8,768]{1,0:T(8,128)S(1)} %add.154), channel_id=1, source_target_pairs={{0,4},{1,5},{2,6},{3,7},{4,0},{5,1},{6,2},{7,3},{8,12},{9,13},{10,... | collective-permute-start | bytes 73736 | tf_op jit(solution)/shard_map/ppermute | solution.py:927
  243.0 5.8 %copy-start.17 = (bf16[256,768]{1,0:T(8,128)(2,1)S(1)}, bf16[256,768]{1,0:T(8,128)(2,1)}, u32[]{:S(2)}) copy-start(bf16[256,768]{1,0:T(8,128)(2,1)} %get-tuple-element.106) | copy-start | bytes 1179652
  243.0 47.0 %all-to-all-start.3 = ((bf16[4,96,2432]{2,1,0:T(8,128)(2,1)}), bf16[4,96,2432]{2,1,0:T(8,128)(2,1)S(1)}, u32[]{:S(2)}, u32[]{:S(2)}) async-start(bf16[4,96,2432]{2,1,0:T(8,128)(2,1)} %merge.1), calls=%async_computation.3 | async-start | bytes 3735552 | tf_op jit(solution)/shard_map/all_to_all | solution.py:1007
  246.7 11.6 %collective-permute-start.12 = (bf16[256,768]{1,0:T(8,128)(2,1)}, bf16[256,768]{1,0:T(8,128)(2,1)S(1)}, u32[]{:S(2)}, u32[]{:S(2)}) collective-permute-start(bf16[256,768]{1,0:T(8,128)(2,1)} %get-tuple-element.104), channel_id=1, source_target_pairs={{0,2},{1,3},{2,0},{3,1},{4,6},{5,7},{6,4},{7,5},{8,10},{9,11},{10,... | collective-permute-start | bytes 1179656 | tf_op jit(solution)/shard_map/ppermute | solution.py:927
  248.2 12.0 %collective-permute-start.13 = (bf16[256,768]{1,0:T(8,128)(2,1)S(1)}, bf16[256,768]{1,0:T(8,128)(2,1)S(1)}, u32[]{:S(2)}, u32[]{:S(2)}) collective-permute-start(bf16[256,768]{1,0:T(8,128)(2,1)S(1)} %copy-done.18), channel_id=1, source_target_pairs={{0,4},{1,5},{2,6},{3,7},{4,0},{5,1},{6,2},{7,3},{8,12},{9,13},{10,... | collective-permute-start | bytes 1179656 | tf_op jit(solution)/shard_map/ppermute | solution.py:927
  248.8 18.2 %collective-permute-start.14 = (bf16[256,768]{1,0:T(8,128)(2,1)S(1)}, bf16[256,768]{1,0:T(8,128)(2,1)S(1)}, u32[]{:S(2)}, u32[]{:S(2)}) collective-permute-start(bf16[256,768]{1,0:T(8,128)(2,1)S(1)} %copy-done.17), channel_id=1, source_target_pairs={{0,6},{1,7},{2,4},{3,5},{4,2},{5,3},{6,0},{7,1},{8,14},{9,15},{10,... | collective-permute-start | bytes 1179656 | tf_op jit(solution)/shard_map/ppermute | solution.py:927
  258.3 8.7 %copy-start.14 = (bf16[256,768]{1,0:T(8,128)(2,1)}, bf16[256,768]{1,0:T(8,128)(2,1)S(1)}, u32[]{:S(2)}) copy-start(bf16[256,768]{1,0:T(8,128)(2,1)S(1)} %collective-permute-done.12.near2_ref) | copy-start | bytes 1179652
  260.2 6.7 %copy-start.15 = (bf16[256,768]{1,0:T(8,128)(2,1)}, bf16[256,768]{1,0:T(8,128)(2,1)S(1)}, u32[]{:S(2)}) copy-start(bf16[256,768]{1,0:T(8,128)(2,1)S(1)} %collective-permute-done.13.away_ref) | copy-start | bytes 1179652
  (9 other events, 13.2 us)
Sparse Core Ops, SparseCore 0:
  13.0 99.8 all-gather.1

commit v4 on v3

--- a/solution.py
+++ b/solution.py
@@ -52,7 +52,7 @@
     copies = narrow_ref.shape[0]
     columns = jnp.transpose(vec_ref[...].astype(F32)).astype(BF16)
     wide_ref[:, :d] = fc_ref[...]
-    wide_ref[:, d : 2 * d] = jnp.transpose(pj_ref[...].astype(F32)).astype(BF16)
+    wide_ref[:, d : 2 * d] = pj_ref[...]
     wide_ref[:, 2 * d : 2 * d + width] = jnp.transpose(out_ref[...].astype(F32)).astype(BF16)
     edge = 2 * d + width
     wide_ref[:, edge:] = jnp.zeros((tall, EXT), BF16)
@@ -605,44 +605,54 @@
     )(*operands)
 
 
-def merge_kernel(side_ref, ak_ref, ac_ref, bk_ref, bc_ref, nk_ref, nc_ref, vec_ref, out_ref, turn_ref):
-    depth, step, cut = ak_ref.shape
+def merge_kernel(place_ref, ak_ref, ac_ref, bk_ref, bc_ref, nk_ref, nc_ref, vec_ref, *rest):
+    n = pl.program_id(0)
+    turn_ref = rest[-1]
+    step, cut = ak_ref.shape[1:]
     at = 2 * cut + nk_ref.shape[2] - EXT
-    turn_ref[...] = jnp.transpose(vec_ref[...])
-    for z in range(depth):
-        out_ref[z, :, :cut] = (ak_ref[z].astype(F32) + ac_ref[z].astype(F32)).astype(BF16)
-        out_ref[z, :, cut : 2 * cut] = (bk_ref[z].astype(F32) + bc_ref[z].astype(F32)).astype(BF16)
-        out_ref[z, :, 2 * cut :] = (nk_ref[z].astype(F32) + nc_ref[z].astype(F32)).astype(BF16)
-        here = pl.ds(pl.multiple_of((2 * z + side_ref[0]) * step, 8), step)
-        out_ref[z, :, at : at + 8] = turn_ref[here, :].astype(BF16)
-
-
-def merge(side, *parts):
+
+    @pl.when(n == 0)
+    def _():
+        turn_ref[...] = jnp.transpose(vec_ref[...])
+
+    here = pl.ds(pl.multiple_of((2 * (n ^ place_ref[1]) + place_ref[0]) * step, 8), step)
+    for m, out_ref in enumerate(rest[:-1]):
+
+        @pl.when(n == m)
+        def _(out_ref=out_ref):
+            out_ref[:, :cut] = (ak_ref[0].astype(F32) + ac_ref[0].astype(F32)).astype(BF16)
+            out_ref[:, cut : 2 * cut] = (bk_ref[0].astype(F32) + bc_ref[0].astype(F32)).astype(BF16)
+            out_ref[:, 2 * cut :] = (nk_ref[0].astype(F32) + nc_ref[0].astype(F32)).astype(BF16)
+            out_ref[:, at : at + 8] = turn_ref[here, :].astype(BF16)
+
+
+def merge(place, *parts):
     depth, step, cut = parts[0].shape
     cols = 2 * cut + parts[4].shape[2]
-    whole = lambda array: pl.BlockSpec(array.shape, lambda i, ix: (0,) * array.ndim)
-    out = jax.ShapeDtypeStruct((depth, step, cols), BF16)
+    piece = lambda array: pl.BlockSpec((1,) + array.shape[1:], lambda n, ix: (n ^ ix[1], 0, 0))
+    whole = lambda array: pl.BlockSpec(array.shape, lambda n, ix: (0, 0))
+    out = jax.ShapeDtypeStruct((step, cols), BF16)
     return pl.pallas_call(
         merge_kernel,
-        out_shape=out,
+        out_shape=(out,) * depth,
         grid_spec=pltpu.PrefetchScalarGridSpec(
             num_scalar_prefetch=1,
-            grid=(1,),
-            in_specs=[whole(p) for p in parts],
-            out_specs=whole(out),
-            scratch_shapes=[pltpu.VMEM(parts[6].shape[::-1], F32)],
+            grid=(depth,),
+            in_specs=[piece(p) for p in parts[:-1]] + [whole(parts[-1])],
+            out_specs=(whole(out),) * depth,
+            scratch_shapes=[pltpu.VMEM(parts[-1].shape[::-1], F32)],
         ),
         compiler_params=params(),
         cost_estimate=cost(0, 6e6),
         name="merge",
-    )(side, *parts)
+    )(place, *parts)
 
 
 def finish_wide(t, fc_ref, pj_ref, out_ref, g_ref, b_ref, ob_ref, pb_ref, fb_ref):
     d = fc_ref.shape[1]
     width = out_ref.shape[0]
     fc_ref[...] = t[:, :d]
-    pj_ref[...] = jnp.transpose(t[:, d : 2 * d])
+    pj_ref[...] = t[:, d : 2 * d]
     rest = jnp.transpose(t[:, 2 * d : 2 * d + width + EXT])
     out_ref[...] = rest[:width]
     g_ref[...] = rest[width : width + 1]
@@ -654,7 +664,7 @@
     fb_ref[...] = t[:rows, at : at + strip]
 
 
-def finish_narrow(t, qkv_ref, qb_ref, vec_ref):
+def finish_narrow(t, qkv_ref, qb_ref, gain_ref, shift_ref):
     width = qkv_ref.shape[2]
     for s in range(3):
         qkv_ref[s] = t[:, s * width : (s + 1) * width]
@@ -662,7 +672,9 @@
     edge = 3 * width + 8
     for s in range(3):
         qb_ref[s] = t[s * heads : (s + 1) * heads, edge : edge + piece]
-    vec_ref[...] = jnp.transpose(t[:, 512:640])[64:72]
+    turned = jnp.transpose(t[:, 512:640])
+    gain_ref[...] = turned[64:65]
+    shift_ref[...] = turned[65:66]
 
 
 def total_of(ref):
@@ -673,24 +685,27 @@
 
 
 def finish_kernel(*refs):
-    total = total_of(refs[0])
-    if len(refs) == 12:
-        edge = total.shape[1] - 640
-        finish_wide(total[:, :edge], *refs[1:9])
-        finish_narrow(total[:, edge:], *refs[9:])
-    else:
-        finish_wide(total, *refs[2:10])
-        finish_narrow(total_of(refs[1]), *refs[10:])
+    parts, outs = refs[:-12], refs[-12:]
+    if len(parts) == 2:
+        finish_wide(total_of(parts[0]), *outs[:8])
+        finish_narrow(total_of(parts[1]), *outs[8:])
+        return
+    total = parts[0][...].astype(F32)
+    for ref in parts[1:]:
+        total = total + ref[...].astype(F32)
+    edge = total.shape[1] - 640
+    finish_wide(total[:, :edge], *outs[:8])
+    finish_narrow(total[:, edge:], *outs[8:])
 
 
 def finish(parts, d, width, fc_bias_shape, qkv_bias_shape):
-    tall = parts[0].shape[1]
+    tall = parts[0].shape[-2]
     sds = lambda *shape: jax.ShapeDtypeStruct(shape, F32)
     return pl.pallas_call(
         finish_kernel,
         out_shape=(
             sds(tall, d),
-            sds(d, tall),
+            sds(tall, d),
             sds(width, tall),
             sds(1, tall),
             sds(1, tall),
@@ -699,7 +714,8 @@
             sds(*fc_bias_shape),
             sds(3, tall, width),
             sds(*qkv_bias_shape),
-            sds(8, tall),
+            sds(1, tall),
+            sds(1, tall),
         ),
         compiler_params=pltpu.CompilerParams(vmem_limit_bytes=SMALL_LIMIT),
         cost_estimate=cost(0, 4e6),
@@ -923,6 +939,12 @@
     width = heads * HD
     lines, strip = fc_bias.shape
 
+    deep = lax.axis_index("dp")
+    depth = lax.axis_size("dp")
+
+    def swap_deep(array, mask):
+        return lax.ppermute(array, "dp", [(n, n ^ mask) for n in range(depth)])
+
     def swap(array, mask):
         return lax.ppermute(array, ("ctx", "tp"), [(n, n ^ mask) for n in range(group)])
 
@@ -930,7 +952,7 @@
     cot = cotangent[:, 0]
 
     vectors = jnp.stack([ln1_gain, ln1_bias, ln2_gain, ln2_bias, out_bias, proj_bias])
-    wide, narrow = pack(fc_weight, proj_weight, out_weight, qkv_weight, vectors, qkv_bias, fc_bias, shards)
+    wide, narrow = pack(fc_weight, proj_weight.T, out_weight, qkv_weight, vectors, qkv_bias, fc_bias, shards)
 
     gathered = lax.all_gather(wide, ("tp", "dp", "ctx"), axis=0, tiled=True)
     gathered = gathered.reshape(parts, d, wide.shape[1])
@@ -951,6 +973,9 @@
     unit = lax.broadcasted_iota(jnp.int32, (1, d), 1)
     order_fc = one_hot_order(unit % 128 // strip * tall + unit // 128, d)
 
+    order_back = order_in.reshape(d, 3, width).transpose(1, 0, 2)
+    far, order_in, order_fc, order_back = barrier((far, order_in, order_fc, order_back))
+
     triple = project(me_array, own, far, w_in, order_in, piece)
     mixed, mixed_turned, level = attend(triple, rows)
     mix = lax.all_to_all(mixed, ("ctx", "tp"), 0, 0, tiled=True)
@@ -963,7 +988,7 @@
     grad_mix = lax.all_to_all(grad_mix, ("ctx", "tp"), 0, 0, tiled=True)
 
     parcels = (n2, cot_rows, gb, mix, act, gl, vec, gfb, order_fc, strip)
-    exchange = tall % 16 == 0
+    exchange = tall % 16 == 0 and depth & (depth - 1) == 0
     if exchange:
         core, row = slot % 2, slot // 2
         index = lambda lane: jnp.stack([(1 - row) * 2 + lane, row * 2 + lane, side]).astype(jnp.int32)
@@ -983,7 +1008,6 @@
         a_send, b_send, grad_triple = barrier((a_send, b_send, grad_triple))
         a_keep, b_keep = plus(a_keep[0], a_came[0]), plus(b_keep[0], b_came[0])
         a_came, b_came = swap(a_send, parts), swap(b_send, 2)
-    order_back = order_in.reshape(d, 3, width).transpose(1, 0, 2)
     back = project_back(me_array, own, far, grad_triple, w_in, order_back, piece, shards if exchange else 0)
     if exchange:
         a_came, b_came, back = barrier((a_came, b_came, back))
@@ -1003,8 +1027,9 @@
         vec_came, near = barrier((vec_came, near))
         vec_in = vec_in + vec_came
         vec_in = vec_in + swap(vec_in, parts)
-        total = merge(side_array, a_keep, a_came, b_keep, b_came, n_keep, n_came, vec_in)
-        totals = (lax.all_to_all(total, "dp", 0, 0, tiled=True),)
+        place = jnp.stack([side, deep]).astype(jnp.int32)
+        totals = merge(place, a_keep, a_came, b_keep, b_came, n_keep, n_came, vec_in)
+        totals = [totals[0]] + [swap_deep(totals[n], n) for n in range(1, depth)]
     else:
         grad_in = back[2].reshape(narrow.shape)
         totals = (grad_wide[None], lax.all_to_all(grad_in, ("dp", "ctx"), 0, 0, tiled=True))
@@ -1013,17 +1038,17 @@
         side_array, tok, near, *arrived, grad_hidden.reshape(micro, rows, d), w_in
     )
     done = finish(totals, d, width, fc_bias.shape, qkv_bias.shape)
-    fc_grad, proj_grad, out_grad, gain2, shift2, out_b, proj_b, fc_b, grad_qkv_weight, grad_qkv_bias, vec_in = done
+    fc_grad, proj_grad, out_grad, gain2, shift2, out_b, proj_b, fc_b, grad_qkv_weight, grad_qkv_bias, *pair = done
     if not exchange:
         mask = parts // 2
         while mask:
-            vec_in = vec_in + swap(vec_in, mask)
+            pair = [v + swap(v, mask) for v in pair]
             mask //= 2
     return (
         y.reshape(micro, 1, rows, d),
         grad_tokens[:, None],
-        vec_in[0],
-        vec_in[1],
+        pair[0][0],
+        pair[1][0],
         grad_qkv_weight,
         grad_qkv_bias,
         out_grad,
@@ -1032,7 +1057,7 @@
         shift2[0],
         fc_grad,
         fc_b,
-        proj_grad,
+        proj_grad.T,
         proj_b[0],
     )
 

time: 305 us -> 304 us (level); the launches traced: 304 us -> 299 us
  local copies, waits for them, and re-layouts: 13.5 us -> 8.9 us
    all_to_all x1 -> x0, waiting for transfers between devices: 17.8 us -> none  [local(): totals = (lax.all_to_all(total, 'dp', 0, 0, tiled=True),)]
    ppermute x17, waiting for transfers between devices: 46.5 us -> 56.9 us  [swap(): lax.ppermute(array, ('ctx', 'tp'), [(n, n ^ mask) for n in range(group)])]
    ppermute x0 -> x3, waiting for transfers between devices: none -> 8.38 us  [swap_deep(): return lax.ppermute(array, 'dp', [(n, n ^ mask) for n in range(depth)])]
    ppermute x0 -> x3, starting transfers between devices: none -> 4.39 us  [swap_deep(): return lax.ppermute(array, 'dp', [(n, n ^ mask) for n in range(depth)])]
    all_to_all x1 -> x0, starting transfers between devices: 3.72 us -> none  [local(): totals = (lax.all_to_all(total, 'dp', 0, 0, tiled=True),)]
    unnamed x40 -> x32, local copies, waits for them, and re-layouts: 10 us -> 6.37 us
  transfers between devices with their start and end apart: 22 -> 24, of which waited for: 12 -> 13; matrix products, arithmetic and copies ran while one was open for 3% -> 4% of each run, Pallas kernels for 35% -> 37%
where the time goes in v4:
time: 304 us; the launch traced here: 299 us
  Pallas kernels  148 us (49%)
  waiting for transfers between devices  83 us (27%)
  starting transfers between devices  32.4 us (11%)
  between operations  14.2 us (5%)
  other arithmetic  12.8 us (4%)
  local copies, waits for them, and re-layouts  8.9 us (3%)
    ppermute x17, waiting for transfers between devices, swap(): lax.ppermute(array, ('ctx', 'tp'), [(n, n ^ mask) for n in range(group)])  56.9 us
    pallas_call x1, Pallas kernels, attend_back(): pl.pallas_call(attend_back_kernel, out_shape=jax.ShapeDtypeStruct(triple....  32 us
    pallas_call x1, Pallas kernels, attend(): pl.pallas_call(attend_kernel, out_shape=(jax.ShapeDtypeStruct((span // ro...  28.7 us
    pallas_call x1, Pallas kernels, middle(): pl.pallas_call(functools.partial(middle_kernel, strip), out_shape=(sds((r...  21.6 us
    pallas_call x2, Pallas kernels, weights(): pl.pallas_call(functools.partial(weights_kernel, mode, strip), out_shape=...  20.7 us
    pallas_call x1, Pallas kernels, project_back(): pl.pallas_call(functools.partial(project_back_kernel, piece), out_shape=(...  14.4 us
    ppermute x17, starting transfers between devices, swap(): lax.ppermute(array, ('ctx', 'tp'), [(n, n ^ mask) for n in range(group)])  14.1 us
    all_to_all x1, waiting for transfers between devices, local(): mix = lax.all_to_all(mixed, ('ctx', 'tp'), 0, 0, tiled=True)  11.1 us
  transfers between devices with their start and end apart: 24, of which 13 were waited for; matrix products, arithmetic and copies ran while one was open for 4% of the time, Pallas kernels for 37%

profile of v4, /device:TPU:0, one launch (start us, length us, event | category | flops | bytes accessed | tf_op | source)
XLA Modules:
  0.0 299.1 jit_solution(1566744036516712369)
XLA Ops:
  8.6 2.4 pack.1
  12.2 3.0 %collective-permute-start.1 = (bf16[256,768]{1,0:T(8,128)(2,1)S(1)}, bf16[256,768]{1,0:T(8,128)(2,1)S(1)}, u32[]{:S(2)}, u32[]{:S(2)}) collective-permute-start(bf16[256,768]{1,0:T(8,128)(2,1)S(1)} %get-tuple-element.162), channel_id=1, source_target_pairs={{0,4},{1,5},{2,6},{3,7},{4,0},{5,1},{6,2},{7,3},{8,12},{9,13},{10,... | collective-permute-start | bytes 1179656 | tf_op jit(solution)/shard_map/ppermute | solution.py:949
  15.2 1.5 collective-permute-start.2
  16.8 6.3 %all-to-all-start = ((bf16[8,96,640]{2,1,0:T(8,128)(2,1)}), bf16[8,96,640]{2,1,0:T(8,128)(2,1)S(1)}, u32[]{:S(2)}, u32[]{:S(2)}) async-start(bf16[8,96,640]{2,1,0:T(8,128)(2,1)} %get-tuple-element.79), calls=%async_computation | async-start | bytes 1966080 | tf_op jit(solution)/shard_map/all_to_all | solution.py:969
  23.0 4.5 %collective-permute-done.1 = bf16[256,768]{1,0:T(8,128)(2,1)S(1)} collective-permute-done((bf16[256,768]{1,0:T(8,128)(2,1)S(1)}, bf16[256,768]{1,0:T(8,128)(2,1)S(1)}, u32[]{:S(2)}, u32[]{:S(2)}) %collective-permute-start.1) | collective-permute-done | bytes 393248 | tf_op jit(solution)/shard_map/ppermute | solution.py:949
  27.6 15.1 %collective-permute-done.2 = bf16[256,768]{1,0:T(8,128)(2,1)} collective-permute-done((bf16[256,768]{1,0:T(8,128)(2,1)S(1)}, bf16[256,768]{1,0:T(8,128)(2,1)}, u32[]{:S(2)}, u32[]{:S(2)}) %collective-permute-start.2) | collective-permute-done | bytes 393248 | tf_op jit(solution)/shard_map/ppermute | solution.py:949
  49.1 6.6 %all-to-all-done = bf16[8,96,640]{2,1,0:T(8,128)(2,1)S(1)} async-done(((bf16[8,96,640]{2,1,0:T(8,128)(2,1)}), bf16[8,96,640]{2,1,0:T(8,128)(2,1)S(1)}, u32[]{:S(2)}, u32[]{:S(2)}) %all-to-all-start) | async-done | bytes 983072 | tf_op jit(solution)/shard_map/all_to_all | solution.py:969
  56.6 10.9 %project.1.q_ref.k_ref.v_ref.qkv_ref = bf16[3,2048,192]{2,1,0:T(8,128)(2,1)} custom-call(s32[2]{0:T(128)} %pad_add_fusion.me_ref, bf16[4,256,768]{2,1,0:T(8,128)(2,1)} %copy-done.2, bf16[4,256,768]{2,1,0:T(8,128)(2,1)} %collective-permute-done.3.far_ref, bf16[768,640]{1,0:T(8,128)(2,1)} %bitcast.51, bf16[768,576]{1,0:T(8,128)(2,1)} %select_convert_fusion.2.order_ref), custom_call_target="tpu_custom_call" | custom-call | flops 1811939328 | bytes 8000000 | tf_op jit(solution)/shard_map/project/pallas_call | solution.py:129
  67.5 28.7 %attend.1 = (bf16[8,192,256]{2,1,0:T(8,128)(2,1)}, f32[192,2048]{1,0:T(8,128)}, f32[8,2048]{1,0:T(8,128)}) custom-call(bf16[3,2048,192]{2,1,0:T(8,128)(2,1)} %project.1.q_ref.k_ref.v_ref.qkv_ref, bf16[3,2048,192]{2,1,0:T(8,128)(2,1)} %project.1.q_ref.k_ref.v_ref.qkv_ref, bf16[3,2048,192]{2,1,0:T(8,128)(2,1)} %project.1.q_ref.k_ref.v_ref.qkv_ref), custom_call_target="tpu_custom_call" | custom-call | flops 3221225472 | bytes 8000000 | tf_op jit(solution)/shard_map/attend/pallas_call | solution.py:216
  96.3 3.9 %all-to-all-start.1 = ((bf16[8,192,256]{2,1,0:T(8,128)(2,1)}), bf16[8,192,256]{2,1,0:T(8,128)(2,1)S(1)}, u32[]{:S(2)}, u32[]{:S(2)}) async-start(bf16[8,192,256]{2,1,0:T(8,128)(2,1)} %get-tuple-element.81), calls=%async_computation.1 | async-start | bytes 1572864 | tf_op jit(solution)/shard_map/all_to_all | solution.py:981
  100.7 11.1 %all-to-all-done.1.mix_ref = bf16[8,192,256]{2,1,0:T(8,128)(2,1)S(1)} async-done(((bf16[8,192,256]{2,1,0:T(8,128)(2,1)}), bf16[8,192,256]{2,1,0:T(8,128)(2,1)S(1)}, u32[]{:S(2)}, u32[]{:S(2)}) %all-to-all-start.1) | async-done | bytes 786464 | tf_op jit(solution)/shard_map/all_to_all | solution.py:981
  112.7 21.6 %middle.1 = (bf16[512,768]{1,0:T(8,128)(2,1)}, f32[512,768]{1,0:T(8,128)}, bf16[8,192,256]{2,1,0:T(8,128)(2,1)}, bf16[512,768]{1,0:T(8,128)(2,1)}, bf16[4,512,76...) custom-call(bf16[512,768]{1,0:T(8,128)(2,1)} %bitcast.59, ...), custom_call_target="tpu_custom_call" | custom-call | flops 10871635968 | bytes 30000000 | tf_op jit(solution)/shard_map/middle/pallas_call | solution.py:458
  134.3 9.4 %weights_send.1 = bf16[2,768,1792]{2,1,0:T(8,128)(2,1)} custom-call(s32[3]{0:T(128)} %add_add_fusion.1.index_ref, bf16[512,768]{1,0:T(8,128)(2,1)} %get-tuple-element.85.n2_ref, bf16[512,768]{1,0:T(8,128)(2,1)} %bitcast.57, bf16[512,768]{1,0:T(8,128)(2,1)} %get-tuple-element.86.gb_ref, bf16[2,4,192,256]{3,2,1,0:T(8,128)(2,1)} %bitcast.54, ...), custom_call_target="tpu_custom_call" | custom-call | flops 2818572288 | bytes 12000000 | tf_op jit(solution)/shard_map/weights_send/pallas_call | solution.py:592
  144.3 3.8 %all-to-all-start.2 = ((bf16[8,192,256]{2,1,0:T(8,128)(2,1)}), bf16[8,192,256]{2,1,0:T(8,128)(2,1)S(1)}, u32[]{:S(2)}, u32[]{:S(2)}) async-start(bf16[8,192,256]{2,1,0:T(8,128)(2,1)} %get-tuple-element.94), calls=%async_computation.2 | async-start | bytes 1572864 | tf_op jit(solution)/shard_map/all_to_all | solution.py:988
  148.0 5.0 %collective-permute-done.4.rest_0_ = bf16[2,768,1792]{2,1,0:T(8,128)(2,1)} collective-permute-done((bf16[2,768,1792]{2,1,0:T(8,128)(2,1)}, bf16[2,768,1792]{2,1,0:T(8,128)(2,1)}, u32[]{:S(2)}, u32[]{:S(2)}) %collective-permute-start.4) | collective-permute-done | bytes 5505056 | tf_op jit(solution)/shard_map/ppermute | solution.py:949
  153.0 11.3 %weights_keep.1 = (bf16[2,4,96,896]{3,2,1,0:T(8,128)(2,1)}, bf16[2,4,96,896]{3,2,1,0:T(8,128)(2,1)}, bf16[2,4,96,896]{3,2,1,0:T(8,128)(2,1)}, bf16[2,4,96,896]{3,2,1,0:T(8,128)(2,1)}) custom-call(s32[3]{0:T(128)} %add_add_fusion.index_ref, bf16[512,768]{1,0:T(8,128)(2,1)} %get-tuple-element.85.n2_ref, bf16[512,768]{1,0:T(8,128)(2,1)} %bitcast.58, ...), custom_call_target="tpu_custom_call" | custom-call | flops 2818572288 | bytes 12000000 | tf_op jit(solution)/shard_map/weights_keep/pallas_call | solution.py:592
  167.3 32.0 %attend_back.1.grad_ref = bf16[3,2048,192]{2,1,0:T(8,128)(2,1)} custom-call(bf16[3,2048,192]{2,1,0:T(8,128)(2,1)} %project.1.q_ref.k_ref.v_ref.qkv_ref, bf16[8,192,256]{2,1,0:T(8,128)(2,1)} %copy-done.6, f32[192,2048]{1,0:T(8,128)} %get-tuple-element.95.ot_ref, f32[8,2048]{1,0:T(8,128)} %get-tuple-element.96.level_ref), custom_call_target="tpu_custom_call" | custom-call | flops 8053063680 | bytes 10000000 | tf_op jit(solution)/shard_map/attend_back/pallas_call | solution.py:337
  199.4 3.4 %fusion.2 = (bf16[4,96,896]{2,1,0:T(8,128)(2,1)}, bf16[4,96,896]{2,1,0:T(8,128)(2,1)}, bf16[4,96,896]{2,1,0:T(8,128)(2,1)}, bf16[4,96,896]{2,1,0:T(8,128)(2,1)}) fusion(bf16[2,4,96,896]{3,2,1,0:T(8,128)(2,1)S(1)} %collective-permute-done.5, bf16[2,4,96,896]{3,2,1,0:T(8,128)(2,1)S(1)} %copy-done.4, bf16[2,4,96,896]{3,2,1,0:T(8,128)(2,1)} %collective-permute-done.6, ...), kind=kLoop, calls=%fused_computation.13 | loop fusion | flops 5505024 | bytes 8257536 | tf_op jit(solution)/shard_map/convert_element_type | solution.py:907
  202.7 1.5 collective-permute-start.7
  204.8 14.4 %project_back.1 = (f32[4,256,768]{2,1,0:T(8,128)}, bf16[4,256,768]{2,1,0:T(8,128)(2,1)}, f32[8,768]{1,0:T(8,128)}, bf16[4,96,640]{2,1,0:T(8,128)(2,1)}, bf16[4,96,640]{2,1,0:T(8,128)(2,1)}) custom-call(s32[2]{0:T(128)} %pad_add_fusion.me_ref, bf16[4,256,768]{2,1,0:T(8,128)(2,1)} %copy-done.2, bf16[4,256,768]{2,1,0:T(8,128)(2,1)} %collective-permute-done.3.far_ref, ...), custom_call_target="tpu_custom_call" | custom-call | flops 3623878656 | bytes 15000000 | tf_op jit(solution)/shard_map/project_back/pallas_call | solution.py:795
  221.9 2.9 collective-permute-done.9
  226.6 4.5 %pair_sum.1 = (f32[256,768]{1,0:T(8,128)}, bf16[256,768]{1,0:T(8,128)(2,1)}, bf16[256,768]{1,0:T(8,128)(2,1)}, bf16[256,768]{1,0:T(8,128)(2,1)}) custom-call(f32[4,256,768]{2,1,0:T(8,128)} %get-tuple-element.113.keep_ref, bf16[4,256,768]{2,1,0:T(8,128)(2,1)} %copy-done.3), custom_call_target="tpu_custom_call" | custom-call | bytes 7000000 | tf_op jit(solution)/shard_map/pair_sum/pallas_call | solution.py:851
  233.1 9.9 %collective-permute-done.11 = f32[8,768]{1,0:T(8,128)S(1)} collective-permute-done((f32[8,768]{1,0:T(8,128)S(1)}, f32[8,768]{1,0:T(8,128)S(1)}, u32[]{:S(2)}, u32[]{:S(2)}) %collective-permute-start.11) | collective-permute-done | bytes 24608 | tf_op jit(solution)/shard_map/ppermute | solution.py:949
  244.2 2.7 collective-permute-done.16
  248.2 5.5 %merge.1 = (bf16[96,2432]{1,0:T(8,128)(2,1)}, bf16[96,2432]{1,0:T(8,128)(2,1)}, bf16[96,2432]{1,0:T(8,128)(2,1)}, bf16[96,2432]{1,0:T(8,128)(2,1)}) custom-call(s32[2]{0:T(128)} %pad_add_fusion.1.place_ref, bf16[4,96,896]{2,1,0:T(8,128)(2,1)} %get-tuple-element.158.ak_ref, bf16[4,96,896]{2,1,0:T(8,128)(2,1)} %copy-done.7, ...), custom_call_target="tpu_custom_call" | custom-call | bytes 6000000 | tf_op jit(solution)/shard_map/merge/pallas_call | solution.py:635
  254.0 2.2 collective-permute-start.18
  256.2 1.9 collective-permute-start.19
  260.1 10.2 %collective-permute-done.13.away_ref = bf16[256,768]{1,0:T(8,128)(2,1)S(1)} collective-permute-done((bf16[256,768]{1,0:T(8,128)(2,1)}, bf16[256,768]{1,0:T(8,128)(2,1)S(1)}, u32[]{:S(2)}, u32[]{:S(2)}) %collective-permute-start.13) | collective-permute-done | bytes 393248 | tf_op jit(solution)/shard_map/ppermute | solution.py:949
  270.3 4.7 %collective-permute-done.14.away2_ref = bf16[256,768]{1,0:T(8,128)(2,1)S(1)} collective-permute-done((bf16[256,768]{1,0:T(8,128)(2,1)}, bf16[256,768]{1,0:T(8,128)(2,1)S(1)}, u32[]{:S(2)}, u32[]{:S(2)}) %collective-permute-start.14) | collective-permute-done | bytes 393248 | tf_op jit(solution)/shard_map/ppermute | solution.py:949
  275.8 4.5 %finish_rows.1 = f32[2,256,768]{2,1,0:T(8,128)} custom-call(s32[1]{0:T(128)} %bitcast.3.side_ref, bf16[2,256,768]{2,1,0:T(8,128)(2,1)} %bitcast.60, f32[256,768]{1,0:T(8,128)} %get-tuple-element.116.near_ref, bf16[256,768]{1,0:T(8,128)(2,1)} %copy-done.13, bf16[256,768]{1,0:T(8,128)(2,1)} %copy-done.14, bf16[256,768]{1,0:T(8,128)(2,1)} %copy-done.15, ...), custom_call_target="tpu_custom_call" | custom-call | bytes 6000000 | tf_op jit(solution)/shard_map/finish_rows/pallas_call | solution.py:882
  280.3 8.4 %collective-permute-done.18.refs_2_ = bf16[96,2432]{1,0:T(8,128)(2,1)S(1)} collective-permute-done((bf16[96,2432]{1,0:T(8,128)(2,1)}, bf16[96,2432]{1,0:T(8,128)(2,1)S(1)}, u32[]{:S(2)}, u32[]{:S(2)}) %collective-permute-start.18) | collective-permute-done | bytes 466976 | tf_op jit(solution)/shard_map/ppermute | solution.py:946
  289.6 2.6 finish.1
  (78 shorter events, 28.6 us)
Async XLA Ops:
  7.2 104.6 %all-gather.2.cloned.1.call-start = ((), (), s32[]{:S(2)}) async-start(), calls=%async_computation.3 | async-start | bytes 11354112 | tf_op jit(solution)/shard_map/all_gather | solution.py:957
  12.2 15.4 %collective-permute-start.1 = (bf16[256,768]{1,0:T(8,128)(2,1)S(1)}, bf16[256,768]{1,0:T(8,128)(2,1)S(1)}, u32[]{:S(2)}, u32[]{:S(2)}) collective-permute-start(bf16[256,768]{1,0:T(8,128)(2,1)S(1)} %get-tuple-element.162), channel_id=1, source_target_pairs={{0,4},{1,5},{2,6},{3,7},{4,0},{5,1},{6,2},{7,3},{8,12},{9,13},{10,... | collective-permute-start | bytes 1179656 | tf_op jit(solution)/shard_map/ppermute | solution.py:949
  15.2 27.5 %collective-permute-start.2 = (bf16[256,768]{1,0:T(8,128)(2,1)S(1)}, bf16[256,768]{1,0:T(8,128)(2,1)}, u32[]{:S(2)}, u32[]{:S(2)}) collective-permute-start(bf16[256,768]{1,0:T(8,128)(2,1)S(1)} %get-tuple-element.162), channel_id=1, source_target_pairs={{0,6},{1,7},{2,4},{3,5},{4,2},{5,3},{6,0},{7,1},{8,14},{9,15},{10,... | collective-permute-start | bytes 1179656 | tf_op jit(solution)/shard_map/ppermute | solution.py:949
  16.7 26.0 %collective-permute-start = (bf16[256,768]{1,0:T(8,128)(2,1)S(1)}, bf16[256,768]{1,0:T(8,128)(2,1)}, u32[]{:S(2)}, u32[]{:S(2)}) collective-permute-start(bf16[256,768]{1,0:T(8,128)(2,1)S(1)} %get-tuple-element.161), channel_id=1, source_target_pairs={{0,2},{1,3},{2,0},{3,1},{4,6},{5,7},{6,4},{7,5},{8,10},{9,11},{10,... | collective-permute-start | bytes 1179656 | tf_op jit(solution)/shard_map/ppermute | solution.py:949
  16.8 38.9 %all-to-all-start = ((bf16[8,96,640]{2,1,0:T(8,128)(2,1)}), bf16[8,96,640]{2,1,0:T(8,128)(2,1)S(1)}, u32[]{:S(2)}, u32[]{:S(2)}) async-start(bf16[8,96,640]{2,1,0:T(8,128)(2,1)} %get-tuple-element.79), calls=%async_computation | async-start | bytes 1966080 | tf_op jit(solution)/shard_map/all_to_all | solution.py:969
  44.0 5.1 %copy-start.2 = (bf16[4,256,768]{2,1,0:T(8,128)(2,1)}, bf16[4,256,768]{2,1,0:T(8,128)(2,1)S(1)}, u32[]{:S(2)}) copy-start(bf16[4,256,768]{2,1,0:T(8,128)(2,1)S(1)} %pad_maximum_fusion.own_ref) | copy-start | bytes 4718596
  44.0 5.1 %collective-permute-start.3 = (bf16[4,256,768]{2,1,0:T(8,128)(2,1)S(1)}, bf16[4,256,768]{2,1,0:T(8,128)(2,1)}, u32[]{:S(2)}, u32[]{:S(2)}) collective-permute-start(bf16[4,256,768]{2,1,0:T(8,128)(2,1)S(1)} %pad_maximum_fusion.own_ref), channel_id=1, source_target_pairs={{0,1},{1,0},{2,3},{3,2},{4,5},{5,4},{6,7},{7,6},{8,9},{9,8},{10,11... | collective-permute-start | bytes 4718600 | tf_op jit(solution)/shard_map/ppermute | solution.py:949
  96.3 15.5 %all-to-all-start.1 = ((bf16[8,192,256]{2,1,0:T(8,128)(2,1)}), bf16[8,192,256]{2,1,0:T(8,128)(2,1)S(1)}, u32[]{:S(2)}, u32[]{:S(2)}) async-start(bf16[8,192,256]{2,1,0:T(8,128)(2,1)} %get-tuple-element.81), calls=%async_computation.1 | async-start | bytes 1572864 | tf_op jit(solution)/shard_map/all_to_all | solution.py:981
  143.6 9.4 %collective-permute-start.4 = (bf16[2,768,1792]{2,1,0:T(8,128)(2,1)}, bf16[2,768,1792]{2,1,0:T(8,128)(2,1)}, u32[]{:S(2)}, u32[]{:S(2)}) collective-permute-start(bf16[2,768,1792]{2,1,0:T(8,128)(2,1)} %weights_send.1), channel_id=1, source_target_pairs={{0,1},{1,0},{2,3},{3,2},{4,5},{5,4},{6,7},{7,6},{8,9},{9,8},{10,11... | collective-permute-start | bytes 16515080 | tf_op jit(solution)/shard_map/ppermute | solution.py:949
  144.3 22.1 %all-to-all-start.2 = ((bf16[8,192,256]{2,1,0:T(8,128)(2,1)}), bf16[8,192,256]{2,1,0:T(8,128)(2,1)S(1)}, u32[]{:S(2)}, u32[]{:S(2)}) async-start(bf16[8,192,256]{2,1,0:T(8,128)(2,1)} %get-tuple-element.94), calls=%async_computation.2 | async-start | bytes 1572864 | tf_op jit(solution)/shard_map/all_to_all | solution.py:988
  164.4 35.0 %collective-permute-start.5 = (bf16[2,4,96,896]{3,2,1,0:T(8,128)(2,1)}, bf16[2,4,96,896]{3,2,1,0:T(8,128)(2,1)S(1)}, u32[]{:S(2)}, u32[]{:S(2)}) collective-permute-start(bf16[2,4,96,896]{3,2,1,0:T(8,128)(2,1)} %get-tuple-element.92), channel_id=1, source_target_pairs={{0,2},{1,3},{2,0},{3,1},{4,6},{5,7},{6,4},{7,5},{8,10},{9,11},{10,... | collective-permute-start | bytes 4128776 | tf_op jit(solution)/shard_map/ppermute | solution.py:949
  165.8 33.5 %collective-permute-start.6 = (bf16[2,4,96,896]{3,2,1,0:T(8,128)(2,1)}, bf16[2,4,96,896]{3,2,1,0:T(8,128)(2,1)}, u32[]{:S(2)}, u32[]{:S(2)}) collective-permute-start(bf16[2,4,96,896]{3,2,1,0:T(8,128)(2,1)} %get-tuple-element.93), channel_id=1, source_target_pairs={{0,4},{1,5},{2,6},{3,7},{4,0},{5,1},{6,2},{7,3},{8,12},{9,13},{10,... | collective-permute-start | bytes 4128776 | tf_op jit(solution)/shard_map/ppermute | solution.py:949
  167.3 32.0 %copy-start.4 = (bf16[2,4,96,896]{3,2,1,0:T(8,128)(2,1)S(1)}, bf16[2,4,96,896]{3,2,1,0:T(8,128)(2,1)}, u32[]{:S(2)}) copy-start(bf16[2,4,96,896]{3,2,1,0:T(8,128)(2,1)} %get-tuple-element.91) | copy-start | bytes 4128772
  167.3 32.0 %copy-start.5 = (bf16[2,4,96,896]{3,2,1,0:T(8,128)(2,1)S(1)}, bf16[2,4,96,896]{3,2,1,0:T(8,128)(2,1)}, u32[]{:S(2)}) copy-start(bf16[2,4,96,896]{3,2,1,0:T(8,128)(2,1)} %get-tuple-element.98) | copy-start | bytes 4128772
  202.7 17.1 %collective-permute-start.7 = (bf16[4,96,896]{2,1,0:T(8,128)(2,1)}, bf16[4,96,896]{2,1,0:T(8,128)(2,1)S(1)}, u32[]{:S(2)}, u32[]{:S(2)}) collective-permute-start(bf16[4,96,896]{2,1,0:T(8,128)(2,1)} %get-tuple-element.101), channel_id=1, source_target_pairs={{0,4},{1,5},{2,6},{3,7},{4,0},{5,1},{6,2},{7,3},{8,12},{9,13},{10,... | collective-permute-start | bytes 2064392 | tf_op jit(solution)/shard_map/ppermute | solution.py:949
  204.2 16.8 %collective-permute-start.8 = (bf16[4,96,896]{2,1,0:T(8,128)(2,1)}, bf16[4,96,896]{2,1,0:T(8,128)(2,1)S(1)}, u32[]{:S(2)}, u32[]{:S(2)}) collective-permute-start(bf16[4,96,896]{2,1,0:T(8,128)(2,1)} %get-tuple-element.102), channel_id=1, source_target_pairs={{0,2},{1,3},{2,0},{3,1},{4,6},{5,7},{6,4},{7,5},{8,10},{9,11},{10,... | collective-permute-start | bytes 2064392 | tf_op jit(solution)/shard_map/ppermute | solution.py:949
  219.9 27.6 %copy-start.7 = (bf16[4,96,896]{2,1,0:T(8,128)(2,1)}, bf16[4,96,896]{2,1,0:T(8,128)(2,1)S(1)}, u32[]{:S(2)}) copy-start(bf16[4,96,896]{2,1,0:T(8,128)(2,1)S(1)} %collective-permute-done.7.ac_ref) | copy-start | bytes 2064388
  221.1 26.4 %copy-start.8 = (bf16[4,96,896]{2,1,0:T(8,128)(2,1)}, bf16[4,96,896]{2,1,0:T(8,128)(2,1)S(1)}, u32[]{:S(2)}) copy-start(bf16[4,96,896]{2,1,0:T(8,128)(2,1)S(1)} %collective-permute-done.8.bc_ref) | copy-start | bytes 2064388
  221.1 4.4 %collective-permute-start.10 = (bf16[4,256,768]{2,1,0:T(8,128)(2,1)}, bf16[4,256,768]{2,1,0:T(8,128)(2,1)S(1)}, u32[]{:S(2)}, u32[]{:S(2)}) collective-permute-start(bf16[4,256,768]{2,1,0:T(8,128)(2,1)} %get-tuple-element.111), channel_id=1, source_target_pairs={{0,1},{1,0},{2,3},{3,2},{4,5},{5,4},{6,7},{7,6},{8,9},{9,8},{10,11... | collective-permute-start | bytes 4718600 | tf_op jit(solution)/shard_map/ppermute | solution.py:949
  221.1 26.4 %collective-permute-start.15 = (bf16[4,96,640]{2,1,0:T(8,128)(2,1)}, bf16[4,96,640]{2,1,0:T(8,128)(2,1)S(1)}, u32[]{:S(2)}, u32[]{:S(2)}) collective-permute-start(bf16[4,96,640]{2,1,0:T(8,128)(2,1)} %get-tuple-element.124), channel_id=1, source_target_pairs={{0,4},{1,5},{2,6},{3,7},{4,0},{5,1},{6,2},{7,3},{8,12},{9,13},{10,... | collective-permute-start | bytes 1474568 | tf_op jit(solution)/shard_map/ppermute | solution.py:949
  221.6 3.1 %collective-permute-start.9 = (f32[8,768]{1,0:T(8,128)}, f32[8,768]{1,0:T(8,128)S(1)}, u32[]{:S(2)}, u32[]{:S(2)}) collective-permute-start(f32[8,768]{1,0:T(8,128)} %get-tuple-element.110), channel_id=1, source_target_pairs={{0,1},{1,0},{2,3},{3,2},{4,5},{5,4},{6,7},{7,6},{8,9},{9,8},{10,11... | collective-permute-start | bytes 73736 | tf_op jit(solution)/shard_map/ppermute | solution.py:949
  231.1 27.6 %collective-permute-start.12 = (bf16[256,768]{1,0:T(8,128)(2,1)}, bf16[256,768]{1,0:T(8,128)(2,1)S(1)}, u32[]{:S(2)}, u32[]{:S(2)}) collective-permute-start(bf16[256,768]{1,0:T(8,128)(2,1)} %get-tuple-element.117), channel_id=1, source_target_pairs={{0,2},{1,3},{2,0},{3,1},{4,6},{5,7},{6,4},{7,5},{8,10},{9,11},{10,... | collective-permute-start | bytes 1179656 | tf_op jit(solution)/shard_map/ppermute | solution.py:949
  231.7 11.3 %collective-permute-start.11 = (f32[8,768]{1,0:T(8,128)S(1)}, f32[8,768]{1,0:T(8,128)S(1)}, u32[]{:S(2)}, u32[]{:S(2)}) collective-permute-start(f32[8,768]{1,0:T(8,128)S(1)} %add.143), channel_id=1, source_target_pairs={{0,2},{1,3},{2,0},{3,1},{4,6},{5,7},{6,4},{7,5},{8,10},{9,11},{10,... | collective-permute-start | bytes 73736 | tf_op jit(solution)/shard_map/ppermute | solution.py:949
  243.0 3.8 %collective-permute-start.16 = (f32[8,768]{1,0:T(8,128)S(1)}, f32[8,768]{1,0:T(8,128)S(1)}, u32[]{:S(2)}, u32[]{:S(2)}) collective-permute-start(f32[8,768]{1,0:T(8,128)S(1)} %add.146), channel_id=1, source_target_pairs={{0,4},{1,5},{2,6},{3,7},{4,0},{5,1},{6,2},{7,3},{8,12},{9,13},{10,... | collective-permute-start | bytes 73736 | tf_op jit(solution)/shard_map/ppermute | solution.py:949
  253.7 26.6 %collective-permute-start.17 = (bf16[96,2432]{1,0:T(8,128)(2,1)}, bf16[96,2432]{1,0:T(8,128)(2,1)S(1)}, u32[]{:S(2)}, u32[]{:S(2)}) collective-permute-start(bf16[96,2432]{1,0:T(8,128)(2,1)} %get-tuple-element.127), channel_id=1, source_target_pairs={{0,8},{8,0},{16,24},{24,16},{1,9},{9,1},{17,25},{25,17},{2,10},{10... | collective-permute-start | bytes 1400840 | tf_op jit(solution)/shard_map/ppermute | solution.py:946
  254.0 34.7 %collective-permute-start.18 = (bf16[96,2432]{1,0:T(8,128)(2,1)}, bf16[96,2432]{1,0:T(8,128)(2,1)S(1)}, u32[]{:S(2)}, u32[]{:S(2)}) collective-permute-start(bf16[96,2432]{1,0:T(8,128)(2,1)} %get-tuple-element.128), channel_id=1, source_target_pairs={{0,16},{8,24},{16,0},{24,8},{1,17},{9,25},{17,1},{25,9},{2,18},{10... | collective-permute-start | bytes 1400840 | tf_op jit(solution)/shard_map/ppermute | solution.py:946
  256.2 32.5 %collective-permute-start.19 = (bf16[96,2432]{1,0:T(8,128)(2,1)}, bf16[96,2432]{1,0:T(8,128)(2,1)S(1)}, u32[]{:S(2)}, u32[]{:S(2)}) collective-permute-start(bf16[96,2432]{1,0:T(8,128)(2,1)} %get-tuple-element.129), channel_id=1, source_target_pairs={{0,24},{8,16},{16,8},{24,0},{1,25},{9,17},{17,9},{25,1},{2,26},{10... | collective-permute-start | bytes 1400840 | tf_op jit(solution)/shard_map/ppermute | solution.py:946
  258.1 12.2 %collective-permute-start.13 = (bf16[256,768]{1,0:T(8,128)(2,1)}, bf16[256,768]{1,0:T(8,128)(2,1)S(1)}, u32[]{:S(2)}, u32[]{:S(2)}) collective-permute-start(bf16[256,768]{1,0:T(8,128)(2,1)} %get-tuple-element.118), channel_id=1, source_target_pairs={{0,4},{1,5},{2,6},{3,7},{4,0},{5,1},{6,2},{7,3},{8,12},{9,13},{10,... | collective-permute-start | bytes 1179656 | tf_op jit(solution)/shard_map/ppermute | solution.py:949
  258.7 16.4 %copy-start.13 = (bf16[256,768]{1,0:T(8,128)(2,1)}, bf16[256,768]{1,0:T(8,128)(2,1)S(1)}, u32[]{:S(2)}) copy-start(bf16[256,768]{1,0:T(8,128)(2,1)S(1)} %collective-permute-done.12.near2_ref) | copy-start | bytes 1179652
  258.7 16.4 %collective-permute-start.14 = (bf16[256,768]{1,0:T(8,128)(2,1)}, bf16[256,768]{1,0:T(8,128)(2,1)S(1)}, u32[]{:S(2)}, u32[]{:S(2)}) collective-permute-start(bf16[256,768]{1,0:T(8,128)(2,1)} %get-tuple-element.119), channel_id=1, source_target_pairs={{0,6},{1,7},{2,4},{3,5},{4,2},{5,3},{6,0},{7,1},{8,14},{9,15},{10,... | collective-permute-start | bytes 1179656 | tf_op jit(solution)/shard_map/ppermute | solution.py:949
  270.3 4.8 %copy-start.14 = (bf16[256,768]{1,0:T(8,128)(2,1)}, bf16[256,768]{1,0:T(8,128)(2,1)S(1)}, u32[]{:S(2)}) copy-start(bf16[256,768]{1,0:T(8,128)(2,1)S(1)} %collective-permute-done.13.away_ref) | copy-start | bytes 1179652
  280.3 8.4 %copy-start.10 = (bf16[96,2432]{1,0:T(8,128)(2,1)}, bf16[96,2432]{1,0:T(8,128)(2,1)S(1)}, u32[]{:S(2)}) copy-start(bf16[96,2432]{1,0:T(8,128)(2,1)S(1)} %collective-permute-done.17.refs_1_) | copy-start | bytes 1400836
  (8 other events, 7.2 us)
Sparse Core Ops, SparseCore 0:
  11.1 100.3 all-gather.1

commit v5 on v2

--- a/solution.py
+++ b/solution.py
@@ -13,6 +13,7 @@
 F32 = jnp.float32
 BF16 = jnp.bfloat16
 VMEM_LIMIT = 60 * 1024 * 1024
+SMALL_LIMIT = 60 * 1024 * 1024
 EXT = 64
 
 
@@ -37,10 +38,8 @@
     return (e - jnp.mean(e, axis=-1, keepdims=True) - n * jnp.mean(e * n, axis=-1, keepdims=True)) * scale
 
 
-def params(steps=1):
-    return pltpu.CompilerParams(
-        dimension_semantics=("arbitrary",) * steps, vmem_limit_bytes=VMEM_LIMIT
-    )
+def params(limit=VMEM_LIMIT):
+    return pltpu.CompilerParams(dimension_semantics=("arbitrary",), vmem_limit_bytes=limit)
 
 
 def cost(flops, moved, exps=0):
@@ -53,7 +52,7 @@
     copies = narrow_ref.shape[0]
     columns = jnp.transpose(vec_ref[...].astype(F32)).astype(BF16)
     wide_ref[:, :d] = fc_ref[...]
-    wide_ref[:, d : 2 * d] = jnp.transpose(pj_ref[...].astype(F32)).astype(BF16)
+    wide_ref[:, d : 2 * d] = pj_ref[...]
     wide_ref[:, 2 * d : 2 * d + width] = jnp.transpose(out_ref[...].astype(F32)).astype(BF16)
     edge = 2 * d + width
     wide_ref[:, edge:] = jnp.zeros((tall, EXT), BF16)
@@ -82,7 +81,7 @@
             jax.ShapeDtypeStruct((tall, 2 * d + width + EXT), BF16),
             jax.ShapeDtypeStruct((copies, tall, 3 * width + EXT), BF16),
         ),
-        compiler_params=pltpu.CompilerParams(vmem_limit_bytes=VMEM_LIMIT),
+        compiler_params=pltpu.CompilerParams(vmem_limit_bytes=SMALL_LIMIT),
         cost_estimate=cost(0, 2e6),
         name="pack",
     )(fc, pj, out, qkv, vec, qb, fb)
@@ -533,11 +532,10 @@
     sum_ref[:, :d] = (dot(nt_ref[...], gl_ref[0]) + came_ref[0, :, :d].astype(F32)).astype(BF16)
     sum_ref[:, d : 2 * d] = (dot(ct_ref[...], act_ref[0]) + came_ref[0, :, d : 2 * d].astype(F32)).astype(BF16)
     depth, step = as_ref.shape[1], as_ref.shape[2]
-    order = halving_order(depth)
     cut = cols // 2
 
     def block(xr, zr):
-        at = ((order[zr] ^ index_ref[2]) * 2 + (xr ^ index_ref[3])) * step
+        at = (zr * 2 + (xr ^ index_ref[2])) * step
         return pl.ds(pl.multiple_of(at, 16), step)
 
     for zr in range(depth):
@@ -555,11 +553,6 @@
         for xr in range(2):
             for zr in range(depth):
                 ak_ref[xr, zr] = sum_ref[block(xr, zr), :cut]
-
-
-def halving_order(count):
-    bits = count.bit_length() - 1
-    return [int(format(n, "b").zfill(bits)[::-1], 2) if bits else 0 for n in range(count)]
 
 
 def weights(mode, index, n2, cot, gb, mix, act, gl, vec, gfb, order, strip, came=None, shards=None):
@@ -612,34 +605,62 @@
     )(*operands)
 
 
-def finish_wide_kernel(ak_ref, ar_ref, bk_ref, br_ref, fc_ref, pj_ref, out_ref, g_ref, b_ref, ob_ref, pb_ref, fb_ref):
-    tall, d = fc_ref.shape
+def wide_sum_kernel(place_ref, ak_ref, ac_ref, bk_ref, bc_ref, keep_ref, send_ref):
+    cut = ak_ref.shape[2]
+    for ref, members in ((send_ref, (1, 2)), (keep_ref, (0, 3))):
+        for n, m in enumerate(members):
+            z = pl.ds(place_ref[0] ^ m, 1)
+            ref[n : n + 1, :, :cut] = (ak_ref[z].astype(F32) + ac_ref[z].astype(F32)).astype(BF16)
+            ref[n : n + 1, :, cut:] = (bk_ref[z].astype(F32) + bc_ref[z].astype(F32)).astype(BF16)
+
+
+def wide_sum(place, *parts):
+    depth, step, cut = parts[0].shape
+    whole = lambda array: pl.BlockSpec(array.shape, lambda i, ix: (0, 0, 0))
+    out = jax.ShapeDtypeStruct((depth // 2, step, 2 * cut), BF16)
+    return pl.pallas_call(
+        wide_sum_kernel,
+        out_shape=(out, out),
+        grid_spec=pltpu.PrefetchScalarGridSpec(
+            num_scalar_prefetch=1,
+            grid=(1,),
+            in_specs=[whole(p) for p in parts],
+            out_specs=(whole(out), whole(out)),
+        ),
+        compiler_params=params(),
+        cost_estimate=cost(0, 4e6),
+        name="wide_sum",
+    )(place, *parts)
+
+
+def finish_wide_kernel(*refs):
+    fc_ref, pj_ref, out_ref, g_ref, b_ref, ob_ref, pb_ref, fb_ref = refs[-8:]
+    d = fc_ref.shape[1]
     width = out_ref.shape[0]
-    cut = ak_ref.shape[1]
-    a = ak_ref[...].astype(F32) + ar_ref[...].astype(F32)
-    b = bk_ref[...].astype(F32) + br_ref[...].astype(F32)
-    fc_ref[...] = a[:, :d]
-    pj_ref[: cut - d, :] = jnp.transpose(a[:, d:])
-    pj_ref[cut - d :, :] = jnp.transpose(b[:, : 2 * d - cut])
-    rest = jnp.transpose(b[:, 2 * d - cut :])
+    t = refs[0][0].astype(F32)
+    for ref in refs[1:-8]:
+        t = t + ref[0].astype(F32)
+    fc_ref[...] = t[:, :d]
+    pj_ref[...] = t[:, d : 2 * d]
+    rest = jnp.transpose(t[:, 2 * d : 2 * d + width + EXT])
     out_ref[...] = rest[:width]
     g_ref[...] = rest[width : width + 1]
     b_ref[...] = rest[width + 1 : width + 2]
     ob_ref[...] = rest[width + 2 : width + 3]
     pb_ref[...] = rest[width + 3 : width + 4]
     rows, strip = fb_ref.shape
-    at = 2 * d - cut + width + 8
-    fb_ref[...] = b[:rows, at : at + strip]
-
-
-def finish_wide(ak, ar, bk, br, d, width, bias_shape):
-    tall = ak.shape[0]
+    at = 2 * d + width + 8
+    fb_ref[...] = t[:rows, at : at + strip]
+
+
+def finish_wide(parts, d, width, bias_shape):
+    tall = parts[0].shape[1]
     sds = lambda *shape: jax.ShapeDtypeStruct(shape, F32)
     return pl.pallas_call(
         finish_wide_kernel,
         out_shape=(
             sds(tall, d),
-            sds(d, tall),
+            sds(tall, d),
             sds(width, tall),
             sds(1, tall),
             sds(1, tall),
@@ -647,10 +668,36 @@
             sds(1, tall),
             sds(*bias_shape),
         ),
-        compiler_params=pltpu.CompilerParams(vmem_limit_bytes=VMEM_LIMIT),
+        compiler_params=pltpu.CompilerParams(vmem_limit_bytes=SMALL_LIMIT),
         cost_estimate=cost(0, 2e6),
         name="finish_wide",
-    )(ak, ar, bk, br)
+    )(*parts)
+
+
+def finish_narrow_kernel(g_ref, qkv_ref, qb_ref, vec_ref):
+    t = g_ref[0].astype(F32)
+    for n in range(1, g_ref.shape[0]):
+        t = t + g_ref[n].astype(F32)
+    width = qkv_ref.shape[2]
+    for s in range(3):
+        qkv_ref[s] = t[:, s * width : (s + 1) * width]
+    heads, piece = qb_ref.shape[1:]
+    edge = 3 * width + 8
+    for s in range(3):
+        qb_ref[s] = t[s * heads : (s + 1) * heads, edge : edge + piece]
+    vec_ref[...] = jnp.transpose(t[:, 512:640])[64:72]
+
+
+def finish_narrow(g, width, bias_shape):
+    tall = g.shape[1]
+    sds = lambda *shape: jax.ShapeDtypeStruct(shape, F32)
+    return pl.pallas_call(
+        finish_narrow_kernel,
+        out_shape=(sds(3, tall, width), sds(*bias_shape), sds(8, tall)),
+        compiler_params=pltpu.CompilerParams(vmem_limit_bytes=SMALL_LIMIT),
+        cost_estimate=cost(0, 2e6),
+        name="finish_narrow",
+    )(g)
 
 
 def project_back_kernel(
@@ -771,36 +818,10 @@
         grid=(half,),
         in_specs=[piece, piece],
         out_specs=(flat,) * half,
-        compiler_params=params(),
+        compiler_params=params(SMALL_LIMIT),
         cost_estimate=cost(0, 7e6),
         name="pair_sum",
     )(keep, came)
-
-
-def finish_narrow_kernel(g_ref, qkv_ref, qb_ref, vec_ref):
-    total = g_ref[0].astype(F32)
-    for n in range(1, g_ref.shape[0]):
-        total = total + g_ref[n].astype(F32)
-    width = qkv_ref.shape[2]
-    for s in range(3):
-        qkv_ref[s] = total[:, s * width : (s + 1) * width]
-    heads, piece = qb_ref.shape[1:]
-    edge = 3 * width + 8
-    for s in range(3):
-        qb_ref[s] = total[s * heads : (s + 1) * heads, edge : edge + piece]
-    vec_ref[...] = jnp.transpose(total[:, 512:640])[64:72]
-
-
-def finish_narrow(g, width, bias_shape):
-    tall = g.shape[1]
-    sds = lambda *shape: jax.ShapeDtypeStruct(shape, F32)
-    return pl.pallas_call(
-        finish_narrow_kernel,
-        out_shape=(sds(3, tall, width), sds(*bias_shape), sds(8, tall)),
-        compiler_params=pltpu.CompilerParams(vmem_limit_bytes=VMEM_LIMIT),
-        cost_estimate=cost(0, 2e6),
-        name="finish_narrow",
-    )(g)
 
 
 def finish_rows_kernel(side_ref, tok_ref, near_ref, near2_ref, away_ref, away2_ref, gh_ref, w_ref, out_ref, gain_ref):
@@ -831,7 +852,7 @@
             out_specs=piece,
             scratch_shapes=[pltpu.VMEM((8, d), F32)],
         ),
-        compiler_params=params(),
+        compiler_params=params(SMALL_LIMIT),
         cost_estimate=cost(0, 6e6),
         name="finish_rows",
     )(side, tok, near, near2, away, away2, gh, w)
@@ -840,6 +861,9 @@
 def one_hot_order(sources, size):
     row = lax.broadcasted_iota(jnp.int32, (size, sources.shape[1]), 0)
     return jnp.where(row == sources, 1.0, 0.0).astype(BF16)
+
+
+barrier = lax.optimization_barrier
 
 
 def plus(a, b):
@@ -870,27 +894,28 @@
     assert micro == sides == 2 and parts == 4
     side = lax.axis_index("ctx")
     slot = lax.axis_index("tp")
-    deep = lax.axis_index("dp")
-    depth = lax.axis_size("dp")
     me = side * parts + slot
-    me_array = jnp.full((1,), me, jnp.int32)
+    me_array = jnp.stack([me, side]).astype(jnp.int32)
     side_array = jnp.full((1,), side, jnp.int32)
     tall = qkv_weight.shape[1]
     heads, piece = qkv_bias.shape[1], qkv_bias.shape[2]
     width = heads * HD
     lines, strip = fc_bias.shape
 
+    deep = lax.axis_index("dp")
+    depth = lax.axis_size("dp")
+
+    def swap_deep(array, mask):
+        return lax.ppermute(array, "dp", [(n, n ^ mask) for n in range(depth)])
+
     def swap(array, mask):
         return lax.ppermute(array, ("ctx", "tp"), [(n, n ^ mask) for n in range(group)])
 
-    def swap_deep(array, mask):
-        return lax.ppermute(array, "dp", [(n, n ^ mask) for n in range(depth)])
-
     tok = tokens[:, 0]
     cot = cotangent[:, 0]
 
     vectors = jnp.stack([ln1_gain, ln1_bias, ln2_gain, ln2_bias, out_bias, proj_bias])
-    wide, narrow = pack(fc_weight, proj_weight, out_weight, qkv_weight, vectors, qkv_bias, fc_bias, shards)
+    wide, narrow = pack(fc_weight, proj_weight.T, out_weight, qkv_weight, vectors, qkv_bias, fc_bias, shards)
 
     gathered = lax.all_gather(wide, ("tp", "dp", "ctx"), axis=0, tiled=True)
     gathered = gathered.reshape(parts, d, wide.shape[1])
@@ -911,6 +936,9 @@
     unit = lax.broadcasted_iota(jnp.int32, (1, d), 1)
     order_fc = one_hot_order(unit % 128 // strip * tall + unit // 128, d)
 
+    order_back = order_in.reshape(d, 3, width).transpose(1, 0, 2)
+    far, order_in, order_fc, order_back = barrier((far, order_in, order_fc, order_back))
+
     triple = project(me_array, own, far, w_in, order_in, piece)
     mixed, mixed_turned, level = attend(triple, rows)
     mix = lax.all_to_all(mixed, ("ctx", "tp"), 0, 0, tiled=True)
@@ -923,51 +951,56 @@
     grad_mix = lax.all_to_all(grad_mix, ("ctx", "tp"), 0, 0, tiled=True)
 
     parcels = (n2, cot_rows, gb, mix, act, gl, vec, gfb, order_fc, strip)
-    cut = wide.shape[1] // 2
-    if tall % 16 == 0 and depth & (depth - 1) == 0:
+    exchange = tall % 16 == 0 and depth == 4
+    if exchange:
         core, row = slot % 2, slot // 2
-        index = lambda lane: jnp.stack([(1 - row) * 2 + lane, row * 2 + lane, deep, side]).astype(jnp.int32)
+        index = lambda lane: jnp.stack([(1 - row) * 2 + lane, row * 2 + lane, side]).astype(jnp.int32)
         came = swap(weights("send", index(1 - core), *parcels), 1)
         a_send, a_keep, b_send, b_keep = weights("keep", index(core), *parcels, came=came, shards=shards)
         a_came, b_came = swap(a_send, 2), swap(b_send, parts)
-        a_send, a_keep = plus(a_keep[1], a_came[1]), plus(a_keep[0], a_came[0])
-        b_send, b_keep = plus(b_keep[1], b_came[1]), plus(b_keep[0], b_came[0])
-        a_came, b_came = swap(a_send, parts), swap(b_send, 2)
-        left, mask = depth, 1
-        while left > 1:
-            left //= 2
-            a_send, a_keep = plus(a_keep[left:], a_came[left:]), plus(a_keep[:left], a_came[:left])
-            b_send, b_keep = plus(b_keep[left:], b_came[left:]), plus(b_keep[:left], b_came[:left])
-            a_came, b_came = swap_deep(a_send, mask), swap_deep(b_send, mask)
-            mask *= 2
-        a_keep, a_came, b_keep, b_came = a_keep[0], a_came[0], b_keep[0], b_came[0]
     else:
         grad_wide = weights("all", jnp.arange(parts, dtype=jnp.int32), *parcels)
         grad_wide = lax.psum_scatter(
             grad_wide.reshape(parts * d, wide.shape[1]), ("tp", "dp", "ctx"), scatter_dimension=0, tiled=True
         )
-        a_keep, b_keep = grad_wide[:, :cut], grad_wide[:, cut:]
-        a_came, b_came = jnp.zeros_like(a_keep), jnp.zeros_like(b_keep)
 
     grad_triple = attend_back(triple, grad_mix, mixed_turned, level)
-    order_back = order_in.reshape(d, 3, width).transpose(1, 0, 2)
+    if exchange:
+        a_came, b_came, grad_triple = barrier((a_came, b_came, grad_triple))
+        a_send, b_send = plus(a_keep[1], a_came[1]), plus(b_keep[1], b_came[1])
+        a_send, b_send, grad_triple = barrier((a_send, b_send, grad_triple))
+        a_keep, b_keep = plus(a_keep[0], a_came[0]), plus(b_keep[0], b_came[0])
+        a_came, b_came = swap(a_send, parts), swap(b_send, 2)
     keep, send, grad_in = project_back(me_array, own, far, grad_triple, w_in, order_back, piece)
-
-    near, *sends = pair_sum(keep, swap(send, 1))
+    if exchange:
+        a_came, b_came, keep, send, grad_in = barrier((a_came, b_came, keep, send, grad_in))
+
+    send_came = swap(send, 1)
+    grad_in = lax.all_to_all(grad_in.reshape(narrow.shape), ("dp", "ctx"), 0, 0, tiled=True)
+    if exchange:
+        place = jnp.full((1,), deep, jnp.int32)
+        z_keep, z_send = wide_sum(place, a_keep, a_came, b_keep, b_came)
+        z_send, send_came = barrier((z_send, send_came))
+        z_came = swap_deep(z_send, 1)
+    near, *sends = pair_sum(keep, send_came)
     arrived = [swap(sends[n - 1], 2 * n) for n in range(1, group // 2)]
 
-    grad_in = lax.all_to_all(grad_in.reshape(narrow.shape), ("dp", "ctx"), 0, 0, tiled=True)
     grad_qkv_weight, grad_qkv_bias, vec_in = finish_narrow(grad_in, width, qkv_bias.shape)
     mask = parts // 2
     while mask:
         vec_in = vec_in + swap(vec_in, mask)
         mask //= 2
 
+    if exchange:
+        z_send = plus(z_keep[1:], z_came[1:])
+        wide_parts = [z_keep, z_came, swap_deep(z_send, 3)]
+    else:
+        wide_parts = [grad_wide[None]]
     grad_tokens = finish_rows(
         side_array, tok, near, *arrived, grad_hidden.reshape(micro, rows, d), w_in
     )
     fc_grad, proj_grad, out_grad, gain2, shift2, out_b, proj_b, fc_b = finish_wide(
-        a_keep, a_came, b_keep, b_came, d, width, fc_bias.shape
+        wide_parts, d, width, fc_bias.shape
     )
     return (
         y.reshape(micro, 1, rows, d),
@@ -982,7 +1015,7 @@
         shift2[0],
         fc_grad,
         fc_b,
-        proj_grad,
+        proj_grad.T,
         proj_b[0],
     )
 

time: 303 us -> 290 us (0.957)
  waiting for transfers between devices: 77.9 us -> 69.1 us
  Pallas kernels: 143 us -> 147 us
  other arithmetic: 16.8 us -> 13.4 us
  local copies, waits for them, and re-layouts: 13.5 us -> 10.2 us
    ppermute x15, waiting for transfers between devices: 59.3 us -> 31.1 us  [swap(): lax.ppermute(array, ('ctx', 'tp'), [(n, n ^ mask) for n in range(group)])]
    ppermute x4 -> x2, waiting for transfers between devices: 0.01 us -> 20.9 us  [swap_deep(): return lax.ppermute(array, 'dp', [(n, n ^ mask) for n in range(depth)])]
    convert_element_type x6 -> x2, other arithmetic: 9.12 us -> 5.2 us  [plus(): return (a.astype(F32) + b.astype(F32)).astype(BF16)]
    unnamed x34 -> x32, local copies, waits for them, and re-layouts: 10.9 us -> 7.15 us
    all_to_all x1, waiting for transfers between devices: 9.23 us -> 5.94 us  [local(): lax.all_to_all(narrow, ('dp', 'ctx'), 0, 0, tiled=True)]
    pallas_call x1 -> x2, Pallas kernels: 2.23 us -> 5.32 us  [the longest x1 2.96 us: wide_sum(): pl.pallas_call(wide_sum_kernel, out_shape=(out, out), grid_spec=pltpu.Pre...]
  transfers between devices with their start and end apart: 24 -> 22, of which waited for: 10 -> 10; matrix products, arithmetic and copies ran while one was open for 6% -> 4% of each run, Pallas kernels for 35% -> 39%
where the time goes in v5:
time: 290 us; the launch traced here: 289 us
  Pallas kernels  147 us (51%)
  waiting for transfers between devices  69.1 us (24%)
  starting transfers between devices  34.6 us (12%)
  between operations  14.2 us (5%)
  other arithmetic  13.4 us (5%)
  local copies, waits for them, and re-layouts  10.2 us (4%)
    pallas_call x1, Pallas kernels, attend_back(): pl.pallas_call(attend_back_kernel, out_shape=jax.ShapeDtypeStruct(triple....  32.1 us
    ppermute x15, waiting for transfers between devices, swap(): lax.ppermute(array, ('ctx', 'tp'), [(n, n ^ mask) for n in range(group)])  31.1 us
    pallas_call x1, Pallas kernels, attend(): pl.pallas_call(attend_kernel, out_shape=(jax.ShapeDtypeStruct((span // ro...  28.8 us
    pallas_call x1, Pallas kernels, middle(): pl.pallas_call(functools.partial(middle_kernel, strip), out_shape=(sds((r...  21.6 us
    ppermute x2, waiting for transfers between devices, swap_deep(): return lax.ppermute(array, 'dp', [(n, n ^ mask) for n in range(depth)])  20.9 us
    pallas_call x2, Pallas kernels, weights(): pl.pallas_call(functools.partial(weights_kernel, mode, strip), out_shape=...  20.7 us
    pallas_call x1, Pallas kernels, project_back(): pl.pallas_call(functools.partial(project_back_kernel, piece), out_shape=(...  14.3 us
    ppermute x15, starting transfers between devices, swap(): lax.ppermute(array, ('ctx', 'tp'), [(n, n ^ mask) for n in range(group)])  12.8 us
  transfers between devices with their start and end apart: 22, of which 10 were waited for; matrix products, arithmetic and copies ran while one was open for 4% of the time, Pallas kernels for 39%

profile of v5, /device:TPU:0, one launch (start us, length us, event | category | flops | bytes accessed | tf_op | source)
XLA Modules:
  0.0 288.7 jit_solution(789315477834295044)
XLA Ops:
  8.6 2.4 pack.1
  12.2 3.0 %collective-permute-start.1 = (bf16[256,768]{1,0:T(8,128)(2,1)S(1)}, bf16[256,768]{1,0:T(8,128)(2,1)S(1)}, u32[]{:S(2)}, u32[]{:S(2)}) collective-permute-start(bf16[256,768]{1,0:T(8,128)(2,1)S(1)} %get-tuple-element.144), channel_id=1, source_target_pairs={{0,4},{1,5},{2,6},{3,7},{4,0},{5,1},{6,2},{7,3},{8,12},{9,13},{10,... | collective-permute-start | bytes 1179656 | tf_op jit(solution)/shard_map/ppermute | solution.py:912
  15.2 1.5 collective-permute-start.2
  16.8 6.3 %all-to-all-start = ((bf16[8,96,640]{2,1,0:T(8,128)(2,1)}), bf16[8,96,640]{2,1,0:T(8,128)(2,1)S(1)}, u32[]{:S(2)}, u32[]{:S(2)}) async-start(bf16[8,96,640]{2,1,0:T(8,128)(2,1)} %get-tuple-element.70), calls=%async_computation | async-start | bytes 1966080 | tf_op jit(solution)/shard_map/all_to_all | solution.py:932
  23.0 4.5 %collective-permute-done.1 = bf16[256,768]{1,0:T(8,128)(2,1)S(1)} collective-permute-done((bf16[256,768]{1,0:T(8,128)(2,1)S(1)}, bf16[256,768]{1,0:T(8,128)(2,1)S(1)}, u32[]{:S(2)}, u32[]{:S(2)}) %collective-permute-start.1) | collective-permute-done | bytes 393248 | tf_op jit(solution)/shard_map/ppermute | solution.py:912
  27.6 15.1 %collective-permute-done.2 = bf16[256,768]{1,0:T(8,128)(2,1)} collective-permute-done((bf16[256,768]{1,0:T(8,128)(2,1)S(1)}, bf16[256,768]{1,0:T(8,128)(2,1)}, u32[]{:S(2)}, u32[]{:S(2)}) %collective-permute-start.2) | collective-permute-done | bytes 393248 | tf_op jit(solution)/shard_map/ppermute | solution.py:912
  47.0 1.5 select_convert_fusion.order_ref
  50.0 5.9 %all-to-all-done = bf16[8,96,640]{2,1,0:T(8,128)(2,1)S(1)} async-done(((bf16[8,96,640]{2,1,0:T(8,128)(2,1)}), bf16[8,96,640]{2,1,0:T(8,128)(2,1)S(1)}, u32[]{:S(2)}, u32[]{:S(2)}) %all-to-all-start) | async-done | bytes 983072 | tf_op jit(solution)/shard_map/all_to_all | solution.py:932
  56.9 10.9 %project.1.q_ref.k_ref.v_ref.qkv_ref = bf16[3,2048,192]{2,1,0:T(8,128)(2,1)} custom-call(s32[2]{0:T(128)} %pad_add_fusion.me_ref, bf16[4,256,768]{2,1,0:T(8,128)(2,1)} %copy-done.2, bf16[4,256,768]{2,1,0:T(8,128)(2,1)} %collective-permute-done.3.far_ref, bf16[768,640]{1,0:T(8,128)(2,1)} %bitcast.54, bf16[768,576]{1,0:T(8,128)(2,1)} %select_convert_fusion.2.order_ref), custom_call_target="tpu_custom_call" | custom-call | flops 1811939328 | bytes 8000000 | tf_op jit(solution)/shard_map/project/pallas_call | solution.py:129
  67.8 28.8 %attend.1 = (bf16[8,192,256]{2,1,0:T(8,128)(2,1)}, f32[192,2048]{1,0:T(8,128)}, f32[8,2048]{1,0:T(8,128)}) custom-call(bf16[3,2048,192]{2,1,0:T(8,128)(2,1)} %project.1.q_ref.k_ref.v_ref.qkv_ref, bf16[3,2048,192]{2,1,0:T(8,128)(2,1)} %project.1.q_ref.k_ref.v_ref.qkv_ref, bf16[3,2048,192]{2,1,0:T(8,128)(2,1)} %project.1.q_ref.k_ref.v_ref.qkv_ref), custom_call_target="tpu_custom_call" | custom-call | flops 3221225472 | bytes 8000000 | tf_op jit(solution)/shard_map/attend/pallas_call | solution.py:216
  96.6 3.9 %all-to-all-start.1 = ((bf16[8,192,256]{2,1,0:T(8,128)(2,1)}), bf16[8,192,256]{2,1,0:T(8,128)(2,1)S(1)}, u32[]{:S(2)}, u32[]{:S(2)}) async-start(bf16[8,192,256]{2,1,0:T(8,128)(2,1)} %get-tuple-element.72), calls=%async_computation.1 | async-start | bytes 1572864 | tf_op jit(solution)/shard_map/all_to_all | solution.py:944
  101.1 11.1 %all-to-all-done.1.mix_ref = bf16[8,192,256]{2,1,0:T(8,128)(2,1)S(1)} async-done(((bf16[8,192,256]{2,1,0:T(8,128)(2,1)}), bf16[8,192,256]{2,1,0:T(8,128)(2,1)S(1)}, u32[]{:S(2)}, u32[]{:S(2)}) %all-to-all-start.1) | async-done | bytes 786464 | tf_op jit(solution)/shard_map/all_to_all | solution.py:944
  113.0 21.6 %middle.1 = (bf16[512,768]{1,0:T(8,128)(2,1)}, f32[512,768]{1,0:T(8,128)}, bf16[8,192,256]{2,1,0:T(8,128)(2,1)}, bf16[512,768]{1,0:T(8,128)(2,1)}, bf16[4,512,76...) custom-call(bf16[512,768]{1,0:T(8,128)(2,1)} %bitcast.62, ...), custom_call_target="tpu_custom_call" | custom-call | flops 10871635968 | bytes 30000000 | tf_op jit(solution)/shard_map/middle/pallas_call | solution.py:458
  134.7 9.4 %weights_send.1 = bf16[2,768,1792]{2,1,0:T(8,128)(2,1)} custom-call(s32[3]{0:T(128)} %add_add_fusion.1.index_ref, bf16[512,768]{1,0:T(8,128)(2,1)} %get-tuple-element.76.n2_ref, bf16[512,768]{1,0:T(8,128)(2,1)} %bitcast.60, bf16[512,768]{1,0:T(8,128)(2,1)} %get-tuple-element.77.gb_ref, bf16[2,4,192,256]{3,2,1,0:T(8,128)(2,1)} %bitcast.57, ...), custom_call_target="tpu_custom_call" | custom-call | flops 2818572288 | bytes 12000000 | tf_op jit(solution)/shard_map/weights_send/pallas_call | solution.py:592
  144.6 3.8 %all-to-all-start.2 = ((bf16[8,192,256]{2,1,0:T(8,128)(2,1)}), bf16[8,192,256]{2,1,0:T(8,128)(2,1)S(1)}, u32[]{:S(2)}, u32[]{:S(2)}) async-start(bf16[8,192,256]{2,1,0:T(8,128)(2,1)} %get-tuple-element.85), calls=%async_computation.2 | async-start | bytes 1572864 | tf_op jit(solution)/shard_map/all_to_all | solution.py:951
  148.4 5.0 %collective-permute-done.4.rest_0_ = bf16[2,768,1792]{2,1,0:T(8,128)(2,1)} collective-permute-done((bf16[2,768,1792]{2,1,0:T(8,128)(2,1)}, bf16[2,768,1792]{2,1,0:T(8,128)(2,1)}, u32[]{:S(2)}, u32[]{:S(2)}) %collective-permute-start.4) | collective-permute-done | bytes 5505056 | tf_op jit(solution)/shard_map/ppermute | solution.py:912
  153.4 11.3 %weights_keep.1 = (bf16[2,4,96,896]{3,2,1,0:T(8,128)(2,1)}, bf16[2,4,96,896]{3,2,1,0:T(8,128)(2,1)}, bf16[2,4,96,896]{3,2,1,0:T(8,128)(2,1)}, bf16[2,4,96,896]{3,2,1,0:T(8,128)(2,1)}) custom-call(s32[3]{0:T(128)} %add_add_fusion.index_ref, bf16[512,768]{1,0:T(8,128)(2,1)} %get-tuple-element.76.n2_ref, bf16[512,768]{1,0:T(8,128)(2,1)} %bitcast.61, ...), custom_call_target="tpu_custom_call" | custom-call | flops 2818572288 | bytes 12000000 | tf_op jit(solution)/shard_map/weights_keep/pallas_call | solution.py:592
  167.7 32.1 %attend_back.1.grad_ref = bf16[3,2048,192]{2,1,0:T(8,128)(2,1)} custom-call(bf16[3,2048,192]{2,1,0:T(8,128)(2,1)} %project.1.q_ref.k_ref.v_ref.qkv_ref, bf16[8,192,256]{2,1,0:T(8,128)(2,1)} %copy-done.8, f32[192,2048]{1,0:T(8,128)} %get-tuple-element.86.ot_ref, f32[8,2048]{1,0:T(8,128)} %get-tuple-element.87.level_ref), custom_call_target="tpu_custom_call" | custom-call | flops 8053063680 | bytes 10000000 | tf_op jit(solution)/shard_map/attend_back/pallas_call | solution.py:337
  199.8 3.4 %fusion.2 = (bf16[4,96,896]{2,1,0:T(8,128)(2,1)}, bf16[4,96,896]{2,1,0:T(8,128)(2,1)}, bf16[4,96,896]{2,1,0:T(8,128)(2,1)}, bf16[4,96,896]{2,1,0:T(8,128)(2,1)}) fusion(bf16[2,4,96,896]{3,2,1,0:T(8,128)(2,1)S(1)} %collective-permute-done.5, bf16[2,4,96,896]{3,2,1,0:T(8,128)(2,1)S(1)} %copy-done.6, bf16[2,4,96,896]{3,2,1,0:T(8,128)(2,1)} %collective-permute-done.6, ...), kind=kLoop, calls=%fused_computation.13 | loop fusion | flops 5505024 | bytes 8257536 | tf_op jit(solution)/shard_map/convert_element_type | solution.py:870
  203.1 1.5 collective-permute-start.7
  205.2 14.3 %project_back.1 = (f32[4,256,768]{2,1,0:T(8,128)}, bf16[4,256,768]{2,1,0:T(8,128)(2,1)}, bf16[768,640]{1,0:T(8,128)(2,1)}) custom-call(s32[2]{0:T(128)} %pad_add_fusion.me_ref, bf16[4,256,768]{2,1,0:T(8,128)(2,1)} %copy-done.2, bf16[4,256,768]{2,1,0:T(8,128)(2,1)} %collective-permute-done.3.far_ref, bf16[3,2048,192]{2,1,0:T(8,128)(2,1)} %attend_back.1.grad_ref, ...), custom_call_target="tpu_custom_call" | custom-call | flops 3623878656 | bytes 15000000 | tf_op jit(solution)/shard_map/project_back/pallas_call | solution.py:759
  222.3 3.8 %all-to-all-start.3 = ((bf16[8,96,640]{2,1,0:T(8,128)(2,1)}), bf16[8,96,640]{2,1,0:T(8,128)(2,1)S(1)}, u32[]{:S(2)}, u32[]{:S(2)}) async-start(bf16[8,96,640]{2,1,0:T(8,128)(2,1)} %bitcast.66), calls=%async_computation.3 | async-start | bytes 1966080 | tf_op jit(solution)/shard_map/all_to_all | solution.py:979
  226.2 3.0 %wide_sum.1 = (bf16[2,96,1792]{2,1,0:T(8,128)(2,1)}, bf16[2,96,1792]{2,1,0:T(8,128)(2,1)}) custom-call(s32[1]{0:T(128)} %bitcast.29.place_ref, bf16[4,96,896]{2,1,0:T(8,128)(2,1)} %get-tuple-element.140.ak_ref, bf16[4,96,896]{2,1,0:T(8,128)(2,1)} %copy-done.9, bf16[4,96,896]{2,1,0:T(8,128)(2,1)} %get-tuple-element.148.bk_ref, bf16[4,96,896]{2,1,0:T(8,128)(2,1)} %copy-done.10), custom_call_target="tpu_custom_call" | custom-call | bytes 4000000 | tf_op jit(solution)/shard_map/wide_sum/pallas_call | solution.py:621
  229.1 1.7 collective-permute-start.15
  230.9 4.5 %pair_sum.1 = (f32[256,768]{1,0:T(8,128)}, bf16[256,768]{1,0:T(8,128)(2,1)}, bf16[256,768]{1,0:T(8,128)(2,1)}, bf16[256,768]{1,0:T(8,128)(2,1)}) custom-call(f32[4,256,768]{2,1,0:T(8,128)} %get-tuple-element.99.keep_ref, bf16[4,256,768]{2,1,0:T(8,128)(2,1)} %copy-done.4), custom_call_target="tpu_custom_call" | custom-call | bytes 7000000 | tf_op jit(solution)/shard_map/pair_sum/pallas_call | solution.py:814
  238.9 20.9 %collective-permute-done.15.refs_1_ = bf16[2,96,1792]{2,1,0:T(8,128)(2,1)} collective-permute-done((bf16[2,96,1792]{2,1,0:T(8,128)(2,1)}, bf16[2,96,1792]{2,1,0:T(8,128)(2,1)}, u32[]{:S(2)}, u32[]{:S(2)}) %collective-permute-start.15) | collective-permute-done | bytes 688160 | tf_op jit(solution)/shard_map/ppermute | solution.py:909
  259.8 1.8 add_convert_fusion.4
  261.6 2.4 collective-permute-start.16
  264.9 2.1 finish_narrow.1
  267.6 3.2 %collective-permute-done.13 = f32[8,96]{1,0:T(8,128)S(1)} collective-permute-done((f32[8,96]{1,0:T(8,128)}, f32[8,96]{1,0:T(8,128)S(1)}, u32[]{:S(2)}, u32[]{:S(2)}) %collective-permute-start.13) | collective-permute-done | bytes 3104 | tf_op jit(solution)/shard_map/ppermute | solution.py:912
  274.3 4.5 %finish_rows.1 = f32[2,256,768]{2,1,0:T(8,128)} custom-call(s32[1]{0:T(128)} %bitcast.3.side_ref, bf16[2,256,768]{2,1,0:T(8,128)(2,1)} %bitcast.63, f32[256,768]{1,0:T(8,128)} %get-tuple-element.105.near_ref, bf16[256,768]{1,0:T(8,128)(2,1)} %copy-done.12, bf16[256,768]{1,0:T(8,128)(2,1)} %copy-done.13, bf16[256,768]{1,0:T(8,128)(2,1)} %copy-done.14, ...), custom_call_target="tpu_custom_call" | custom-call | bytes 6000000 | tf_op jit(solution)/shard_map/finish_rows/pallas_call | solution.py:845
  279.5 2.4 finish_wide.1
  (75 shorter events, 27.0 us)
Async XLA Ops:
  7.2 105.0 %all-gather.2.cloned.1.call-start = ((), (), s32[]{:S(2)}) async-start(), calls=%async_computation.4 | async-start | bytes 11354112 | tf_op jit(solution)/shard_map/all_gather | solution.py:920
  12.2 15.4 %collective-permute-start.1 = (bf16[256,768]{1,0:T(8,128)(2,1)S(1)}, bf16[256,768]{1,0:T(8,128)(2,1)S(1)}, u32[]{:S(2)}, u32[]{:S(2)}) collective-permute-start(bf16[256,768]{1,0:T(8,128)(2,1)S(1)} %get-tuple-element.144), channel_id=1, source_target_pairs={{0,4},{1,5},{2,6},{3,7},{4,0},{5,1},{6,2},{7,3},{8,12},{9,13},{10,... | collective-permute-start | bytes 1179656 | tf_op jit(solution)/shard_map/ppermute | solution.py:912
  15.2 27.5 %collective-permute-start.2 = (bf16[256,768]{1,0:T(8,128)(2,1)S(1)}, bf16[256,768]{1,0:T(8,128)(2,1)}, u32[]{:S(2)}, u32[]{:S(2)}) collective-permute-start(bf16[256,768]{1,0:T(8,128)(2,1)S(1)} %get-tuple-element.144), channel_id=1, source_target_pairs={{0,6},{1,7},{2,4},{3,5},{4,2},{5,3},{6,0},{7,1},{8,14},{9,15},{10,... | collective-permute-start | bytes 1179656 | tf_op jit(solution)/shard_map/ppermute | solution.py:912
  16.7 26.0 %collective-permute-start = (bf16[256,768]{1,0:T(8,128)(2,1)S(1)}, bf16[256,768]{1,0:T(8,128)(2,1)S(1)}, u32[]{:S(2)}, u32[]{:S(2)}) collective-permute-start(bf16[256,768]{1,0:T(8,128)(2,1)S(1)} %get-tuple-element.143), channel_id=1, source_target_pairs={{0,2},{1,3},{2,0},{3,1},{4,6},{5,7},{6,4},{7,5},{8,10},{9,11},{10,... | collective-permute-start | bytes 1179656 | tf_op jit(solution)/shard_map/ppermute | solution.py:912
  16.8 39.1 %all-to-all-start = ((bf16[8,96,640]{2,1,0:T(8,128)(2,1)}), bf16[8,96,640]{2,1,0:T(8,128)(2,1)S(1)}, u32[]{:S(2)}, u32[]{:S(2)}) async-start(bf16[8,96,640]{2,1,0:T(8,128)(2,1)} %get-tuple-element.70), calls=%async_computation | async-start | bytes 1966080 | tf_op jit(solution)/shard_map/all_to_all | solution.py:932
  44.8 5.2 %copy-start.2 = (bf16[4,256,768]{2,1,0:T(8,128)(2,1)}, bf16[4,256,768]{2,1,0:T(8,128)(2,1)S(1)}, u32[]{:S(2)}) copy-start(bf16[4,256,768]{2,1,0:T(8,128)(2,1)S(1)} %pad_maximum_fusion.own_ref) | copy-start | bytes 4718596
  44.8 5.2 %collective-permute-start.3 = (bf16[4,256,768]{2,1,0:T(8,128)(2,1)S(1)}, bf16[4,256,768]{2,1,0:T(8,128)(2,1)}, u32[]{:S(2)}, u32[]{:S(2)}) collective-permute-start(bf16[4,256,768]{2,1,0:T(8,128)(2,1)S(1)} %pad_maximum_fusion.own_ref), channel_id=1, source_target_pairs={{0,1},{1,0},{2,3},{3,2},{4,5},{5,4},{6,7},{7,6},{8,9},{9,8},{10,11... | collective-permute-start | bytes 4718600 | tf_op jit(solution)/shard_map/ppermute | solution.py:912
  55.9 1.0 copy-start
  96.6 15.6 %all-to-all-start.1 = ((bf16[8,192,256]{2,1,0:T(8,128)(2,1)}), bf16[8,192,256]{2,1,0:T(8,128)(2,1)S(1)}, u32[]{:S(2)}, u32[]{:S(2)}) async-start(bf16[8,192,256]{2,1,0:T(8,128)(2,1)} %get-tuple-element.72), calls=%async_computation.1 | async-start | bytes 1572864 | tf_op jit(solution)/shard_map/all_to_all | solution.py:944
  144.0 9.4 %collective-permute-start.4 = (bf16[2,768,1792]{2,1,0:T(8,128)(2,1)}, bf16[2,768,1792]{2,1,0:T(8,128)(2,1)}, u32[]{:S(2)}, u32[]{:S(2)}) collective-permute-start(bf16[2,768,1792]{2,1,0:T(8,128)(2,1)} %weights_send.1), channel_id=1, source_target_pairs={{0,1},{1,0},{2,3},{3,2},{4,5},{5,4},{6,7},{7,6},{8,9},{9,8},{10,11... | collective-permute-start | bytes 16515080 | tf_op jit(solution)/shard_map/ppermute | solution.py:912
  144.6 22.1 %all-to-all-start.2 = ((bf16[8,192,256]{2,1,0:T(8,128)(2,1)}), bf16[8,192,256]{2,1,0:T(8,128)(2,1)S(1)}, u32[]{:S(2)}, u32[]{:S(2)}) async-start(bf16[8,192,256]{2,1,0:T(8,128)(2,1)} %get-tuple-element.85), calls=%async_computation.2 | async-start | bytes 1572864 | tf_op jit(solution)/shard_map/all_to_all | solution.py:951
  164.7 35.0 %collective-permute-start.5 = (bf16[2,4,96,896]{3,2,1,0:T(8,128)(2,1)}, bf16[2,4,96,896]{3,2,1,0:T(8,128)(2,1)S(1)}, u32[]{:S(2)}, u32[]{:S(2)}) collective-permute-start(bf16[2,4,96,896]{3,2,1,0:T(8,128)(2,1)} %get-tuple-element.83), channel_id=1, source_target_pairs={{0,2},{1,3},{2,0},{3,1},{4,6},{5,7},{6,4},{7,5},{8,10},{9,11},{10,... | collective-permute-start | bytes 4128776 | tf_op jit(solution)/shard_map/ppermute | solution.py:912
  166.2 33.5 %collective-permute-start.6 = (bf16[2,4,96,896]{3,2,1,0:T(8,128)(2,1)}, bf16[2,4,96,896]{3,2,1,0:T(8,128)(2,1)}, u32[]{:S(2)}, u32[]{:S(2)}) collective-permute-start(bf16[2,4,96,896]{3,2,1,0:T(8,128)(2,1)} %get-tuple-element.84), channel_id=1, source_target_pairs={{0,4},{1,5},{2,6},{3,7},{4,0},{5,1},{6,2},{7,3},{8,12},{9,13},{10,... | collective-permute-start | bytes 4128776 | tf_op jit(solution)/shard_map/ppermute | solution.py:912
  166.8 0.9 copy-start.8
  167.7 32.1 %copy-start.6 = (bf16[2,4,96,896]{3,2,1,0:T(8,128)(2,1)S(1)}, bf16[2,4,96,896]{3,2,1,0:T(8,128)(2,1)}, u32[]{:S(2)}) copy-start(bf16[2,4,96,896]{3,2,1,0:T(8,128)(2,1)} %get-tuple-element.82) | copy-start | bytes 4128772
  167.7 32.1 %copy-start.7 = (bf16[2,4,96,896]{3,2,1,0:T(8,128)(2,1)S(1)}, bf16[2,4,96,896]{3,2,1,0:T(8,128)(2,1)}, u32[]{:S(2)}) copy-start(bf16[2,4,96,896]{3,2,1,0:T(8,128)(2,1)} %get-tuple-element.89) | copy-start | bytes 4128772
  203.1 17.1 %collective-permute-start.7 = (bf16[4,96,896]{2,1,0:T(8,128)(2,1)}, bf16[4,96,896]{2,1,0:T(8,128)(2,1)S(1)}, u32[]{:S(2)}, u32[]{:S(2)}) collective-permute-start(bf16[4,96,896]{2,1,0:T(8,128)(2,1)} %get-tuple-element.92), channel_id=1, source_target_pairs={{0,4},{1,5},{2,6},{3,7},{4,0},{5,1},{6,2},{7,3},{8,12},{9,13},{10,... | collective-permute-start | bytes 2064392 | tf_op jit(solution)/shard_map/ppermute | solution.py:912
  204.6 16.8 %collective-permute-start.8 = (bf16[4,96,896]{2,1,0:T(8,128)(2,1)}, bf16[4,96,896]{2,1,0:T(8,128)(2,1)S(1)}, u32[]{:S(2)}, u32[]{:S(2)}) collective-permute-start(bf16[4,96,896]{2,1,0:T(8,128)(2,1)} %get-tuple-element.93), channel_id=1, source_target_pairs={{0,2},{1,3},{2,0},{3,1},{4,6},{5,7},{6,4},{7,5},{8,10},{9,11},{10,... | collective-permute-start | bytes 2064392 | tf_op jit(solution)/shard_map/ppermute | solution.py:912
  220.3 5.9 %copy-start.9 = (bf16[4,96,896]{2,1,0:T(8,128)(2,1)}, bf16[4,96,896]{2,1,0:T(8,128)(2,1)S(1)}, u32[]{:S(2)}) copy-start(bf16[4,96,896]{2,1,0:T(8,128)(2,1)S(1)} %collective-permute-done.7.ac_ref) | copy-start | bytes 2064388
  222.3 6.8 %collective-permute-start.9 = (bf16[4,256,768]{2,1,0:T(8,128)(2,1)}, bf16[4,256,768]{2,1,0:T(8,128)(2,1)S(1)}, u32[]{:S(2)}, u32[]{:S(2)}) collective-permute-start(bf16[4,256,768]{2,1,0:T(8,128)(2,1)} %get-tuple-element.103), channel_id=1, source_target_pairs={{0,1},{1,0},{2,3},{3,2},{4,5},{5,4},{6,7},{7,6},{8,9},{9,8},{10,11... | collective-permute-start | bytes 4718600 | tf_op jit(solution)/shard_map/ppermute | solution.py:912
  222.3 41.7 %all-to-all-start.3 = ((bf16[8,96,640]{2,1,0:T(8,128)(2,1)}), bf16[8,96,640]{2,1,0:T(8,128)(2,1)S(1)}, u32[]{:S(2)}, u32[]{:S(2)}) async-start(bf16[8,96,640]{2,1,0:T(8,128)(2,1)} %bitcast.66), calls=%async_computation.3 | async-start | bytes 1966080 | tf_op jit(solution)/shard_map/all_to_all | solution.py:979
  229.1 1.7 copy-start.4
  229.1 30.7 %copy-start.5 = (bf16[2,96,1792]{2,1,0:T(8,128)(2,1)S(1)}, bf16[2,96,1792]{2,1,0:T(8,128)(2,1)}, u32[]{:S(2)}) copy-start(bf16[2,96,1792]{2,1,0:T(8,128)(2,1)} %get-tuple-element.114.refs_0_) | copy-start | bytes 2064388
  229.1 30.7 %collective-permute-start.15 = (bf16[2,96,1792]{2,1,0:T(8,128)(2,1)}, bf16[2,96,1792]{2,1,0:T(8,128)(2,1)}, u32[]{:S(2)}, u32[]{:S(2)}) collective-permute-start(bf16[2,96,1792]{2,1,0:T(8,128)(2,1)} %get-tuple-element.115), channel_id=1, source_target_pairs={{0,8},{8,0},{16,24},{24,16},{1,9},{9,1},{17,25},{25,17},{2,10},{10... | collective-permute-start | bytes 2064392 | tf_op jit(solution)/shard_map/ppermute | solution.py:909
  235.4 37.8 %collective-permute-start.10 = (bf16[256,768]{1,0:T(8,128)(2,1)}, bf16[256,768]{1,0:T(8,128)(2,1)S(1)}, u32[]{:S(2)}, u32[]{:S(2)}) collective-permute-start(bf16[256,768]{1,0:T(8,128)(2,1)} %get-tuple-element.106), channel_id=1, source_target_pairs={{0,2},{1,3},{2,0},{3,1},{4,6},{5,7},{6,4},{7,5},{8,10},{9,11},{10,... | collective-permute-start | bytes 1179656 | tf_op jit(solution)/shard_map/ppermute | solution.py:912
  236.4 36.9 %collective-permute-start.11 = (bf16[256,768]{1,0:T(8,128)(2,1)}, bf16[256,768]{1,0:T(8,128)(2,1)S(1)}, u32[]{:S(2)}, u32[]{:S(2)}) collective-permute-start(bf16[256,768]{1,0:T(8,128)(2,1)} %get-tuple-element.107), channel_id=1, source_target_pairs={{0,4},{1,5},{2,6},{3,7},{4,0},{5,1},{6,2},{7,3},{8,12},{9,13},{10,... | collective-permute-start | bytes 1179656 | tf_op jit(solution)/shard_map/ppermute | solution.py:912
  237.8 35.4 %collective-permute-start.12 = (bf16[256,768]{1,0:T(8,128)(2,1)}, bf16[256,768]{1,0:T(8,128)(2,1)S(1)}, u32[]{:S(2)}, u32[]{:S(2)}) collective-permute-start(bf16[256,768]{1,0:T(8,128)(2,1)} %get-tuple-element.108), channel_id=1, source_target_pairs={{0,6},{1,7},{2,4},{3,5},{4,2},{5,3},{6,0},{7,1},{8,14},{9,15},{10,... | collective-permute-start | bytes 1179656 | tf_op jit(solution)/shard_map/ppermute | solution.py:912
  261.6 17.2 %collective-permute-start.16 = (bf16[1,96,1792]{2,1,0:T(8,128)(2,1)}, bf16[1,96,1792]{2,1,0:T(8,128)(2,1)S(1)}, u32[]{:S(2)}, u32[]{:S(2)}) collective-permute-start(bf16[1,96,1792]{2,1,0:T(8,128)(2,1)} %add_convert_fusion.4), channel_id=1, source_target_pairs={{0,24},{8,16},{16,8},{24,0},{1,25},{9,17},{17,9},{25,1},{2,26},{10... | collective-permute-start | bytes 1032200 | tf_op jit(solution)/shard_map/ppermute | solution.py:909
  264.0 0.9 copy-start.3
  267.0 3.8 %collective-permute-start.13 = (f32[8,96]{1,0:T(8,128)}, f32[8,96]{1,0:T(8,128)S(1)}, u32[]{:S(2)}, u32[]{:S(2)}) collective-permute-start(f32[8,96]{1,0:T(8,128)} %get-tuple-element.111), channel_id=1, source_target_pairs={{0,2},{1,3},{2,0},{3,1},{4,6},{5,7},{6,4},{7,5},{8,10},{9,11},{10,... | collective-permute-start | bytes 9224 | tf_op jit(solution)/shard_map/ppermute | solution.py:912
  271.5 1.2 collective-permute-start.14
  273.3 1.1 copy-start.14
  (6 other events, 4.9 us)
Sparse Core Ops, SparseCore 0:
  11.1 100.1 all-gather.1

commit v6 on v5

--- a/solution.py
+++ b/solution.py
@@ -46,11 +46,13 @@
     return pl.CostEstimate(flops=int(flops), bytes_accessed=int(moved), transcendentals=int(exps))
 
 
-def pack_kernel(fc_ref, pj_ref, out_ref, qkv_ref, vec_ref, qb_ref, fb_ref, wide_ref, narrow_ref):
+def pack_kernel(fc_ref, pj_ref, out_ref, qkv_ref, qb_ref, fb_ref, *rest):
+    vec_refs, wide_ref, narrow_ref = rest[:-2], rest[-2], rest[-1]
     tall, d = fc_ref.shape
     width = out_ref.shape[0]
     copies = narrow_ref.shape[0]
-    columns = jnp.transpose(vec_ref[...].astype(F32)).astype(BF16)
+    vectors = jnp.concatenate([ref[...].astype(F32) for ref in vec_refs] + [jnp.zeros((2, tall), F32)], axis=0)
+    columns = jnp.transpose(vectors).astype(BF16)
     wide_ref[:, :d] = fc_ref[...]
     wide_ref[:, d : 2 * d] = pj_ref[...]
     wide_ref[:, 2 * d : 2 * d + width] = jnp.transpose(out_ref[...].astype(F32)).astype(BF16)
@@ -84,7 +86,7 @@
         compiler_params=pltpu.CompilerParams(vmem_limit_bytes=SMALL_LIMIT),
         cost_estimate=cost(0, 2e6),
         name="pack",
-    )(fc, pj, out, qkv, vec, qb, fb)
+    )(fc, pj, out, qkv, qb, fb, *vec)
 
 
 def pick_rows(table, period):
@@ -605,27 +607,30 @@
     )(*operands)
 
 
-def wide_sum_kernel(place_ref, ak_ref, ac_ref, bk_ref, bc_ref, keep_ref, send_ref):
-    cut = ak_ref.shape[2]
-    for ref, members in ((send_ref, (1, 2)), (keep_ref, (0, 3))):
-        for n, m in enumerate(members):
-            z = pl.ds(place_ref[0] ^ m, 1)
-            ref[n : n + 1, :, :cut] = (ak_ref[z].astype(F32) + ac_ref[z].astype(F32)).astype(BF16)
-            ref[n : n + 1, :, cut:] = (bk_ref[z].astype(F32) + bc_ref[z].astype(F32)).astype(BF16)
+def wide_sum_kernel(place_ref, *refs):
+    for i, masks in enumerate(((1, 3), (3, 1))):
+        mine_ref, first_ref, second_ref = refs[3 * i : 3 * i + 3]
+        keep_ref, send_ref = refs[6 + 2 * i : 8 + 2 * i]
+        for ref, base in ((send_ref, masks[0]), (keep_ref, 0)):
+            for n, m in enumerate((base, base ^ masks[1])):
+                z = pl.ds(place_ref[0] ^ m, 1)
+                total = mine_ref[0, z].astype(F32) + first_ref[0, z].astype(F32)
+                ref[n : n + 1] = (total + second_ref[z].astype(F32)).astype(BF16)
 
 
 def wide_sum(place, *parts):
-    depth, step, cut = parts[0].shape
-    whole = lambda array: pl.BlockSpec(array.shape, lambda i, ix: (0, 0, 0))
-    out = jax.ShapeDtypeStruct((depth // 2, step, 2 * cut), BF16)
+    depth, step, cut = parts[2].shape
+    first = pl.BlockSpec((1, depth, step, cut), lambda i, ix: (0, 0, 0, 0))
+    last = pl.BlockSpec((depth, step, cut), lambda i, ix: (0, 0, 0))
+    out = jax.ShapeDtypeStruct((depth // 2, step, cut), BF16)
     return pl.pallas_call(
         wide_sum_kernel,
-        out_shape=(out, out),
+        out_shape=(out,) * 4,
         grid_spec=pltpu.PrefetchScalarGridSpec(
             num_scalar_prefetch=1,
             grid=(1,),
-            in_specs=[whole(p) for p in parts],
-            out_specs=(whole(out), whole(out)),
+            in_specs=[first, first, last] * 2,
+            out_specs=(pl.BlockSpec(out.shape, lambda i, ix: (0, 0, 0)),) * 4,
         ),
         compiler_params=params(),
         cost_estimate=cost(0, 4e6),
@@ -637,9 +642,14 @@
     fc_ref, pj_ref, out_ref, g_ref, b_ref, ob_ref, pb_ref, fb_ref = refs[-8:]
     d = fc_ref.shape[1]
     width = out_ref.shape[0]
-    t = refs[0][0].astype(F32)
-    for ref in refs[1:-8]:
-        t = t + ref[0].astype(F32)
+    halves = []
+    count = (len(refs) - 8) // 2
+    for parts in (refs[:count], refs[count : 2 * count]):
+        t = parts[0][0].astype(F32)
+        for ref in parts[1:]:
+            t = t + ref[0].astype(F32)
+        halves.append(t)
+    t = jnp.concatenate(halves, axis=1)
     fc_ref[...] = t[:, :d]
     pj_ref[...] = t[:, d : 2 * d]
     rest = jnp.transpose(t[:, 2 * d : 2 * d + width + EXT])
@@ -914,7 +924,7 @@
     tok = tokens[:, 0]
     cot = cotangent[:, 0]
 
-    vectors = jnp.stack([ln1_gain, ln1_bias, ln2_gain, ln2_bias, out_bias, proj_bias])
+    vectors = [v[None] for v in (ln1_gain, ln1_bias, ln2_gain, ln2_bias, out_bias, proj_bias)]
     wide, narrow = pack(fc_weight, proj_weight.T, out_weight, qkv_weight, vectors, qkv_bias, fc_bias, shards)
 
     gathered = lax.all_gather(wide, ("tp", "dp", "ctx"), axis=0, tiled=True)
@@ -969,22 +979,23 @@
         a_came, b_came, grad_triple = barrier((a_came, b_came, grad_triple))
         a_send, b_send = plus(a_keep[1], a_came[1]), plus(b_keep[1], b_came[1])
         a_send, b_send, grad_triple = barrier((a_send, b_send, grad_triple))
-        a_keep, b_keep = plus(a_keep[0], a_came[0]), plus(b_keep[0], b_came[0])
-        a_came, b_came = swap(a_send, parts), swap(b_send, 2)
+        a_last, b_last = swap(a_send, parts), swap(b_send, 2)
     keep, send, grad_in = project_back(me_array, own, far, grad_triple, w_in, order_back, piece)
     if exchange:
-        a_came, b_came, keep, send, grad_in = barrier((a_came, b_came, keep, send, grad_in))
+        a_last, b_last, keep, send, grad_in = barrier((a_last, b_last, keep, send, grad_in))
 
     send_came = swap(send, 1)
     grad_in = lax.all_to_all(grad_in.reshape(narrow.shape), ("dp", "ctx"), 0, 0, tiled=True)
     if exchange:
         place = jnp.full((1,), deep, jnp.int32)
-        z_keep, z_send = wide_sum(place, a_keep, a_came, b_keep, b_came)
-        z_send, send_came = barrier((z_send, send_came))
-        z_came = swap_deep(z_send, 1)
+        a_kept, a_send, b_kept, b_send = wide_sum(place, a_keep, a_came, a_last, b_keep, b_came, b_last)
+        a_send, send_came = barrier((a_send, send_came))
+        a_came, b_came = swap_deep(a_send, 1), swap_deep(b_send, 3)
     near, *sends = pair_sum(keep, send_came)
     arrived = [swap(sends[n - 1], 2 * n) for n in range(1, group // 2)]
 
+    if exchange:
+        grad_in, a_came, b_came, near = barrier((grad_in, a_came, b_came, near))
     grad_qkv_weight, grad_qkv_bias, vec_in = finish_narrow(grad_in, width, qkv_bias.shape)
     mask = parts // 2
     while mask:
@@ -992,10 +1003,12 @@
         mask //= 2
 
     if exchange:
-        z_send = plus(z_keep[1:], z_came[1:])
-        wide_parts = [z_keep, z_came, swap_deep(z_send, 3)]
+        a_last = swap_deep(plus(a_kept[1:], a_came[1:]), 3)
+        b_last = swap_deep(plus(b_kept[1:], b_came[1:]), 1)
+        wide_parts = [a_kept, a_came, a_last, b_kept, b_came, b_last]
     else:
-        wide_parts = [grad_wide[None]]
+        cut = wide.shape[1] // 2
+        wide_parts = [grad_wide[None, :, :cut], grad_wide[None, :, cut:]]
     grad_tokens = finish_rows(
         side_array, tok, near, *arrived, grad_hidden.reshape(micro, rows, d), w_in
     )

time: 290 us -> 293 us (1.010)
  starting transfers between devices: 34.6 us -> 43.7 us
  waiting for transfers between devices: 69.1 us -> 63.3 us
    ppermute x2 -> x4, starting transfers between devices: 4.09 us -> 13.3 us  [swap_deep(): return lax.ppermute(array, 'dp', [(n, n ^ mask) for n in range(depth)])]
    ppermute x2 -> x4, waiting for transfers between devices: 20.9 us -> 13.7 us  [swap_deep(): return lax.ppermute(array, 'dp', [(n, n ^ mask) for n in range(depth)])]
    all_to_all x1, waiting for transfers between devices: 0.01 us -> 4.16 us  [local(): lax.all_to_all(grad_in.reshape(narrow.shape), ('dp', 'ctx'), 0, 0, tiled=...]
    ppermute x15, waiting for transfers between devices: 31.1 us -> 27.6 us  [swap(): lax.ppermute(array, ('ctx', 'tp'), [(n, n ^ mask) for n in range(group)])]
    unnamed x32 -> x38, local copies, waits for them, and re-layouts: 7.15 us -> 7.78 us
  transfers between devices with their start and end apart: 22 -> 24, of which waited for: 10 -> 12; matrix products, arithmetic and copies ran while one was open for 4% -> 4% of each run, Pallas kernels for 39% -> 38%
where the time goes in v6:
time: 293 us; the launch traced here: 291 us
  Pallas kernels  148 us (51%)
  waiting for transfers between devices  63.3 us (22%)
  starting transfers between devices  43.7 us (15%)
  between operations  14.3 us (5%)
  other arithmetic  12.1 us (4%)
  local copies, waits for them, and re-layouts  9.5 us (3%)
    pallas_call x1, Pallas kernels, attend_back(): pl.pallas_call(attend_back_kernel, out_shape=jax.ShapeDtypeStruct(triple....  32.1 us
    pallas_call x1, Pallas kernels, attend(): pl.pallas_call(attend_kernel, out_shape=(jax.ShapeDtypeStruct((span // ro...  28.8 us
    ppermute x15, waiting for transfers between devices, swap(): lax.ppermute(array, ('ctx', 'tp'), [(n, n ^ mask) for n in range(group)])  27.6 us
    pallas_call x1, Pallas kernels, middle(): pl.pallas_call(functools.partial(middle_kernel, strip), out_shape=(sds((r...  21.6 us
    pallas_call x2, Pallas kernels, weights(): pl.pallas_call(functools.partial(weights_kernel, mode, strip), out_shape=...  20.8 us
    pallas_call x1, Pallas kernels, project_back(): pl.pallas_call(functools.partial(project_back_kernel, piece), out_shape=(...  14.3 us
    ppermute x4, waiting for transfers between devices, swap_deep(): return lax.ppermute(array, 'dp', [(n, n ^ mask) for n in range(depth)])  13.7 us
    ppermute x4, starting transfers between devices, swap_deep(): return lax.ppermute(array, 'dp', [(n, n ^ mask) for n in range(depth)])  13.3 us
  transfers between devices with their start and end apart: 24, of which 12 were waited for; matrix products, arithmetic and copies ran while one was open for 4% of the time, Pallas kernels for 38%

profile of v6, /device:TPU:0, one launch (start us, length us, event | category | flops | bytes accessed | tf_op | source)
XLA Modules:
  0.0 290.6 jit_solution(3258988876218945944)
XLA Ops:
  7.2 2.5 pack.1
  10.9 3.0 %collective-permute-start.1 = (bf16[256,768]{1,0:T(8,128)(2,1)S(1)}, bf16[256,768]{1,0:T(8,128)(2,1)S(1)}, u32[]{:S(2)}, u32[]{:S(2)}) collective-permute-start(bf16[256,768]{1,0:T(8,128)(2,1)S(1)} %get-tuple-element.152), channel_id=1, source_target_pairs={{0,4},{1,5},{2,6},{3,7},{4,0},{5,1},{6,2},{7,3},{8,12},{9,13},{10,... | collective-permute-start | bytes 1179656 | tf_op jit(solution)/shard_map/ppermute | solution.py:922
  14.0 1.5 collective-permute-start.2
  15.5 6.3 %all-to-all-start = ((bf16[8,96,640]{2,1,0:T(8,128)(2,1)}), bf16[8,96,640]{2,1,0:T(8,128)(2,1)S(1)}, u32[]{:S(2)}, u32[]{:S(2)}) async-start(bf16[8,96,640]{2,1,0:T(8,128)(2,1)} %get-tuple-element.76), calls=%async_computation | async-start | bytes 1966080 | tf_op jit(solution)/shard_map/all_to_all | solution.py:942
  21.8 3.9 %collective-permute-done.1 = bf16[256,768]{1,0:T(8,128)(2,1)S(1)} collective-permute-done((bf16[256,768]{1,0:T(8,128)(2,1)S(1)}, bf16[256,768]{1,0:T(8,128)(2,1)S(1)}, u32[]{:S(2)}, u32[]{:S(2)}) %collective-permute-start.1) | collective-permute-done | bytes 393248 | tf_op jit(solution)/shard_map/ppermute | solution.py:922
  25.7 16.5 %collective-permute-done.2 = bf16[256,768]{1,0:T(8,128)(2,1)} collective-permute-done((bf16[256,768]{1,0:T(8,128)(2,1)S(1)}, bf16[256,768]{1,0:T(8,128)(2,1)}, u32[]{:S(2)}, u32[]{:S(2)}) %collective-permute-start.2) | collective-permute-done | bytes 393248 | tf_op jit(solution)/shard_map/ppermute | solution.py:922
  46.5 1.5 select_convert_fusion.order_ref
  49.4 7.0 %all-to-all-done = bf16[8,96,640]{2,1,0:T(8,128)(2,1)S(1)} async-done(((bf16[8,96,640]{2,1,0:T(8,128)(2,1)}), bf16[8,96,640]{2,1,0:T(8,128)(2,1)S(1)}, u32[]{:S(2)}, u32[]{:S(2)}) %all-to-all-start) | async-done | bytes 983072 | tf_op jit(solution)/shard_map/all_to_all | solution.py:942
  57.4 10.9 %project.1.q_ref.k_ref.v_ref.qkv_ref = bf16[3,2048,192]{2,1,0:T(8,128)(2,1)} custom-call(s32[2]{0:T(128)} %pad_add_fusion.me_ref, bf16[4,256,768]{2,1,0:T(8,128)(2,1)} %copy-done.2, bf16[4,256,768]{2,1,0:T(8,128)(2,1)} %collective-permute-done.3.far_ref, bf16[768,640]{1,0:T(8,128)(2,1)} %bitcast.50, bf16[768,576]{1,0:T(8,128)(2,1)} %select_convert_fusion.2.order_ref), custom_call_target="tpu_custom_call" | custom-call | flops 1811939328 | bytes 8000000 | tf_op jit(solution)/shard_map/project/pallas_call | solution.py:131
  68.4 28.8 %attend.1 = (bf16[8,192,256]{2,1,0:T(8,128)(2,1)}, f32[192,2048]{1,0:T(8,128)}, f32[8,2048]{1,0:T(8,128)}) custom-call(bf16[3,2048,192]{2,1,0:T(8,128)(2,1)} %project.1.q_ref.k_ref.v_ref.qkv_ref, bf16[3,2048,192]{2,1,0:T(8,128)(2,1)} %project.1.q_ref.k_ref.v_ref.qkv_ref, bf16[3,2048,192]{2,1,0:T(8,128)(2,1)} %project.1.q_ref.k_ref.v_ref.qkv_ref), custom_call_target="tpu_custom_call" | custom-call | flops 3221225472 | bytes 8000000 | tf_op jit(solution)/shard_map/attend/pallas_call | solution.py:218
  97.1 3.7 %all-to-all-start.1 = ((bf16[8,192,256]{2,1,0:T(8,128)(2,1)}), bf16[8,192,256]{2,1,0:T(8,128)(2,1)S(1)}, u32[]{:S(2)}, u32[]{:S(2)}) async-start(bf16[8,192,256]{2,1,0:T(8,128)(2,1)} %get-tuple-element.78), calls=%async_computation.1 | async-start | bytes 1572864 | tf_op jit(solution)/shard_map/all_to_all | solution.py:954
  101.5 10.8 %all-to-all-done.1.mix_ref = bf16[8,192,256]{2,1,0:T(8,128)(2,1)S(1)} async-done(((bf16[8,192,256]{2,1,0:T(8,128)(2,1)}), bf16[8,192,256]{2,1,0:T(8,128)(2,1)S(1)}, u32[]{:S(2)}, u32[]{:S(2)}) %all-to-all-start.1) | async-done | bytes 786464 | tf_op jit(solution)/shard_map/all_to_all | solution.py:954
  113.2 21.6 %middle.1 = (bf16[512,768]{1,0:T(8,128)(2,1)}, f32[512,768]{1,0:T(8,128)}, bf16[8,192,256]{2,1,0:T(8,128)(2,1)}, bf16[512,768]{1,0:T(8,128)(2,1)}, bf16[4,512,76...) custom-call(bf16[512,768]{1,0:T(8,128)(2,1)} %bitcast.58, ...), custom_call_target="tpu_custom_call" | custom-call | flops 10871635968 | bytes 30000000 | tf_op jit(solution)/shard_map/middle/pallas_call | solution.py:460
  134.8 9.4 %weights_send.1 = bf16[2,768,1792]{2,1,0:T(8,128)(2,1)} custom-call(s32[3]{0:T(128)} %add_add_fusion.1.index_ref, bf16[512,768]{1,0:T(8,128)(2,1)} %get-tuple-element.82.n2_ref, bf16[512,768]{1,0:T(8,128)(2,1)} %bitcast.56, bf16[512,768]{1,0:T(8,128)(2,1)} %get-tuple-element.83.gb_ref, bf16[2,4,192,256]{3,2,1,0:T(8,128)(2,1)} %bitcast.53, ...), custom_call_target="tpu_custom_call" | custom-call | flops 2818572288 | bytes 12000000 | tf_op jit(solution)/shard_map/weights_send/pallas_call | solution.py:594
  144.8 3.8 %all-to-all-start.2 = ((bf16[8,192,256]{2,1,0:T(8,128)(2,1)}), bf16[8,192,256]{2,1,0:T(8,128)(2,1)S(1)}, u32[]{:S(2)}, u32[]{:S(2)}) async-start(bf16[8,192,256]{2,1,0:T(8,128)(2,1)} %get-tuple-element.91), calls=%async_computation.2 | async-start | bytes 1572864 | tf_op jit(solution)/shard_map/all_to_all | solution.py:961
  148.6 5.0 %collective-permute-done.4.rest_0_ = bf16[2,768,1792]{2,1,0:T(8,128)(2,1)} collective-permute-done((bf16[2,768,1792]{2,1,0:T(8,128)(2,1)}, bf16[2,768,1792]{2,1,0:T(8,128)(2,1)}, u32[]{:S(2)}, u32[]{:S(2)}) %collective-permute-start.4) | collective-permute-done | bytes 5505056 | tf_op jit(solution)/shard_map/ppermute | solution.py:922
  153.6 11.4 %weights_keep.1 = (bf16[2,4,96,896]{3,2,1,0:T(8,128)(2,1)}, bf16[2,4,96,896]{3,2,1,0:T(8,128)(2,1)}, bf16[2,4,96,896]{3,2,1,0:T(8,128)(2,1)}, bf16[2,4,96,896]{3,2,1,0:T(8,128)(2,1)}) custom-call(s32[3]{0:T(128)} %add_add_fusion.index_ref, bf16[512,768]{1,0:T(8,128)(2,1)} %get-tuple-element.82.n2_ref, bf16[512,768]{1,0:T(8,128)(2,1)} %bitcast.57, ...), custom_call_target="tpu_custom_call" | custom-call | flops 2818572288 | bytes 12000000 | tf_op jit(solution)/shard_map/weights_keep/pallas_call | solution.py:594
  167.9 32.1 %attend_back.1.grad_ref = bf16[3,2048,192]{2,1,0:T(8,128)(2,1)} custom-call(bf16[3,2048,192]{2,1,0:T(8,128)(2,1)} %project.1.q_ref.k_ref.v_ref.qkv_ref, bf16[8,192,256]{2,1,0:T(8,128)(2,1)} %copy-done.7, f32[192,2048]{1,0:T(8,128)} %get-tuple-element.92.ot_ref, f32[8,2048]{1,0:T(8,128)} %get-tuple-element.93.level_ref), custom_call_target="tpu_custom_call" | custom-call | flops 8053063680 | bytes 10000000 | tf_op jit(solution)/shard_map/attend_back/pallas_call | solution.py:339
  200.0 2.8 fusion
  202.8 1.5 collective-permute-start.7
  204.8 14.3 %project_back.1 = (f32[4,256,768]{2,1,0:T(8,128)}, bf16[4,256,768]{2,1,0:T(8,128)(2,1)}, bf16[768,640]{1,0:T(8,128)(2,1)}) custom-call(s32[2]{0:T(128)} %pad_add_fusion.me_ref, bf16[4,256,768]{2,1,0:T(8,128)(2,1)} %copy-done.2, bf16[4,256,768]{2,1,0:T(8,128)(2,1)} %collective-permute-done.3.far_ref, bf16[3,2048,192]{2,1,0:T(8,128)(2,1)} %attend_back.1.grad_ref, ...), custom_call_target="tpu_custom_call" | custom-call | flops 3623878656 | bytes 15000000 | tf_op jit(solution)/shard_map/project_back/pallas_call | solution.py:769
  222.0 3.8 %all-to-all-start.3 = ((bf16[8,96,640]{2,1,0:T(8,128)(2,1)}), bf16[8,96,640]{2,1,0:T(8,128)(2,1)S(1)}, u32[]{:S(2)}, u32[]{:S(2)}) async-start(bf16[8,96,640]{2,1,0:T(8,128)(2,1)} %bitcast.62), calls=%async_computation.3 | async-start | bytes 1966080 | tf_op jit(solution)/shard_map/all_to_all | solution.py:988
  225.8 3.4 %wide_sum.1 = (bf16[2,96,896]{2,1,0:T(8,128)(2,1)}, bf16[2,96,896]{2,1,0:T(8,128)(2,1)}, bf16[2,96,896]{2,1,0:T(8,128)(2,1)}, bf16[2,96,896]{2,1,0:T(8,128)(2,1)}) custom-call(s32[1]{0:T(128)} %bitcast.30.place_ref, bf16[2,4,96,896]{3,2,1,0:T(8,128)(2,1)} %get-tuple-element.88.refs_0_, bf16[2,4,96,896]{3,2,1,0:T(8,128)(2,1)} %collective-permute-done.5.refs_1_, ...), custom_call_target="tpu_custom_call" | custom-call | bytes 4000000 | tf_op jit(solution)/shard_map/wide_sum/pallas_call | solution.py:626
  229.2 3.5 %collective-permute-start.11 = (bf16[2,96,896]{2,1,0:T(8,128)(2,1)}, bf16[2,96,896]{2,1,0:T(8,128)(2,1)S(1)}, u32[]{:S(2)}, u32[]{:S(2)}) collective-permute-start(bf16[2,96,896]{2,1,0:T(8,128)(2,1)} %get-tuple-element.111), channel_id=1, source_target_pairs={{0,24},{8,16},{16,8},{24,0},{1,25},{9,17},{17,9},{25,1},{2,26},{10... | collective-permute-start | bytes 1032200 | tf_op jit(solution)/shard_map/ppermute | solution.py:919
  233.8 4.5 %pair_sum.1 = (f32[256,768]{1,0:T(8,128)}, bf16[256,768]{1,0:T(8,128)(2,1)}, bf16[256,768]{1,0:T(8,128)(2,1)}, bf16[256,768]{1,0:T(8,128)(2,1)}) custom-call(f32[4,256,768]{2,1,0:T(8,128)} %get-tuple-element.112.keep_ref, bf16[4,256,768]{2,1,0:T(8,128)(2,1)} %copy-done.6), custom_call_target="tpu_custom_call" | custom-call | bytes 7000000 | tf_op jit(solution)/shard_map/pair_sum/pallas_call | solution.py:824
  241.8 12.7 %collective-permute-done.11.refs_4_ = bf16[2,96,896]{2,1,0:T(8,128)(2,1)S(1)} collective-permute-done((bf16[2,96,896]{2,1,0:T(8,128)(2,1)}, bf16[2,96,896]{2,1,0:T(8,128)(2,1)S(1)}, u32[]{:S(2)}, u32[]{:S(2)}) %collective-permute-start.11) | collective-permute-done | bytes 344096 | tf_op jit(solution)/shard_map/ppermute | solution.py:919
  254.5 4.2 %all-to-all-done.3.g_ref = bf16[8,96,640]{2,1,0:T(8,128)(2,1)S(1)} async-done(((bf16[8,96,640]{2,1,0:T(8,128)(2,1)}), bf16[8,96,640]{2,1,0:T(8,128)(2,1)S(1)}, u32[]{:S(2)}, u32[]{:S(2)}) %all-to-all-start.3) | async-done | bytes 983072 | tf_op jit(solution)/shard_map/all_to_all | solution.py:988
  259.6 2.1 finish_narrow.1
  262.3 7.6 %collective-permute-start.18 = (bf16[1,96,896]{2,1,0:T(8,128)(2,1)S(1)}, bf16[1,96,896]{2,1,0:T(8,128)(2,1)S(1)}, u32[]{:S(2)}, u32[]{:S(2)}) collective-permute-start(bf16[1,96,896]{2,1,0:T(8,128)(2,1)S(1)} %add_convert_fusion.2), channel_id=1, source_target_pairs={{0,8},{8,0},{16,24},{24,16},{1,9},{9,1},{17,25},{25,17},{2,10},{10... | collective-permute-start | bytes 516104 | tf_op jit(solution)/shard_map/ppermute | solution.py:919
  271.8 2.3 collective-permute-start.17
  275.6 4.5 %finish_rows.1 = f32[2,256,768]{2,1,0:T(8,128)} custom-call(s32[1]{0:T(128)} %bitcast.3.side_ref, bf16[2,256,768]{2,1,0:T(8,128)(2,1)} %bitcast.59, f32[256,768]{1,0:T(8,128)} %get-tuple-element.115.near_ref, bf16[256,768]{1,0:T(8,128)(2,1)} %copy-done.14, bf16[256,768]{1,0:T(8,128)(2,1)} %copy-done.15, bf16[256,768]{1,0:T(8,128)(2,1)} %copy-done.16, ...), custom_call_target="tpu_custom_call" | custom-call | bytes 6000000 | tf_op jit(solution)/shard_map/finish_rows/pallas_call | solution.py:855
  281.4 2.3 finish_wide.1
  (85 shorter events, 27.3 us)
Async XLA Ops:
  7.2 105.1 %all-gather.2.cloned.1.call-start = ((), (), s32[]{:S(2)}) async-start(), calls=%async_computation.4 | async-start | bytes 11354112 | tf_op jit(solution)/shard_map/all_gather | solution.py:930
  10.9 14.7 %collective-permute-start.1 = (bf16[256,768]{1,0:T(8,128)(2,1)S(1)}, bf16[256,768]{1,0:T(8,128)(2,1)S(1)}, u32[]{:S(2)}, u32[]{:S(2)}) collective-permute-start(bf16[256,768]{1,0:T(8,128)(2,1)S(1)} %get-tuple-element.152), channel_id=1, source_target_pairs={{0,4},{1,5},{2,6},{3,7},{4,0},{5,1},{6,2},{7,3},{8,12},{9,13},{10,... | collective-permute-start | bytes 1179656 | tf_op jit(solution)/shard_map/ppermute | solution.py:922
  14.0 28.2 %collective-permute-start.2 = (bf16[256,768]{1,0:T(8,128)(2,1)S(1)}, bf16[256,768]{1,0:T(8,128)(2,1)}, u32[]{:S(2)}, u32[]{:S(2)}) collective-permute-start(bf16[256,768]{1,0:T(8,128)(2,1)S(1)} %get-tuple-element.152), channel_id=1, source_target_pairs={{0,6},{1,7},{2,4},{3,5},{4,2},{5,3},{6,0},{7,1},{8,14},{9,15},{10,... | collective-permute-start | bytes 1179656 | tf_op jit(solution)/shard_map/ppermute | solution.py:922
  15.5 26.7 %collective-permute-start = (bf16[256,768]{1,0:T(8,128)(2,1)S(1)}, bf16[256,768]{1,0:T(8,128)(2,1)S(1)}, u32[]{:S(2)}, u32[]{:S(2)}) collective-permute-start(bf16[256,768]{1,0:T(8,128)(2,1)S(1)} %get-tuple-element.151), channel_id=1, source_target_pairs={{0,2},{1,3},{2,0},{3,1},{4,6},{5,7},{6,4},{7,5},{8,10},{9,11},{10,... | collective-permute-start | bytes 1179656 | tf_op jit(solution)/shard_map/ppermute | solution.py:922
  15.5 41.0 %all-to-all-start = ((bf16[8,96,640]{2,1,0:T(8,128)(2,1)}), bf16[8,96,640]{2,1,0:T(8,128)(2,1)S(1)}, u32[]{:S(2)}, u32[]{:S(2)}) async-start(bf16[8,96,640]{2,1,0:T(8,128)(2,1)} %get-tuple-element.76), calls=%async_computation | async-start | bytes 1966080 | tf_op jit(solution)/shard_map/all_to_all | solution.py:942
  44.2 5.2 %copy-start.2 = (bf16[4,256,768]{2,1,0:T(8,128)(2,1)}, bf16[4,256,768]{2,1,0:T(8,128)(2,1)S(1)}, u32[]{:S(2)}) copy-start(bf16[4,256,768]{2,1,0:T(8,128)(2,1)S(1)} %pad_maximum_fusion.own_ref) | copy-start | bytes 4718596
  44.2 5.2 %collective-permute-start.3 = (bf16[4,256,768]{2,1,0:T(8,128)(2,1)S(1)}, bf16[4,256,768]{2,1,0:T(8,128)(2,1)}, u32[]{:S(2)}, u32[]{:S(2)}) collective-permute-start(bf16[4,256,768]{2,1,0:T(8,128)(2,1)S(1)} %pad_maximum_fusion.own_ref), channel_id=1, source_target_pairs={{0,1},{1,0},{2,3},{3,2},{4,5},{5,4},{6,7},{7,6},{8,9},{9,8},{10,11... | collective-permute-start | bytes 4718600 | tf_op jit(solution)/shard_map/ppermute | solution.py:922
  97.1 15.1 %all-to-all-start.1 = ((bf16[8,192,256]{2,1,0:T(8,128)(2,1)}), bf16[8,192,256]{2,1,0:T(8,128)(2,1)S(1)}, u32[]{:S(2)}, u32[]{:S(2)}) async-start(bf16[8,192,256]{2,1,0:T(8,128)(2,1)} %get-tuple-element.78), calls=%async_computation.1 | async-start | bytes 1572864 | tf_op jit(solution)/shard_map/all_to_all | solution.py:954
  144.2 9.4 %collective-permute-start.4 = (bf16[2,768,1792]{2,1,0:T(8,128)(2,1)}, bf16[2,768,1792]{2,1,0:T(8,128)(2,1)}, u32[]{:S(2)}, u32[]{:S(2)}) collective-permute-start(bf16[2,768,1792]{2,1,0:T(8,128)(2,1)} %weights_send.1), channel_id=1, source_target_pairs={{0,1},{1,0},{2,3},{3,2},{4,5},{5,4},{6,7},{7,6},{8,9},{9,8},{10,11... | collective-permute-start | bytes 16515080 | tf_op jit(solution)/shard_map/ppermute | solution.py:922
  144.8 22.2 %all-to-all-start.2 = ((bf16[8,192,256]{2,1,0:T(8,128)(2,1)}), bf16[8,192,256]{2,1,0:T(8,128)(2,1)S(1)}, u32[]{:S(2)}, u32[]{:S(2)}) async-start(bf16[8,192,256]{2,1,0:T(8,128)(2,1)} %get-tuple-element.91), calls=%async_computation.2 | async-start | bytes 1572864 | tf_op jit(solution)/shard_map/all_to_all | solution.py:961
  165.0 35.0 %collective-permute-start.5 = (bf16[2,4,96,896]{3,2,1,0:T(8,128)(2,1)}, bf16[2,4,96,896]{3,2,1,0:T(8,128)(2,1)}, u32[]{:S(2)}, u32[]{:S(2)}) collective-permute-start(bf16[2,4,96,896]{3,2,1,0:T(8,128)(2,1)} %get-tuple-element.89), channel_id=1, source_target_pairs={{0,2},{1,3},{2,0},{3,1},{4,6},{5,7},{6,4},{7,5},{8,10},{9,11},{10,... | collective-permute-start | bytes 4128776 | tf_op jit(solution)/shard_map/ppermute | solution.py:922
  166.4 33.5 %collective-permute-start.6 = (bf16[2,4,96,896]{3,2,1,0:T(8,128)(2,1)}, bf16[2,4,96,896]{3,2,1,0:T(8,128)(2,1)}, u32[]{:S(2)}, u32[]{:S(2)}) collective-permute-start(bf16[2,4,96,896]{3,2,1,0:T(8,128)(2,1)} %get-tuple-element.90), channel_id=1, source_target_pairs={{0,4},{1,5},{2,6},{3,7},{4,0},{5,1},{6,2},{7,3},{8,12},{9,13},{10,... | collective-permute-start | bytes 4128776 | tf_op jit(solution)/shard_map/ppermute | solution.py:922
  167.9 32.1 %copy-start.4 = (bf16[2,4,96,896]{3,2,1,0:T(8,128)(2,1)S(1)}, bf16[2,4,96,896]{3,2,1,0:T(8,128)(2,1)}, u32[]{:S(2)}) copy-start(bf16[2,4,96,896]{3,2,1,0:T(8,128)(2,1)} %get-tuple-element.88.refs_0_) | copy-start | bytes 4128772
  167.9 32.1 %copy-start.5 = (bf16[2,4,96,896]{3,2,1,0:T(8,128)(2,1)S(1)}, bf16[2,4,96,896]{3,2,1,0:T(8,128)(2,1)}, u32[]{:S(2)}) copy-start(bf16[2,4,96,896]{3,2,1,0:T(8,128)(2,1)} %get-tuple-element.95.refs_3_) | copy-start | bytes 4128772
  202.8 17.1 %collective-permute-start.7 = (bf16[4,96,896]{2,1,0:T(8,128)(2,1)}, bf16[4,96,896]{2,1,0:T(8,128)(2,1)S(1)}, u32[]{:S(2)}, u32[]{:S(2)}) collective-permute-start(bf16[4,96,896]{2,1,0:T(8,128)(2,1)} %get-tuple-element.98), channel_id=1, source_target_pairs={{0,4},{1,5},{2,6},{3,7},{4,0},{5,1},{6,2},{7,3},{8,12},{9,13},{10,... | collective-permute-start | bytes 2064392 | tf_op jit(solution)/shard_map/ppermute | solution.py:922
  204.3 16.8 %collective-permute-start.8 = (bf16[4,96,896]{2,1,0:T(8,128)(2,1)}, bf16[4,96,896]{2,1,0:T(8,128)(2,1)S(1)}, u32[]{:S(2)}, u32[]{:S(2)}) collective-permute-start(bf16[4,96,896]{2,1,0:T(8,128)(2,1)} %get-tuple-element.99), channel_id=1, source_target_pairs={{0,2},{1,3},{2,0},{3,1},{4,6},{5,7},{6,4},{7,5},{8,10},{9,11},{10,... | collective-permute-start | bytes 2064392 | tf_op jit(solution)/shard_map/ppermute | solution.py:922
  219.9 5.9 %copy-start.11 = (bf16[4,96,896]{2,1,0:T(8,128)(2,1)}, bf16[4,96,896]{2,1,0:T(8,128)(2,1)S(1)}, u32[]{:S(2)}) copy-start(bf16[4,96,896]{2,1,0:T(8,128)(2,1)S(1)} %collective-permute-done.7.refs_2_) | copy-start | bytes 2064388
  222.0 10.7 %collective-permute-start.9 = (bf16[4,256,768]{2,1,0:T(8,128)(2,1)}, bf16[4,256,768]{2,1,0:T(8,128)(2,1)S(1)}, u32[]{:S(2)}, u32[]{:S(2)}) collective-permute-start(bf16[4,256,768]{2,1,0:T(8,128)(2,1)} %get-tuple-element.109), channel_id=1, source_target_pairs={{0,1},{1,0},{2,3},{3,2},{4,5},{5,4},{6,7},{7,6},{8,9},{9,8},{10,11... | collective-permute-start | bytes 4718600 | tf_op jit(solution)/shard_map/ppermute | solution.py:922
  222.0 36.7 %all-to-all-start.3 = ((bf16[8,96,640]{2,1,0:T(8,128)(2,1)}), bf16[8,96,640]{2,1,0:T(8,128)(2,1)S(1)}, u32[]{:S(2)}, u32[]{:S(2)}) async-start(bf16[8,96,640]{2,1,0:T(8,128)(2,1)} %bitcast.62), calls=%async_computation.3 | async-start | bytes 1966080 | tf_op jit(solution)/shard_map/all_to_all | solution.py:988
  229.2 25.3 %collective-permute-start.11 = (bf16[2,96,896]{2,1,0:T(8,128)(2,1)}, bf16[2,96,896]{2,1,0:T(8,128)(2,1)S(1)}, u32[]{:S(2)}, u32[]{:S(2)}) collective-permute-start(bf16[2,96,896]{2,1,0:T(8,128)(2,1)} %get-tuple-element.111), channel_id=1, source_target_pairs={{0,24},{8,16},{16,8},{24,0},{1,25},{9,17},{17,9},{25,1},{2,26},{10... | collective-permute-start | bytes 1032200 | tf_op jit(solution)/shard_map/ppermute | solution.py:919
  232.7 1.1 copy-start.6
  232.7 29.6 %copy-start.9 = (bf16[2,96,896]{2,1,0:T(8,128)(2,1)S(1)}, bf16[2,96,896]{2,1,0:T(8,128)(2,1)}, u32[]{:S(2)}) copy-start(bf16[2,96,896]{2,1,0:T(8,128)(2,1)} %get-tuple-element.126.refs_3_) | copy-start | bytes 1032196
  232.7 26.7 %collective-permute-start.10 = (bf16[2,96,896]{2,1,0:T(8,128)(2,1)}, bf16[2,96,896]{2,1,0:T(8,128)(2,1)}, u32[]{:S(2)}, u32[]{:S(2)}) collective-permute-start(bf16[2,96,896]{2,1,0:T(8,128)(2,1)} %get-tuple-element.110), channel_id=1, source_target_pairs={{0,8},{8,0},{16,24},{24,16},{1,9},{9,1},{17,25},{25,17},{2,10},{10... | collective-permute-start | bytes 1032200 | tf_op jit(solution)/shard_map/ppermute | solution.py:919
  238.3 32.3 %copy-start.8 = (bf16[2,96,896]{2,1,0:T(8,128)(2,1)S(1)}, bf16[2,96,896]{2,1,0:T(8,128)(2,1)}, u32[]{:S(2)}) copy-start(bf16[2,96,896]{2,1,0:T(8,128)(2,1)} %get-tuple-element.124.refs_0_) | copy-start | bytes 1032196
  238.3 36.2 %collective-permute-start.12 = (bf16[256,768]{1,0:T(8,128)(2,1)}, bf16[256,768]{1,0:T(8,128)(2,1)S(1)}, u32[]{:S(2)}, u32[]{:S(2)}) collective-permute-start(bf16[256,768]{1,0:T(8,128)(2,1)} %get-tuple-element.116), channel_id=1, source_target_pairs={{0,2},{1,3},{2,0},{3,1},{4,6},{5,7},{6,4},{7,5},{8,10},{9,11},{10,... | collective-permute-start | bytes 1179656 | tf_op jit(solution)/shard_map/ppermute | solution.py:922
  238.9 35.7 %collective-permute-start.13 = (bf16[256,768]{1,0:T(8,128)(2,1)}, bf16[256,768]{1,0:T(8,128)(2,1)S(1)}, u32[]{:S(2)}, u32[]{:S(2)}) collective-permute-start(bf16[256,768]{1,0:T(8,128)(2,1)} %get-tuple-element.117), channel_id=1, source_target_pairs={{0,4},{1,5},{2,6},{3,7},{4,0},{5,1},{6,2},{7,3},{8,12},{9,13},{10,... | collective-permute-start | bytes 1179656 | tf_op jit(solution)/shard_map/ppermute | solution.py:922
  240.3 34.2 %collective-permute-start.14 = (bf16[256,768]{1,0:T(8,128)(2,1)}, bf16[256,768]{1,0:T(8,128)(2,1)S(1)}, u32[]{:S(2)}, u32[]{:S(2)}) collective-permute-start(bf16[256,768]{1,0:T(8,128)(2,1)} %get-tuple-element.118), channel_id=1, source_target_pairs={{0,6},{1,7},{2,4},{3,5},{4,2},{5,3},{6,0},{7,1},{8,14},{9,15},{10,... | collective-permute-start | bytes 1179656 | tf_op jit(solution)/shard_map/ppermute | solution.py:922
  254.5 25.8 %copy-start.10 = (bf16[2,96,896]{2,1,0:T(8,128)(2,1)}, bf16[2,96,896]{2,1,0:T(8,128)(2,1)S(1)}, u32[]{:S(2)}) copy-start(bf16[2,96,896]{2,1,0:T(8,128)(2,1)S(1)} %collective-permute-done.11.refs_4_) | copy-start | bytes 1032196
  261.7 8.2 %collective-permute-start.15 = (f32[8,96]{1,0:T(8,128)}, f32[8,96]{1,0:T(8,128)S(1)}, u32[]{:S(2)}, u32[]{:S(2)}) collective-permute-start(f32[8,96]{1,0:T(8,128)} %get-tuple-element.121), channel_id=1, source_target_pairs={{0,2},{1,3},{2,0},{3,1},{4,6},{5,7},{6,4},{7,5},{8,10},{9,11},{10,... | collective-permute-start | bytes 9224 | tf_op jit(solution)/shard_map/ppermute | solution.py:922
  262.3 17.7 %collective-permute-start.18 = (bf16[1,96,896]{2,1,0:T(8,128)(2,1)S(1)}, bf16[1,96,896]{2,1,0:T(8,128)(2,1)S(1)}, u32[]{:S(2)}, u32[]{:S(2)}) collective-permute-start(bf16[1,96,896]{2,1,0:T(8,128)(2,1)S(1)} %add_convert_fusion.2), channel_id=1, source_target_pairs={{0,8},{8,0},{16,24},{24,16},{1,9},{9,1},{17,25},{25,17},{2,10},{10... | collective-permute-start | bytes 516104 | tf_op jit(solution)/shard_map/ppermute | solution.py:919
  270.6 1.2 collective-permute-start.16
  271.8 8.6 %collective-permute-start.17 = (bf16[1,96,896]{2,1,0:T(8,128)(2,1)S(1)}, bf16[1,96,896]{2,1,0:T(8,128)(2,1)S(1)}, u32[]{:S(2)}, u32[]{:S(2)}) collective-permute-start(bf16[1,96,896]{2,1,0:T(8,128)(2,1)S(1)} %add_convert_fusion.3), channel_id=1, source_target_pairs={{0,24},{8,16},{16,8},{24,0},{1,25},{9,17},{17,9},{25,1},{2,26},{10... | collective-permute-start | bytes 516104 | tf_op jit(solution)/shard_map/ppermute | solution.py:919
  (11 other events, 9.3 us)
Sparse Core Ops, SparseCore 0:
  11.0 99.0 all-gather.1

commit v7 on v6

--- a/solution.py
+++ b/solution.py
@@ -995,26 +995,27 @@
     arrived = [swap(sends[n - 1], 2 * n) for n in range(1, group // 2)]
 
     if exchange:
-        grad_in, a_came, b_came, near = barrier((grad_in, a_came, b_came, near))
-    grad_qkv_weight, grad_qkv_bias, vec_in = finish_narrow(grad_in, width, qkv_bias.shape)
-    mask = parts // 2
-    while mask:
-        vec_in = vec_in + swap(vec_in, mask)
-        mask //= 2
-
-    if exchange:
-        a_last = swap_deep(plus(a_kept[1:], a_came[1:]), 3)
-        b_last = swap_deep(plus(b_kept[1:], b_came[1:]), 1)
+        a_came, b_came, near = barrier((a_came, b_came, near))
+        a_send, b_send = plus(a_kept[1:], a_came[1:]), plus(b_kept[1:], b_came[1:])
+        a_send, b_send, grad_in = barrier((a_send, b_send, grad_in))
+        a_last, b_last = swap_deep(a_send, 3), swap_deep(b_send, 1)
         wide_parts = [a_kept, a_came, a_last, b_kept, b_came, b_last]
     else:
         cut = wide.shape[1] // 2
         wide_parts = [grad_wide[None, :, :cut], grad_wide[None, :, cut:]]
+    grad_qkv_weight, grad_qkv_bias, vec_in = finish_narrow(grad_in, width, qkv_bias.shape)
+    vec_came = swap(vec_in, 2)
     grad_tokens = finish_rows(
         side_array, tok, near, *arrived, grad_hidden.reshape(micro, rows, d), w_in
     )
+    vec_came, grad_tokens = barrier((vec_came, grad_tokens))
+    vec_in = vec_in + vec_came
+    vec_came = swap(vec_in, 1)
     fc_grad, proj_grad, out_grad, gain2, shift2, out_b, proj_b, fc_b = finish_wide(
         wide_parts, d, width, fc_bias.shape
     )
+    vec_came, fc_grad = barrier((vec_came, fc_grad))
+    vec_in = vec_in + vec_came
     return (
         y.reshape(micro, 1, rows, d),
         grad_tokens[:, None],

time: 293 us -> 293 us (level)
    all_to_all x1, waiting for transfers between devices: 4.16 us -> 0.01 us  [local(): lax.all_to_all(grad_in.reshape(narrow.shape), ('dp', 'ctx'), 0, 0, tiled=...]
    ppermute x4, waiting for transfers between devices: 13.7 us -> 17.6 us  [swap_deep(): return lax.ppermute(array, 'dp', [(n, n ^ mask) for n in range(depth)])]
    unnamed x38 -> x42, local copies, waits for them, and re-layouts: 7.78 us -> 7.78 us
  transfers between devices with their start and end apart: 24 -> 24, of which waited for: 12 -> 9; matrix products, arithmetic and copies ran while one was open for 4% -> 3% of each run, Pallas kernels for 38% -> 39%
where the time goes in v7:
time: 293 us; the launch traced here: 292 us
  Pallas kernels  148 us (51%)
  waiting for transfers between devices  62.8 us (21%)
  starting transfers between devices  46.5 us (16%)
  between operations  14.4 us (5%)
  other arithmetic  11.4 us (4%)
  local copies, waits for them, and re-layouts  9.5 us (3%)
    pallas_call x1, Pallas kernels, attend_back(): pl.pallas_call(attend_back_kernel, out_shape=jax.ShapeDtypeStruct(triple....  32.1 us
    pallas_call x1, Pallas kernels, attend(): pl.pallas_call(attend_kernel, out_shape=(jax.ShapeDtypeStruct((span // ro...  28.7 us
    ppermute x15, waiting for transfers between devices, swap(): lax.ppermute(array, ('ctx', 'tp'), [(n, n ^ mask) for n in range(group)])  27.3 us
    pallas_call x1, Pallas kernels, middle(): pl.pallas_call(functools.partial(middle_kernel, strip), out_shape=(sds((r...  21.6 us
    pallas_call x2, Pallas kernels, weights(): pl.pallas_call(functools.partial(weights_kernel, mode, strip), out_shape=...  20.7 us
    ppermute x4, waiting for transfers between devices, swap_deep(): return lax.ppermute(array, 'dp', [(n, n ^ mask) for n in range(depth)])  17.6 us
    ppermute x4, starting transfers between devices, swap_deep(): return lax.ppermute(array, 'dp', [(n, n ^ mask) for n in range(depth)])  16.1 us
    pallas_call x1, Pallas kernels, project_back(): pl.pallas_call(functools.partial(project_back_kernel, piece), out_shape=(...  14.3 us
  transfers between devices with their start and end apart: 24, of which 9 were waited for; matrix products, arithmetic and copies ran while one was open for 3% of the time, Pallas kernels for 39%

profile of v7, /device:TPU:0, one launch (start us, length us, event | category | flops | bytes accessed | tf_op | source)
XLA Modules:
  0.0 292.1 jit_solution(6111142567677516593)
XLA Ops:
  7.2 2.5 pack.1
  10.9 3.0 %collective-permute-start.1 = (bf16[256,768]{1,0:T(8,128)(2,1)S(1)}, bf16[256,768]{1,0:T(8,128)(2,1)S(1)}, u32[]{:S(2)}, u32[]{:S(2)}) collective-permute-start(bf16[256,768]{1,0:T(8,128)(2,1)S(1)} %get-tuple-element.164), channel_id=1, source_target_pairs={{0,4},{1,5},{2,6},{3,7},{4,0},{5,1},{6,2},{7,3},{8,12},{9,13},{10,... | collective-permute-start | bytes 1179656 | tf_op jit(solution)/shard_map/ppermute | solution.py:922
  14.0 1.5 collective-permute-start.2
  15.5 6.3 %all-to-all-start = ((bf16[8,96,640]{2,1,0:T(8,128)(2,1)}), bf16[8,96,640]{2,1,0:T(8,128)(2,1)S(1)}, u32[]{:S(2)}, u32[]{:S(2)}) async-start(bf16[8,96,640]{2,1,0:T(8,128)(2,1)} %get-tuple-element.82), calls=%async_computation | async-start | bytes 1966080 | tf_op jit(solution)/shard_map/all_to_all | solution.py:942
  21.8 3.9 %collective-permute-done.1 = bf16[256,768]{1,0:T(8,128)(2,1)S(1)} collective-permute-done((bf16[256,768]{1,0:T(8,128)(2,1)S(1)}, bf16[256,768]{1,0:T(8,128)(2,1)S(1)}, u32[]{:S(2)}, u32[]{:S(2)}) %collective-permute-start.1) | collective-permute-done | bytes 393248 | tf_op jit(solution)/shard_map/ppermute | solution.py:922
  25.7 16.4 %collective-permute-done.2 = bf16[256,768]{1,0:T(8,128)(2,1)S(1)} collective-permute-done((bf16[256,768]{1,0:T(8,128)(2,1)S(1)}, bf16[256,768]{1,0:T(8,128)(2,1)S(1)}, u32[]{:S(2)}, u32[]{:S(2)}) %collective-permute-start.2) | collective-permute-done | bytes 393248 | tf_op jit(solution)/shard_map/ppermute | solution.py:922
  49.4 7.1 %all-to-all-done = bf16[8,96,640]{2,1,0:T(8,128)(2,1)S(1)} async-done(((bf16[8,96,640]{2,1,0:T(8,128)(2,1)}), bf16[8,96,640]{2,1,0:T(8,128)(2,1)S(1)}, u32[]{:S(2)}, u32[]{:S(2)}) %all-to-all-start) | async-done | bytes 983072 | tf_op jit(solution)/shard_map/all_to_all | solution.py:942
  57.5 10.9 %project.1.q_ref.k_ref.v_ref.qkv_ref = bf16[3,2048,192]{2,1,0:T(8,128)(2,1)} custom-call(s32[2]{0:T(128)} %pad_add_fusion.me_ref, bf16[4,256,768]{2,1,0:T(8,128)(2,1)} %copy-done.2, bf16[4,256,768]{2,1,0:T(8,128)(2,1)} %collective-permute-done.3.far_ref, bf16[768,640]{1,0:T(8,128)(2,1)} %bitcast.50, bf16[768,576]{1,0:T(8,128)(2,1)} %select_convert_fusion.2.order_ref), custom_call_target="tpu_custom_call" | custom-call | flops 1811939328 | bytes 8000000 | tf_op jit(solution)/shard_map/project/pallas_call | solution.py:131
  68.4 28.7 %attend.1 = (bf16[8,192,256]{2,1,0:T(8,128)(2,1)}, f32[192,2048]{1,0:T(8,128)}, f32[8,2048]{1,0:T(8,128)}) custom-call(bf16[3,2048,192]{2,1,0:T(8,128)(2,1)} %project.1.q_ref.k_ref.v_ref.qkv_ref, bf16[3,2048,192]{2,1,0:T(8,128)(2,1)} %project.1.q_ref.k_ref.v_ref.qkv_ref, bf16[3,2048,192]{2,1,0:T(8,128)(2,1)} %project.1.q_ref.k_ref.v_ref.qkv_ref), custom_call_target="tpu_custom_call" | custom-call | flops 3221225472 | bytes 8000000 | tf_op jit(solution)/shard_map/attend/pallas_call | solution.py:218
  97.1 3.7 %all-to-all-start.1 = ((bf16[8,192,256]{2,1,0:T(8,128)(2,1)}), bf16[8,192,256]{2,1,0:T(8,128)(2,1)S(1)}, u32[]{:S(2)}, u32[]{:S(2)}) async-start(bf16[8,192,256]{2,1,0:T(8,128)(2,1)} %get-tuple-element.84), calls=%async_computation.1 | async-start | bytes 1572864 | tf_op jit(solution)/shard_map/all_to_all | solution.py:954
  101.5 10.8 %all-to-all-done.1.mix_ref = bf16[8,192,256]{2,1,0:T(8,128)(2,1)S(1)} async-done(((bf16[8,192,256]{2,1,0:T(8,128)(2,1)}), bf16[8,192,256]{2,1,0:T(8,128)(2,1)S(1)}, u32[]{:S(2)}, u32[]{:S(2)}) %all-to-all-start.1) | async-done | bytes 786464 | tf_op jit(solution)/shard_map/all_to_all | solution.py:954
  113.2 21.6 %middle.1 = (bf16[512,768]{1,0:T(8,128)(2,1)}, f32[512,768]{1,0:T(8,128)}, bf16[8,192,256]{2,1,0:T(8,128)(2,1)}, bf16[512,768]{1,0:T(8,128)(2,1)}, bf16[4,512,76...) custom-call(bf16[512,768]{1,0:T(8,128)(2,1)} %bitcast.58, ...), custom_call_target="tpu_custom_call" | custom-call | flops 10871635968 | bytes 30000000 | tf_op jit(solution)/shard_map/middle/pallas_call | solution.py:460
  134.8 9.4 %weights_send.1 = bf16[2,768,1792]{2,1,0:T(8,128)(2,1)} custom-call(s32[3]{0:T(128)} %add_add_fusion.1.index_ref, bf16[512,768]{1,0:T(8,128)(2,1)} %get-tuple-element.88.n2_ref, bf16[512,768]{1,0:T(8,128)(2,1)} %bitcast.56, bf16[512,768]{1,0:T(8,128)(2,1)} %get-tuple-element.89.gb_ref, bf16[2,4,192,256]{3,2,1,0:T(8,128)(2,1)} %bitcast.53, ...), custom_call_target="tpu_custom_call" | custom-call | flops 2818572288 | bytes 12000000 | tf_op jit(solution)/shard_map/weights_send/pallas_call | solution.py:594
  144.8 3.8 %all-to-all-start.2 = ((bf16[8,192,256]{2,1,0:T(8,128)(2,1)}), bf16[8,192,256]{2,1,0:T(8,128)(2,1)S(1)}, u32[]{:S(2)}, u32[]{:S(2)}) async-start(bf16[8,192,256]{2,1,0:T(8,128)(2,1)} %get-tuple-element.97), calls=%async_computation.2 | async-start | bytes 1572864 | tf_op jit(solution)/shard_map/all_to_all | solution.py:961
  148.5 5.0 %collective-permute-done.4.rest_0_ = bf16[2,768,1792]{2,1,0:T(8,128)(2,1)} collective-permute-done((bf16[2,768,1792]{2,1,0:T(8,128)(2,1)}, bf16[2,768,1792]{2,1,0:T(8,128)(2,1)}, u32[]{:S(2)}, u32[]{:S(2)}) %collective-permute-start.4) | collective-permute-done | bytes 5505056 | tf_op jit(solution)/shard_map/ppermute | solution.py:922
  153.5 11.4 %weights_keep.1 = (bf16[2,4,96,896]{3,2,1,0:T(8,128)(2,1)}, bf16[2,4,96,896]{3,2,1,0:T(8,128)(2,1)}, bf16[2,4,96,896]{3,2,1,0:T(8,128)(2,1)}, bf16[2,4,96,896]{3,2,1,0:T(8,128)(2,1)}) custom-call(s32[3]{0:T(128)} %add_add_fusion.index_ref, bf16[512,768]{1,0:T(8,128)(2,1)} %get-tuple-element.88.n2_ref, bf16[512,768]{1,0:T(8,128)(2,1)} %bitcast.57, ...), custom_call_target="tpu_custom_call" | custom-call | flops 2818572288 | bytes 12000000 | tf_op jit(solution)/shard_map/weights_keep/pallas_call | solution.py:594
  164.9 1.5 collective-permute-start.5
  167.8 32.1 %attend_back.1.grad_ref = bf16[3,2048,192]{2,1,0:T(8,128)(2,1)} custom-call(bf16[3,2048,192]{2,1,0:T(8,128)(2,1)} %project.1.q_ref.k_ref.v_ref.qkv_ref, bf16[8,192,256]{2,1,0:T(8,128)(2,1)} %copy-done.7, f32[192,2048]{1,0:T(8,128)} %get-tuple-element.98.ot_ref, f32[8,2048]{1,0:T(8,128)} %get-tuple-element.99.level_ref), custom_call_target="tpu_custom_call" | custom-call | flops 8053063680 | bytes 10000000 | tf_op jit(solution)/shard_map/attend_back/pallas_call | solution.py:339
  199.9 2.8 fusion
  202.7 1.5 collective-permute-start.7
  204.8 14.3 %project_back.1 = (f32[4,256,768]{2,1,0:T(8,128)}, bf16[4,256,768]{2,1,0:T(8,128)(2,1)}, bf16[768,640]{1,0:T(8,128)(2,1)}) custom-call(s32[2]{0:T(128)} %pad_add_fusion.me_ref, bf16[4,256,768]{2,1,0:T(8,128)(2,1)} %copy-done.2, bf16[4,256,768]{2,1,0:T(8,128)(2,1)} %collective-permute-done.3.far_ref, bf16[3,2048,192]{2,1,0:T(8,128)(2,1)} %attend_back.1.grad_ref, ...), custom_call_target="tpu_custom_call" | custom-call | flops 3623878656 | bytes 15000000 | tf_op jit(solution)/shard_map/project_back/pallas_call | solution.py:769
  221.9 3.8 %all-to-all-start.3 = ((bf16[8,96,640]{2,1,0:T(8,128)(2,1)}), bf16[8,96,640]{2,1,0:T(8,128)(2,1)S(1)}, u32[]{:S(2)}, u32[]{:S(2)}) async-start(bf16[8,96,640]{2,1,0:T(8,128)(2,1)} %bitcast.62), calls=%async_computation.3 | async-start | bytes 1966080 | tf_op jit(solution)/shard_map/all_to_all | solution.py:988
  225.8 3.4 %wide_sum.1 = (bf16[2,96,896]{2,1,0:T(8,128)(2,1)}, bf16[2,96,896]{2,1,0:T(8,128)(2,1)}, bf16[2,96,896]{2,1,0:T(8,128)(2,1)}, bf16[2,96,896]{2,1,0:T(8,128)(2,1)}) custom-call(s32[1]{0:T(128)} %bitcast.21.place_ref, bf16[2,4,96,896]{3,2,1,0:T(8,128)(2,1)} %get-tuple-element.94.refs_0_, bf16[2,4,96,896]{3,2,1,0:T(8,128)(2,1)} %collective-permute-done.5.refs_1_, ...), custom_call_target="tpu_custom_call" | custom-call | bytes 4000000 | tf_op jit(solution)/shard_map/wide_sum/pallas_call | solution.py:626
  229.2 3.5 %collective-permute-start.11 = (bf16[2,96,896]{2,1,0:T(8,128)(2,1)}, bf16[2,96,896]{2,1,0:T(8,128)(2,1)S(1)}, u32[]{:S(2)}, u32[]{:S(2)}) collective-permute-start(bf16[2,96,896]{2,1,0:T(8,128)(2,1)} %get-tuple-element.117), channel_id=1, source_target_pairs={{0,24},{8,16},{16,8},{24,0},{1,25},{9,17},{17,9},{25,1},{2,26},{10... | collective-permute-start | bytes 1032200 | tf_op jit(solution)/shard_map/ppermute | solution.py:919
  233.8 4.5 %pair_sum.1 = (f32[256,768]{1,0:T(8,128)}, bf16[256,768]{1,0:T(8,128)(2,1)}, bf16[256,768]{1,0:T(8,128)(2,1)}, bf16[256,768]{1,0:T(8,128)(2,1)}) custom-call(f32[4,256,768]{2,1,0:T(8,128)} %get-tuple-element.118.keep_ref, bf16[4,256,768]{2,1,0:T(8,128)(2,1)} %copy-done.6), custom_call_target="tpu_custom_call" | custom-call | bytes 7000000 | tf_op jit(solution)/shard_map/pair_sum/pallas_call | solution.py:824
  241.7 12.7 %collective-permute-done.11.refs_4_ = bf16[2,96,896]{2,1,0:T(8,128)(2,1)S(1)} collective-permute-done((bf16[2,96,896]{2,1,0:T(8,128)(2,1)}, bf16[2,96,896]{2,1,0:T(8,128)(2,1)S(1)}, u32[]{:S(2)}, u32[]{:S(2)}) %collective-permute-start.11) | collective-permute-done | bytes 344096 | tf_op jit(solution)/shard_map/ppermute | solution.py:919
  254.5 4.9 %collective-permute-done.10.refs_1_ = bf16[2,96,896]{2,1,0:T(8,128)(2,1)} collective-permute-done((bf16[2,96,896]{2,1,0:T(8,128)(2,1)}, bf16[2,96,896]{2,1,0:T(8,128)(2,1)}, u32[]{:S(2)}, u32[]{:S(2)}) %collective-permute-start.10) | collective-permute-done | bytes 344096 | tf_op jit(solution)/shard_map/ppermute | solution.py:919
  260.4 2.4 collective-permute-start.17
  262.9 10.1 %collective-permute-start.18 = (bf16[1,96,896]{2,1,0:T(8,128)(2,1)S(1)}, bf16[1,96,896]{2,1,0:T(8,128)(2,1)S(1)}, u32[]{:S(2)}, u32[]{:S(2)}) collective-permute-start(bf16[1,96,896]{2,1,0:T(8,128)(2,1)S(1)} %add_convert_fusion.2), channel_id=1, source_target_pairs={{0,8},{8,0},{16,24},{24,16},{1,9},{9,1},{17,25},{25,17},{2,10},{10... | collective-permute-start | bytes 516104 | tf_op jit(solution)/shard_map/ppermute | solution.py:919
  273.0 2.1 finish_narrow.1
  276.5 4.5 %finish_rows.1 = f32[2,256,768]{2,1,0:T(8,128)} custom-call(s32[1]{0:T(128)} %bitcast.3.side_ref, bf16[2,256,768]{2,1,0:T(8,128)(2,1)} %bitcast.59, f32[256,768]{1,0:T(8,128)} %get-tuple-element.127.near_ref, bf16[256,768]{1,0:T(8,128)(2,1)} %copy-done.15, bf16[256,768]{1,0:T(8,128)(2,1)} %copy-done.16, bf16[256,768]{1,0:T(8,128)(2,1)} %copy-done.17, ...), custom_call_target="tpu_custom_call" | custom-call | bytes 6000000 | tf_op jit(solution)/shard_map/finish_rows/pallas_call | solution.py:855
  282.4 2.3 finish_wide.1
  (89 shorter events, 25.5 us)
Async XLA Ops:
  7.2 105.1 %all-gather.2.cloned.1.call-start = ((), (), s32[]{:S(2)}) async-start(), calls=%async_computation.4 | async-start | bytes 11354112 | tf_op jit(solution)/shard_map/all_gather | solution.py:930
  10.9 14.7 %collective-permute-start.1 = (bf16[256,768]{1,0:T(8,128)(2,1)S(1)}, bf16[256,768]{1,0:T(8,128)(2,1)S(1)}, u32[]{:S(2)}, u32[]{:S(2)}) collective-permute-start(bf16[256,768]{1,0:T(8,128)(2,1)S(1)} %get-tuple-element.164), channel_id=1, source_target_pairs={{0,4},{1,5},{2,6},{3,7},{4,0},{5,1},{6,2},{7,3},{8,12},{9,13},{10,... | collective-permute-start | bytes 1179656 | tf_op jit(solution)/shard_map/ppermute | solution.py:922
  14.0 28.1 %collective-permute-start.2 = (bf16[256,768]{1,0:T(8,128)(2,1)S(1)}, bf16[256,768]{1,0:T(8,128)(2,1)S(1)}, u32[]{:S(2)}, u32[]{:S(2)}) collective-permute-start(bf16[256,768]{1,0:T(8,128)(2,1)S(1)} %get-tuple-element.164), channel_id=1, source_target_pairs={{0,6},{1,7},{2,4},{3,5},{4,2},{5,3},{6,0},{7,1},{8,14},{9,15},{10,... | collective-permute-start | bytes 1179656 | tf_op jit(solution)/shard_map/ppermute | solution.py:922
  15.5 26.6 %collective-permute-start = (bf16[256,768]{1,0:T(8,128)(2,1)S(1)}, bf16[256,768]{1,0:T(8,128)(2,1)S(1)}, u32[]{:S(2)}, u32[]{:S(2)}) collective-permute-start(bf16[256,768]{1,0:T(8,128)(2,1)S(1)} %get-tuple-element.163), channel_id=1, source_target_pairs={{0,2},{1,3},{2,0},{3,1},{4,6},{5,7},{6,4},{7,5},{8,10},{9,11},{10,... | collective-permute-start | bytes 1179656 | tf_op jit(solution)/shard_map/ppermute | solution.py:922
  15.5 41.0 %all-to-all-start = ((bf16[8,96,640]{2,1,0:T(8,128)(2,1)}), bf16[8,96,640]{2,1,0:T(8,128)(2,1)S(1)}, u32[]{:S(2)}, u32[]{:S(2)}) async-start(bf16[8,96,640]{2,1,0:T(8,128)(2,1)} %get-tuple-element.82), calls=%async_computation | async-start | bytes 1966080 | tf_op jit(solution)/shard_map/all_to_all | solution.py:942
  44.2 5.2 %copy-start.2 = (bf16[4,256,768]{2,1,0:T(8,128)(2,1)}, bf16[4,256,768]{2,1,0:T(8,128)(2,1)S(1)}, u32[]{:S(2)}) copy-start(bf16[4,256,768]{2,1,0:T(8,128)(2,1)S(1)} %pad_maximum_fusion.own_ref) | copy-start | bytes 4718596
  44.2 5.2 %collective-permute-start.3 = (bf16[4,256,768]{2,1,0:T(8,128)(2,1)S(1)}, bf16[4,256,768]{2,1,0:T(8,128)(2,1)}, u32[]{:S(2)}, u32[]{:S(2)}) collective-permute-start(bf16[4,256,768]{2,1,0:T(8,128)(2,1)S(1)} %pad_maximum_fusion.own_ref), channel_id=1, source_target_pairs={{0,1},{1,0},{2,3},{3,2},{4,5},{5,4},{6,7},{7,6},{8,9},{9,8},{10,11... | collective-permute-start | bytes 4718600 | tf_op jit(solution)/shard_map/ppermute | solution.py:922
  97.1 15.1 %all-to-all-start.1 = ((bf16[8,192,256]{2,1,0:T(8,128)(2,1)}), bf16[8,192,256]{2,1,0:T(8,128)(2,1)S(1)}, u32[]{:S(2)}, u32[]{:S(2)}) async-start(bf16[8,192,256]{2,1,0:T(8,128)(2,1)} %get-tuple-element.84), calls=%async_computation.1 | async-start | bytes 1572864 | tf_op jit(solution)/shard_map/all_to_all | solution.py:954
  144.2 9.4 %collective-permute-start.4 = (bf16[2,768,1792]{2,1,0:T(8,128)(2,1)}, bf16[2,768,1792]{2,1,0:T(8,128)(2,1)}, u32[]{:S(2)}, u32[]{:S(2)}) collective-permute-start(bf16[2,768,1792]{2,1,0:T(8,128)(2,1)} %weights_send.1), channel_id=1, source_target_pairs={{0,1},{1,0},{2,3},{3,2},{4,5},{5,4},{6,7},{7,6},{8,9},{9,8},{10,11... | collective-permute-start | bytes 16515080 | tf_op jit(solution)/shard_map/ppermute | solution.py:922
  144.8 22.1 %all-to-all-start.2 = ((bf16[8,192,256]{2,1,0:T(8,128)(2,1)}), bf16[8,192,256]{2,1,0:T(8,128)(2,1)S(1)}, u32[]{:S(2)}, u32[]{:S(2)}) async-start(bf16[8,192,256]{2,1,0:T(8,128)(2,1)} %get-tuple-element.97), calls=%async_computation.2 | async-start | bytes 1572864 | tf_op jit(solution)/shard_map/all_to_all | solution.py:961
  164.9 35.0 %collective-permute-start.5 = (bf16[2,4,96,896]{3,2,1,0:T(8,128)(2,1)}, bf16[2,4,96,896]{3,2,1,0:T(8,128)(2,1)}, u32[]{:S(2)}, u32[]{:S(2)}) collective-permute-start(bf16[2,4,96,896]{3,2,1,0:T(8,128)(2,1)} %get-tuple-element.95), channel_id=1, source_target_pairs={{0,2},{1,3},{2,0},{3,1},{4,6},{5,7},{6,4},{7,5},{8,10},{9,11},{10,... | collective-permute-start | bytes 4128776 | tf_op jit(solution)/shard_map/ppermute | solution.py:922
  166.4 33.5 %collective-permute-start.6 = (bf16[2,4,96,896]{3,2,1,0:T(8,128)(2,1)}, bf16[2,4,96,896]{3,2,1,0:T(8,128)(2,1)}, u32[]{:S(2)}, u32[]{:S(2)}) collective-permute-start(bf16[2,4,96,896]{3,2,1,0:T(8,128)(2,1)} %get-tuple-element.96), channel_id=1, source_target_pairs={{0,4},{1,5},{2,6},{3,7},{4,0},{5,1},{6,2},{7,3},{8,12},{9,13},{10,... | collective-permute-start | bytes 4128776 | tf_op jit(solution)/shard_map/ppermute | solution.py:922
  167.8 32.1 %copy-start.4 = (bf16[2,4,96,896]{3,2,1,0:T(8,128)(2,1)S(1)}, bf16[2,4,96,896]{3,2,1,0:T(8,128)(2,1)}, u32[]{:S(2)}) copy-start(bf16[2,4,96,896]{3,2,1,0:T(8,128)(2,1)} %get-tuple-element.94.refs_0_) | copy-start | bytes 4128772
  167.8 32.1 %copy-start.5 = (bf16[2,4,96,896]{3,2,1,0:T(8,128)(2,1)S(1)}, bf16[2,4,96,896]{3,2,1,0:T(8,128)(2,1)}, u32[]{:S(2)}) copy-start(bf16[2,4,96,896]{3,2,1,0:T(8,128)(2,1)} %get-tuple-element.101.refs_3_) | copy-start | bytes 4128772
  202.7 17.1 %collective-permute-start.7 = (bf16[4,96,896]{2,1,0:T(8,128)(2,1)}, bf16[4,96,896]{2,1,0:T(8,128)(2,1)S(1)}, u32[]{:S(2)}, u32[]{:S(2)}) collective-permute-start(bf16[4,96,896]{2,1,0:T(8,128)(2,1)} %get-tuple-element.104), channel_id=1, source_target_pairs={{0,4},{1,5},{2,6},{3,7},{4,0},{5,1},{6,2},{7,3},{8,12},{9,13},{10,... | collective-permute-start | bytes 2064392 | tf_op jit(solution)/shard_map/ppermute | solution.py:922
  204.2 16.8 %collective-permute-start.8 = (bf16[4,96,896]{2,1,0:T(8,128)(2,1)}, bf16[4,96,896]{2,1,0:T(8,128)(2,1)S(1)}, u32[]{:S(2)}, u32[]{:S(2)}) collective-permute-start(bf16[4,96,896]{2,1,0:T(8,128)(2,1)} %get-tuple-element.105), channel_id=1, source_target_pairs={{0,2},{1,3},{2,0},{3,1},{4,6},{5,7},{6,4},{7,5},{8,10},{9,11},{10,... | collective-permute-start | bytes 2064392 | tf_op jit(solution)/shard_map/ppermute | solution.py:922
  219.8 5.9 %copy-start.11 = (bf16[4,96,896]{2,1,0:T(8,128)(2,1)}, bf16[4,96,896]{2,1,0:T(8,128)(2,1)S(1)}, u32[]{:S(2)}) copy-start(bf16[4,96,896]{2,1,0:T(8,128)(2,1)S(1)} %collective-permute-done.7.refs_2_) | copy-start | bytes 2064388
  221.9 10.7 %collective-permute-start.9 = (bf16[4,256,768]{2,1,0:T(8,128)(2,1)}, bf16[4,256,768]{2,1,0:T(8,128)(2,1)S(1)}, u32[]{:S(2)}, u32[]{:S(2)}) collective-permute-start(bf16[4,256,768]{2,1,0:T(8,128)(2,1)} %get-tuple-element.115), channel_id=1, source_target_pairs={{0,1},{1,0},{2,3},{3,2},{4,5},{5,4},{6,7},{7,6},{8,9},{9,8},{10,11... | collective-permute-start | bytes 4718600 | tf_op jit(solution)/shard_map/ppermute | solution.py:922
  221.9 38.5 %all-to-all-start.3 = ((bf16[8,96,640]{2,1,0:T(8,128)(2,1)}), bf16[8,96,640]{2,1,0:T(8,128)(2,1)S(1)}, u32[]{:S(2)}, u32[]{:S(2)}) async-start(bf16[8,96,640]{2,1,0:T(8,128)(2,1)} %bitcast.62), calls=%async_computation.3 | async-start | bytes 1966080 | tf_op jit(solution)/shard_map/all_to_all | solution.py:988
  229.2 25.3 %collective-permute-start.11 = (bf16[2,96,896]{2,1,0:T(8,128)(2,1)}, bf16[2,96,896]{2,1,0:T(8,128)(2,1)S(1)}, u32[]{:S(2)}, u32[]{:S(2)}) collective-permute-start(bf16[2,96,896]{2,1,0:T(8,128)(2,1)} %get-tuple-element.117), channel_id=1, source_target_pairs={{0,24},{8,16},{16,8},{24,0},{1,25},{9,17},{17,9},{25,1},{2,26},{10... | collective-permute-start | bytes 1032200 | tf_op jit(solution)/shard_map/ppermute | solution.py:919
  232.6 26.8 %copy-start.9 = (bf16[2,96,896]{2,1,0:T(8,128)(2,1)S(1)}, bf16[2,96,896]{2,1,0:T(8,128)(2,1)}, u32[]{:S(2)}) copy-start(bf16[2,96,896]{2,1,0:T(8,128)(2,1)} %get-tuple-element.122.refs_3_) | copy-start | bytes 1032196
  232.6 26.8 %copy-start.8 = (bf16[2,96,896]{2,1,0:T(8,128)(2,1)S(1)}, bf16[2,96,896]{2,1,0:T(8,128)(2,1)}, u32[]{:S(2)}) copy-start(bf16[2,96,896]{2,1,0:T(8,128)(2,1)} %get-tuple-element.113.refs_0_) | copy-start | bytes 1032196
  232.6 26.7 %collective-permute-start.10 = (bf16[2,96,896]{2,1,0:T(8,128)(2,1)}, bf16[2,96,896]{2,1,0:T(8,128)(2,1)}, u32[]{:S(2)}, u32[]{:S(2)}) collective-permute-start(bf16[2,96,896]{2,1,0:T(8,128)(2,1)} %get-tuple-element.116), channel_id=1, source_target_pairs={{0,8},{8,0},{16,24},{24,16},{1,9},{9,1},{17,25},{25,17},{2,10},{10... | collective-permute-start | bytes 1032200 | tf_op jit(solution)/shard_map/ppermute | solution.py:919
  238.3 36.8 %collective-permute-start.13 = (bf16[256,768]{1,0:T(8,128)(2,1)}, bf16[256,768]{1,0:T(8,128)(2,1)S(1)}, u32[]{:S(2)}, u32[]{:S(2)}) collective-permute-start(bf16[256,768]{1,0:T(8,128)(2,1)} %get-tuple-element.128), channel_id=1, source_target_pairs={{0,2},{1,3},{2,0},{3,1},{4,6},{5,7},{6,4},{7,5},{8,10},{9,11},{10,... | collective-permute-start | bytes 1179656 | tf_op jit(solution)/shard_map/ppermute | solution.py:922
  238.8 36.8 %collective-permute-start.14 = (bf16[256,768]{1,0:T(8,128)(2,1)}, bf16[256,768]{1,0:T(8,128)(2,1)S(1)}, u32[]{:S(2)}, u32[]{:S(2)}) collective-permute-start(bf16[256,768]{1,0:T(8,128)(2,1)} %get-tuple-element.129), channel_id=1, source_target_pairs={{0,4},{1,5},{2,6},{3,7},{4,0},{5,1},{6,2},{7,3},{8,12},{9,13},{10,... | collective-permute-start | bytes 1179656 | tf_op jit(solution)/shard_map/ppermute | solution.py:922
  240.3 35.3 %collective-permute-start.15 = (bf16[256,768]{1,0:T(8,128)(2,1)}, bf16[256,768]{1,0:T(8,128)(2,1)S(1)}, u32[]{:S(2)}, u32[]{:S(2)}) collective-permute-start(bf16[256,768]{1,0:T(8,128)(2,1)} %get-tuple-element.130), channel_id=1, source_target_pairs={{0,6},{1,7},{2,4},{3,5},{4,2},{5,3},{6,0},{7,1},{8,14},{9,15},{10,... | collective-permute-start | bytes 1179656 | tf_op jit(solution)/shard_map/ppermute | solution.py:922
  254.5 5.0 %copy-start.10 = (bf16[2,96,896]{2,1,0:T(8,128)(2,1)}, bf16[2,96,896]{2,1,0:T(8,128)(2,1)S(1)}, u32[]{:S(2)}) copy-start(bf16[2,96,896]{2,1,0:T(8,128)(2,1)S(1)} %collective-permute-done.11.refs_4_) | copy-start | bytes 1032196
  260.4 12.5 %copy-start.3 = (bf16[8,96,640]{2,1,0:T(8,128)(2,1)}, bf16[8,96,640]{2,1,0:T(8,128)(2,1)S(1)}, u32[]{:S(2)}) copy-start(bf16[8,96,640]{2,1,0:T(8,128)(2,1)S(1)} %all-to-all-done.3.g_ref) | copy-start | bytes 2949124
  260.4 20.6 %collective-permute-start.17 = (bf16[1,96,896]{2,1,0:T(8,128)(2,1)S(1)}, bf16[1,96,896]{2,1,0:T(8,128)(2,1)S(1)}, u32[]{:S(2)}, u32[]{:S(2)}) collective-permute-start(bf16[1,96,896]{2,1,0:T(8,128)(2,1)S(1)} %add_convert_fusion.3), channel_id=1, source_target_pairs={{0,24},{8,16},{16,8},{24,0},{1,25},{9,17},{17,9},{25,1},{2,26},{10... | collective-permute-start | bytes 516104 | tf_op jit(solution)/shard_map/ppermute | solution.py:919
  262.9 18.2 %collective-permute-start.18 = (bf16[1,96,896]{2,1,0:T(8,128)(2,1)S(1)}, bf16[1,96,896]{2,1,0:T(8,128)(2,1)S(1)}, u32[]{:S(2)}, u32[]{:S(2)}) collective-permute-start(bf16[1,96,896]{2,1,0:T(8,128)(2,1)S(1)} %add_convert_fusion.2), channel_id=1, source_target_pairs={{0,8},{8,0},{16,24},{24,16},{1,9},{9,1},{17,25},{25,17},{2,10},{10... | collective-permute-start | bytes 516104 | tf_op jit(solution)/shard_map/ppermute | solution.py:919
  275.1 5.9 %collective-permute-start.12 = (f32[8,96]{1,0:T(8,128)}, f32[8,96]{1,0:T(8,128)S(1)}, u32[]{:S(2)}, u32[]{:S(2)}) collective-permute-start(f32[8,96]{1,0:T(8,128)} %get-tuple-element.126), channel_id=1, source_target_pairs={{0,2},{1,3},{2,0},{3,1},{4,6},{5,7},{6,4},{7,5},{8,10},{9,11},{10,... | collective-permute-start | bytes 9224 | tf_op jit(solution)/shard_map/ppermute | solution.py:922
  281.0 3.8 %collective-permute-start.16 = (f32[8,96]{1,0:T(8,128)S(1)}, f32[8,96]{1,0:T(8,128)S(1)}, u32[]{:S(2)}, u32[]{:S(2)}) collective-permute-start(f32[8,96]{1,0:T(8,128)S(1)} %add.140), channel_id=1, source_target_pairs={{0,1},{1,0},{2,3},{3,2},{4,5},{5,4},{6,7},{7,6},{8,9},{9,8},{10,11... | collective-permute-start | bytes 9224 | tf_op jit(solution)/shard_map/ppermute | solution.py:922
  (13 other events, 14.6 us)
Sparse Core Ops, SparseCore 0:
  11.0 99.1 all-gather.1

commit v8 on v7

--- a/solution.py
+++ b/solution.py
@@ -608,29 +608,30 @@
 
 
 def wide_sum_kernel(place_ref, *refs):
-    for i, masks in enumerate(((1, 3), (3, 1))):
+    keep_ref, send_ref = refs[6:]
+    cut = keep_ref.shape[2] // 2
+    for i in range(2):
         mine_ref, first_ref, second_ref = refs[3 * i : 3 * i + 3]
-        keep_ref, send_ref = refs[6 + 2 * i : 8 + 2 * i]
-        for ref, base in ((send_ref, masks[0]), (keep_ref, 0)):
-            for n, m in enumerate((base, base ^ masks[1])):
+        for ref, members in ((send_ref, (1, 2)), (keep_ref, (0, 3))):
+            for n, m in enumerate(members):
                 z = pl.ds(place_ref[0] ^ m, 1)
                 total = mine_ref[0, z].astype(F32) + first_ref[0, z].astype(F32)
-                ref[n : n + 1] = (total + second_ref[z].astype(F32)).astype(BF16)
+                ref[n : n + 1, :, i * cut : (i + 1) * cut] = (total + second_ref[z].astype(F32)).astype(BF16)
 
 
 def wide_sum(place, *parts):
     depth, step, cut = parts[2].shape
     first = pl.BlockSpec((1, depth, step, cut), lambda i, ix: (0, 0, 0, 0))
     last = pl.BlockSpec((depth, step, cut), lambda i, ix: (0, 0, 0))
-    out = jax.ShapeDtypeStruct((depth // 2, step, cut), BF16)
+    out = jax.ShapeDtypeStruct((depth // 2, step, 2 * cut), BF16)
     return pl.pallas_call(
         wide_sum_kernel,
-        out_shape=(out,) * 4,
+        out_shape=(out, out),
         grid_spec=pltpu.PrefetchScalarGridSpec(
             num_scalar_prefetch=1,
             grid=(1,),
             in_specs=[first, first, last] * 2,
-            out_specs=(pl.BlockSpec(out.shape, lambda i, ix: (0, 0, 0)),) * 4,
+            out_specs=(pl.BlockSpec(out.shape, lambda i, ix: (0, 0, 0)),) * 2,
         ),
         compiler_params=params(),
         cost_estimate=cost(0, 4e6),
@@ -642,14 +643,9 @@
     fc_ref, pj_ref, out_ref, g_ref, b_ref, ob_ref, pb_ref, fb_ref = refs[-8:]
     d = fc_ref.shape[1]
     width = out_ref.shape[0]
-    halves = []
-    count = (len(refs) - 8) // 2
-    for parts in (refs[:count], refs[count : 2 * count]):
-        t = parts[0][0].astype(F32)
-        for ref in parts[1:]:
-            t = t + ref[0].astype(F32)
-        halves.append(t)
-    t = jnp.concatenate(halves, axis=1)
+    t = refs[0][0].astype(F32)
+    for ref in refs[1:-8]:
+        t = t + ref[0].astype(F32)
     fc_ref[...] = t[:, :d]
     pj_ref[...] = t[:, d : 2 * d]
     rest = jnp.transpose(t[:, 2 * d : 2 * d + width + EXT])
@@ -988,21 +984,19 @@
     grad_in = lax.all_to_all(grad_in.reshape(narrow.shape), ("dp", "ctx"), 0, 0, tiled=True)
     if exchange:
         place = jnp.full((1,), deep, jnp.int32)
-        a_kept, a_send, b_kept, b_send = wide_sum(place, a_keep, a_came, a_last, b_keep, b_came, b_last)
-        a_send, send_came = barrier((a_send, send_came))
-        a_came, b_came = swap_deep(a_send, 1), swap_deep(b_send, 3)
+        z_kept, z_send = wide_sum(place, a_keep, a_came, a_last, b_keep, b_came, b_last)
+        z_send, send_came = barrier((z_send, send_came))
+        z_came = swap_deep(z_send, 1)
     near, *sends = pair_sum(keep, send_came)
     arrived = [swap(sends[n - 1], 2 * n) for n in range(1, group // 2)]
 
     if exchange:
-        a_came, b_came, near = barrier((a_came, b_came, near))
-        a_send, b_send = plus(a_kept[1:], a_came[1:]), plus(b_kept[1:], b_came[1:])
-        a_send, b_send, grad_in = barrier((a_send, b_send, grad_in))
-        a_last, b_last = swap_deep(a_send, 3), swap_deep(b_send, 1)
-        wide_parts = [a_kept, a_came, a_last, b_kept, b_came, b_last]
+        z_came, near = barrier((z_came, near))
+        z_send = plus(z_kept[1:], z_came[1:])
+        z_send, grad_in = barrier((z_send, grad_in))
+        wide_parts = [z_kept, z_came, swap_deep(z_send, 3)]
     else:
-        cut = wide.shape[1] // 2
-        wide_parts = [grad_wide[None, :, :cut], grad_wide[None, :, cut:]]
+        wide_parts = [grad_wide[None]]
     grad_qkv_weight, grad_qkv_bias, vec_in = finish_narrow(grad_in, width, qkv_bias.shape)
     vec_came = swap(vec_in, 2)
     grad_tokens = finish_rows(

time: 293 us -> 288 us (0.983); the launches traced: 292 us -> 283 us
  starting transfers between devices: 46.5 us -> 34.6 us
  waiting for transfers between devices: 62.8 us -> 66.3 us
    ppermute x4 -> x2, starting transfers between devices: 16.1 us -> 4.15 us  [swap_deep(): return lax.ppermute(array, 'dp', [(n, n ^ mask) for n in range(depth)])]
    ppermute x4 -> x2, waiting for transfers between devices: 17.6 us -> 21.1 us  [swap_deep(): return lax.ppermute(array, 'dp', [(n, n ^ mask) for n in range(depth)])]
    unnamed x42 -> x36, local copies, waits for them, and re-layouts: 7.78 us -> 6.35 us
  transfers between devices with their start and end apart: 24 -> 22, of which waited for: 9 -> 9; matrix products, arithmetic and copies ran while one was open for 3% -> 3% of each run, Pallas kernels for 39% -> 41%
where the time goes in v8:
time: 288 us; the launch traced here: 283 us
  Pallas kernels  148 us (51%)
  waiting for transfers between devices  66.3 us (23%)
  starting transfers between devices  34.6 us (12%)
  between operations  14.3 us (5%)
  other arithmetic  11.4 us (4%)
  local copies, waits for them, and re-layouts  8.06 us (3%)
    pallas_call x1, Pallas kernels, attend_back(): pl.pallas_call(attend_back_kernel, out_shape=jax.ShapeDtypeStruct(triple....  32.1 us
    pallas_call x1, Pallas kernels, attend(): pl.pallas_call(attend_kernel, out_shape=(jax.ShapeDtypeStruct((span // ro...  28.7 us
    ppermute x15, waiting for transfers between devices, swap(): lax.ppermute(array, ('ctx', 'tp'), [(n, n ^ mask) for n in range(group)])  27.3 us
    pallas_call x1, Pallas kernels, middle(): pl.pallas_call(functools.partial(middle_kernel, strip), out_shape=(sds((r...  21.6 us
    ppermute x2, waiting for transfers between devices, swap_deep(): return lax.ppermute(array, 'dp', [(n, n ^ mask) for n in range(depth)])  21.1 us
    pallas_call x2, Pallas kernels, weights(): pl.pallas_call(functools.partial(weights_kernel, mode, strip), out_shape=...  20.8 us
    pallas_call x1, Pallas kernels, project_back(): pl.pallas_call(functools.partial(project_back_kernel, piece), out_shape=(...  14.3 us
    ppermute x15, starting transfers between devices, swap(): lax.ppermute(array, ('ctx', 'tp'), [(n, n ^ mask) for n in range(group)])  12.8 us
  transfers between devices with their start and end apart: 22, of which 9 were waited for; matrix products, arithmetic and copies ran while one was open for 3% of the time, Pallas kernels for 41%

profile of v8, /device:TPU:0, one launch (start us, length us, event | category | flops | bytes accessed | tf_op | source)
XLA Modules:
  0.0 282.5 jit_solution(4308492159087507406)
XLA Ops:
  7.2 2.5 pack.1
  10.9 3.0 %collective-permute-start.1 = (bf16[256,768]{1,0:T(8,128)(2,1)S(1)}, bf16[256,768]{1,0:T(8,128)(2,1)S(1)}, u32[]{:S(2)}, u32[]{:S(2)}) collective-permute-start(bf16[256,768]{1,0:T(8,128)(2,1)S(1)} %get-tuple-element.156), channel_id=1, source_target_pairs={{0,4},{1,5},{2,6},{3,7},{4,0},{5,1},{6,2},{7,3},{8,12},{9,13},{10,... | collective-permute-start | bytes 1179656 | tf_op jit(solution)/shard_map/ppermute | solution.py:918
  14.0 1.5 collective-permute-start.2
  15.5 6.3 %all-to-all-start = ((bf16[8,96,640]{2,1,0:T(8,128)(2,1)}), bf16[8,96,640]{2,1,0:T(8,128)(2,1)S(1)}, u32[]{:S(2)}, u32[]{:S(2)}) async-start(bf16[8,96,640]{2,1,0:T(8,128)(2,1)} %get-tuple-element.78), calls=%async_computation | async-start | bytes 1966080 | tf_op jit(solution)/shard_map/all_to_all | solution.py:938
  21.8 3.9 %collective-permute-done.1 = bf16[256,768]{1,0:T(8,128)(2,1)S(1)} collective-permute-done((bf16[256,768]{1,0:T(8,128)(2,1)S(1)}, bf16[256,768]{1,0:T(8,128)(2,1)S(1)}, u32[]{:S(2)}, u32[]{:S(2)}) %collective-permute-start.1) | collective-permute-done | bytes 393248 | tf_op jit(solution)/shard_map/ppermute | solution.py:918
  25.7 16.4 %collective-permute-done.2 = bf16[256,768]{1,0:T(8,128)(2,1)S(1)} collective-permute-done((bf16[256,768]{1,0:T(8,128)(2,1)S(1)}, bf16[256,768]{1,0:T(8,128)(2,1)S(1)}, u32[]{:S(2)}, u32[]{:S(2)}) %collective-permute-start.2) | collective-permute-done | bytes 393248 | tf_op jit(solution)/shard_map/ppermute | solution.py:918
  46.4 1.5 select_convert_fusion.order_ref
  49.4 7.1 %all-to-all-done = bf16[8,96,640]{2,1,0:T(8,128)(2,1)S(1)} async-done(((bf16[8,96,640]{2,1,0:T(8,128)(2,1)}), bf16[8,96,640]{2,1,0:T(8,128)(2,1)S(1)}, u32[]{:S(2)}, u32[]{:S(2)}) %all-to-all-start) | async-done | bytes 983072 | tf_op jit(solution)/shard_map/all_to_all | solution.py:938
  57.5 10.9 %project.1.q_ref.k_ref.v_ref.qkv_ref = bf16[3,2048,192]{2,1,0:T(8,128)(2,1)} custom-call(s32[2]{0:T(128)} %pad_add_fusion.me_ref, bf16[4,256,768]{2,1,0:T(8,128)(2,1)} %copy-done.2, bf16[4,256,768]{2,1,0:T(8,128)(2,1)} %collective-permute-done.3.far_ref, bf16[768,640]{1,0:T(8,128)(2,1)} %bitcast.50, bf16[768,576]{1,0:T(8,128)(2,1)} %select_convert_fusion.2.order_ref), custom_call_target="tpu_custom_call" | custom-call | flops 1811939328 | bytes 8000000 | tf_op jit(solution)/shard_map/project/pallas_call | solution.py:131
  68.4 28.7 %attend.1 = (bf16[8,192,256]{2,1,0:T(8,128)(2,1)}, f32[192,2048]{1,0:T(8,128)}, f32[8,2048]{1,0:T(8,128)}) custom-call(bf16[3,2048,192]{2,1,0:T(8,128)(2,1)} %project.1.q_ref.k_ref.v_ref.qkv_ref, bf16[3,2048,192]{2,1,0:T(8,128)(2,1)} %project.1.q_ref.k_ref.v_ref.qkv_ref, bf16[3,2048,192]{2,1,0:T(8,128)(2,1)} %project.1.q_ref.k_ref.v_ref.qkv_ref), custom_call_target="tpu_custom_call" | custom-call | flops 3221225472 | bytes 8000000 | tf_op jit(solution)/shard_map/attend/pallas_call | solution.py:218
  97.1 3.7 %all-to-all-start.1 = ((bf16[8,192,256]{2,1,0:T(8,128)(2,1)}), bf16[8,192,256]{2,1,0:T(8,128)(2,1)S(1)}, u32[]{:S(2)}, u32[]{:S(2)}) async-start(bf16[8,192,256]{2,1,0:T(8,128)(2,1)} %get-tuple-element.80), calls=%async_computation.1 | async-start | bytes 1572864 | tf_op jit(solution)/shard_map/all_to_all | solution.py:950
  101.5 10.8 %all-to-all-done.1.mix_ref = bf16[8,192,256]{2,1,0:T(8,128)(2,1)S(1)} async-done(((bf16[8,192,256]{2,1,0:T(8,128)(2,1)}), bf16[8,192,256]{2,1,0:T(8,128)(2,1)S(1)}, u32[]{:S(2)}, u32[]{:S(2)}) %all-to-all-start.1) | async-done | bytes 786464 | tf_op jit(solution)/shard_map/all_to_all | solution.py:950
  113.1 21.6 %middle.1 = (bf16[512,768]{1,0:T(8,128)(2,1)}, f32[512,768]{1,0:T(8,128)}, bf16[8,192,256]{2,1,0:T(8,128)(2,1)}, bf16[512,768]{1,0:T(8,128)(2,1)}, bf16[4,512,76...) custom-call(bf16[512,768]{1,0:T(8,128)(2,1)} %bitcast.58, ...), custom_call_target="tpu_custom_call" | custom-call | flops 10871635968 | bytes 30000000 | tf_op jit(solution)/shard_map/middle/pallas_call | solution.py:460
  134.8 9.4 %weights_send.1 = bf16[2,768,1792]{2,1,0:T(8,128)(2,1)} custom-call(s32[3]{0:T(128)} %add_add_fusion.1.index_ref, bf16[512,768]{1,0:T(8,128)(2,1)} %get-tuple-element.84.n2_ref, bf16[512,768]{1,0:T(8,128)(2,1)} %bitcast.56, bf16[512,768]{1,0:T(8,128)(2,1)} %get-tuple-element.85.gb_ref, bf16[2,4,192,256]{3,2,1,0:T(8,128)(2,1)} %bitcast.53, ...), custom_call_target="tpu_custom_call" | custom-call | flops 2818572288 | bytes 12000000 | tf_op jit(solution)/shard_map/weights_send/pallas_call | solution.py:594
  144.7 3.8 %all-to-all-start.2 = ((bf16[8,192,256]{2,1,0:T(8,128)(2,1)}), bf16[8,192,256]{2,1,0:T(8,128)(2,1)S(1)}, u32[]{:S(2)}, u32[]{:S(2)}) async-start(bf16[8,192,256]{2,1,0:T(8,128)(2,1)} %get-tuple-element.93), calls=%async_computation.2 | async-start | bytes 1572864 | tf_op jit(solution)/shard_map/all_to_all | solution.py:957
  148.5 5.0 %collective-permute-done.4.rest_0_ = bf16[2,768,1792]{2,1,0:T(8,128)(2,1)} collective-permute-done((bf16[2,768,1792]{2,1,0:T(8,128)(2,1)}, bf16[2,768,1792]{2,1,0:T(8,128)(2,1)}, u32[]{:S(2)}, u32[]{:S(2)}) %collective-permute-start.4) | collective-permute-done | bytes 5505056 | tf_op jit(solution)/shard_map/ppermute | solution.py:918
  153.5 11.4 %weights_keep.1 = (bf16[2,4,96,896]{3,2,1,0:T(8,128)(2,1)}, bf16[2,4,96,896]{3,2,1,0:T(8,128)(2,1)}, bf16[2,4,96,896]{3,2,1,0:T(8,128)(2,1)}, bf16[2,4,96,896]{3,2,1,0:T(8,128)(2,1)}) custom-call(s32[3]{0:T(128)} %add_add_fusion.index_ref, bf16[512,768]{1,0:T(8,128)(2,1)} %get-tuple-element.84.n2_ref, bf16[512,768]{1,0:T(8,128)(2,1)} %bitcast.57, ...), custom_call_target="tpu_custom_call" | custom-call | flops 2818572288 | bytes 12000000 | tf_op jit(solution)/shard_map/weights_keep/pallas_call | solution.py:594
  164.9 1.5 collective-permute-start.5
  167.8 32.1 %attend_back.1.grad_ref = bf16[3,2048,192]{2,1,0:T(8,128)(2,1)} custom-call(bf16[3,2048,192]{2,1,0:T(8,128)(2,1)} %project.1.q_ref.k_ref.v_ref.qkv_ref, bf16[8,192,256]{2,1,0:T(8,128)(2,1)} %copy-done.8, f32[192,2048]{1,0:T(8,128)} %get-tuple-element.94.ot_ref, f32[8,2048]{1,0:T(8,128)} %get-tuple-element.95.level_ref), custom_call_target="tpu_custom_call" | custom-call | flops 8053063680 | bytes 10000000 | tf_op jit(solution)/shard_map/attend_back/pallas_call | solution.py:339
  199.9 2.8 fusion
  202.7 1.5 collective-permute-start.7
  204.7 14.3 %project_back.1 = (f32[4,256,768]{2,1,0:T(8,128)}, bf16[4,256,768]{2,1,0:T(8,128)(2,1)}, bf16[768,640]{1,0:T(8,128)(2,1)}) custom-call(s32[2]{0:T(128)} %pad_add_fusion.me_ref, bf16[4,256,768]{2,1,0:T(8,128)(2,1)} %copy-done.2, bf16[4,256,768]{2,1,0:T(8,128)(2,1)} %collective-permute-done.3.far_ref, bf16[3,2048,192]{2,1,0:T(8,128)(2,1)} %attend_back.1.grad_ref, ...), custom_call_target="tpu_custom_call" | custom-call | flops 3623878656 | bytes 15000000 | tf_op jit(solution)/shard_map/project_back/pallas_call | solution.py:765
  221.9 3.8 %all-to-all-start.3 = ((bf16[8,96,640]{2,1,0:T(8,128)(2,1)}), bf16[8,96,640]{2,1,0:T(8,128)(2,1)S(1)}, u32[]{:S(2)}, u32[]{:S(2)}) async-start(bf16[8,96,640]{2,1,0:T(8,128)(2,1)} %bitcast.62), calls=%async_computation.3 | async-start | bytes 1966080 | tf_op jit(solution)/shard_map/all_to_all | solution.py:984
  225.8 3.6 %wide_sum.1 = (bf16[2,96,1792]{2,1,0:T(8,128)(2,1)}, bf16[2,96,1792]{2,1,0:T(8,128)(2,1)}) custom-call(s32[1]{0:T(128)} %bitcast.21.place_ref, bf16[2,4,96,896]{3,2,1,0:T(8,128)(2,1)} %get-tuple-element.90.refs_0_, bf16[2,4,96,896]{3,2,1,0:T(8,128)(2,1)} %collective-permute-done.5.refs_1_, bf16[4,96,896]{2,1,0:T(8,128)(2,1)} %copy-done.9, ...), custom_call_target="tpu_custom_call" | custom-call | bytes 4000000 | tf_op jit(solution)/shard_map/wide_sum/pallas_call | solution.py:627
  229.4 1.7 collective-permute-start.10
  231.1 4.5 %pair_sum.1 = (f32[256,768]{1,0:T(8,128)}, bf16[256,768]{1,0:T(8,128)(2,1)}, bf16[256,768]{1,0:T(8,128)(2,1)}, bf16[256,768]{1,0:T(8,128)(2,1)}) custom-call(f32[4,256,768]{2,1,0:T(8,128)} %get-tuple-element.113.keep_ref, bf16[4,256,768]{2,1,0:T(8,128)(2,1)} %copy-done.6), custom_call_target="tpu_custom_call" | custom-call | bytes 7000000 | tf_op jit(solution)/shard_map/pair_sum/pallas_call | solution.py:820
  236.2 1.5 collective-permute-start.13
  239.1 20.3 %collective-permute-done.10.refs_1_ = bf16[2,96,1792]{2,1,0:T(8,128)(2,1)} collective-permute-done((bf16[2,96,1792]{2,1,0:T(8,128)(2,1)}, bf16[2,96,1792]{2,1,0:T(8,128)(2,1)}, u32[]{:S(2)}, u32[]{:S(2)}) %collective-permute-start.10) | collective-permute-done | bytes 688160 | tf_op jit(solution)/shard_map/ppermute | solution.py:915
  260.5 2.4 collective-permute-start.16
  262.9 2.1 finish_narrow.1
  266.6 4.5 %finish_rows.1 = f32[2,256,768]{2,1,0:T(8,128)} custom-call(s32[1]{0:T(128)} %bitcast.3.side_ref, bf16[2,256,768]{2,1,0:T(8,128)(2,1)} %bitcast.59, f32[256,768]{1,0:T(8,128)} %get-tuple-element.120.near_ref, bf16[256,768]{1,0:T(8,128)(2,1)} %copy-done.13, bf16[256,768]{1,0:T(8,128)(2,1)} %copy-done.14, bf16[256,768]{1,0:T(8,128)(2,1)} %copy-done.15, ...), custom_call_target="tpu_custom_call" | custom-call | bytes 6000000 | tf_op jit(solution)/shard_map/finish_rows/pallas_call | solution.py:851
  272.8 2.4 finish_wide.1
  (78 shorter events, 22.0 us)
Async XLA Ops:
  7.2 105.1 %all-gather.2.cloned.1.call-start = ((), (), s32[]{:S(2)}) async-start(), calls=%async_computation.4 | async-start | bytes 11354112 | tf_op jit(solution)/shard_map/all_gather | solution.py:926
  10.9 14.7 %collective-permute-start.1 = (bf16[256,768]{1,0:T(8,128)(2,1)S(1)}, bf16[256,768]{1,0:T(8,128)(2,1)S(1)}, u32[]{:S(2)}, u32[]{:S(2)}) collective-permute-start(bf16[256,768]{1,0:T(8,128)(2,1)S(1)} %get-tuple-element.156), channel_id=1, source_target_pairs={{0,4},{1,5},{2,6},{3,7},{4,0},{5,1},{6,2},{7,3},{8,12},{9,13},{10,... | collective-permute-start | bytes 1179656 | tf_op jit(solution)/shard_map/ppermute | solution.py:918
  14.0 28.1 %collective-permute-start.2 = (bf16[256,768]{1,0:T(8,128)(2,1)S(1)}, bf16[256,768]{1,0:T(8,128)(2,1)S(1)}, u32[]{:S(2)}, u32[]{:S(2)}) collective-permute-start(bf16[256,768]{1,0:T(8,128)(2,1)S(1)} %get-tuple-element.156), channel_id=1, source_target_pairs={{0,6},{1,7},{2,4},{3,5},{4,2},{5,3},{6,0},{7,1},{8,14},{9,15},{10,... | collective-permute-start | bytes 1179656 | tf_op jit(solution)/shard_map/ppermute | solution.py:918
  15.5 26.6 %collective-permute-start = (bf16[256,768]{1,0:T(8,128)(2,1)S(1)}, bf16[256,768]{1,0:T(8,128)(2,1)S(1)}, u32[]{:S(2)}, u32[]{:S(2)}) collective-permute-start(bf16[256,768]{1,0:T(8,128)(2,1)S(1)} %get-tuple-element.155), channel_id=1, source_target_pairs={{0,2},{1,3},{2,0},{3,1},{4,6},{5,7},{6,4},{7,5},{8,10},{9,11},{10,... | collective-permute-start | bytes 1179656 | tf_op jit(solution)/shard_map/ppermute | solution.py:918
  15.5 41.0 %all-to-all-start = ((bf16[8,96,640]{2,1,0:T(8,128)(2,1)}), bf16[8,96,640]{2,1,0:T(8,128)(2,1)S(1)}, u32[]{:S(2)}, u32[]{:S(2)}) async-start(bf16[8,96,640]{2,1,0:T(8,128)(2,1)} %get-tuple-element.78), calls=%async_computation | async-start | bytes 1966080 | tf_op jit(solution)/shard_map/all_to_all | solution.py:938
  44.2 5.2 %copy-start.2 = (bf16[4,256,768]{2,1,0:T(8,128)(2,1)}, bf16[4,256,768]{2,1,0:T(8,128)(2,1)S(1)}, u32[]{:S(2)}) copy-start(bf16[4,256,768]{2,1,0:T(8,128)(2,1)S(1)} %pad_maximum_fusion.own_ref) | copy-start | bytes 4718596
  44.2 5.2 %collective-permute-start.3 = (bf16[4,256,768]{2,1,0:T(8,128)(2,1)S(1)}, bf16[4,256,768]{2,1,0:T(8,128)(2,1)}, u32[]{:S(2)}, u32[]{:S(2)}) collective-permute-start(bf16[4,256,768]{2,1,0:T(8,128)(2,1)S(1)} %pad_maximum_fusion.own_ref), channel_id=1, source_target_pairs={{0,1},{1,0},{2,3},{3,2},{4,5},{5,4},{6,7},{7,6},{8,9},{9,8},{10,11... | collective-permute-start | bytes 4718600 | tf_op jit(solution)/shard_map/ppermute | solution.py:918
  56.5 1.0 copy-start
  97.1 15.1 %all-to-all-start.1 = ((bf16[8,192,256]{2,1,0:T(8,128)(2,1)}), bf16[8,192,256]{2,1,0:T(8,128)(2,1)S(1)}, u32[]{:S(2)}, u32[]{:S(2)}) async-start(bf16[8,192,256]{2,1,0:T(8,128)(2,1)} %get-tuple-element.80), calls=%async_computation.1 | async-start | bytes 1572864 | tf_op jit(solution)/shard_map/all_to_all | solution.py:950
  144.1 9.4 %collective-permute-start.4 = (bf16[2,768,1792]{2,1,0:T(8,128)(2,1)}, bf16[2,768,1792]{2,1,0:T(8,128)(2,1)}, u32[]{:S(2)}, u32[]{:S(2)}) collective-permute-start(bf16[2,768,1792]{2,1,0:T(8,128)(2,1)} %weights_send.1), channel_id=1, source_target_pairs={{0,1},{1,0},{2,3},{3,2},{4,5},{5,4},{6,7},{7,6},{8,9},{9,8},{10,11... | collective-permute-start | bytes 16515080 | tf_op jit(solution)/shard_map/ppermute | solution.py:918
  144.7 22.2 %all-to-all-start.2 = ((bf16[8,192,256]{2,1,0:T(8,128)(2,1)}), bf16[8,192,256]{2,1,0:T(8,128)(2,1)S(1)}, u32[]{:S(2)}, u32[]{:S(2)}) async-start(bf16[8,192,256]{2,1,0:T(8,128)(2,1)} %get-tuple-element.93), calls=%async_computation.2 | async-start | bytes 1572864 | tf_op jit(solution)/shard_map/all_to_all | solution.py:957
  164.9 35.0 %collective-permute-start.5 = (bf16[2,4,96,896]{3,2,1,0:T(8,128)(2,1)}, bf16[2,4,96,896]{3,2,1,0:T(8,128)(2,1)}, u32[]{:S(2)}, u32[]{:S(2)}) collective-permute-start(bf16[2,4,96,896]{3,2,1,0:T(8,128)(2,1)} %get-tuple-element.91), channel_id=1, source_target_pairs={{0,2},{1,3},{2,0},{3,1},{4,6},{5,7},{6,4},{7,5},{8,10},{9,11},{10,... | collective-permute-start | bytes 4128776 | tf_op jit(solution)/shard_map/ppermute | solution.py:918
  166.4 33.5 %collective-permute-start.6 = (bf16[2,4,96,896]{3,2,1,0:T(8,128)(2,1)}, bf16[2,4,96,896]{3,2,1,0:T(8,128)(2,1)}, u32[]{:S(2)}, u32[]{:S(2)}) collective-permute-start(bf16[2,4,96,896]{3,2,1,0:T(8,128)(2,1)} %get-tuple-element.92), channel_id=1, source_target_pairs={{0,4},{1,5},{2,6},{3,7},{4,0},{5,1},{6,2},{7,3},{8,12},{9,13},{10,... | collective-permute-start | bytes 4128776 | tf_op jit(solution)/shard_map/ppermute | solution.py:918
  167.8 32.1 %copy-start.4 = (bf16[2,4,96,896]{3,2,1,0:T(8,128)(2,1)S(1)}, bf16[2,4,96,896]{3,2,1,0:T(8,128)(2,1)}, u32[]{:S(2)}) copy-start(bf16[2,4,96,896]{3,2,1,0:T(8,128)(2,1)} %get-tuple-element.90.refs_0_) | copy-start | bytes 4128772
  167.8 32.1 %copy-start.5 = (bf16[2,4,96,896]{3,2,1,0:T(8,128)(2,1)S(1)}, bf16[2,4,96,896]{3,2,1,0:T(8,128)(2,1)}, u32[]{:S(2)}) copy-start(bf16[2,4,96,896]{3,2,1,0:T(8,128)(2,1)} %get-tuple-element.97.refs_3_) | copy-start | bytes 4128772
  202.7 17.1 %collective-permute-start.7 = (bf16[4,96,896]{2,1,0:T(8,128)(2,1)}, bf16[4,96,896]{2,1,0:T(8,128)(2,1)S(1)}, u32[]{:S(2)}, u32[]{:S(2)}) collective-permute-start(bf16[4,96,896]{2,1,0:T(8,128)(2,1)} %get-tuple-element.100), channel_id=1, source_target_pairs={{0,4},{1,5},{2,6},{3,7},{4,0},{5,1},{6,2},{7,3},{8,12},{9,13},{10,... | collective-permute-start | bytes 2064392 | tf_op jit(solution)/shard_map/ppermute | solution.py:918
  204.2 16.8 %collective-permute-start.8 = (bf16[4,96,896]{2,1,0:T(8,128)(2,1)}, bf16[4,96,896]{2,1,0:T(8,128)(2,1)S(1)}, u32[]{:S(2)}, u32[]{:S(2)}) collective-permute-start(bf16[4,96,896]{2,1,0:T(8,128)(2,1)} %get-tuple-element.101), channel_id=1, source_target_pairs={{0,2},{1,3},{2,0},{3,1},{4,6},{5,7},{6,4},{7,5},{8,10},{9,11},{10,... | collective-permute-start | bytes 2064392 | tf_op jit(solution)/shard_map/ppermute | solution.py:918
  219.8 5.9 %copy-start.9 = (bf16[4,96,896]{2,1,0:T(8,128)(2,1)}, bf16[4,96,896]{2,1,0:T(8,128)(2,1)S(1)}, u32[]{:S(2)}) copy-start(bf16[4,96,896]{2,1,0:T(8,128)(2,1)S(1)} %collective-permute-done.7.refs_2_) | copy-start | bytes 2064388
  221.9 7.4 %collective-permute-start.9 = (bf16[4,256,768]{2,1,0:T(8,128)(2,1)}, bf16[4,256,768]{2,1,0:T(8,128)(2,1)S(1)}, u32[]{:S(2)}, u32[]{:S(2)}) collective-permute-start(bf16[4,256,768]{2,1,0:T(8,128)(2,1)} %get-tuple-element.111), channel_id=1, source_target_pairs={{0,1},{1,0},{2,3},{3,2},{4,5},{5,4},{6,7},{7,6},{8,9},{9,8},{10,11... | collective-permute-start | bytes 4718600 | tf_op jit(solution)/shard_map/ppermute | solution.py:918
  221.9 38.5 %all-to-all-start.3 = ((bf16[8,96,640]{2,1,0:T(8,128)(2,1)}), bf16[8,96,640]{2,1,0:T(8,128)(2,1)S(1)}, u32[]{:S(2)}, u32[]{:S(2)}) async-start(bf16[8,96,640]{2,1,0:T(8,128)(2,1)} %bitcast.62), calls=%async_computation.3 | async-start | bytes 1966080 | tf_op jit(solution)/shard_map/all_to_all | solution.py:984
  229.4 1.7 copy-start.6
  229.4 30.0 %copy-start.7 = (bf16[2,96,1792]{2,1,0:T(8,128)(2,1)S(1)}, bf16[2,96,1792]{2,1,0:T(8,128)(2,1)}, u32[]{:S(2)}) copy-start(bf16[2,96,1792]{2,1,0:T(8,128)(2,1)} %get-tuple-element.109.refs_0_) | copy-start | bytes 2064388
  229.4 30.0 %collective-permute-start.10 = (bf16[2,96,1792]{2,1,0:T(8,128)(2,1)}, bf16[2,96,1792]{2,1,0:T(8,128)(2,1)}, u32[]{:S(2)}, u32[]{:S(2)}) collective-permute-start(bf16[2,96,1792]{2,1,0:T(8,128)(2,1)} %get-tuple-element.112), channel_id=1, source_target_pairs={{0,8},{8,0},{16,24},{24,16},{1,9},{9,1},{17,25},{25,17},{2,10},{10... | collective-permute-start | bytes 2064392 | tf_op jit(solution)/shard_map/ppermute | solution.py:915
  235.6 29.9 %collective-permute-start.12 = (bf16[256,768]{1,0:T(8,128)(2,1)}, bf16[256,768]{1,0:T(8,128)(2,1)S(1)}, u32[]{:S(2)}, u32[]{:S(2)}) collective-permute-start(bf16[256,768]{1,0:T(8,128)(2,1)} %get-tuple-element.121), channel_id=1, source_target_pairs={{0,2},{1,3},{2,0},{3,1},{4,6},{5,7},{6,4},{7,5},{8,10},{9,11},{10,... | collective-permute-start | bytes 1179656 | tf_op jit(solution)/shard_map/ppermute | solution.py:918
  236.2 29.4 %collective-permute-start.13 = (bf16[256,768]{1,0:T(8,128)(2,1)}, bf16[256,768]{1,0:T(8,128)(2,1)S(1)}, u32[]{:S(2)}, u32[]{:S(2)}) collective-permute-start(bf16[256,768]{1,0:T(8,128)(2,1)} %get-tuple-element.122), channel_id=1, source_target_pairs={{0,4},{1,5},{2,6},{3,7},{4,0},{5,1},{6,2},{7,3},{8,12},{9,13},{10,... | collective-permute-start | bytes 1179656 | tf_op jit(solution)/shard_map/ppermute | solution.py:918
  237.7 27.9 %collective-permute-start.14 = (bf16[256,768]{1,0:T(8,128)(2,1)}, bf16[256,768]{1,0:T(8,128)(2,1)S(1)}, u32[]{:S(2)}, u32[]{:S(2)}) collective-permute-start(bf16[256,768]{1,0:T(8,128)(2,1)} %get-tuple-element.123), channel_id=1, source_target_pairs={{0,6},{1,7},{2,4},{3,5},{4,2},{5,3},{6,0},{7,1},{8,14},{9,15},{10,... | collective-permute-start | bytes 1179656 | tf_op jit(solution)/shard_map/ppermute | solution.py:918
  260.5 2.5 copy-start.3
  260.5 11.6 %collective-permute-start.16 = (bf16[1,96,1792]{2,1,0:T(8,128)(2,1)S(1)}, bf16[1,96,1792]{2,1,0:T(8,128)(2,1)S(1)}, u32[]{:S(2)}, u32[]{:S(2)}) collective-permute-start(bf16[1,96,1792]{2,1,0:T(8,128)(2,1)S(1)} %add_convert_fusion.2), channel_id=1, source_target_pairs={{0,24},{8,16},{16,8},{24,0},{1,25},{9,17},{17,9},{25,1},{2,26},{10... | collective-permute-start | bytes 1032200 | tf_op jit(solution)/shard_map/ppermute | solution.py:915
  265.0 6.1 %collective-permute-start.11 = (f32[8,96]{1,0:T(8,128)}, f32[8,96]{1,0:T(8,128)S(1)}, u32[]{:S(2)}, u32[]{:S(2)}) collective-permute-start(f32[8,96]{1,0:T(8,128)} %get-tuple-element.119), channel_id=1, source_target_pairs={{0,2},{1,3},{2,0},{3,1},{4,6},{5,7},{6,4},{7,5},{8,10},{9,11},{10,... | collective-permute-start | bytes 9224 | tf_op jit(solution)/shard_map/ppermute | solution.py:918
  265.6 1.0 copy-start.15
  266.6 4.5 %copy-start.17 = (f32[8,96]{1,0:T(8,128)S(1)}, f32[8,96]{1,0:T(8,128)}, u32[]{:S(2)}) copy-start(f32[8,96]{1,0:T(8,128)} %get-tuple-element.119) | copy-start | bytes 9220
  271.1 4.0 %collective-permute-start.15 = (f32[8,96]{1,0:T(8,128)S(1)}, f32[8,96]{1,0:T(8,128)S(1)}, u32[]{:S(2)}, u32[]{:S(2)}) collective-permute-start(f32[8,96]{1,0:T(8,128)S(1)} %add.136), channel_id=1, source_target_pairs={{0,1},{1,0},{2,3},{3,2},{4,5},{5,4},{6,7},{7,6},{8,9},{9,8},{10,11... | collective-permute-start | bytes 9224 | tf_op jit(solution)/shard_map/ppermute | solution.py:918
  (8 other events, 6.7 us)
Sparse Core Ops, SparseCore 0:
  11.0 99.0 all-gather.1

commit v9 on v8

--- a/solution.py
+++ b/solution.py
@@ -743,7 +743,7 @@
 
     @pl.when(jnp.logical_not(far))
     def _():
-        keep_ref[0] = part
+        keep_ref[0] = part.astype(BF16)
 
     @pl.when(i == steps - 1)
     def _():
@@ -765,7 +765,7 @@
     return pl.pallas_call(
         functools.partial(project_back_kernel, piece),
         out_shape=(
-            sds((half, rows, d), F32),
+            sds((half, rows, d), BF16),
             sds((half, rows, d), BF16),
             sds(w.shape, BF16),
         ),
@@ -800,7 +800,7 @@
 
 def pair_kernel(keep_ref, came_ref, own_ref, *send_refs):
     n = pl.program_id(0)
-    total = keep_ref[0] + came_ref[0].astype(F32)
+    total = keep_ref[0].astype(F32) + came_ref[0].astype(F32)
 
     @pl.when(n == 0)
     def _():

time: 288 us -> 288 us (level)
  transfers between devices with their start and end apart: 22 -> 22, of which waited for: 9 -> 9; matrix products, arithmetic and copies ran while one was open for 3% -> 3% of each run, Pallas kernels for 41% -> 40%
where the time goes in v9:
time: 288 us; the launch traced here: 282 us
  Pallas kernels  147 us (51%)
  waiting for transfers between devices  66.9 us (23%)
  starting transfers between devices  34.6 us (12%)
  between operations  14.3 us (5%)
  other arithmetic  11.3 us (4%)
  local copies, waits for them, and re-layouts  7.98 us (3%)
    pallas_call x1, Pallas kernels, attend_back(): pl.pallas_call(attend_back_kernel, out_shape=jax.ShapeDtypeStruct(triple....  32 us
    pallas_call x1, Pallas kernels, attend(): pl.pallas_call(attend_kernel, out_shape=(jax.ShapeDtypeStruct((span // ro...  28.7 us
    ppermute x15, waiting for transfers between devices, swap(): lax.ppermute(array, ('ctx', 'tp'), [(n, n ^ mask) for n in range(group)])  27.6 us
    pallas_call x1, Pallas kernels, middle(): pl.pallas_call(functools.partial(middle_kernel, strip), out_shape=(sds((r...  21.6 us
    ppermute x2, waiting for transfers between devices, swap_deep(): return lax.ppermute(array, 'dp', [(n, n ^ mask) for n in range(depth)])  21.4 us
    pallas_call x2, Pallas kernels, weights(): pl.pallas_call(functools.partial(weights_kernel, mode, strip), out_shape=...  20.7 us
    pallas_call x1, Pallas kernels, project_back(): pl.pallas_call(functools.partial(project_back_kernel, piece), out_shape=(...  14 us
    ppermute x15, starting transfers between devices, swap(): lax.ppermute(array, ('ctx', 'tp'), [(n, n ^ mask) for n in range(group)])  12.8 us
  transfers between devices with their start and end apart: 22, of which 9 were waited for; matrix products, arithmetic and copies ran while one was open for 3% of the time, Pallas kernels for 40%

profile of v9, /device:TPU:0, one launch (start us, length us, event | category | flops | bytes accessed | tf_op | source)
XLA Modules:
  0.0 282.3 jit_solution(18069851231357280276)
XLA Ops:
  7.2 2.5 pack.1
  11.0 3.0 %collective-permute-start.1 = (bf16[256,768]{1,0:T(8,128)(2,1)S(1)}, bf16[256,768]{1,0:T(8,128)(2,1)S(1)}, u32[]{:S(2)}, u32[]{:S(2)}) collective-permute-start(bf16[256,768]{1,0:T(8,128)(2,1)S(1)} %get-tuple-element.156), channel_id=1, source_target_pairs={{0,4},{1,5},{2,6},{3,7},{4,0},{5,1},{6,2},{7,3},{8,12},{9,13},{10,... | collective-permute-start | bytes 1179656 | tf_op jit(solution)/shard_map/ppermute | solution.py:918
  14.0 1.5 collective-permute-start.2
  15.6 6.3 %all-to-all-start = ((bf16[8,96,640]{2,1,0:T(8,128)(2,1)}), bf16[8,96,640]{2,1,0:T(8,128)(2,1)S(1)}, u32[]{:S(2)}, u32[]{:S(2)}) async-start(bf16[8,96,640]{2,1,0:T(8,128)(2,1)} %get-tuple-element.78), calls=%async_computation | async-start | bytes 1966080 | tf_op jit(solution)/shard_map/all_to_all | solution.py:938
  21.8 3.9 %collective-permute-done.1 = bf16[256,768]{1,0:T(8,128)(2,1)S(1)} collective-permute-done((bf16[256,768]{1,0:T(8,128)(2,1)S(1)}, bf16[256,768]{1,0:T(8,128)(2,1)S(1)}, u32[]{:S(2)}, u32[]{:S(2)}) %collective-permute-start.1) | collective-permute-done | bytes 393248 | tf_op jit(solution)/shard_map/ppermute | solution.py:918
  25.7 16.4 %collective-permute-done.2 = bf16[256,768]{1,0:T(8,128)(2,1)S(1)} collective-permute-done((bf16[256,768]{1,0:T(8,128)(2,1)S(1)}, bf16[256,768]{1,0:T(8,128)(2,1)S(1)}, u32[]{:S(2)}, u32[]{:S(2)}) %collective-permute-start.2) | collective-permute-done | bytes 393248 | tf_op jit(solution)/shard_map/ppermute | solution.py:918
  46.5 1.5 select_convert_fusion.order_ref
  49.4 7.1 %all-to-all-done = bf16[8,96,640]{2,1,0:T(8,128)(2,1)S(1)} async-done(((bf16[8,96,640]{2,1,0:T(8,128)(2,1)}), bf16[8,96,640]{2,1,0:T(8,128)(2,1)S(1)}, u32[]{:S(2)}, u32[]{:S(2)}) %all-to-all-start) | async-done | bytes 983072 | tf_op jit(solution)/shard_map/all_to_all | solution.py:938
  57.5 10.9 %project.1.q_ref.k_ref.v_ref.qkv_ref = bf16[3,2048,192]{2,1,0:T(8,128)(2,1)} custom-call(s32[2]{0:T(128)} %pad_add_fusion.me_ref, bf16[4,256,768]{2,1,0:T(8,128)(2,1)} %copy-done.2, bf16[4,256,768]{2,1,0:T(8,128)(2,1)} %collective-permute-done.3.far_ref, bf16[768,640]{1,0:T(8,128)(2,1)} %bitcast.50, bf16[768,576]{1,0:T(8,128)(2,1)} %select_convert_fusion.2.order_ref), custom_call_target="tpu_custom_call" | custom-call | flops 1811939328 | bytes 8000000 | tf_op jit(solution)/shard_map/project/pallas_call | solution.py:131
  68.4 28.7 %attend.1 = (bf16[8,192,256]{2,1,0:T(8,128)(2,1)}, f32[192,2048]{1,0:T(8,128)}, f32[8,2048]{1,0:T(8,128)}) custom-call(bf16[3,2048,192]{2,1,0:T(8,128)(2,1)} %project.1.q_ref.k_ref.v_ref.qkv_ref, bf16[3,2048,192]{2,1,0:T(8,128)(2,1)} %project.1.q_ref.k_ref.v_ref.qkv_ref, bf16[3,2048,192]{2,1,0:T(8,128)(2,1)} %project.1.q_ref.k_ref.v_ref.qkv_ref), custom_call_target="tpu_custom_call" | custom-call | flops 3221225472 | bytes 8000000 | tf_op jit(solution)/shard_map/attend/pallas_call | solution.py:218
  97.1 3.7 %all-to-all-start.1 = ((bf16[8,192,256]{2,1,0:T(8,128)(2,1)}), bf16[8,192,256]{2,1,0:T(8,128)(2,1)S(1)}, u32[]{:S(2)}, u32[]{:S(2)}) async-start(bf16[8,192,256]{2,1,0:T(8,128)(2,1)} %get-tuple-element.80), calls=%async_computation.1 | async-start | bytes 1572864 | tf_op jit(solution)/shard_map/all_to_all | solution.py:950
  101.4 10.8 %all-to-all-done.1.mix_ref = bf16[8,192,256]{2,1,0:T(8,128)(2,1)S(1)} async-done(((bf16[8,192,256]{2,1,0:T(8,128)(2,1)}), bf16[8,192,256]{2,1,0:T(8,128)(2,1)S(1)}, u32[]{:S(2)}, u32[]{:S(2)}) %all-to-all-start.1) | async-done | bytes 786464 | tf_op jit(solution)/shard_map/all_to_all | solution.py:950
  113.1 21.6 %middle.1 = (bf16[512,768]{1,0:T(8,128)(2,1)}, f32[512,768]{1,0:T(8,128)}, bf16[8,192,256]{2,1,0:T(8,128)(2,1)}, bf16[512,768]{1,0:T(8,128)(2,1)}, bf16[4,512,76...) custom-call(bf16[512,768]{1,0:T(8,128)(2,1)} %bitcast.58, ...), custom_call_target="tpu_custom_call" | custom-call | flops 10871635968 | bytes 30000000 | tf_op jit(solution)/shard_map/middle/pallas_call | solution.py:460
  134.8 9.4 %weights_send.1 = bf16[2,768,1792]{2,1,0:T(8,128)(2,1)} custom-call(s32[3]{0:T(128)} %add_add_fusion.1.index_ref, bf16[512,768]{1,0:T(8,128)(2,1)} %get-tuple-element.84.n2_ref, bf16[512,768]{1,0:T(8,128)(2,1)} %bitcast.56, bf16[512,768]{1,0:T(8,128)(2,1)} %get-tuple-element.85.gb_ref, bf16[2,4,192,256]{3,2,1,0:T(8,128)(2,1)} %bitcast.53, ...), custom_call_target="tpu_custom_call" | custom-call | flops 2818572288 | bytes 12000000 | tf_op jit(solution)/shard_map/weights_send/pallas_call | solution.py:594
  144.7 3.8 %all-to-all-start.2 = ((bf16[8,192,256]{2,1,0:T(8,128)(2,1)}), bf16[8,192,256]{2,1,0:T(8,128)(2,1)S(1)}, u32[]{:S(2)}, u32[]{:S(2)}) async-start(bf16[8,192,256]{2,1,0:T(8,128)(2,1)} %get-tuple-element.93), calls=%async_computation.2 | async-start | bytes 1572864 | tf_op jit(solution)/shard_map/all_to_all | solution.py:957
  148.5 5.0 %collective-permute-done.4.rest_0_ = bf16[2,768,1792]{2,1,0:T(8,128)(2,1)} collective-permute-done((bf16[2,768,1792]{2,1,0:T(8,128)(2,1)}, bf16[2,768,1792]{2,1,0:T(8,128)(2,1)}, u32[]{:S(2)}, u32[]{:S(2)}) %collective-permute-start.4) | collective-permute-done | bytes 5505056 | tf_op jit(solution)/shard_map/ppermute | solution.py:918
  153.5 11.3 %weights_keep.1 = (bf16[2,4,96,896]{3,2,1,0:T(8,128)(2,1)}, bf16[2,4,96,896]{3,2,1,0:T(8,128)(2,1)}, bf16[2,4,96,896]{3,2,1,0:T(8,128)(2,1)}, bf16[2,4,96,896]{3,2,1,0:T(8,128)(2,1)}) custom-call(s32[3]{0:T(128)} %add_add_fusion.index_ref, bf16[512,768]{1,0:T(8,128)(2,1)} %get-tuple-element.84.n2_ref, bf16[512,768]{1,0:T(8,128)(2,1)} %bitcast.57, ...), custom_call_target="tpu_custom_call" | custom-call | flops 2818572288 | bytes 12000000 | tf_op jit(solution)/shard_map/weights_keep/pallas_call | solution.py:594
  164.8 1.5 collective-permute-start.5
  167.7 32.0 %attend_back.1.grad_ref = bf16[3,2048,192]{2,1,0:T(8,128)(2,1)} custom-call(bf16[3,2048,192]{2,1,0:T(8,128)(2,1)} %project.1.q_ref.k_ref.v_ref.qkv_ref, bf16[8,192,256]{2,1,0:T(8,128)(2,1)} %copy-done.8, f32[192,2048]{1,0:T(8,128)} %get-tuple-element.94.ot_ref, f32[8,2048]{1,0:T(8,128)} %get-tuple-element.95.level_ref), custom_call_target="tpu_custom_call" | custom-call | flops 8053063680 | bytes 10000000 | tf_op jit(solution)/shard_map/attend_back/pallas_call | solution.py:339
  199.7 2.7 fusion
  202.5 1.5 collective-permute-start.7
  204.5 14.0 %project_back.1 = (bf16[4,256,768]{2,1,0:T(8,128)(2,1)}, bf16[4,256,768]{2,1,0:T(8,128)(2,1)}, bf16[768,640]{1,0:T(8,128)(2,1)}) custom-call(s32[2]{0:T(128)} %pad_add_fusion.me_ref, bf16[4,256,768]{2,1,0:T(8,128)(2,1)} %copy-done.2, bf16[4,256,768]{2,1,0:T(8,128)(2,1)} %collective-permute-done.3.far_ref, bf16[3,2048,192]{2,1,0:T(8,128)(2,1)} %attend_back.1.grad_ref, ...), custom_call_target="tpu_custom_call" | custom-call | flops 3623878656 | bytes 15000000 | tf_op jit(solution)/shard_map/project_back/pallas_call | solution.py:765
  221.7 3.8 %all-to-all-start.3 = ((bf16[8,96,640]{2,1,0:T(8,128)(2,1)}), bf16[8,96,640]{2,1,0:T(8,128)(2,1)S(1)}, u32[]{:S(2)}, u32[]{:S(2)}) async-start(bf16[8,96,640]{2,1,0:T(8,128)(2,1)} %bitcast.62), calls=%async_computation.3 | async-start | bytes 1966080 | tf_op jit(solution)/shard_map/all_to_all | solution.py:984
  225.5 3.6 %wide_sum.1 = (bf16[2,96,1792]{2,1,0:T(8,128)(2,1)}, bf16[2,96,1792]{2,1,0:T(8,128)(2,1)}) custom-call(s32[1]{0:T(128)} %bitcast.21.place_ref, bf16[2,4,96,896]{3,2,1,0:T(8,128)(2,1)} %get-tuple-element.90.refs_0_, bf16[2,4,96,896]{3,2,1,0:T(8,128)(2,1)} %collective-permute-done.5.refs_1_, bf16[4,96,896]{2,1,0:T(8,128)(2,1)} %copy-done.9, ...), custom_call_target="tpu_custom_call" | custom-call | bytes 4000000 | tf_op jit(solution)/shard_map/wide_sum/pallas_call | solution.py:627
  229.2 1.7 collective-permute-start.10
  230.9 4.3 %pair_sum.1 = (f32[256,768]{1,0:T(8,128)}, bf16[256,768]{1,0:T(8,128)(2,1)}, bf16[256,768]{1,0:T(8,128)(2,1)}, bf16[256,768]{1,0:T(8,128)(2,1)}) custom-call(bf16[4,256,768]{2,1,0:T(8,128)(2,1)} %get-tuple-element.113.keep_ref, bf16[4,256,768]{2,1,0:T(8,128)(2,1)} %copy-done.6), custom_call_target="tpu_custom_call" | custom-call | bytes 7000000 | tf_op jit(solution)/shard_map/pair_sum/pallas_call | solution.py:820
  235.7 1.5 collective-permute-start.13
  238.6 20.5 %collective-permute-done.10.refs_1_ = bf16[2,96,1792]{2,1,0:T(8,128)(2,1)} collective-permute-done((bf16[2,96,1792]{2,1,0:T(8,128)(2,1)}, bf16[2,96,1792]{2,1,0:T(8,128)(2,1)}, u32[]{:S(2)}, u32[]{:S(2)}) %collective-permute-start.10) | collective-permute-done | bytes 688160 | tf_op jit(solution)/shard_map/ppermute | solution.py:915
  260.2 2.4 collective-permute-start.16
  262.7 2.1 finish_narrow.1
  266.4 4.5 %finish_rows.1 = f32[2,256,768]{2,1,0:T(8,128)} custom-call(s32[1]{0:T(128)} %bitcast.3.side_ref, bf16[2,256,768]{2,1,0:T(8,128)(2,1)} %bitcast.59, f32[256,768]{1,0:T(8,128)} %get-tuple-element.120.near_ref, bf16[256,768]{1,0:T(8,128)(2,1)} %copy-done.13, bf16[256,768]{1,0:T(8,128)(2,1)} %copy-done.14, bf16[256,768]{1,0:T(8,128)(2,1)} %copy-done.15, ...), custom_call_target="tpu_custom_call" | custom-call | bytes 6000000 | tf_op jit(solution)/shard_map/finish_rows/pallas_call | solution.py:851
  272.6 2.4 finish_wide.1
  (78 shorter events, 22.2 us)
Async XLA Ops:
  7.2 105.1 %all-gather.2.cloned.1.call-start = ((), (), s32[]{:S(2)}) async-start(), calls=%async_computation.4 | async-start | bytes 11354112 | tf_op jit(solution)/shard_map/all_gather | solution.py:926
  11.0 14.7 %collective-permute-start.1 = (bf16[256,768]{1,0:T(8,128)(2,1)S(1)}, bf16[256,768]{1,0:T(8,128)(2,1)S(1)}, u32[]{:S(2)}, u32[]{:S(2)}) collective-permute-start(bf16[256,768]{1,0:T(8,128)(2,1)S(1)} %get-tuple-element.156), channel_id=1, source_target_pairs={{0,4},{1,5},{2,6},{3,7},{4,0},{5,1},{6,2},{7,3},{8,12},{9,13},{10,... | collective-permute-start | bytes 1179656 | tf_op jit(solution)/shard_map/ppermute | solution.py:918
  14.0 28.0 %collective-permute-start.2 = (bf16[256,768]{1,0:T(8,128)(2,1)S(1)}, bf16[256,768]{1,0:T(8,128)(2,1)S(1)}, u32[]{:S(2)}, u32[]{:S(2)}) collective-permute-start(bf16[256,768]{1,0:T(8,128)(2,1)S(1)} %get-tuple-element.156), channel_id=1, source_target_pairs={{0,6},{1,7},{2,4},{3,5},{4,2},{5,3},{6,0},{7,1},{8,14},{9,15},{10,... | collective-permute-start | bytes 1179656 | tf_op jit(solution)/shard_map/ppermute | solution.py:918
  15.5 26.6 %collective-permute-start = (bf16[256,768]{1,0:T(8,128)(2,1)S(1)}, bf16[256,768]{1,0:T(8,128)(2,1)S(1)}, u32[]{:S(2)}, u32[]{:S(2)}) collective-permute-start(bf16[256,768]{1,0:T(8,128)(2,1)S(1)} %get-tuple-element.155), channel_id=1, source_target_pairs={{0,2},{1,3},{2,0},{3,1},{4,6},{5,7},{6,4},{7,5},{8,10},{9,11},{10,... | collective-permute-start | bytes 1179656 | tf_op jit(solution)/shard_map/ppermute | solution.py:918
  15.6 41.0 %all-to-all-start = ((bf16[8,96,640]{2,1,0:T(8,128)(2,1)}), bf16[8,96,640]{2,1,0:T(8,128)(2,1)S(1)}, u32[]{:S(2)}, u32[]{:S(2)}) async-start(bf16[8,96,640]{2,1,0:T(8,128)(2,1)} %get-tuple-element.78), calls=%async_computation | async-start | bytes 1966080 | tf_op jit(solution)/shard_map/all_to_all | solution.py:938
  44.3 5.2 %copy-start.2 = (bf16[4,256,768]{2,1,0:T(8,128)(2,1)}, bf16[4,256,768]{2,1,0:T(8,128)(2,1)S(1)}, u32[]{:S(2)}) copy-start(bf16[4,256,768]{2,1,0:T(8,128)(2,1)S(1)} %pad_maximum_fusion.own_ref) | copy-start | bytes 4718596
  44.3 5.2 %collective-permute-start.3 = (bf16[4,256,768]{2,1,0:T(8,128)(2,1)S(1)}, bf16[4,256,768]{2,1,0:T(8,128)(2,1)}, u32[]{:S(2)}, u32[]{:S(2)}) collective-permute-start(bf16[4,256,768]{2,1,0:T(8,128)(2,1)S(1)} %pad_maximum_fusion.own_ref), channel_id=1, source_target_pairs={{0,1},{1,0},{2,3},{3,2},{4,5},{5,4},{6,7},{7,6},{8,9},{9,8},{10,11... | collective-permute-start | bytes 4718600 | tf_op jit(solution)/shard_map/ppermute | solution.py:918
  56.5 0.9 copy-start
  97.1 15.1 %all-to-all-start.1 = ((bf16[8,192,256]{2,1,0:T(8,128)(2,1)}), bf16[8,192,256]{2,1,0:T(8,128)(2,1)S(1)}, u32[]{:S(2)}, u32[]{:S(2)}) async-start(bf16[8,192,256]{2,1,0:T(8,128)(2,1)} %get-tuple-element.80), calls=%async_computation.1 | async-start | bytes 1572864 | tf_op jit(solution)/shard_map/all_to_all | solution.py:950
  144.1 9.4 %collective-permute-start.4 = (bf16[2,768,1792]{2,1,0:T(8,128)(2,1)}, bf16[2,768,1792]{2,1,0:T(8,128)(2,1)}, u32[]{:S(2)}, u32[]{:S(2)}) collective-permute-start(bf16[2,768,1792]{2,1,0:T(8,128)(2,1)} %weights_send.1), channel_id=1, source_target_pairs={{0,1},{1,0},{2,3},{3,2},{4,5},{5,4},{6,7},{7,6},{8,9},{9,8},{10,11... | collective-permute-start | bytes 16515080 | tf_op jit(solution)/shard_map/ppermute | solution.py:918
  144.7 22.1 %all-to-all-start.2 = ((bf16[8,192,256]{2,1,0:T(8,128)(2,1)}), bf16[8,192,256]{2,1,0:T(8,128)(2,1)S(1)}, u32[]{:S(2)}, u32[]{:S(2)}) async-start(bf16[8,192,256]{2,1,0:T(8,128)(2,1)} %get-tuple-element.93), calls=%async_computation.2 | async-start | bytes 1572864 | tf_op jit(solution)/shard_map/all_to_all | solution.py:957
  164.8 34.9 %collective-permute-start.5 = (bf16[2,4,96,896]{3,2,1,0:T(8,128)(2,1)}, bf16[2,4,96,896]{3,2,1,0:T(8,128)(2,1)}, u32[]{:S(2)}, u32[]{:S(2)}) collective-permute-start(bf16[2,4,96,896]{3,2,1,0:T(8,128)(2,1)} %get-tuple-element.91), channel_id=1, source_target_pairs={{0,2},{1,3},{2,0},{3,1},{4,6},{5,7},{6,4},{7,5},{8,10},{9,11},{10,... | collective-permute-start | bytes 4128776 | tf_op jit(solution)/shard_map/ppermute | solution.py:918
  166.3 33.4 %collective-permute-start.6 = (bf16[2,4,96,896]{3,2,1,0:T(8,128)(2,1)}, bf16[2,4,96,896]{3,2,1,0:T(8,128)(2,1)}, u32[]{:S(2)}, u32[]{:S(2)}) collective-permute-start(bf16[2,4,96,896]{3,2,1,0:T(8,128)(2,1)} %get-tuple-element.92), channel_id=1, source_target_pairs={{0,4},{1,5},{2,6},{3,7},{4,0},{5,1},{6,2},{7,3},{8,12},{9,13},{10,... | collective-permute-start | bytes 4128776 | tf_op jit(solution)/shard_map/ppermute | solution.py:918
  167.7 32.0 %copy-start.4 = (bf16[2,4,96,896]{3,2,1,0:T(8,128)(2,1)S(1)}, bf16[2,4,96,896]{3,2,1,0:T(8,128)(2,1)}, u32[]{:S(2)}) copy-start(bf16[2,4,96,896]{3,2,1,0:T(8,128)(2,1)} %get-tuple-element.90.refs_0_) | copy-start | bytes 4128772
  167.7 32.0 %copy-start.5 = (bf16[2,4,96,896]{3,2,1,0:T(8,128)(2,1)S(1)}, bf16[2,4,96,896]{3,2,1,0:T(8,128)(2,1)}, u32[]{:S(2)}) copy-start(bf16[2,4,96,896]{3,2,1,0:T(8,128)(2,1)} %get-tuple-element.97.refs_3_) | copy-start | bytes 4128772
  202.5 17.1 %collective-permute-start.7 = (bf16[4,96,896]{2,1,0:T(8,128)(2,1)}, bf16[4,96,896]{2,1,0:T(8,128)(2,1)S(1)}, u32[]{:S(2)}, u32[]{:S(2)}) collective-permute-start(bf16[4,96,896]{2,1,0:T(8,128)(2,1)} %get-tuple-element.100), channel_id=1, source_target_pairs={{0,4},{1,5},{2,6},{3,7},{4,0},{5,1},{6,2},{7,3},{8,12},{9,13},{10,... | collective-permute-start | bytes 2064392 | tf_op jit(solution)/shard_map/ppermute | solution.py:918
  204.0 16.8 %collective-permute-start.8 = (bf16[4,96,896]{2,1,0:T(8,128)(2,1)}, bf16[4,96,896]{2,1,0:T(8,128)(2,1)S(1)}, u32[]{:S(2)}, u32[]{:S(2)}) collective-permute-start(bf16[4,96,896]{2,1,0:T(8,128)(2,1)} %get-tuple-element.101), channel_id=1, source_target_pairs={{0,2},{1,3},{2,0},{3,1},{4,6},{5,7},{6,4},{7,5},{8,10},{9,11},{10,... | collective-permute-start | bytes 2064392 | tf_op jit(solution)/shard_map/ppermute | solution.py:918
  219.6 5.9 %copy-start.9 = (bf16[4,96,896]{2,1,0:T(8,128)(2,1)}, bf16[4,96,896]{2,1,0:T(8,128)(2,1)S(1)}, u32[]{:S(2)}) copy-start(bf16[4,96,896]{2,1,0:T(8,128)(2,1)S(1)} %collective-permute-done.7.refs_2_) | copy-start | bytes 2064388
  221.7 7.5 %collective-permute-start.9 = (bf16[4,256,768]{2,1,0:T(8,128)(2,1)}, bf16[4,256,768]{2,1,0:T(8,128)(2,1)S(1)}, u32[]{:S(2)}, u32[]{:S(2)}) collective-permute-start(bf16[4,256,768]{2,1,0:T(8,128)(2,1)} %get-tuple-element.111), channel_id=1, source_target_pairs={{0,1},{1,0},{2,3},{3,2},{4,5},{5,4},{6,7},{7,6},{8,9},{9,8},{10,11... | collective-permute-start | bytes 4718600 | tf_op jit(solution)/shard_map/ppermute | solution.py:918
  221.7 38.5 %all-to-all-start.3 = ((bf16[8,96,640]{2,1,0:T(8,128)(2,1)}), bf16[8,96,640]{2,1,0:T(8,128)(2,1)S(1)}, u32[]{:S(2)}, u32[]{:S(2)}) async-start(bf16[8,96,640]{2,1,0:T(8,128)(2,1)} %bitcast.62), calls=%async_computation.3 | async-start | bytes 1966080 | tf_op jit(solution)/shard_map/all_to_all | solution.py:984
  229.1 1.7 copy-start.6
  229.1 30.0 %copy-start.7 = (bf16[2,96,1792]{2,1,0:T(8,128)(2,1)S(1)}, bf16[2,96,1792]{2,1,0:T(8,128)(2,1)}, u32[]{:S(2)}) copy-start(bf16[2,96,1792]{2,1,0:T(8,128)(2,1)} %get-tuple-element.109.refs_0_) | copy-start | bytes 2064388
  229.2 30.0 %collective-permute-start.10 = (bf16[2,96,1792]{2,1,0:T(8,128)(2,1)}, bf16[2,96,1792]{2,1,0:T(8,128)(2,1)}, u32[]{:S(2)}, u32[]{:S(2)}) collective-permute-start(bf16[2,96,1792]{2,1,0:T(8,128)(2,1)} %get-tuple-element.112), channel_id=1, source_target_pairs={{0,8},{8,0},{16,24},{24,16},{1,9},{9,1},{17,25},{25,17},{2,10},{10... | collective-permute-start | bytes 2064392 | tf_op jit(solution)/shard_map/ppermute | solution.py:915
  235.1 30.2 %collective-permute-start.12 = (bf16[256,768]{1,0:T(8,128)(2,1)}, bf16[256,768]{1,0:T(8,128)(2,1)S(1)}, u32[]{:S(2)}, u32[]{:S(2)}) collective-permute-start(bf16[256,768]{1,0:T(8,128)(2,1)} %get-tuple-element.121), channel_id=1, source_target_pairs={{0,2},{1,3},{2,0},{3,1},{4,6},{5,7},{6,4},{7,5},{8,10},{9,11},{10,... | collective-permute-start | bytes 1179656 | tf_op jit(solution)/shard_map/ppermute | solution.py:918
  235.7 29.6 %collective-permute-start.13 = (bf16[256,768]{1,0:T(8,128)(2,1)}, bf16[256,768]{1,0:T(8,128)(2,1)S(1)}, u32[]{:S(2)}, u32[]{:S(2)}) collective-permute-start(bf16[256,768]{1,0:T(8,128)(2,1)} %get-tuple-element.122), channel_id=1, source_target_pairs={{0,4},{1,5},{2,6},{3,7},{4,0},{5,1},{6,2},{7,3},{8,12},{9,13},{10,... | collective-permute-start | bytes 1179656 | tf_op jit(solution)/shard_map/ppermute | solution.py:918
  237.2 28.2 %collective-permute-start.14 = (bf16[256,768]{1,0:T(8,128)(2,1)}, bf16[256,768]{1,0:T(8,128)(2,1)S(1)}, u32[]{:S(2)}, u32[]{:S(2)}) collective-permute-start(bf16[256,768]{1,0:T(8,128)(2,1)} %get-tuple-element.123), channel_id=1, source_target_pairs={{0,6},{1,7},{2,4},{3,5},{4,2},{5,3},{6,0},{7,1},{8,14},{9,15},{10,... | collective-permute-start | bytes 1179656 | tf_op jit(solution)/shard_map/ppermute | solution.py:918
  260.2 2.5 copy-start.3
  260.2 11.6 %collective-permute-start.16 = (bf16[1,96,1792]{2,1,0:T(8,128)(2,1)S(1)}, bf16[1,96,1792]{2,1,0:T(8,128)(2,1)S(1)}, u32[]{:S(2)}, u32[]{:S(2)}) collective-permute-start(bf16[1,96,1792]{2,1,0:T(8,128)(2,1)S(1)} %add_convert_fusion.2), channel_id=1, source_target_pairs={{0,24},{8,16},{16,8},{24,0},{1,25},{9,17},{17,9},{25,1},{2,26},{10... | collective-permute-start | bytes 1032200 | tf_op jit(solution)/shard_map/ppermute | solution.py:915
  264.8 6.1 %collective-permute-start.11 = (f32[8,96]{1,0:T(8,128)}, f32[8,96]{1,0:T(8,128)S(1)}, u32[]{:S(2)}, u32[]{:S(2)}) collective-permute-start(f32[8,96]{1,0:T(8,128)} %get-tuple-element.119), channel_id=1, source_target_pairs={{0,2},{1,3},{2,0},{3,1},{4,6},{5,7},{6,4},{7,5},{8,10},{9,11},{10,... | collective-permute-start | bytes 9224 | tf_op jit(solution)/shard_map/ppermute | solution.py:918
  265.4 1.0 copy-start.15
  266.4 4.5 %copy-start.17 = (f32[8,96]{1,0:T(8,128)S(1)}, f32[8,96]{1,0:T(8,128)}, u32[]{:S(2)}) copy-start(f32[8,96]{1,0:T(8,128)} %get-tuple-element.119) | copy-start | bytes 9220
  270.9 4.1 %collective-permute-start.15 = (f32[8,96]{1,0:T(8,128)S(1)}, f32[8,96]{1,0:T(8,128)S(1)}, u32[]{:S(2)}, u32[]{:S(2)}) collective-permute-start(f32[8,96]{1,0:T(8,128)S(1)} %add.136), channel_id=1, source_target_pairs={{0,1},{1,0},{2,3},{3,2},{4,5},{5,4},{6,7},{7,6},{8,9},{9,8},{10,11... | collective-permute-start | bytes 9224 | tf_op jit(solution)/shard_map/ppermute | solution.py:918
  (8 other events, 6.7 us)
Sparse Core Ops, SparseCore 0:
  11.0 99.1 all-gather.1
